TPU v7x, 128 devices: a whole 4x4x4 slice. The times are simulated.
128 devices in a mesh: row: 16 (over x, y), col: 8 (over z, core).
Axes of the slice: x: 4, y: 4, z: 4, core: 2. Of those that a mesh axis runs over, the one named last changes fastest.
Arguments:
- counts: int32 [8192, 8192], P('row', 'col'), may hold values from 1 to 5
- sample_weights: float32 [8192, 8192], P('row', 'col'), may hold values from 0.045 to 54
- classes: int32 [8192, 8192], P('row', 'col'), may hold values from 0 to 3
- class_radius: int32 [4], replicated, may hold values from 8 to 64, as said below
Outputs:
- density_first: float32 [8192, 8192], P('row', 'col')
- density_second: float32 [8192, 8192], P('row', 'col')
Inputs may be any that keep to these rules, and one draw needn't show every extreme that they name: `class_radius`: the radii rise strictly from class 0 to class 3, and class 3's radius is 64.
All inputs are finite; a program needn't handle non-finite values.
Results may differ from a plain program's by a relative error of at most 0.0001.
Values sent between devices are 32-bit elements; how exact they have to be, the bound alone decides.
No kernel may reach another device: no remote copies, remote signals or barrier semaphores. Data moves between devices by JAX's collectives and lax.ppermute only.
A program may use at most 128 MiB of HBM per device.

v0:
```python
import functools

import jax
import jax.numpy as jnp
from jax import lax
from jax.experimental import pallas as pl
from jax.experimental.pallas import tpu as pltpu
from jax.sharding import PartitionSpec as P

REACH = 64
PILOT_RADIUS = 32
CLASSES = 4
BACKGROUND = 0.5
TILE = 256
BAND = TILE + 2 * REACH
F32 = jnp.float32
BF16 = jnp.bfloat16
MIB = 1 << 20


def call(kernel, outs, args, smem=(), limit=24):
    vmem = pl.BlockSpec(memory_space=pltpu.VMEM)
    scalar = pl.BlockSpec(memory_space=pltpu.SMEM)
    return pl.pallas_call(
        kernel,
        out_shape=[jax.ShapeDtypeStruct(s, d) for s, d in outs],
        in_specs=[scalar if i in smem else vmem for i in range(len(args))],
        out_specs=[vmem] * len(outs),
        compiler_params=pltpu.CompilerParams(vmem_limit_bytes=limit * MIB),
    )(*args)


def split(value):
    high = value.astype(BF16)
    return high, (value - high.astype(F32)).astype(BF16)


def dot(a, b):
    return jnp.dot(a, b, preferred_element_type=F32)


def bands_kernel(radius_ref, high_ref, low_ref, stack_ref, rim_ref):
    def iota(shape, dim):
        return lax.broadcasted_iota(jnp.int32, shape, dim)

    lane = iota((8, 128), 1).astype(F32)
    tap = jnp.where(iota((8, 128), 0) == 0, jnp.where(lane == 0, 1.0, 2.0), 0.0)
    shift = (iota((BAND, TILE), 0) - REACH - iota((BAND, TILE), 1)).astype(F32)
    row, column = iota((128, 128), 0), iota((128, 128), 1)
    upper = row < 64
    same = upper == (column < 64)
    rim_shift = (row - column + jnp.where(upper, REACH, -REACH)).astype(F32)
    for c in range(CLASSES + 1):
        radius = F32(PILOT_RADIUS) if c == CLASSES else radius_ref[c].astype(F32)
        radius = jnp.full((1, 1), radius, F32)
        inverse = 1.0 / (2.0 * (0.5 * radius) * (0.5 * radius))

        def shape_of(d):
            return jnp.where(jnp.abs(d) <= radius, jnp.exp(-(d * d) * inverse), 0.0)

        total = jnp.sum(shape_of(lane) * tap, axis=(0, 1), keepdims=True)
        high, low = split(shape_of(shift) / total)
        high_ref[c * BAND : (c + 1) * BAND, :] = high
        low_ref[c * BAND : (c + 1) * BAND, :] = low
        stack_ref[c, :, 0:TILE] = high
        stack_ref[c, :, TILE : 2 * TILE] = low
        stack_ref[c, :, 2 * TILE :] = high
        high, low = split(jnp.where(same, shape_of(rim_shift) / total, 0.0))
        rim_ref[c, :, 0:128] = high
        rim_ref[c, :, 128:256] = high
        rim_ref[c, :, 256:384] = low


def masked(pieces, labels, c):
    if labels is None:
        return pieces
    keep = labels == c
    return [jnp.where(keep, piece, jnp.zeros_like(piece)) for piece in pieces]


def rows_kernel(*refs, bands, labelled):
    field_ref, refs = refs[0], refs[1:]
    label_ref, refs = (refs[0], refs[1:]) if labelled else (None, refs)
    stack_ref, high_ref, low_ref, edge_ref = refs
    rows, columns = field_ref.shape
    for n in range(columns // TILE):
        at = slice(n * TILE, (n + 1) * TILE)
        pieces = split(field_ref[:, at])
        labels = label_ref[:, at] if labelled else None
        for slot, c in enumerate(bands):
            high, low = masked(pieces, labels, c)

            def part(t, start):
                own = slice(t * TILE, (t + 1) * TILE)
                right = jnp.concatenate([high[own], high[own], low[own]], axis=0)
                return dot(stack_ref[c, start : start + TILE + REACH, :], right)

            first, second = part(0, REACH), part(1, 0)
            edge_ref[slot, 0:REACH, at] = first[0:REACH]
            edge_ref[slot, REACH:, at] = second[TILE:]
            cut = TILE - REACH
            for target, value in (
                (0, first[REACH:cut]),
                (cut - REACH, first[cut:] + second[: 2 * REACH]),
                (cut + REACH, second[2 * REACH : TILE]),
            ):
                value_high, value_low = split(value)
                high_ref[slot, target : target + value.shape[0], at] = value_high
                low_ref[slot, target : target + value.shape[0], at] = value_low


def swept(parts, bands, high_ref, low_ref, inputs, taps, outputs):
    stacked = [
        jnp.concatenate([ref[c * BAND + taps.start : c * BAND + taps.stop, outputs] for c in bands])
        for ref in (high_ref, low_ref)
    ]
    results = []
    for high_part, low_part in parts:
        high, low = (
            jnp.concatenate([ref[slot, :, inputs] for slot in range(len(bands))], axis=1)
            for ref in (high_part, low_part)
        )
        results.append(dot(high, stacked[0]) + dot(high, stacked[1]) + dot(low, stacked[0]))
    return results


def place(target_ref, at, inner, edge):
    rows = target_ref.shape[0]
    target_ref[0:REACH, at] = edge[0:REACH]
    target_ref[REACH : rows - REACH, at] = inner
    target_ref[rows - REACH :, at] = edge[REACH:]


def edges_kernel(*refs, bands, labelled):
    partial_ref, top_ref, bottom_ref, refs = refs[0], refs[1], refs[2], refs[3:]
    if labelled:
        top_label_ref, bottom_label_ref, refs = refs[0], refs[1], refs[2:]
    inner_high, inner_low, rim_ref, band_high, band_low, refs = *refs[:5], refs[5:]
    edge_high, edge_low, left_ref, right_ref, send_left, send_right = refs
    columns = top_ref.shape[1]
    for n in range(columns // TILE):
        at = slice(n * TILE, (n + 1) * TILE)
        pieces = split(jnp.concatenate([top_ref[:, at], bottom_ref[:, at]]))
        labels = None
        if labelled:
            labels = jnp.concatenate([top_label_ref[:, at], bottom_label_ref[:, at]])
            labels = labels.astype(F32).astype(BF16)
        for slot, c in enumerate(bands):
            high, low = masked(pieces, labels, c)
            right = jnp.concatenate([high, low, high], axis=0)
            value = partial_ref[slot, :, at] + dot(rim_ref[c], right)
            edge_high[slot, :, at], edge_low[slot, :, at] = split(value)
    parts = ((inner_high, inner_low), (edge_high, edge_low))
    sides = (
        (left_ref, slice(0, TILE), slice(128, BAND), slice(0, TILE)),
        (right_ref, slice(columns - 128, columns), slice(0, 128), slice(0, 128)),
    )
    for target, inputs, taps, outputs in sides:
        inner, edge = swept(parts, bands, band_high, band_low, inputs, taps, outputs)
        place(target, slice(None), inner, edge)
    half = left_ref.shape[0] // 2
    lower = lax.broadcasted_iota(jnp.int32, (half, 128), 1) < REACH
    left = left_ref[:, 0:128]
    send_left[...] = jnp.where(lower, left[:half], pltpu.roll(left[half:], REACH, 1))
    right = right_ref[...]
    send_right[...] = jnp.where(lower, pltpu.roll(right[:half], REACH, 1), right[half:])


def middle_kernel(inner_high, inner_low, edge_high, edge_low, band_high, band_low, out_ref, *, bands):
    parts = ((inner_high, inner_low), (edge_high, edge_low))
    for j in range(out_ref.shape[1] // TILE):
        inputs = slice(j * TILE + 128, j * TILE + 128 + BAND)
        inner, edge = swept(
            parts, bands, band_high, band_low, inputs, slice(0, BAND), slice(0, TILE)
        )
        place(out_ref, slice(j * TILE, (j + 1) * TILE), inner, edge)


def gathered(left_ref, middle_ref, right_ref, from_left, from_right, at):
    half = left_ref.shape[0] // 2
    lane = lax.broadcasted_iota(jnp.int32, (at.stop - at.start, 128), 1)
    local = slice(at.start % half, at.start % half + at.stop - at.start)
    come_left, come_right = from_left[local], from_right[local]
    if at.start < half:
        come_left = pltpu.roll(come_left, REACH, 1)
    else:
        come_right = pltpu.roll(come_right, REACH, 1)
    first = left_ref[at, 0:128] + jnp.where(lane >= REACH, come_left, 0.0)
    last = right_ref[at, :] + jnp.where(lane < REACH, come_right, 0.0)
    blocks = [first, left_ref[at, 128:256]]
    blocks += [middle_ref[at, k : k + 128] for k in range(0, middle_ref.shape[1], 128)]
    blocks += [last]
    turned = [pltpu.roll(block, REACH, 1) for block in blocks]
    return [jnp.where(lane < REACH, a, b) for a, b in zip(turned[:-1], turned[1:])]


def finish_kernel(*refs, scaled, density, following, totals):
    left_ref, middle_ref, right_ref, from_left, from_right, refs = *refs[:5], refs[5:]
    if scaled:
        log_ref, mass_total_ref, refs = refs[0], refs[1], refs[2:]
        inverse = jnp.exp(-(log_ref[0:1, :] / mass_total_ref[1:2, :]))
    if following:
        mass_ref, refs = refs[0], refs[1:]
    if density:
        density_ref, refs = refs[0], refs[1:]
    if following:
        adapted_ref, top_ref, bottom_ref, stat_ref = refs
    rows = left_ref.shape[0]
    step = 64
    log_sum = jnp.zeros((8, 128), F32)
    mass_sum = jnp.zeros((8, 128), F32)
    for start in range(0, rows, step):
        at = slice(start, start + step)
        blocks = gathered(left_ref, middle_ref, right_ref, from_left, from_right, at)
        for k, block in enumerate(blocks):
            lanes = slice(k * 128, (k + 1) * 128)
            if scaled:
                block = block * inverse
            if density:
                density_ref[at, lanes] = block
            if following:
                pilot = block + BACKGROUND
                mass = mass_ref[at, lanes]
                value = mass * pilot
                adapted_ref[at, lanes] = value
                if start == 0:
                    top_ref[:, lanes] = value
                if start == rows - step:
                    bottom_ref[:, lanes] = value
                terms = mass * jnp.log(pilot)
                log_sum += jnp.sum(terms.reshape(step // 8, 8, 128), axis=0)
                if totals:
                    mass_sum += jnp.sum(mass.reshape(step // 8, 8, 128), axis=0)
    if following:
        log_sum = jnp.sum(log_sum, axis=(0, 1), keepdims=True)
        mass_sum = jnp.sum(mass_sum, axis=(0, 1), keepdims=True)
        row = lax.broadcasted_iota(jnp.int32, (8, 128), 0)
        stat_ref[...] = jnp.where(row == 0, log_sum, jnp.where(row == 1, mass_sum, 0.0))


def shift_pair(up, down, axis):
    count = lax.axis_size(axis)
    forward = [(i, i + 1) for i in range(count - 1)]
    backward = [(i + 1, i) for i in range(count - 1)]
    return lax.ppermute(down, axis, forward), lax.ppermute(up, axis, backward)


def total_over(stat):
    for axis in ("row", "col"):
        distance = 1
        while distance < lax.axis_size(axis):
            pairs = [(i, i ^ distance) for i in range(lax.axis_size(axis))]
            stat = stat + lax.ppermute(stat, axis, pairs)
            distance *= 2
    return stat


def smooth(field, halo, labels, label_halo, tables, bands):
    high, low, stack, rim = tables
    rows, columns = field.shape
    count = len(bands)
    labelled = labels is not None
    inner = (count, rows - 2 * REACH, columns)
    edge = (count, 2 * REACH, columns)
    args = [field] + ([labels] if labelled else []) + [stack]
    inner_high, inner_low, partial = call(
        functools.partial(rows_kernel, bands=bands, labelled=labelled),
        [(inner, BF16), (inner, BF16), (edge, F32)],
        args,
    )
    args = [partial, *halo, *(label_halo if labelled else ()), inner_high, inner_low]
    args += [rim, high, low]
    edge_high, edge_low, left, right, send_left, send_right = call(
        functools.partial(edges_kernel, bands=bands, labelled=labelled),
        [(edge, BF16), (edge, BF16), ((rows, TILE), F32), ((rows, 128), F32)]
        + [((rows // 2, 128), F32)] * 2,
        args,
    )
    from_left, from_right = shift_pair(send_left, send_right, "col")
    (middle,) = call(
        functools.partial(middle_kernel, bands=bands),
        [((rows, columns - TILE), F32)],
        [inner_high, inner_low, edge_high, edge_low, high, low],
    )
    return left, middle, right, from_left, from_right


def body(counts, sample_weights, classes, class_radius):
    rows, columns = counts.shape
    top = counts[:REACH].astype(F32) * sample_weights[:REACH]
    bottom = counts[rows - REACH :].astype(F32) * sample_weights[rows - REACH :]
    mass_halo = shift_pair(top, bottom, "row")
    label_halo = shift_pair(classes[:REACH], classes[rows - REACH :], "row")
    mass = counts.astype(F32) * sample_weights
    labels = classes.astype(F32).astype(BF16)
    wide = (CLASSES + 1) * BAND
    tables = call(
        bands_kernel,
        [
            ((wide, TILE), BF16),
            ((wide, TILE), BF16),
            ((CLASSES + 1, BAND, 3 * TILE), BF16),
            ((CLASSES + 1, 128, 384), BF16),
        ],
        [class_radius],
        smem=(0,),
    )
    plane = ((rows, columns), F32)
    rim = ((REACH, columns), F32)
    stat = ((8, 128), F32)
    every = tuple(range(CLASSES))

    pieces = smooth(mass, mass_halo, None, None, tables, (CLASSES,))
    adapted, top, bottom, first_stat = call(
        functools.partial(finish_kernel, scaled=False, density=False, following=True, totals=True),
        [plane, rim, rim, stat],
        [*pieces, mass],
    )
    halo = shift_pair(top, bottom, "row")
    first_total = total_over(first_stat)
    pieces = smooth(adapted, halo, labels, label_halo, tables, every)
    density_first, adapted, top, bottom, second_stat = call(
        functools.partial(finish_kernel, scaled=True, density=True, following=True, totals=False),
        [plane, plane, rim, rim, stat],
        [*pieces, first_total, first_total, mass],
    )
    halo = shift_pair(top, bottom, "row")
    second_total = total_over(second_stat)
    pieces = smooth(adapted, halo, labels, label_halo, tables, every)
    (density_second,) = call(
        functools.partial(finish_kernel, scaled=True, density=True, following=False, totals=False),
        [plane],
        [*pieces, second_total, first_total],
    )
    return density_first, density_second


def solution(mesh):
    spec = P("row", "col")
    return jax.shard_map(
        body,
        mesh=mesh,
        in_specs=(spec, spec, spec, P()),
        out_specs=(spec, spec),
        check_vma=False,
    )
```

profile of v0, /device:TPU:26, one launch (start us, length us, event | category | flops | bytes accessed | tf_op | source)
XLA Modules:
  0.0 143.0 jit_solution(10084186983861262991)
XLA Ops:
  4.6 5.3 %collective-permute-start = (f32[64,1024]{1,0:T(8,128)S(1)}, f32[64,1024]{1,0:T(8,128)S(1)}, u32[]{:S(2)}, u32[]{:S(2)}) collective-permute-start(f32[64,1024]{1,0:T(8,128)S(1)} %get-tuple-element.83), channel_id=1, source_target_pairs={{0,8},{8,16},{16,24},{24,32},{32,40},{40,48},{48,56},{56,64},{64,7... | collective-permute-start | bytes 786440 | tf_op jit(solution)/shard_map/ppermute | solution.py:245
  12.5 2.8 %convert_multiply_fusion.refs_0_.refs_5_.refs_7_ = f32[512,1024]{1,0:T(8,128)S(1)} fusion(f32[512,1024]{1,0:T(8,128)} %param.5, s32[512,1024]{1,0:T(8,128)} %param.4), kind=kLoop, calls=%fused_computation.1 | loop fusion | flops 1048576 | bytes 6291456 | tf_op jit(solution)/shard_map/mul | solution.py:294
  21.8 6.0 %collective-permute-start.6 = (s32[64,1024]{1,0:T(8,128)S(1)}, s32[64,1024]{1,0:T(8,128)S(1)}, u32[]{:S(2)}, u32[]{:S(2)}) collective-permute-start(s32[64,1024]{1,0:T(8,128)S(1)} %get-tuple-element.85), channel_id=1, source_target_pairs={{0,8},{8,16},{16,24},{24,32},{32,40},{40,48},{48,56},{56,64},{64,7... | collective-permute-start | bytes 786440 | tf_op jit(solution)/shard_map/ppermute | solution.py:245
  30.4 3.0 %collective-permute-start.4 = (f32[64,1024]{1,0:T(8,128)S(1)}, f32[64,1024]{1,0:T(8,128)S(1)}, u32[]{:S(2)}, u32[]{:S(2)}) collective-permute-start(f32[64,1024]{1,0:T(8,128)S(1)} %get-tuple-element.57), channel_id=1, source_target_pairs={{0,8},{8,16},{16,24},{24,32},{32,40},{40,48},{48,56},{56,64},{64,7... | collective-permute-start | bytes 786440 | tf_op jit(solution)/shard_map/ppermute | solution.py:245
  33.4 3.0 %collective-permute-start.5 = (f32[64,1024]{1,0:T(8,128)S(1)}, f32[64,1024]{1,0:T(8,128)S(1)}, u32[]{:S(2)}, u32[]{:S(2)}) collective-permute-start(f32[64,1024]{1,0:T(8,128)S(1)} %get-tuple-element.58), channel_id=1, source_target_pairs={{8,0},{16,8},{24,16},{32,24},{40,32},{48,40},{56,48},{64,56},{72,6... | collective-permute-start | bytes 786440 | tf_op jit(solution)/shard_map/ppermute | solution.py:245
  36.7 4.5 %shard_map.64 = (bf16[4,384,1024]{2,1,0:T(8,128)(2,1)S(1)}, bf16[4,384,1024]{2,1,0:T(8,128)(2,1)S(1)}, f32[4,128,1024]{2,1,0:T(8,128)S(1)}) custom-call(f32[512,1024]{1,0:T(8,128)S(1)} %get-tuple-element.55.refs_0_, bf16[512,1024]{1,0:T(8,128)(2,1)S(1)} %convert_convert_fusion.refs_1_, bf16[5,384,768]{2,1,0:T(8,128)(2,1)S(1)} %get-tuple-element.42.refs_1_.refs_2_), custom_call_target="tpu_custom_call" | custom-call | tf_op jit(solution)/shard_map/pallas_call | solution.py:24
  41.2 3.9 %collective-permute-done.5.refs_2_ = f32[64,1024]{1,0:T(8,128)S(1)} collective-permute-done((f32[64,1024]{1,0:T(8,128)S(1)}, f32[64,1024]{1,0:T(8,128)S(1)}, u32[]{:S(2)}, u32[]{:S(2)}) %collective-permute-start.5) | collective-permute-done | bytes 262176 | tf_op jit(solution)/shard_map/ppermute | solution.py:245
  47.2 3.2 %collective-permute-start.8 = (f32[256,128]{1,0:T(8,128)S(1)}, f32[256,128]{1,0:T(8,128)S(1)}, u32[]{:S(2)}, u32[]{:S(2)}) collective-permute-start(f32[256,128]{1,0:T(8,128)S(1)} %get-tuple-element.65), channel_id=1, source_target_pairs={{0,1},{1,2},{2,3},{3,4},{4,5},{5,6},{6,7},{8,9},{9,10},{10,11},{11... | collective-permute-start | bytes 393224 | tf_op jit(solution)/shard_map/ppermute | solution.py:245
  51.9 3.6 %collective-permute-done.10 = f32[8,128]{1,0:T(8,128)S(1)} collective-permute-done((f32[8,128]{1,0:T(8,128)S(1)}, f32[8,128]{1,0:T(8,128)S(1)}, u32[]{:S(2)}, u32[]{:S(2)}) %collective-permute-start.10) | collective-permute-done | bytes 4128 | tf_op jit(solution)/shard_map/ppermute | solution.py:253
  55.5 5.1 %collective-permute-done.11 = f32[8,128]{1,0:T(8,128)S(1)} collective-permute-done((f32[8,128]{1,0:T(8,128)S(1)}, f32[8,128]{1,0:T(8,128)S(1)}, u32[]{:S(2)}, u32[]{:S(2)}) %collective-permute-start.11) | collective-permute-done | bytes 4128 | tf_op jit(solution)/shard_map/ppermute | solution.py:253
  61.1 3.1 %collective-permute-done.12 = f32[8,128]{1,0:T(8,128)S(1)} collective-permute-done((f32[8,128]{1,0:T(8,128)S(1)}, f32[8,128]{1,0:T(8,128)S(1)}, u32[]{:S(2)}, u32[]{:S(2)}) %collective-permute-start.12) | collective-permute-done | bytes 4128 | tf_op jit(solution)/shard_map/ppermute | solution.py:253
  65.1 4.2 %collective-permute-done.13 = f32[8,128]{1,0:T(8,128)S(1)} collective-permute-done((f32[8,128]{1,0:T(8,128)S(1)}, f32[8,128]{1,0:T(8,128)S(1)}, u32[]{:S(2)}, u32[]{:S(2)}) %collective-permute-start.13) | collective-permute-done | bytes 4128 | tf_op jit(solution)/shard_map/ppermute | solution.py:253
  70.5 5.9 %collective-permute-start.15 = (f32[8,128]{1,0:T(8,128)S(1)}, f32[8,128]{1,0:T(8,128)S(1)}, u32[]{:S(2)}, u32[]{:S(2)}) collective-permute-start(f32[8,128]{1,0:T(8,128)S(1)} %add.46), channel_id=1, source_target_pairs={{0,2},{1,3},{2,0},{3,1},{4,6},{5,7},{6,4},{7,5},{8,10},{9,11},{10,... | collective-permute-start | bytes 12296 | tf_op jit(solution)/shard_map/ppermute | solution.py:253
  78.0 3.7 %collective-permute-start.16 = (f32[8,128]{1,0:T(8,128)S(1)}, f32[8,128]{1,0:T(8,128)S(1)}, u32[]{:S(2)}, u32[]{:S(2)}) collective-permute-start(f32[8,128]{1,0:T(8,128)S(1)} %add.47), channel_id=1, source_target_pairs={{0,4},{1,5},{2,6},{3,7},{4,0},{5,1},{6,2},{7,3},{8,12},{9,13},{10,... | collective-permute-start | bytes 12296 | tf_op jit(solution)/shard_map/ppermute | solution.py:253
  83.3 3.8 %shard_map.66.refs_1_ = f32[512,768]{1,0:T(8,128)S(1)} custom-call(bf16[4,384,1024]{2,1,0:T(8,128)(2,1)S(1)} %get-tuple-element.59.refs_5_.inner_high, bf16[4,384,1024]{2,1,0:T(8,128)(2,1)S(1)} %get-tuple-element.60.refs_6_.inner_low, bf16[4,128,1024]{2,1,0:T(8,128)(2,1)S(1)} %get-tuple-element.62.edge_high, ...), custom_call_target="tpu_custom_call" | custom-call | tf_op jit(solution)/shard_map/pallas_call | solution.py:24
  91.3 4.1 %collective-permute-start.18 = (f32[64,1024]{1,0:T(8,128)S(1)}, f32[64,1024]{1,0:T(8,128)S(1)}, u32[]{:S(2)}, u32[]{:S(2)}) collective-permute-start(f32[64,1024]{1,0:T(8,128)S(1)} %get-tuple-element.72), channel_id=1, source_target_pairs={{8,0},{16,8},{24,16},{32,24},{40,32},{48,40},{56,48},{64,56},{72,6... | collective-permute-start | bytes 786440 | tf_op jit(solution)/shard_map/ppermute | solution.py:245
  95.4 4.6 %shard_map.68 = (bf16[4,384,1024]{2,1,0:T(8,128)(2,1)S(1)}, bf16[4,384,1024]{2,1,0:T(8,128)(2,1)S(1)}, f32[4,128,1024]{2,1,0:T(8,128)S(1)}) custom-call(f32[512,1024]{1,0:T(8,128)S(1)} %get-tuple-element.69.refs_0_, bf16[512,1024]{1,0:T(8,128)(2,1)S(1)} %convert_convert_fusion.refs_1_, bf16[5,384,768]{2,1,0:T(8,128)(2,1)S(1)} %get-tuple-element.42.refs_1_.refs_2_), custom_call_target="tpu_custom_call" | custom-call | tf_op jit(solution)/shard_map/pallas_call | solution.py:24
  106.6 3.6 %collective-permute-done.21 = f32[8,128]{1,0:T(8,128)S(1)} collective-permute-done((f32[8,128]{1,0:T(8,128)S(1)}, f32[8,128]{1,0:T(8,128)S(1)}, u32[]{:S(2)}, u32[]{:S(2)}) %collective-permute-start.21) | collective-permute-done | bytes 4128 | tf_op jit(solution)/shard_map/ppermute | solution.py:253
  110.2 5.1 %collective-permute-done.22 = f32[8,128]{1,0:T(8,128)S(1)} collective-permute-done((f32[8,128]{1,0:T(8,128)S(1)}, f32[8,128]{1,0:T(8,128)S(1)}, u32[]{:S(2)}, u32[]{:S(2)}) %collective-permute-start.22) | collective-permute-done | bytes 4128 | tf_op jit(solution)/shard_map/ppermute | solution.py:253
  115.8 3.1 %collective-permute-done.23 = f32[8,128]{1,0:T(8,128)S(1)} collective-permute-done((f32[8,128]{1,0:T(8,128)S(1)}, f32[8,128]{1,0:T(8,128)S(1)}, u32[]{:S(2)}, u32[]{:S(2)}) %collective-permute-start.23) | collective-permute-done | bytes 4128 | tf_op jit(solution)/shard_map/ppermute | solution.py:253
  119.8 4.2 %collective-permute-done.24 = f32[8,128]{1,0:T(8,128)S(1)} collective-permute-done((f32[8,128]{1,0:T(8,128)S(1)}, f32[8,128]{1,0:T(8,128)S(1)}, u32[]{:S(2)}, u32[]{:S(2)}) %collective-permute-start.24) | collective-permute-done | bytes 4128 | tf_op jit(solution)/shard_map/ppermute | solution.py:253
  125.2 4.8 %collective-permute-start.26 = (f32[8,128]{1,0:T(8,128)S(1)}, f32[8,128]{1,0:T(8,128)S(1)}, u32[]{:S(2)}, u32[]{:S(2)}) collective-permute-start(f32[8,128]{1,0:T(8,128)S(1)} %add.53), channel_id=1, source_target_pairs={{0,2},{1,3},{2,0},{3,1},{4,6},{5,7},{6,4},{7,5},{8,10},{9,11},{10,... | collective-permute-start | bytes 12296 | tf_op jit(solution)/shard_map/ppermute | solution.py:253
  131.6 3.7 %collective-permute-start.27 = (f32[8,128]{1,0:T(8,128)S(1)}, f32[8,128]{1,0:T(8,128)S(1)}, u32[]{:S(2)}, u32[]{:S(2)}) collective-permute-start(f32[8,128]{1,0:T(8,128)S(1)} %add.54), channel_id=1, source_target_pairs={{0,4},{1,5},{2,6},{3,7},{4,0},{5,1},{6,2},{7,3},{8,12},{9,13},{10,... | collective-permute-start | bytes 12296 | tf_op jit(solution)/shard_map/ppermute | solution.py:253
  136.9 3.8 %shard_map.70.refs_1_ = f32[512,768]{1,0:T(8,128)S(1)} custom-call(bf16[4,384,1024]{2,1,0:T(8,128)(2,1)S(1)} %get-tuple-element.73.refs_5_.inner_high, bf16[4,384,1024]{2,1,0:T(8,128)(2,1)S(1)} %get-tuple-element.74.refs_6_.inner_low, bf16[4,128,1024]{2,1,0:T(8,128)(2,1)S(1)} %get-tuple-element.76.edge_high, ...), custom_call_target="tpu_custom_call" | custom-call | tf_op jit(solution)/shard_map/pallas_call | solution.py:24
  (67 shorter events, 43.7 us)
Async XLA Ops:
  1.9 14.6 %collective-permute-start.1 = (f32[64,1024]{1,0:T(8,128)S(1)}, f32[64,1024]{1,0:T(8,128)S(1)}, u32[]{:S(2)}, u32[]{:S(2)}) collective-permute-start(f32[64,1024]{1,0:T(8,128)S(1)} %get-tuple-element.82), channel_id=1, source_target_pairs={{8,0},{16,8},{24,16},{32,24},{40,32},{48,40},{56,48},{64,56},{72,6... | collective-permute-start | bytes 786440 | tf_op jit(solution)/shard_map/ppermute | solution.py:245
  4.6 12.0 %collective-permute-start = (f32[64,1024]{1,0:T(8,128)S(1)}, f32[64,1024]{1,0:T(8,128)S(1)}, u32[]{:S(2)}, u32[]{:S(2)}) collective-permute-start(f32[64,1024]{1,0:T(8,128)S(1)} %get-tuple-element.83), channel_id=1, source_target_pairs={{0,8},{8,16},{16,24},{24,32},{32,40},{40,48},{48,56},{56,64},{64,7... | collective-permute-start | bytes 786440 | tf_op jit(solution)/shard_map/ppermute | solution.py:245
  17.2 12.0 %collective-permute-start.2 = (f32[256,128]{1,0:T(8,128)S(1)}, f32[256,128]{1,0:T(8,128)S(1)}, u32[]{:S(2)}, u32[]{:S(2)}) collective-permute-start(f32[256,128]{1,0:T(8,128)S(1)} %get-tuple-element.53), channel_id=1, source_target_pairs={{0,1},{1,2},{2,3},{3,4},{4,5},{5,6},{6,7},{8,9},{9,10},{10,11},{11... | collective-permute-start | bytes 393224 | tf_op jit(solution)/shard_map/ppermute | solution.py:245
  18.6 10.7 %collective-permute-start.3 = (f32[256,128]{1,0:T(8,128)S(1)}, f32[256,128]{1,0:T(8,128)S(1)}, u32[]{:S(2)}, u32[]{:S(2)}) collective-permute-start(f32[256,128]{1,0:T(8,128)S(1)} %get-tuple-element.54), channel_id=1, source_target_pairs={{1,0},{2,1},{3,2},{4,3},{5,4},{6,5},{7,6},{9,8},{10,9},{11,10},{12... | collective-permute-start | bytes 393224 | tf_op jit(solution)/shard_map/ppermute | solution.py:245
  19.9 21.3 %collective-permute-start.7 = (s32[64,1024]{1,0:T(8,128)S(1)}, s32[64,1024]{1,0:T(8,128)S(1)}, u32[]{:S(2)}, u32[]{:S(2)}) collective-permute-start(s32[64,1024]{1,0:T(8,128)S(1)} %get-tuple-element.84), channel_id=1, source_target_pairs={{8,0},{16,8},{24,16},{32,24},{40,32},{48,40},{56,48},{64,56},{72,6... | collective-permute-start | bytes 786440 | tf_op jit(solution)/shard_map/ppermute | solution.py:245
  21.8 19.4 %collective-permute-start.6 = (s32[64,1024]{1,0:T(8,128)S(1)}, s32[64,1024]{1,0:T(8,128)S(1)}, u32[]{:S(2)}, u32[]{:S(2)}) collective-permute-start(s32[64,1024]{1,0:T(8,128)S(1)} %get-tuple-element.85), channel_id=1, source_target_pairs={{0,8},{8,16},{16,24},{24,32},{32,40},{40,48},{48,56},{56,64},{64,7... | collective-permute-start | bytes 786440 | tf_op jit(solution)/shard_map/ppermute | solution.py:245
  30.4 10.9 %collective-permute-start.4 = (f32[64,1024]{1,0:T(8,128)S(1)}, f32[64,1024]{1,0:T(8,128)S(1)}, u32[]{:S(2)}, u32[]{:S(2)}) collective-permute-start(f32[64,1024]{1,0:T(8,128)S(1)} %get-tuple-element.57), channel_id=1, source_target_pairs={{0,8},{8,16},{16,24},{24,32},{32,40},{40,48},{48,56},{56,64},{64,7... | collective-permute-start | bytes 786440 | tf_op jit(solution)/shard_map/ppermute | solution.py:245
  33.4 11.7 %collective-permute-start.5 = (f32[64,1024]{1,0:T(8,128)S(1)}, f32[64,1024]{1,0:T(8,128)S(1)}, u32[]{:S(2)}, u32[]{:S(2)}) collective-permute-start(f32[64,1024]{1,0:T(8,128)S(1)} %get-tuple-element.58), channel_id=1, source_target_pairs={{8,0},{16,8},{24,16},{32,24},{40,32},{48,40},{56,48},{64,56},{72,6... | collective-permute-start | bytes 786440 | tf_op jit(solution)/shard_map/ppermute | solution.py:245
  47.2 39.8 %collective-permute-start.8 = (f32[256,128]{1,0:T(8,128)S(1)}, f32[256,128]{1,0:T(8,128)S(1)}, u32[]{:S(2)}, u32[]{:S(2)}) collective-permute-start(f32[256,128]{1,0:T(8,128)S(1)} %get-tuple-element.65), channel_id=1, source_target_pairs={{0,1},{1,2},{2,3},{3,4},{4,5},{5,6},{6,7},{8,9},{9,10},{10,11},{11... | collective-permute-start | bytes 393224 | tf_op jit(solution)/shard_map/ppermute | solution.py:245
  50.5 36.6 %collective-permute-start.9 = (f32[256,128]{1,0:T(8,128)S(1)}, f32[256,128]{1,0:T(8,128)S(1)}, u32[]{:S(2)}, u32[]{:S(2)}) collective-permute-start(f32[256,128]{1,0:T(8,128)S(1)} %get-tuple-element.66), channel_id=1, source_target_pairs={{1,0},{2,1},{3,2},{4,3},{5,4},{6,5},{7,6},{9,8},{10,9},{11,10},{12... | collective-permute-start | bytes 393224 | tf_op jit(solution)/shard_map/ppermute | solution.py:245
  51.8 3.7 %collective-permute-start.10 = (f32[8,128]{1,0:T(8,128)S(1)}, f32[8,128]{1,0:T(8,128)S(1)}, u32[]{:S(2)}, u32[]{:S(2)}) collective-permute-start(f32[8,128]{1,0:T(8,128)S(1)} %get-tuple-element.67), channel_id=1, source_target_pairs={{0,8},{8,0},{16,24},{24,16},{32,40},{40,32},{48,56},{56,48},{64,72... | collective-permute-start | bytes 12296 | tf_op jit(solution)/shard_map/ppermute | solution.py:253
  55.4 5.1 %collective-permute-start.11 = (f32[8,128]{1,0:T(8,128)S(1)}, f32[8,128]{1,0:T(8,128)S(1)}, u32[]{:S(2)}, u32[]{:S(2)}) collective-permute-start(f32[8,128]{1,0:T(8,128)S(1)} %add.42), channel_id=1, source_target_pairs={{0,16},{8,24},{16,0},{24,8},{32,48},{40,56},{48,32},{56,40},{64,80... | collective-permute-start | bytes 12296 | tf_op jit(solution)/shard_map/ppermute | solution.py:253
  64.2 5.1 %collective-permute-start.13 = (f32[8,128]{1,0:T(8,128)S(1)}, f32[8,128]{1,0:T(8,128)S(1)}, u32[]{:S(2)}, u32[]{:S(2)}) collective-permute-start(f32[8,128]{1,0:T(8,128)S(1)} %add.44), channel_id=1, source_target_pairs={{0,64},{8,72},{16,80},{24,88},{32,96},{40,104},{48,112},{56,120},{... | collective-permute-start | bytes 12296 | tf_op jit(solution)/shard_map/ppermute | solution.py:253
  70.5 7.5 %collective-permute-start.15 = (f32[8,128]{1,0:T(8,128)S(1)}, f32[8,128]{1,0:T(8,128)S(1)}, u32[]{:S(2)}, u32[]{:S(2)}) collective-permute-start(f32[8,128]{1,0:T(8,128)S(1)} %add.46), channel_id=1, source_target_pairs={{0,2},{1,3},{2,0},{3,1},{4,6},{5,7},{6,4},{7,5},{8,10},{9,11},{10,... | collective-permute-start | bytes 12296 | tf_op jit(solution)/shard_map/ppermute | solution.py:253
  78.0 5.3 %collective-permute-start.16 = (f32[8,128]{1,0:T(8,128)S(1)}, f32[8,128]{1,0:T(8,128)S(1)}, u32[]{:S(2)}, u32[]{:S(2)}) collective-permute-start(f32[8,128]{1,0:T(8,128)S(1)} %add.47), channel_id=1, source_target_pairs={{0,4},{1,5},{2,6},{3,7},{4,0},{5,1},{6,2},{7,3},{8,12},{9,13},{10,... | collective-permute-start | bytes 12296 | tf_op jit(solution)/shard_map/ppermute | solution.py:253
  89.4 10.7 %collective-permute-start.17 = (f32[64,1024]{1,0:T(8,128)S(1)}, f32[64,1024]{1,0:T(8,128)S(1)}, u32[]{:S(2)}, u32[]{:S(2)}) collective-permute-start(f32[64,1024]{1,0:T(8,128)S(1)} %get-tuple-element.71), channel_id=1, source_target_pairs={{0,8},{8,16},{16,24},{24,32},{32,40},{40,48},{48,56},{56,64},{64,7... | collective-permute-start | bytes 786440 | tf_op jit(solution)/shard_map/ppermute | solution.py:245
  91.3 10.4 %collective-permute-start.18 = (f32[64,1024]{1,0:T(8,128)S(1)}, f32[64,1024]{1,0:T(8,128)S(1)}, u32[]{:S(2)}, u32[]{:S(2)}) collective-permute-start(f32[64,1024]{1,0:T(8,128)S(1)} %get-tuple-element.72), channel_id=1, source_target_pairs={{8,0},{16,8},{24,16},{32,24},{40,32},{48,40},{56,48},{64,56},{72,6... | collective-permute-start | bytes 786440 | tf_op jit(solution)/shard_map/ppermute | solution.py:245
  103.9 36.8 %collective-permute-start.19 = (f32[256,128]{1,0:T(8,128)S(1)}, f32[256,128]{1,0:T(8,128)S(1)}, u32[]{:S(2)}, u32[]{:S(2)}) collective-permute-start(f32[256,128]{1,0:T(8,128)S(1)} %get-tuple-element.79), channel_id=1, source_target_pairs={{0,1},{1,2},{2,3},{3,4},{4,5},{5,6},{6,7},{8,9},{9,10},{10,11},{11... | collective-permute-start | bytes 393224 | tf_op jit(solution)/shard_map/ppermute | solution.py:245
  105.2 35.5 %collective-permute-start.20 = (f32[256,128]{1,0:T(8,128)S(1)}, f32[256,128]{1,0:T(8,128)S(1)}, u32[]{:S(2)}, u32[]{:S(2)}) collective-permute-start(f32[256,128]{1,0:T(8,128)S(1)} %get-tuple-element.80), channel_id=1, source_target_pairs={{1,0},{2,1},{3,2},{4,3},{5,4},{6,5},{7,6},{9,8},{10,9},{11,10},{12... | collective-permute-start | bytes 393224 | tf_op jit(solution)/shard_map/ppermute | solution.py:245
  106.5 3.7 %collective-permute-start.21 = (f32[8,128]{1,0:T(8,128)S(1)}, f32[8,128]{1,0:T(8,128)S(1)}, u32[]{:S(2)}, u32[]{:S(2)}) collective-permute-start(f32[8,128]{1,0:T(8,128)S(1)} %get-tuple-element.81), channel_id=1, source_target_pairs={{0,8},{8,0},{16,24},{24,16},{32,40},{40,32},{48,56},{56,48},{64,72... | collective-permute-start | bytes 12296 | tf_op jit(solution)/shard_map/ppermute | solution.py:253
  110.2 5.1 %collective-permute-start.22 = (f32[8,128]{1,0:T(8,128)S(1)}, f32[8,128]{1,0:T(8,128)S(1)}, u32[]{:S(2)}, u32[]{:S(2)}) collective-permute-start(f32[8,128]{1,0:T(8,128)S(1)} %add.49), channel_id=1, source_target_pairs={{0,16},{8,24},{16,0},{24,8},{32,48},{40,56},{48,32},{56,40},{64,80... | collective-permute-start | bytes 12296 | tf_op jit(solution)/shard_map/ppermute | solution.py:253
  118.9 5.1 %collective-permute-start.24 = (f32[8,128]{1,0:T(8,128)S(1)}, f32[8,128]{1,0:T(8,128)S(1)}, u32[]{:S(2)}, u32[]{:S(2)}) collective-permute-start(f32[8,128]{1,0:T(8,128)S(1)} %add.51), channel_id=1, source_target_pairs={{0,64},{8,72},{16,80},{24,88},{32,96},{40,104},{48,112},{56,120},{... | collective-permute-start | bytes 12296 | tf_op jit(solution)/shard_map/ppermute | solution.py:253
  125.2 6.4 %collective-permute-start.26 = (f32[8,128]{1,0:T(8,128)S(1)}, f32[8,128]{1,0:T(8,128)S(1)}, u32[]{:S(2)}, u32[]{:S(2)}) collective-permute-start(f32[8,128]{1,0:T(8,128)S(1)} %add.53), channel_id=1, source_target_pairs={{0,2},{1,3},{2,0},{3,1},{4,6},{5,7},{6,4},{7,5},{8,10},{9,11},{10,... | collective-permute-start | bytes 12296 | tf_op jit(solution)/shard_map/ppermute | solution.py:253
  131.6 5.3 %collective-permute-start.27 = (f32[8,128]{1,0:T(8,128)S(1)}, f32[8,128]{1,0:T(8,128)S(1)}, u32[]{:S(2)}, u32[]{:S(2)}) collective-permute-start(f32[8,128]{1,0:T(8,128)S(1)} %add.54), channel_id=1, source_target_pairs={{0,4},{1,5},{2,6},{3,7},{4,0},{5,1},{6,2},{7,3},{8,12},{9,13},{10,... | collective-permute-start | bytes 12296 | tf_op jit(solution)/shard_map/ppermute | solution.py:253
  (6 other events, 13.6 us)
where the time goes:
time: 143 us
  starting transfers between devices  58.8 us (41%)
  waiting for transfers between devices  46.2 us (32%)
  Pallas kernels  31.9 us (22%)
  other arithmetic  4.39 us (3%)
    ppermute x14, waiting for transfers between devices, total_over(): stat = stat + lax.ppermute(stat, axis, pairs)  40.7 us
    ppermute x14, starting transfers between devices, shift_pair(): return (lax.ppermute(down, axis, forward), lax.ppermute(up, axis, backward))  37.7 us
    pallas_call x13, Pallas kernels, call(): pl.pallas_call(kernel, out_shape=[jax.ShapeDtypeStruct(s, d) for s, d in...  31.9 us
    ppermute x14, starting transfers between devices, total_over(): stat = stat + lax.ppermute(stat, axis, pairs)  21.1 us
    ppermute x14, waiting for transfers between devices, shift_pair(): return (lax.ppermute(down, axis, forward), lax.ppermute(up, axis, backward))  5.54 us
  transfers between devices with their start and end apart: 28, of which 16 were waited for; matrix products, arithmetic and copies ran while one was open for 2% of the time, Pallas kernels for 16%

commit v1 on v0

v1 whole, which is shorter than its diff:
```python
import functools

import jax
import jax.numpy as jnp
from jax import lax
from jax.experimental import pallas as pl
from jax.experimental.pallas import tpu as pltpu
from jax.sharding import PartitionSpec as P


REACH = 64
PILOT_RADIUS = 32
CLASSES = 4
BACKGROUND = 0.5
TILE = 256
BAND = TILE + 2 * REACH
F32 = jnp.float32
BF16 = jnp.bfloat16
MIB = 1 << 20


def call(kernel, outs, args, smem=(), limit=24, flops=100_000_000):
    vmem = pl.BlockSpec(memory_space=pltpu.VMEM)
    scalar = pl.BlockSpec(memory_space=pltpu.SMEM)
    return pl.pallas_call(
        kernel,
        out_shape=[jax.ShapeDtypeStruct(s, d) for s, d in outs],
        in_specs=[scalar if i in smem else vmem for i in range(len(args))],
        out_specs=[vmem] * len(outs),
        compiler_params=pltpu.CompilerParams(vmem_limit_bytes=limit * MIB),
        cost_estimate=pl.CostEstimate(flops=flops, transcendentals=0, bytes_accessed=4 * MIB),
    )(*args)


def split(value):
    high = value.astype(BF16)
    return high, (value - high.astype(F32)).astype(BF16)


def dot(a, b):
    return jnp.dot(a, b, preferred_element_type=F32)


def bands_kernel(radius_ref, high_ref, low_ref, stack_ref, rim_ref):
    def iota(shape, dim):
        return lax.broadcasted_iota(jnp.int32, shape, dim)

    lane = iota((8, 128), 1).astype(F32)
    tap = jnp.where(iota((8, 128), 0) == 0, jnp.where(lane == 0, 1.0, 2.0), 0.0)
    shift = (iota((BAND, TILE), 0) - REACH - iota((BAND, TILE), 1)).astype(F32)
    row, column = iota((128, 128), 0), iota((128, 128), 1)
    upper = row < 64
    same = upper == (column < 64)
    rim_shift = (row - column + jnp.where(upper, REACH, -REACH)).astype(F32)
    for c in range(CLASSES + 1):
        radius = F32(PILOT_RADIUS) if c == CLASSES else radius_ref[c].astype(F32)
        radius = jnp.full((1, 1), radius, F32)
        inverse = 1.0 / (2.0 * (0.5 * radius) * (0.5 * radius))

        def shape_of(d):
            return jnp.where(jnp.abs(d) <= radius, jnp.exp(-(d * d) * inverse), 0.0)

        total = jnp.sum(shape_of(lane) * tap, axis=(0, 1), keepdims=True)
        high, low = split(shape_of(shift) / total)
        high_ref[c * BAND : (c + 1) * BAND, :] = high
        low_ref[c * BAND : (c + 1) * BAND, :] = low
        stack_ref[c, :, 0:TILE] = high
        stack_ref[c, :, TILE : 2 * TILE] = low
        stack_ref[c, :, 2 * TILE :] = high
        high, low = split(jnp.where(same, shape_of(rim_shift) / total, 0.0))
        rim_ref[c, :, 0:128] = high
        rim_ref[c, :, 128:256] = high
        rim_ref[c, :, 256:384] = low


def masked(pieces, labels, c):
    if labels is None:
        return pieces
    keep = labels == c
    return [jnp.where(keep, piece, jnp.zeros_like(piece)) for piece in pieces]


def rows_kernel(*refs, bands, labelled):
    field_ref, refs = refs[0], refs[1:]
    label_ref, refs = (refs[0], refs[1:]) if labelled else (None, refs)
    stack_ref, high_ref, low_ref, edge_ref = refs
    _, columns = field_ref.shape
    for n in range(columns // TILE):
        at = slice(n * TILE, (n + 1) * TILE)
        pieces = split(field_ref[:, at])
        labels = label_ref[:, at] if labelled else None
        for slot, c in enumerate(bands):
            high, low = masked(pieces, labels, c)

            def part(t, start):
                own = slice(t * TILE, (t + 1) * TILE)
                right = jnp.concatenate([high[own], high[own], low[own]], axis=0)
                return dot(stack_ref[c, start : start + TILE + REACH, :], right)

            first, second = part(0, REACH), part(1, 0)
            edge_ref[slot, 0:REACH, at] = first[0:REACH]
            edge_ref[slot, REACH:, at] = second[TILE:]
            cut = TILE - REACH
            for target, value in (
                (0, first[REACH:cut]),
                (cut - REACH, first[cut:] + second[: 2 * REACH]),
                (cut + REACH, second[2 * REACH : TILE]),
            ):
                value_high, value_low = split(value)
                high_ref[slot, target : target + value.shape[0], at] = value_high
                low_ref[slot, target : target + value.shape[0], at] = value_low


def swept(parts, bands, high_ref, low_ref, inputs, taps, outputs):
    stacked = [
        jnp.concatenate([ref[c * BAND + taps.start : c * BAND + taps.stop, outputs] for c in bands])
        for ref in (high_ref, low_ref)
    ]
    results = []
    for part in parts:
        high, low = (
            jnp.concatenate([ref[slot, :, inputs] for ref, slot in side], axis=1) for side in part
        )
        results.append(dot(high, stacked[0]) + dot(high, stacked[1]) + dot(low, stacked[0]))
    return results


def place(target_ref, at, inner, edge):
    rows = target_ref.shape[0]
    target_ref[0:REACH, at] = edge[0:REACH]
    target_ref[REACH : rows - REACH, at] = inner
    target_ref[rows - REACH :, at] = edge[REACH:]


def take(refs, *counts):
    groups = []
    for count in counts:
        groups.append(list(refs[:count]))
        refs = refs[count:]
    return *groups, list(refs)


def slots_of(refs, groups):
    return [(ref, slot) for ref, group in zip(refs, groups) for slot in range(len(group))]


def chosen(odd_ref, when_odd, when_even):
    return jnp.where(odd_ref[0:1, 0:1] > 0.5, when_odd, when_even)


def edges_kernel(*refs, groups, labelled):
    count = len(groups)
    refs, (odd_row, odd_column), halo, labels_in, partials, highs, lows, tables, outs = (
        None,
        *take(refs, 2, 2, 2 * labelled, count, count, count, 3),
    )
    rim_ref, band_high, band_low = tables
    edge_high, edge_low, left_ref, right_ref, send_a, send_b = outs
    bands = [c for group in groups for c in group]
    partial_slots = slots_of(partials, groups)
    columns = halo[0].shape[1]
    for n in range(columns // TILE):
        at = slice(n * TILE, (n + 1) * TILE)

        def joined(pair):
            first, second = pair[0][:, at].astype(F32), pair[1][:, at].astype(F32)
            top = chosen(odd_row, first, second)
            bottom = chosen(odd_row, second, first)
            missing = REACH - first.shape[0]
            if missing:
                zeros = jnp.zeros((missing, TILE), F32)
                return jnp.concatenate([zeros, top, bottom, zeros])
            return jnp.concatenate([top, bottom])

        pieces = split(joined(halo))
        labels = joined(labels_in).astype(BF16) if labelled else None
        for slot, c in enumerate(bands):
            high, low = masked(pieces, labels, c)
            right = jnp.concatenate([high, low, high], axis=0)
            source, at_slot = partial_slots[slot]
            value = source[at_slot, :, at] + dot(rim_ref[c], right)
            edge_high[slot, :, at], edge_low[slot, :, at] = split(value)
    parts = parts_of(highs, lows, edge_high, edge_low, groups)
    sides = (
        (left_ref, slice(0, TILE), slice(128, BAND), slice(0, TILE)),
        (right_ref, slice(columns - 128, columns), slice(0, 128), slice(0, 128)),
    )
    for target, inputs, taps, outputs in sides:
        inner, edge = swept(parts, bands, band_high, band_low, inputs, taps, outputs)
        place(target, slice(None), inner, edge)
    half = left_ref.shape[0] // 2
    lower = lax.broadcasted_iota(jnp.int32, (half, 128), 1) < REACH
    left = left_ref[:, 0:128]
    left = jnp.where(lower, left[:half], pltpu.roll(left[half:], REACH, 1))
    right = right_ref[...]
    right = jnp.where(lower, pltpu.roll(right[:half], REACH, 1), right[half:])
    send_a[...] = chosen(odd_column, left, right)
    send_b[...] = chosen(odd_column, right, left)


def parts_of(highs, lows, edge_high, edge_low, groups):
    whole = [[c for group in groups for c in group]]
    return (
        (slots_of(highs, groups), slots_of(lows, groups)),
        (slots_of([edge_high], whole), slots_of([edge_low], whole)),
    )


def middle_kernel(*refs, groups, blocks):
    count = len(groups)
    highs, lows, (edge_high, edge_low, band_high, band_low), (out_ref,) = take(refs, count, count, 4)
    bands = [c for group in groups for c in group]
    parts = parts_of(highs, lows, edge_high, edge_low, groups)
    for slot, j in enumerate(blocks):
        inputs = slice(j * TILE + 128, j * TILE + 128 + BAND)
        inner, edge = swept(
            parts, bands, band_high, band_low, inputs, slice(0, BAND), slice(0, TILE)
        )
        place(out_ref, slice(slot * TILE, (slot + 1) * TILE), inner, edge)


def gathered(pieces, come, odd, at):
    left_ref, middles, right_ref = pieces
    half = left_ref.shape[0] // 2
    lane = lax.broadcasted_iota(jnp.int32, (at.stop - at.start, 128), 1)
    local = slice(at.start % half, at.start % half + at.stop - at.start)
    come_left = chosen(odd, come[0][local], come[1][local])
    come_right = chosen(odd, come[1][local], come[0][local])
    if at.start < half:
        come_left = pltpu.roll(come_left, REACH, 1)
    else:
        come_right = pltpu.roll(come_right, REACH, 1)
    first = left_ref[at, 0:128] + jnp.where(lane >= REACH, come_left, 0.0)
    last = right_ref[at, :] + jnp.where(lane < REACH, come_right, 0.0)
    blocks = [first, left_ref[at, 128:256]]
    for middle_ref in middles:
        blocks += [middle_ref[at, k : k + 128] for k in range(0, middle_ref.shape[1], 128)]
    blocks += [last]
    turned = [pltpu.roll(block, REACH, 1) for block in blocks]
    return [jnp.where(lane < REACH, a, b) for a, b in zip(turned[:-1], turned[1:])]


def finish_kernel(*refs, middles, scaled, density, following, totals):
    (odd_row, odd_column), (left_ref,), middle_refs, (right_ref,), come, refs = take(
        refs, 2, 1, middles, 1, 2
    )
    pieces = (left_ref, middle_refs, right_ref)
    if scaled:
        (log_ref, mass_total_ref), refs = take(refs, 2)
        inverse = jnp.exp(-(log_ref[0:1, :] / mass_total_ref[1:2, :]))
    if following:
        (mass_ref,), refs = take(refs, 1)
    if density:
        (density_ref,), refs = take(refs, 1)
    if following:
        adapted_ref, send_a, send_b, stat_ref = refs
    rows = left_ref.shape[0]
    step = 64
    log_sum = jnp.zeros((8, 128), F32)
    mass_sum = jnp.zeros((8, 128), F32)
    for start in range(0, rows, step):
        at = slice(start, start + step)
        for k, block in enumerate(gathered(pieces, come, odd_column, at)):
            lanes = slice(k * 128, (k + 1) * 128)
            if scaled:
                block = block * inverse
            if density:
                density_ref[at, lanes] = block
            if following:
                pilot = block + BACKGROUND
                mass = mass_ref[at, lanes]
                adapted_ref[at, lanes] = mass * pilot
                terms = mass * jnp.log(pilot)
                log_sum += jnp.sum(terms.reshape(step // 8, 8, 128), axis=0)
                if totals:
                    mass_sum += jnp.sum(mass.reshape(step // 8, 8, 128), axis=0)
    if following:
        top, bottom = adapted_ref[0:REACH], adapted_ref[rows - REACH :]
        send_a[...] = chosen(odd_row, top, bottom)
        send_b[...] = chosen(odd_row, bottom, top)
        log_sum = jnp.sum(log_sum, axis=(0, 1), keepdims=True)
        mass_sum = jnp.sum(mass_sum, axis=(0, 1), keepdims=True)
        row = lax.broadcasted_iota(jnp.int32, (8, 128), 0)
        stat_ref[...] = jnp.where(row == 0, log_sum, jnp.where(row == 1, mass_sum, 0.0))


def exchange(first, second, axis):
    results = []
    for offset, value in ((0, first), (1, second)):
        pairs = []
        for i in range(offset, lax.axis_size(axis) - 1, 2):
            pairs += [(i, i + 1), (i + 1, i)]
        results.append(lax.ppermute(value, axis, pairs))
    return results


HOPS = {1: (), 2: (1,), 4: (1, 3), 8: (1, 2, 6), 16: (4, 12, 1, 3)}


def total_over(stat):
    for axis in ("col", "row"):
        for hop in HOPS[lax.axis_size(axis)]:
            pairs = [(i, i ^ hop) for i in range(lax.axis_size(axis))]
            stat = stat + lax.ppermute(stat, axis, pairs)
    return stat


def smooth(field, halo, labels, label_halo, tables, odd, groups, blocks):
    high, low, stack, rim = tables
    rows, columns = field.shape
    labelled = labels is not None
    bands = [c for group in groups for c in group]
    highs, lows, partials = [], [], []
    for group in groups:
        inner = (len(group), rows - 2 * REACH, columns)
        edge = (len(group), 2 * REACH, columns)
        results = call(
            functools.partial(rows_kernel, bands=group, labelled=labelled),
            [(inner, BF16), (inner, BF16), (edge, F32)],
            [field] + ([labels] if labelled else []) + [stack],
            flops=len(group) * 1_000_000_000,
        )
        for results_of, result in zip((highs, lows, partials), results):
            results_of.append(result)
    edge = (len(bands), 2 * REACH, columns)
    edge_high, edge_low, left, right, send_a, send_b = call(
        functools.partial(edges_kernel, groups=groups, labelled=labelled),
        [(edge, BF16), (edge, BF16), ((rows, TILE), F32), ((rows, 128), F32)]
        + [((rows // 2, 128), F32)] * 2,
        [*odd, *halo, *(label_halo if labelled else ()), *partials, *highs, *lows]
        + [rim, high, low],
        flops=len(bands) * 500_000_000,
    )
    come = exchange(send_a, send_b, "col")
    middles = []
    for part in blocks:
        middles += call(
            functools.partial(middle_kernel, groups=groups, blocks=part),
            [((rows, len(part) * TILE), F32)],
            [*highs, *lows, edge_high, edge_low, high, low],
            flops=len(bands) * len(part) * 250_000_000,
        )
    return [*odd, left, *middles, right, *come]


def finish(pieces, extra, outs, **flags):
    return call(
        functools.partial(finish_kernel, middles=len(pieces) - 6, **flags),
        outs,
        [*pieces, *extra],
        flops=500_000_000,
    )


def body(counts, sample_weights, classes, class_radius):
    rows, columns = counts.shape
    is_odd = [(lax.axis_index(axis) & 1).astype(F32) for axis in ("row", "col")]
    odd = [jnp.full((8, 128), value, F32) for value in is_odd]
    plane = ((rows, columns), F32)
    rim = ((REACH, columns), F32)
    stat = ((8, 128), F32)
    groups = ((0,), (1, 2), (3,))
    blocks = tuple((j,) for j in range(columns // TILE - 1))

    def ends(array, width):
        top, bottom = array[:width], array[rows - width :]
        return [jnp.where(is_odd[0] > 0.5, *pair) for pair in ((top, bottom), (bottom, top))]

    sends = [
        number.astype(F32) * weight
        for number, weight in zip(ends(counts, PILOT_RADIUS), ends(sample_weights, PILOT_RADIUS))
    ]
    mass_halo = exchange(*sends, "row")
    label_halo = exchange(*ends(classes, REACH), "row")
    mass = counts.astype(F32) * sample_weights
    labels = classes.astype(F32).astype(BF16)
    wide = (CLASSES + 1) * BAND
    tables = call(
        bands_kernel,
        [
            ((wide, TILE), BF16),
            ((wide, TILE), BF16),
            ((CLASSES + 1, BAND, 3 * TILE), BF16),
            ((CLASSES + 1, 128, 384), BF16),
        ],
        [class_radius],
        smem=(0,),
        flops=500_000_000,
    )
    pieces = smooth(
        mass, mass_halo, None, None, tables, odd, ((CLASSES,),), (sum(blocks, ()),)
    )
    adapted, *sends, first_stat = finish(
        pieces,
        [mass],
        [plane, rim, rim, stat],
        scaled=False,
        density=False,
        following=True,
        totals=True,
    )
    halo = exchange(*sends, "row")
    first_total = total_over(first_stat)
    pieces = smooth(adapted, halo, labels, label_halo, tables, odd, groups, blocks)
    density_first, adapted, *sends, second_stat = finish(
        pieces,
        [first_total, first_total, mass],
        [plane, plane, rim, rim, stat],
        scaled=True,
        density=True,
        following=True,
        totals=False,
    )
    halo = exchange(*sends, "row")
    second_total = total_over(second_stat)
    pieces = smooth(adapted, halo, labels, label_halo, tables, odd, groups, blocks)
    (density_second,) = finish(
        pieces,
        [second_total, first_total],
        [plane],
        scaled=True,
        density=True,
        following=False,
        totals=False,
    )
    return density_first, density_second


def solution(mesh):
    spec = P("row", "col")
    return jax.shard_map(
        body,
        mesh=mesh,
        in_specs=(spec, spec, spec, P()),
        out_specs=(spec, spec),
        check_vma=False,
    )
```

time: 143 us -> 107 us (0.75)
  the two profiles are of different devices: /device:TPU:26 before, /device:TPU:1 now
where the time goes in v1:
time: 107 us
  starting transfers between devices  51.9 us (49%)
  Pallas kernels  34.6 us (32%)
  waiting for transfers between devices  15.1 us (14%)
  other arithmetic  4.11 us (4%)
    pallas_call x21, Pallas kernels, call(): pl.pallas_call(kernel, out_shape=[jax.ShapeDtypeStruct(s, d) for s, d in...  34.6 us
    ppermute x14, starting transfers between devices, exchange(): results.append(lax.ppermute(value, axis, pairs))  31.3 us
    ppermute x14, starting transfers between devices, total_over(): stat = stat + lax.ppermute(stat, axis, pairs)  20.6 us
    ppermute x14, waiting for transfers between devices, total_over(): stat = stat + lax.ppermute(stat, axis, pairs)  13.6 us
    mul x1, other arithmetic, body(): mass = counts.astype(F32) * sample_weights  2.65 us
  transfers between devices with their start and end apart: 28, of which 13 were waited for; matrix products, arithmetic and copies ran while one was open for 3% of the time, Pallas kernels for 22%

profile of v1, /device:TPU:1, one launch (start us, length us, event | category | flops | bytes accessed | tf_op | source)
XLA Modules:
  0.0 106.7 jit_solution(2044818550257617037)
XLA Ops:
  2.5 4.7 %collective-permute-start = (f32[32,1024]{1,0:T(8,128)S(1)}, f32[32,1024]{1,0:T(8,128)S(1)}, u32[]{:S(2)}, u32[]{:S(2)}) collective-permute-start(f32[32,1024]{1,0:T(8,128)S(1)} %get-tuple-element.107), channel_id=1, source_target_pairs={{0,8},{8,0},{16,24},{24,16},{32,40},{40,32},{48,56},{56,48},{64,72... | collective-permute-start | bytes 393224 | tf_op jit(solution)/shard_map/ppermute | solution.py:293
  7.2 2.6 %convert_multiply_fusion.refs_0_.refs_7_.refs_11_ = f32[512,1024]{1,0:T(8,128)S(1)} fusion(f32[512,1024]{1,0:T(8,128)} %param.5, s32[512,1024]{1,0:T(8,128)} %param.4), kind=kLoop, calls=%fused_computation.1 | loop fusion | flops 1048576 | bytes 6291456 | tf_op jit(solution)/shard_map/mul | solution.py:375
  9.9 1.9 %shard_map.59 = (bf16[1920,256]{1,0:T(8,128)(2,1)S(1)}, bf16[1920,256]{1,0:T(8,128)(2,1)S(1)}, bf16[5,384,768]{2,1,0:T(8,128)(2,1)S(1)}, bf16[5,128,384]{2,1,0:T(8,128)(2,1)S(1)}) custom-call(s32[4]{0:T(128)S(1)} %copy-done), custom_call_target="tpu_custom_call" | custom-call | flops 500000000 | bytes 4194304 | tf_op jit(solution)/shard_map/pallas_call | solution.py:25
  15.2 3.5 %collective-permute-start.3 = (f32[256,128]{1,0:T(8,128)S(1)}, f32[256,128]{1,0:T(8,128)S(1)}, u32[]{:S(2)}, u32[]{:S(2)}) collective-permute-start(f32[256,128]{1,0:T(8,128)S(1)} %get-tuple-element.66), channel_id=1, source_target_pairs={{1,2},{2,1},{3,4},{4,3},{5,6},{6,5},{9,10},{10,9},{11,12},{12,11},... | collective-permute-start | bytes 393224 | tf_op jit(solution)/shard_map/ppermute | solution.py:293
  23.8 1.6 %collective-permute-start.11 = (f32[8,128]{1,0:T(8,128)S(1)}, f32[8,128]{1,0:T(8,128)S(1)}, u32[]{:S(2)}, u32[]{:S(2)}) collective-permute-start(f32[8,128]{1,0:T(8,128)S(1)} %add.42), channel_id=1, source_target_pairs={{0,2},{1,3},{2,0},{3,1},{4,6},{5,7},{6,4},{7,5},{8,10},{9,11},{10,... | collective-permute-start | bytes 12296 | tf_op jit(solution)/shard_map/ppermute | solution.py:304
  26.5 3.3 %collective-permute-start.12 = (f32[8,128]{1,0:T(8,128)S(1)}, f32[8,128]{1,0:T(8,128)S(1)}, u32[]{:S(2)}, u32[]{:S(2)}) collective-permute-start(f32[8,128]{1,0:T(8,128)S(1)} %add.43), channel_id=1, source_target_pairs={{0,6},{1,7},{2,4},{3,5},{4,2},{5,3},{6,0},{7,1},{8,14},{9,15},{10,... | collective-permute-start | bytes 12296 | tf_op jit(solution)/shard_map/ppermute | solution.py:304
  30.5 3.2 %collective-permute-start.6 = (s32[64,1024]{1,0:T(8,128)S(1)}, s32[64,1024]{1,0:T(8,128)S(1)}, u32[]{:S(2)}, u32[]{:S(2)}) collective-permute-start(s32[64,1024]{1,0:T(8,128)S(1)} %get-tuple-element.109), channel_id=1, source_target_pairs={{0,8},{8,0},{16,24},{24,16},{32,40},{40,32},{48,56},{56,48},{64,72... | collective-permute-start | bytes 786440 | tf_op jit(solution)/shard_map/ppermute | solution.py:293
  36.4 2.1 %collective-permute-done.13 = f32[8,128]{1,0:T(8,128)S(1)} collective-permute-done((f32[8,128]{1,0:T(8,128)S(1)}, f32[8,128]{1,0:T(8,128)S(1)}, u32[]{:S(2)}, u32[]{:S(2)}) %collective-permute-start.13) | collective-permute-done | bytes 4128 | tf_op jit(solution)/shard_map/ppermute | solution.py:304
  38.5 3.3 %collective-permute-start.14 = (f32[8,128]{1,0:T(8,128)S(1)}, f32[8,128]{1,0:T(8,128)S(1)}, u32[]{:S(2)}, u32[]{:S(2)}) collective-permute-start(f32[8,128]{1,0:T(8,128)S(1)} %add.45), channel_id=1, source_target_pairs={{0,96},{8,104},{16,112},{24,120},{32,64},{40,72},{48,80},{56,88},{... | collective-permute-start | bytes 12296 | tf_op jit(solution)/shard_map/ppermute | solution.py:304
  41.8 2.5 %shard_map.65 = (bf16[2,384,1024]{2,1,0:T(8,128)(2,1)S(1)}, bf16[2,384,1024]{2,1,0:T(8,128)(2,1)S(1)}, f32[2,128,1024]{2,1,0:T(8,128)S(1)}) custom-call(f32[512,1024]{1,0:T(8,128)S(1)} %get-tuple-element.69.refs_0_, bf16[512,1024]{1,0:T(8,128)(2,1)S(1)} %convert_convert_fusion.refs_1_, bf16[5,384,768]{2,1,0:T(8,128)(2,1)S(1)} %get-tuple-element.54.refs_1_.refs_2_), custom_call_target="tpu_custom_call" | custom-call | flops 2000000000 | bytes 4194304 | tf_op jit(solution)/shard_map/pallas_call | solution.py:25
  50.6 2.3 %shard_map.67 = (bf16[4,128,1024]{2,1,0:T(8,128)(2,1)S(1)}, bf16[4,128,1024]{2,1,0:T(8,128)(2,1)S(1)}, f32[512,256]{1,0:T(8,128)S(1)}, f32[512,128]{1,0:T(8,128)...) custom-call(f32[8,128]{1,0:T(8,128)S(1)} %broadcast_in_dim.6.refs_0_, f32[8,128]{1,0:T(8,128)S(1)} %broadcast_in_dim.7.refs_1_, ...), custom_call_target="tpu_custom_call" | custom-call | flops 2000000000 | bytes 4194304 | tf_op jit(solution)/shard_map/pallas_call | solution.py:25
  52.9 5.6 %collective-permute-start.8 = (f32[256,128]{1,0:T(8,128)S(1)}, f32[256,128]{1,0:T(8,128)S(1)}, u32[]{:S(2)}, u32[]{:S(2)}) collective-permute-start(f32[256,128]{1,0:T(8,128)S(1)} %get-tuple-element.83), channel_id=1, source_target_pairs={{0,1},{1,0},{2,3},{3,2},{4,5},{5,4},{6,7},{7,6},{8,9},{9,8},{10,11... | collective-permute-start | bytes 393224 | tf_op jit(solution)/shard_map/ppermute | solution.py:293
  58.4 1.9 %collective-permute-start.9 = (f32[256,128]{1,0:T(8,128)S(1)}, f32[256,128]{1,0:T(8,128)S(1)}, u32[]{:S(2)}, u32[]{:S(2)}) collective-permute-start(f32[256,128]{1,0:T(8,128)S(1)} %get-tuple-element.84), channel_id=1, source_target_pairs={{1,2},{2,1},{3,4},{4,3},{5,6},{6,5},{9,10},{10,9},{11,12},{12,11},... | collective-permute-start | bytes 393224 | tf_op jit(solution)/shard_map/ppermute | solution.py:293
  64.7 2.3 %shard_map.71 = (f32[512,1024]{1,0:T(8,128)}, f32[512,1024]{1,0:T(8,128)S(1)}, f32[64,1024]{1,0:T(8,128)S(1)}, f32[64,1024]{1,0:T(8,128)S(1)}, f32[8,128]{1,0:T(8,128)S(1)}) custom-call(f32[8,128]{1,0:T(8,128)S(1)} %broadcast_in_dim.6.refs_0_, f32[8,128]{1,0:T(8,128)S(1)} %broadcast_in_dim.7.refs_1_, f32[512,256]{1,0:T(8,128)S(1)} %get-tuple-element.79.refs_2_, ...), custom_call_target="tpu_custom_call" | custom-call | flops 500000000 | bytes 4194304 | tf_op jit(solution)/shard_map/pallas_call | solution.py:25
  68.2 1.5 %collective-permute-start.22 = (f32[8,128]{1,0:T(8,128)S(1)}, f32[8,128]{1,0:T(8,128)S(1)}, u32[]{:S(2)}, u32[]{:S(2)}) collective-permute-start(f32[8,128]{1,0:T(8,128)S(1)} %add.49), channel_id=1, source_target_pairs={{0,2},{1,3},{2,0},{3,1},{4,6},{5,7},{6,4},{7,5},{8,10},{9,11},{10,... | collective-permute-start | bytes 12296 | tf_op jit(solution)/shard_map/ppermute | solution.py:304
  71.0 3.4 %collective-permute-done.23 = f32[8,128]{1,0:T(8,128)S(1)} collective-permute-done((f32[8,128]{1,0:T(8,128)S(1)}, f32[8,128]{1,0:T(8,128)S(1)}, u32[]{:S(2)}, u32[]{:S(2)}) %collective-permute-start.23) | collective-permute-done | bytes 4128 | tf_op jit(solution)/shard_map/ppermute | solution.py:304
  74.4 2.0 %collective-permute-start.24 = (f32[8,128]{1,0:T(8,128)S(1)}, f32[8,128]{1,0:T(8,128)S(1)}, u32[]{:S(2)}, u32[]{:S(2)}) collective-permute-start(f32[8,128]{1,0:T(8,128)S(1)} %add.51), channel_id=1, source_target_pairs={{0,32},{8,40},{16,48},{24,56},{32,0},{40,8},{48,16},{56,24},{64,96... | collective-permute-start | bytes 12296 | tf_op jit(solution)/shard_map/ppermute | solution.py:304
  77.3 3.6 %collective-permute-start.25 = (f32[8,128]{1,0:T(8,128)S(1)}, f32[8,128]{1,0:T(8,128)S(1)}, u32[]{:S(2)}, u32[]{:S(2)}) collective-permute-start(f32[8,128]{1,0:T(8,128)S(1)} %add.52), channel_id=1, source_target_pairs={{0,96},{8,104},{16,112},{24,120},{32,64},{40,72},{48,80},{56,88},{... | collective-permute-start | bytes 12296 | tf_op jit(solution)/shard_map/ppermute | solution.py:304
  80.9 2.5 %shard_map.73 = (bf16[2,384,1024]{2,1,0:T(8,128)(2,1)S(1)}, bf16[2,384,1024]{2,1,0:T(8,128)(2,1)S(1)}, f32[2,128,1024]{2,1,0:T(8,128)S(1)}) custom-call(f32[512,1024]{1,0:T(8,128)S(1)} %get-tuple-element.89.refs_0_, bf16[512,1024]{1,0:T(8,128)(2,1)S(1)} %convert_convert_fusion.refs_1_, bf16[5,384,768]{2,1,0:T(8,128)(2,1)S(1)} %get-tuple-element.54.refs_1_.refs_2_), custom_call_target="tpu_custom_call" | custom-call | flops 2000000000 | bytes 4194304 | tf_op jit(solution)/shard_map/pallas_call | solution.py:25
  89.9 2.3 %shard_map.75 = (bf16[4,128,1024]{2,1,0:T(8,128)(2,1)S(1)}, bf16[4,128,1024]{2,1,0:T(8,128)(2,1)S(1)}, f32[512,256]{1,0:T(8,128)S(1)}, f32[512,128]{1,0:T(8,128)...) custom-call(f32[8,128]{1,0:T(8,128)S(1)} %broadcast_in_dim.6.refs_0_, f32[8,128]{1,0:T(8,128)S(1)} %broadcast_in_dim.7.refs_1_, ...), custom_call_target="tpu_custom_call" | custom-call | flops 2000000000 | bytes 4194304 | tf_op jit(solution)/shard_map/pallas_call | solution.py:25
  92.2 5.6 %collective-permute-start.19 = (f32[256,128]{1,0:T(8,128)S(1)}, f32[256,128]{1,0:T(8,128)S(1)}, u32[]{:S(2)}, u32[]{:S(2)}) collective-permute-start(f32[256,128]{1,0:T(8,128)S(1)} %get-tuple-element.103), channel_id=1, source_target_pairs={{0,1},{1,0},{2,3},{3,2},{4,5},{5,4},{6,7},{7,6},{8,9},{9,8},{10,11... | collective-permute-start | bytes 393224 | tf_op jit(solution)/shard_map/ppermute | solution.py:293
  97.8 2.2 %collective-permute-start.20 = (f32[256,128]{1,0:T(8,128)S(1)}, f32[256,128]{1,0:T(8,128)S(1)}, u32[]{:S(2)}, u32[]{:S(2)}) collective-permute-start(f32[256,128]{1,0:T(8,128)S(1)} %get-tuple-element.104), channel_id=1, source_target_pairs={{1,2},{2,1},{3,4},{4,3},{5,6},{6,5},{9,10},{10,9},{11,12},{12,11},... | collective-permute-start | bytes 393224 | tf_op jit(solution)/shard_map/ppermute | solution.py:293
  101.5 1.4 %shard_map.77.refs_4_ = f32[512,256]{1,0:T(8,128)S(1)} custom-call(bf16[1,384,1024]{2,1,0:T(8,128)(2,1)S(1)} %get-tuple-element.93.refs_9_.refs_0_, bf16[2,384,1024]{2,1,0:T(8,128)(2,1)S(1)} %get-tuple-element.94.refs_10_.refs_1_, bf16[1,384,1024]{2,1,0:T(8,128)(2,1)S(1)} %get-tuple-element.95.refs_11_.refs_2_, ...), custom_call_target="tpu_custom_call" | custom-call | flops 1000000000 | bytes 4194304 | tf_op jit(solution)/shard_map/pallas_call | solution.py:25
  104.4 2.3 %shard_map.79 = f32[512,1024]{1,0:T(8,128)} custom-call(f32[8,128]{1,0:T(8,128)S(1)} %broadcast_in_dim.6.refs_0_, f32[8,128]{1,0:T(8,128)S(1)} %broadcast_in_dim.7.refs_1_, f32[512,256]{1,0:T(8,128)S(1)} %get-tuple-element.99.refs_2_, f32[512,256]{1,0:T(8,128)S(1)} %shard_map.76.refs_3_, f32[512,256]{1,0:T(8,128)S(1)} %shard_map.77.refs_4_, ...), custom_call_target="tpu_custom_call" | custom-call | flops 500000000 | bytes 4194304 | tf_op jit(solution)/shard_map/pallas_call | solution.py:25
  (77 shorter events, 38.0 us)
Async XLA Ops:
  1.8 11.3 %collective-permute-start.1 = (f32[32,1024]{1,0:T(8,128)S(1)}, f32[32,1024]{1,0:T(8,128)S(1)}, u32[]{:S(2)}, u32[]{:S(2)}) collective-permute-start(f32[32,1024]{1,0:T(8,128)S(1)} %get-tuple-element.106), channel_id=1, source_target_pairs={{8,16},{16,8},{24,32},{32,24},{40,48},{48,40},{56,64},{64,56},{72,... | collective-permute-start | bytes 393224 | tf_op jit(solution)/shard_map/ppermute | solution.py:293
  2.5 10.6 %collective-permute-start = (f32[32,1024]{1,0:T(8,128)S(1)}, f32[32,1024]{1,0:T(8,128)S(1)}, u32[]{:S(2)}, u32[]{:S(2)}) collective-permute-start(f32[32,1024]{1,0:T(8,128)S(1)} %get-tuple-element.107), channel_id=1, source_target_pairs={{0,8},{8,0},{16,24},{24,16},{32,40},{40,32},{48,56},{56,48},{64,72... | collective-permute-start | bytes 393224 | tf_op jit(solution)/shard_map/ppermute | solution.py:293
  13.9 6.2 %collective-permute-start.2 = (f32[256,128]{1,0:T(8,128)S(1)}, f32[256,128]{1,0:T(8,128)S(1)}, u32[]{:S(2)}, u32[]{:S(2)}) collective-permute-start(f32[256,128]{1,0:T(8,128)S(1)} %get-tuple-element.65), channel_id=1, source_target_pairs={{0,1},{1,0},{2,3},{3,2},{4,5},{5,4},{6,7},{7,6},{8,9},{9,8},{10,11... | collective-permute-start | bytes 393224 | tf_op jit(solution)/shard_map/ppermute | solution.py:293
  15.2 6.3 %collective-permute-start.3 = (f32[256,128]{1,0:T(8,128)S(1)}, f32[256,128]{1,0:T(8,128)S(1)}, u32[]{:S(2)}, u32[]{:S(2)}) collective-permute-start(f32[256,128]{1,0:T(8,128)S(1)} %get-tuple-element.66), channel_id=1, source_target_pairs={{1,2},{2,1},{3,4},{4,3},{5,6},{6,5},{9,10},{10,9},{11,12},{12,11},... | collective-permute-start | bytes 393224 | tf_op jit(solution)/shard_map/ppermute | solution.py:293
  23.8 2.6 %collective-permute-start.11 = (f32[8,128]{1,0:T(8,128)S(1)}, f32[8,128]{1,0:T(8,128)S(1)}, u32[]{:S(2)}, u32[]{:S(2)}) collective-permute-start(f32[8,128]{1,0:T(8,128)S(1)} %add.42), channel_id=1, source_target_pairs={{0,2},{1,3},{2,0},{3,1},{4,6},{5,7},{6,4},{7,5},{8,10},{9,11},{10,... | collective-permute-start | bytes 12296 | tf_op jit(solution)/shard_map/ppermute | solution.py:304
  26.5 7.2 %collective-permute-start.12 = (f32[8,128]{1,0:T(8,128)S(1)}, f32[8,128]{1,0:T(8,128)S(1)}, u32[]{:S(2)}, u32[]{:S(2)}) collective-permute-start(f32[8,128]{1,0:T(8,128)S(1)} %add.43), channel_id=1, source_target_pairs={{0,6},{1,7},{2,4},{3,5},{4,2},{5,3},{6,0},{7,1},{8,14},{9,15},{10,... | collective-permute-start | bytes 12296 | tf_op jit(solution)/shard_map/ppermute | solution.py:304
  29.8 20.8 %collective-permute-start.7 = (s32[64,1024]{1,0:T(8,128)S(1)}, s32[64,1024]{1,0:T(8,128)S(1)}, u32[]{:S(2)}, u32[]{:S(2)}) collective-permute-start(s32[64,1024]{1,0:T(8,128)S(1)} %get-tuple-element.108), channel_id=1, source_target_pairs={{8,16},{16,8},{24,32},{32,24},{40,48},{48,40},{56,64},{64,56},{72,... | collective-permute-start | bytes 786440 | tf_op jit(solution)/shard_map/ppermute | solution.py:293
  30.5 20.1 %collective-permute-start.6 = (s32[64,1024]{1,0:T(8,128)S(1)}, s32[64,1024]{1,0:T(8,128)S(1)}, u32[]{:S(2)}, u32[]{:S(2)}) collective-permute-start(s32[64,1024]{1,0:T(8,128)S(1)} %get-tuple-element.109), channel_id=1, source_target_pairs={{0,8},{8,0},{16,24},{24,16},{32,40},{40,32},{48,56},{56,48},{64,72... | collective-permute-start | bytes 786440 | tf_op jit(solution)/shard_map/ppermute | solution.py:293
  33.7 4.8 %collective-permute-start.13 = (f32[8,128]{1,0:T(8,128)S(1)}, f32[8,128]{1,0:T(8,128)S(1)}, u32[]{:S(2)}, u32[]{:S(2)}) collective-permute-start(f32[8,128]{1,0:T(8,128)S(1)} %add.44), channel_id=1, source_target_pairs={{0,32},{8,40},{16,48},{24,56},{32,0},{40,8},{48,16},{56,24},{64,96... | collective-permute-start | bytes 12296 | tf_op jit(solution)/shard_map/ppermute | solution.py:304
  35.1 15.5 %collective-permute-start.4 = (f32[64,1024]{1,0:T(8,128)S(1)}, f32[64,1024]{1,0:T(8,128)S(1)}, u32[]{:S(2)}, u32[]{:S(2)}) collective-permute-start(f32[64,1024]{1,0:T(8,128)S(1)} %get-tuple-element.67), channel_id=1, source_target_pairs={{0,8},{8,0},{16,24},{24,16},{32,40},{40,32},{48,56},{56,48},{64,72... | collective-permute-start | bytes 786440 | tf_op jit(solution)/shard_map/ppermute | solution.py:293
  35.7 14.9 %collective-permute-start.5 = (f32[64,1024]{1,0:T(8,128)S(1)}, f32[64,1024]{1,0:T(8,128)S(1)}, u32[]{:S(2)}, u32[]{:S(2)}) collective-permute-start(f32[64,1024]{1,0:T(8,128)S(1)} %get-tuple-element.68), channel_id=1, source_target_pairs={{8,16},{16,8},{24,32},{32,24},{40,48},{48,40},{56,64},{64,56},{72,... | collective-permute-start | bytes 786440 | tf_op jit(solution)/shard_map/ppermute | solution.py:293
  38.5 5.8 %collective-permute-start.14 = (f32[8,128]{1,0:T(8,128)S(1)}, f32[8,128]{1,0:T(8,128)S(1)}, u32[]{:S(2)}, u32[]{:S(2)}) collective-permute-start(f32[8,128]{1,0:T(8,128)S(1)} %add.45), channel_id=1, source_target_pairs={{0,96},{8,104},{16,112},{24,120},{32,64},{40,72},{48,80},{56,88},{... | collective-permute-start | bytes 12296 | tf_op jit(solution)/shard_map/ppermute | solution.py:304
  46.9 3.7 %collective-permute-start.16 = (f32[8,128]{1,0:T(8,128)S(1)}, f32[8,128]{1,0:T(8,128)S(1)}, u32[]{:S(2)}, u32[]{:S(2)}) collective-permute-start(f32[8,128]{1,0:T(8,128)S(1)} %add.47), channel_id=1, source_target_pairs={{0,24},{8,16},{16,8},{24,0},{32,56},{40,48},{48,40},{56,32},{64,88... | collective-permute-start | bytes 12296 | tf_op jit(solution)/shard_map/ppermute | solution.py:304
  52.9 11.8 %collective-permute-start.8 = (f32[256,128]{1,0:T(8,128)S(1)}, f32[256,128]{1,0:T(8,128)S(1)}, u32[]{:S(2)}, u32[]{:S(2)}) collective-permute-start(f32[256,128]{1,0:T(8,128)S(1)} %get-tuple-element.83), channel_id=1, source_target_pairs={{0,1},{1,0},{2,3},{3,2},{4,5},{5,4},{6,7},{7,6},{8,9},{9,8},{10,11... | collective-permute-start | bytes 393224 | tf_op jit(solution)/shard_map/ppermute | solution.py:293
  58.4 6.3 %collective-permute-start.9 = (f32[256,128]{1,0:T(8,128)S(1)}, f32[256,128]{1,0:T(8,128)S(1)}, u32[]{:S(2)}, u32[]{:S(2)}) collective-permute-start(f32[256,128]{1,0:T(8,128)S(1)} %get-tuple-element.84), channel_id=1, source_target_pairs={{1,2},{2,1},{3,4},{4,3},{5,6},{6,5},{9,10},{10,9},{11,12},{12,11},... | collective-permute-start | bytes 393224 | tf_op jit(solution)/shard_map/ppermute | solution.py:293
  70.7 3.7 %collective-permute-start.23 = (f32[8,128]{1,0:T(8,128)S(1)}, f32[8,128]{1,0:T(8,128)S(1)}, u32[]{:S(2)}, u32[]{:S(2)}) collective-permute-start(f32[8,128]{1,0:T(8,128)S(1)} %add.50), channel_id=1, source_target_pairs={{0,6},{1,7},{2,4},{3,5},{4,2},{5,3},{6,0},{7,1},{8,14},{9,15},{10,... | collective-permute-start | bytes 12296 | tf_op jit(solution)/shard_map/ppermute | solution.py:304
  74.4 3.0 %collective-permute-start.24 = (f32[8,128]{1,0:T(8,128)S(1)}, f32[8,128]{1,0:T(8,128)S(1)}, u32[]{:S(2)}, u32[]{:S(2)}) collective-permute-start(f32[8,128]{1,0:T(8,128)S(1)} %add.51), channel_id=1, source_target_pairs={{0,32},{8,40},{16,48},{24,56},{32,0},{40,8},{48,16},{56,24},{64,96... | collective-permute-start | bytes 12296 | tf_op jit(solution)/shard_map/ppermute | solution.py:304
  76.3 13.6 %collective-permute-start.17 = (f32[64,1024]{1,0:T(8,128)S(1)}, f32[64,1024]{1,0:T(8,128)S(1)}, u32[]{:S(2)}, u32[]{:S(2)}) collective-permute-start(f32[64,1024]{1,0:T(8,128)S(1)} %get-tuple-element.87), channel_id=1, source_target_pairs={{0,8},{8,0},{16,24},{24,16},{32,40},{40,32},{48,56},{56,48},{64,72... | collective-permute-start | bytes 786440 | tf_op jit(solution)/shard_map/ppermute | solution.py:293
  76.3 13.6 %collective-permute-start.18 = (f32[64,1024]{1,0:T(8,128)S(1)}, f32[64,1024]{1,0:T(8,128)S(1)}, u32[]{:S(2)}, u32[]{:S(2)}) collective-permute-start(f32[64,1024]{1,0:T(8,128)S(1)} %get-tuple-element.88), channel_id=1, source_target_pairs={{8,16},{16,8},{24,32},{32,24},{40,48},{48,40},{56,64},{64,56},{72,... | collective-permute-start | bytes 786440 | tf_op jit(solution)/shard_map/ppermute | solution.py:293
  77.3 6.1 %collective-permute-start.25 = (f32[8,128]{1,0:T(8,128)S(1)}, f32[8,128]{1,0:T(8,128)S(1)}, u32[]{:S(2)}, u32[]{:S(2)}) collective-permute-start(f32[8,128]{1,0:T(8,128)S(1)} %add.52), channel_id=1, source_target_pairs={{0,96},{8,104},{16,112},{24,120},{32,64},{40,72},{48,80},{56,88},{... | collective-permute-start | bytes 12296 | tf_op jit(solution)/shard_map/ppermute | solution.py:304
  83.4 2.8 %collective-permute-start.26 = (f32[8,128]{1,0:T(8,128)S(1)}, f32[8,128]{1,0:T(8,128)S(1)}, u32[]{:S(2)}, u32[]{:S(2)}) collective-permute-start(f32[8,128]{1,0:T(8,128)S(1)} %add.53), channel_id=1, source_target_pairs={{0,8},{8,0},{16,24},{24,16},{32,40},{40,32},{48,56},{56,48},{64,72... | collective-permute-start | bytes 12296 | tf_op jit(solution)/shard_map/ppermute | solution.py:304
  86.2 3.7 %collective-permute-start.27 = (f32[8,128]{1,0:T(8,128)S(1)}, f32[8,128]{1,0:T(8,128)S(1)}, u32[]{:S(2)}, u32[]{:S(2)}) collective-permute-start(f32[8,128]{1,0:T(8,128)S(1)} %add.54), channel_id=1, source_target_pairs={{0,24},{8,16},{16,8},{24,0},{32,56},{40,48},{48,40},{56,32},{64,88... | collective-permute-start | bytes 12296 | tf_op jit(solution)/shard_map/ppermute | solution.py:304
  92.2 12.2 %collective-permute-start.19 = (f32[256,128]{1,0:T(8,128)S(1)}, f32[256,128]{1,0:T(8,128)S(1)}, u32[]{:S(2)}, u32[]{:S(2)}) collective-permute-start(f32[256,128]{1,0:T(8,128)S(1)} %get-tuple-element.103), channel_id=1, source_target_pairs={{0,1},{1,0},{2,3},{3,2},{4,5},{5,4},{6,7},{7,6},{8,9},{9,8},{10,11... | collective-permute-start | bytes 393224 | tf_op jit(solution)/shard_map/ppermute | solution.py:293
  97.8 6.6 %collective-permute-start.20 = (f32[256,128]{1,0:T(8,128)S(1)}, f32[256,128]{1,0:T(8,128)S(1)}, u32[]{:S(2)}, u32[]{:S(2)}) collective-permute-start(f32[256,128]{1,0:T(8,128)S(1)} %get-tuple-element.104), channel_id=1, source_target_pairs={{1,2},{2,1},{3,4},{4,3},{5,6},{6,5},{9,10},{10,9},{11,12},{12,11},... | collective-permute-start | bytes 393224 | tf_op jit(solution)/shard_map/ppermute | solution.py:293
  (6 other events, 23.1 us)

commit v2 on v1

v2 whole, which is shorter than its diff:
```python
import functools

import jax
import jax.numpy as jnp
from jax import lax
from jax.experimental import pallas as pl
from jax.experimental.pallas import tpu as pltpu
from jax.sharding import PartitionSpec as P


REACH = 64
PILOT_RADIUS = 32
CLASSES = 4
BACKGROUND = 0.5
TILE = 256
BAND = TILE + 2 * REACH
STEP = 64
F32 = jnp.float32
BF16 = jnp.bfloat16
MIB = 1 << 20
HBM = pl.BlockSpec(memory_space=pltpu.HBM)
VMEM = pl.BlockSpec(memory_space=pltpu.VMEM)
SMEM = pl.BlockSpec(memory_space=pltpu.SMEM)


def call(kernel, outs, args, ins=None, out_specs=None, scratch=(), limit=24, flops=100_000_000):
    return pl.pallas_call(
        kernel,
        out_shape=[jax.ShapeDtypeStruct(s, d) for s, d in outs],
        in_specs=ins or [VMEM] * len(args),
        out_specs=out_specs or [VMEM] * len(outs),
        scratch_shapes=scratch,
        compiler_params=pltpu.CompilerParams(vmem_limit_bytes=limit * MIB),
        cost_estimate=pl.CostEstimate(flops=flops, transcendentals=0, bytes_accessed=4 * MIB),
    )(*args)


def iota(shape, dim):
    return lax.broadcasted_iota(jnp.int32, shape, dim)


def split(value):
    high = value.astype(BF16)
    return high, (value - high.astype(F32)).astype(BF16)


def dot(a, b):
    return jnp.dot(a, b, preferred_element_type=F32)


def take(refs, *counts):
    groups = []
    for count in counts:
        groups.append(list(refs[:count]))
        refs = refs[count:]
    return *groups, list(refs)


def chosen(flag, when_set, when_clear):
    return jnp.where(flag > 0.5, when_set, when_clear)


def flags_of(axis):
    index = lax.axis_index(axis)
    last = lax.axis_size(axis) - 1
    values = (index & 1, jnp.minimum(index, 1), jnp.minimum(last - index, 1))
    return [jnp.full((1, 1), value.astype(F32), F32) for value in values]


def fill_bands(radius_ref, high_ref, low_ref, stack_ref, rim_ref):
    lane = iota((8, 128), 1).astype(F32)
    tap = jnp.where(iota((8, 128), 0) == 0, jnp.where(lane == 0, 1.0, 2.0), 0.0)
    shift = (iota((BAND, TILE), 0) - REACH - iota((BAND, TILE), 1)).astype(F32)
    row, column = iota((128, 128), 0), iota((128, 128), 1)
    upper = row < 64
    same = upper == (column < 64)
    rim_shift = (row - column + jnp.where(upper, REACH, -REACH)).astype(F32)
    for c in range(CLASSES + 1):
        radius = F32(PILOT_RADIUS) if c == CLASSES else radius_ref[c].astype(F32)
        radius = jnp.full((1, 1), radius, F32)
        inverse = 1.0 / (2.0 * (0.5 * radius) * (0.5 * radius))

        def shape_of(d):
            return jnp.where(jnp.abs(d) <= radius, jnp.exp(-(d * d) * inverse), 0.0)

        total = jnp.sum(shape_of(lane) * tap, axis=(0, 1), keepdims=True)
        high, low = split(shape_of(shift) / total)
        high_ref[c * BAND : (c + 1) * BAND, :] = high
        low_ref[c * BAND : (c + 1) * BAND, :] = low
        stack_ref[c, :, 0:TILE] = high
        stack_ref[c, :, TILE : 2 * TILE] = low
        stack_ref[c, :, 2 * TILE :] = high
        high, low = split(jnp.where(same, shape_of(rim_shift) / total, 0.0))
        rim_ref[c, :, 0:128] = high
        rim_ref[c, :, 128:256] = high
        rim_ref[c, :, 256:384] = low


def prepare_kernel(*refs):
    (radius_ref, *fields), tables, outs, scratch = take(refs, 4, 4, 4)
    mass_ref, label_ref, send_a, send_b = outs
    *local, arrived = scratch
    copies = [
        pltpu.make_async_copy(field, kept, arrived.at[n])
        for n, (field, kept) in enumerate(zip(fields, local))
    ]
    for copy in copies:
        copy.start()
    fill_bands(radius_ref, *tables)
    counts, weights, classes = local
    copies[0].wait()
    copies[1].wait()
    rows = counts.shape[0]
    for start in range(0, rows, STEP):
        at = slice(start, start + STEP)
        mass_ref[at] = counts[at].astype(F32) * weights[at]
    copies[2].wait()
    for start in range(0, rows, STEP):
        at = slice(start, start + STEP)
        label_ref[at] = classes[at].astype(F32).astype(BF16)
    odd = flags_of("row")[0]
    top, bottom = classes[0:REACH], classes[rows - REACH :]
    send_a[...] = chosen(odd, top, bottom)
    send_b[...] = chosen(odd, bottom, top)


def masked(pieces, labels, c):
    if labels is None:
        return pieces
    keep = labels == c
    return [jnp.where(keep, piece, jnp.zeros_like(piece)) for piece in pieces]


def rows_kernel(*refs, bands, labelled):
    (field_ref,), label_refs, (stack_ref, high_ref, low_ref, edge_ref) = take(refs, 1, labelled)
    _, columns = field_ref.shape
    for n in range(columns // TILE):
        at = slice(n * TILE, (n + 1) * TILE)
        pieces = split(field_ref[:, at])
        labels = label_refs[0][:, at] if labelled else None
        for slot, c in enumerate(bands):
            high, low = masked(pieces, labels, c)

            def part(t, start):
                own = slice(t * TILE, (t + 1) * TILE)
                right = jnp.concatenate([high[own], high[own], low[own]], axis=0)
                return dot(stack_ref[c, start : start + TILE + REACH, :], right)

            first, second = part(0, REACH), part(1, 0)
            edge_ref[slot, 0:REACH, at] = first[0:REACH]
            edge_ref[slot, REACH:, at] = second[TILE:]
            cut = TILE - REACH
            for target, value in (
                (0, first[REACH:cut]),
                (cut - REACH, first[cut:] + second[: 2 * REACH]),
                (cut + REACH, second[2 * REACH : TILE]),
            ):
                value_high, value_low = split(value)
                high_ref[slot, target : target + value.shape[0], at] = value_high
                low_ref[slot, target : target + value.shape[0], at] = value_low


def kept_row(start, rows):
    if start < REACH:
        return rows - 2 * REACH + start
    return start if start >= rows - REACH else start - REACH


def stacked_left(sides, inputs, start, stop, inner):
    refs, edge_ref = sides
    pieces = []
    slot = 0
    for ref in refs:
        for own in range(ref.shape[0]):
            rows = []
            if start < inner:
                rows.append(ref[own, start : min(stop, inner), inputs])
            if stop > inner:
                rows.append(edge_ref[slot, max(start, inner) - inner : stop - inner, inputs])
            pieces.append(rows[0] if len(rows) == 1 else jnp.concatenate(rows))
            slot += 1
    return jnp.concatenate(pieces, axis=1)


def swept(highs, lows, bands, band_refs, inputs, taps, outputs, start, stop, inner):
    right_high, right_low = (
        jnp.concatenate([ref[c * BAND + taps.start : c * BAND + taps.stop, outputs] for c in bands])
        for ref in band_refs
    )
    high = stacked_left(highs, inputs, start, stop, inner)
    low = stacked_left(lows, inputs, start, stop, inner)
    return dot(high, right_high) + dot(high, right_low) + dot(low, right_high)


def edges_kernel(*refs, groups, labelled):
    count = len(groups)
    halo, labels_in, partials, highs, lows, (rim_ref, *band_refs), outs = take(
        refs, 2, 2 * labelled, count, count, count, 3
    )
    edge_high, edge_low, left_ref, right_ref, send_a, send_b = outs
    bands = [c for group in groups for c in group]
    sources = [(ref, own) for ref in partials for own in range(ref.shape[0])]
    columns = halo[0].shape[1]
    odd_row, has_top, has_bottom = flags_of("row")
    odd_column = flags_of("col")[0]
    for n in range(columns // TILE):
        at = slice(n * TILE, (n + 1) * TILE)

        def joined(pair):
            first, second = pair[0][:, at].astype(F32), pair[1][:, at].astype(F32)
            top = chosen(has_top, chosen(odd_row, first, second), 0.0)
            bottom = chosen(has_bottom, chosen(odd_row, second, first), 0.0)
            missing = REACH - first.shape[0]
            if missing:
                zeros = jnp.zeros((missing, TILE), F32)
                return jnp.concatenate([zeros, top, bottom, zeros])
            return jnp.concatenate([top, bottom])

        pieces = split(joined(halo))
        labels = joined(labels_in).astype(BF16) if labelled else None
        for slot, c in enumerate(bands):
            high, low = masked(pieces, labels, c)
            right = jnp.concatenate([high, low, high], axis=0)
            source, own = sources[slot]
            value = source[own, :, at] + dot(rim_ref[c], right)
            edge_high[slot, :, at], edge_low[slot, :, at] = split(value)
    rows = left_ref.shape[0]
    inner = rows - 2 * REACH
    sides = (
        (left_ref, slice(0, TILE), slice(128, BAND), slice(0, TILE)),
        (right_ref, slice(columns - 128, columns), slice(0, 128), slice(0, 128)),
    )
    for target, *window in sides:
        target[...] = swept(
            (highs, edge_high), (lows, edge_low), bands, band_refs, *window, 0, rows, inner
        )
    half = rows // 2
    lower = iota((half, 128), 1) < REACH
    left = left_ref[:, 0:128]
    left = jnp.where(lower, left[:half], pltpu.roll(left[half:], REACH, 1))
    right = right_ref[...]
    right = jnp.where(lower, pltpu.roll(right[:half], REACH, 1), right[half:])
    send_a[...] = chosen(odd_column, left, right)
    send_b[...] = chosen(odd_column, right, left)


def middle_kernel(*refs, groups, start):
    count = len(groups)
    highs, lows, (edge_high, edge_low), band_refs, (out_ref,) = take(refs, count, count, 2, 2)
    bands = [c for group in groups for c in group]
    inner = highs[0].shape[1]
    stop = start + out_ref.shape[0]
    for j in range(out_ref.shape[1] // TILE):
        inputs = slice(j * TILE + 128, j * TILE + 128 + BAND)
        out_ref[:, j * TILE : (j + 1) * TILE] = swept(
            (highs, edge_high),
            (lows, edge_low),
            bands,
            band_refs,
            inputs,
            slice(0, BAND),
            slice(0, TILE),
            start,
            stop,
            inner,
        )


def gathered(pieces, come, flags, start):
    left_ref, middles, right_ref = pieces
    odd, has_left, has_right = flags
    rows = left_ref.shape[0]
    half = rows // 2
    kept = kept_row(start, rows)
    at = slice(kept, kept + STEP)
    lane = iota((STEP, 128), 1)
    local = slice(kept % half, kept % half + STEP)
    come_left = chosen(has_left, chosen(odd, come[0][local], come[1][local]), 0.0)
    come_right = chosen(has_right, chosen(odd, come[1][local], come[0][local]), 0.0)
    if kept < half:
        come_left = pltpu.roll(come_left, REACH, 1)
    else:
        come_right = pltpu.roll(come_right, REACH, 1)
    first = left_ref[at, 0:128] + jnp.where(lane >= REACH, come_left, 0.0)
    last = right_ref[at, :] + jnp.where(lane < REACH, come_right, 0.0)
    each = middles[0].shape[0]
    middle_ref = middles[kept // each]
    own = slice(kept % each, kept % each + STEP)
    blocks = [first, left_ref[at, 128:256]]
    blocks += [middle_ref[own, k : k + 128] for k in range(0, middle_ref.shape[1], 128)]
    blocks += [last]
    turned = [pltpu.roll(block, REACH, 1) for block in blocks]
    return [jnp.where(lane < REACH, a, b) for a, b in zip(turned[:-1], turned[1:])]


def finish_kernel(*refs, middles, scaled, following, totals):
    (left_ref,), middle_refs, (right_ref,), come, refs = take(refs, 1, middles, 1, 2)
    pieces = (left_ref, middle_refs, right_ref)
    totals_in, mass_in, density_out, refs = take(refs, 2 * scaled, following, scaled)
    adapted_out, refs = take(refs, 4 * following)
    if scaled:
        inverse = jnp.exp(-(totals_in[0][0:1, :] / totals_in[1][1:2, :]))
        staged, done = refs
    rows = left_ref.shape[0]
    column_flags = flags_of("col")
    log_sum = jnp.zeros((8, 128), F32)
    mass_sum = jnp.zeros((8, 128), F32)
    copies = []
    for number, start in enumerate(range(0, rows, STEP)):
        at = slice(start, start + STEP)
        for k, block in enumerate(gathered(pieces, come, column_flags, start)):
            lanes = slice(k * 128, (k + 1) * 128)
            if scaled:
                block = block * inverse
                staged[at, lanes] = block
            if following:
                pilot = block + BACKGROUND
                mass = mass_in[0][at, lanes]
                adapted_out[0][at, lanes] = mass * pilot
                terms = mass * jnp.log(pilot)
                log_sum += jnp.sum(terms.reshape(STEP // 8, 8, 128), axis=0)
                if totals:
                    mass_sum += jnp.sum(mass.reshape(STEP // 8, 8, 128), axis=0)
        if scaled:
            copy = pltpu.make_async_copy(staged.at[at], density_out[0].at[at], done.at[number])
            copy.start()
            copies.append(copy)
    if following:
        adapted_ref, send_a, send_b, stat_ref = adapted_out
        odd_row = flags_of("row")[0]
        top, bottom = adapted_ref[0:REACH], adapted_ref[rows - REACH :]
        send_a[...] = chosen(odd_row, top, bottom)
        send_b[...] = chosen(odd_row, bottom, top)
        log_sum = jnp.sum(log_sum, axis=(0, 1), keepdims=True)
        mass_sum = jnp.sum(mass_sum, axis=(0, 1), keepdims=True)
        row = iota((8, 128), 0)
        stat_ref[...] = jnp.where(row == 0, log_sum, jnp.where(row == 1, mass_sum, 0.0))
    for copy in copies:
        copy.wait()


def exchange(first, second, axis):
    results = []
    count = lax.axis_size(axis)
    for offset, value in ((0, first), (1, second)):
        pairs = []
        for i in range(offset, count, 2):
            pairs += [(i, (i + 1) % count), ((i + 1) % count, i)]
        results.append(lax.ppermute(value, axis, pairs))
    return results


HOPS = {1: (), 2: (1,), 4: (1, 3), 8: (1, 2, 6), 16: (4, 12, 1, 3)}


def total_over(stat):
    for axis in ("col", "row"):
        for hop in HOPS[lax.axis_size(axis)]:
            pairs = [(i, i ^ hop) for i in range(lax.axis_size(axis))]
            stat = stat + lax.ppermute(stat, axis, pairs)
    return stat


def smooth(field, halo, labels, label_halo, tables, groups, cuts):
    high, low, stack, rim = tables
    rows, columns = field.shape
    labelled = labels is not None
    bands = [c for group in groups for c in group]
    highs, lows, partials = [], [], []
    for group in groups:
        inner = (len(group), rows - 2 * REACH, columns)
        edge = (len(group), 2 * REACH, columns)
        results = call(
            functools.partial(rows_kernel, bands=group, labelled=labelled),
            [(inner, BF16), (inner, BF16), (edge, F32)],
            [field] + ([labels] if labelled else []) + [stack],
            flops=len(group) * 1_000_000_000,
        )
        for results_of, result in zip((highs, lows, partials), results):
            results_of.append(result)
    edge = (len(bands), 2 * REACH, columns)
    edge_high, edge_low, left, right, send_a, send_b = call(
        functools.partial(edges_kernel, groups=groups, labelled=labelled),
        [(edge, BF16), (edge, BF16), ((rows, TILE), F32), ((rows, 128), F32)]
        + [((rows // 2, 128), F32)] * 2,
        [*halo, *(label_halo if labelled else ()), *partials, *highs, *lows]
        + [rim, high, low],
        flops=len(bands) * 500_000_000,
    )
    come = exchange(send_a, send_b, "col")
    middles = []
    for number in range(cuts):
        middles += call(
            functools.partial(middle_kernel, groups=groups, start=number * (rows // cuts)),
            [((rows // cuts, columns - TILE), F32)],
            [*highs, *lows, edge_high, edge_low, high, low],
            flops=len(bands) * 750_000_000 // cuts,
        )
    return [left, *middles, right, *come]


def finish(pieces, extra, scaled, following, totals, shape):
    plane, rim, stat = (shape, F32), ((REACH, shape[1]), F32), ((8, 128), F32)
    outs = [plane] * scaled + [plane, rim, rim, stat] * following
    scratch = []
    if scaled:
        scratch = [pltpu.VMEM(shape, F32), pltpu.SemaphoreType.DMA((shape[0] // STEP,))]
    return call(
        functools.partial(
            finish_kernel,
            middles=len(pieces) - 4,
            scaled=scaled,
            following=following,
            totals=totals,
        ),
        outs,
        [*pieces, *extra],
        out_specs=[HBM] * scaled + [VMEM] * (4 * following),
        scratch=scratch,
        flops=500_000_000,
    )


def body(counts, sample_weights, classes, class_radius):
    shape = rows, columns = counts.shape
    is_odd = (lax.axis_index("row") & 1).astype(F32)
    groups = ((0, 1), (2, 3))
    rim = (REACH, columns)

    def ends(array, width):
        top, bottom = array[:width], array[rows - width :]
        return [jnp.where(is_odd > 0.5, *pair) for pair in ((top, bottom), (bottom, top))]

    sends = [
        number.astype(F32) * weight
        for number, weight in zip(ends(counts, PILOT_RADIUS), ends(sample_weights, PILOT_RADIUS))
    ]
    mass_halo = exchange(*sends, "row")
    wide = (CLASSES + 1) * BAND
    *tables, mass, labels, label_a, label_b = call(
        prepare_kernel,
        [
            ((wide, TILE), BF16),
            ((wide, TILE), BF16),
            ((CLASSES + 1, BAND, 3 * TILE), BF16),
            ((CLASSES + 1, 128, 384), BF16),
            (shape, F32),
            (shape, BF16),
            (rim, jnp.int32),
            (rim, jnp.int32),
        ],
        [class_radius]
        + [
            pltpu.with_memory_space_constraint(field, pltpu.HBM)
            for field in (counts, sample_weights, classes)
        ],
        ins=[SMEM, HBM, HBM, HBM],
        scratch=[
            pltpu.VMEM(shape, jnp.int32),
            pltpu.VMEM(shape, F32),
            pltpu.VMEM(shape, jnp.int32),
            pltpu.SemaphoreType.DMA((3,)),
        ],
        flops=500_000_000,
    )
    label_halo = exchange(label_a, label_b, "row")
    pieces = smooth(mass, mass_halo, None, None, tables, ((CLASSES,),), 1)
    adapted, *sends, first_stat = finish(pieces, [mass], False, True, True, shape)
    halo = exchange(*sends, "row")
    first_total = total_over(first_stat)
    pieces = smooth(adapted, halo, labels, label_halo, tables, groups, 2)
    density_first, adapted, *sends, second_stat = finish(
        pieces, [first_total, first_total, mass], True, True, False, shape
    )
    halo = exchange(*sends, "row")
    second_total = total_over(second_stat)
    pieces = smooth(adapted, halo, labels, label_halo, tables, groups, 2)
    (density_second,) = finish(
        pieces, [second_total, first_total], True, False, False, shape
    )
    return density_first, density_second


def solution(mesh):
    spec = P("row", "col")
    return jax.shard_map(
        body,
        mesh=mesh,
        in_specs=(spec, spec, spec, P()),
        out_specs=(spec, spec),
        check_vma=False,
    )
```

time: 107 us -> 100 us (0.935)
  starting transfers between devices: 51.9 us -> 43.4 us
  waiting for transfers between devices: 15.1 us -> 20 us
  other arithmetic: 4.11 us -> 1.18 us
    ppermute x14, starting transfers between devices: 20.6 us -> 14.6 us  [total_over(): stat = stat + lax.ppermute(stat, axis, pairs)]
    ppermute x14, waiting for transfers between devices: 13.6 us -> 17.3 us  [total_over(): stat = stat + lax.ppermute(stat, axis, pairs)]
    mul x1 -> x0, other arithmetic: 2.65 us -> none  [body(): mass = counts.astype(F32) * sample_weights]
    ppermute x14, starting transfers between devices: 31.3 us -> 28.7 us  [exchange(): results.append(lax.ppermute(value, axis, pairs))]
    ppermute x14, waiting for transfers between devices: 1.49 us -> 2.78 us  [exchange(): results.append(lax.ppermute(value, axis, pairs))]
    pallas_call x21 -> x17, Pallas kernels: 34.6 us -> 33.8 us  [call(): pl.pallas_call(kernel, out_shape=[jax.ShapeDtypeStruct(s, d) for s, d in...]
  transfers between devices with their start and end apart: 28 -> 28, of which waited for: 13 -> 15; matrix products, arithmetic and copies ran while one was open for 3% -> 0% of each run, Pallas kernels for 22% -> 24%
where the time goes in v2:
time: 100 us
  starting transfers between devices  43.4 us (43%)
  Pallas kernels  33.8 us (34%)
  waiting for transfers between devices  20 us (20%)
  other arithmetic  1.18 us (1%)
  between operations  1.04 us (1%)
    pallas_call x17, Pallas kernels, call(): pl.pallas_call(kernel, out_shape=[jax.ShapeDtypeStruct(s, d) for s, d in...  33.8 us
    ppermute x14, starting transfers between devices, exchange(): results.append(lax.ppermute(value, axis, pairs))  28.7 us
    ppermute x14, waiting for transfers between devices, total_over(): stat = stat + lax.ppermute(stat, axis, pairs)  17.3 us
    ppermute x14, starting transfers between devices, total_over(): stat = stat + lax.ppermute(stat, axis, pairs)  14.6 us
    ppermute x14, waiting for transfers between devices, exchange(): results.append(lax.ppermute(value, axis, pairs))  2.78 us
  transfers between devices with their start and end apart: 28, of which 15 were waited for; matrix products, arithmetic and copies ran while one was open for 0% of the time, Pallas kernels for 24%

profile of v2, /device:TPU:1, one launch (start us, length us, event | category | flops | bytes accessed | tf_op | source)
XLA Modules:
  0.0 100.0 jit_solution(4141345176704138817)
XLA Ops:
  1.8 5.8 %collective-permute-start.1 = (f32[32,1024]{1,0:T(8,128)S(1)}, f32[32,1024]{1,0:T(8,128)S(1)}, u32[]{:S(2)}, u32[]{:S(2)}) collective-permute-start(f32[32,1024]{1,0:T(8,128)S(1)} %get-tuple-element.102), channel_id=1, source_target_pairs={{8,16},{16,8},{24,32},{32,24},{40,48},{48,40},{56,64},{64,56},{72,... | collective-permute-start | bytes 393224 | tf_op jit(solution)/shard_map/ppermute | solution.py:349
  8.3 4.0 %shard_map.59 = (bf16[1920,256]{1,0:T(8,128)(2,1)S(1)}, bf16[1920,256]{1,0:T(8,128)(2,1)S(1)}, bf16[5,384,768]{2,1,0:T(8,128)(2,1)S(1)}, bf16[5,128,384]{2,1,0:T...) custom-call(s32[4]{0:T(128)S(1)} %copy-done, ...), custom_call_target="tpu_custom_call" | custom-call | flops 500000000 | bytes 4194304 | tf_op jit(solution)/shard_map/pallas_call | solution.py:27
  20.7 2.5 %collective-permute-start.10 = (f32[8,128]{1,0:T(8,128)S(1)}, f32[8,128]{1,0:T(8,128)S(1)}, u32[]{:S(2)}, u32[]{:S(2)}) collective-permute-start(f32[8,128]{1,0:T(8,128)S(1)} %get-tuple-element.84), channel_id=1, source_target_pairs={{0,1},{1,0},{2,3},{3,2},{4,5},{5,4},{6,7},{7,6},{8,9},{9,8},{10,11... | collective-permute-start | bytes 12296 | tf_op jit(solution)/shard_map/ppermute | solution.py:360
  24.0 2.5 %collective-permute-done.11 = f32[8,128]{1,0:T(8,128)S(1)} collective-permute-done((f32[8,128]{1,0:T(8,128)S(1)}, f32[8,128]{1,0:T(8,128)S(1)}, u32[]{:S(2)}, u32[]{:S(2)}) %collective-permute-start.11) | collective-permute-done | bytes 4128 | tf_op jit(solution)/shard_map/ppermute | solution.py:360
  26.5 2.9 %collective-permute-start.12 = (f32[8,128]{1,0:T(8,128)S(1)}, f32[8,128]{1,0:T(8,128)S(1)}, u32[]{:S(2)}, u32[]{:S(2)}) collective-permute-start(f32[8,128]{1,0:T(8,128)S(1)} %add.43), channel_id=1, source_target_pairs={{0,6},{1,7},{2,4},{3,5},{4,2},{5,3},{6,0},{7,1},{8,14},{9,15},{10,... | collective-permute-start | bytes 12296 | tf_op jit(solution)/shard_map/ppermute | solution.py:360
  30.4 2.5 %collective-permute-done.13 = f32[8,128]{1,0:T(8,128)S(1)} collective-permute-done((f32[8,128]{1,0:T(8,128)S(1)}, f32[8,128]{1,0:T(8,128)S(1)}, u32[]{:S(2)}, u32[]{:S(2)}) %collective-permute-start.13) | collective-permute-done | bytes 4128 | tf_op jit(solution)/shard_map/ppermute | solution.py:360
  36.4 3.5 %collective-permute-start.5 = (f32[64,1024]{1,0:T(8,128)S(1)}, f32[64,1024]{1,0:T(8,128)S(1)}, u32[]{:S(2)}, u32[]{:S(2)}) collective-permute-start(f32[64,1024]{1,0:T(8,128)S(1)} %get-tuple-element.67), channel_id=1, source_target_pairs={{8,16},{16,8},{24,32},{32,24},{40,48},{48,40},{56,64},{64,56},{72,... | collective-permute-start | bytes 786440 | tf_op jit(solution)/shard_map/ppermute | solution.py:349
  40.0 2.4 %shard_map.65 = (bf16[2,384,1024]{2,1,0:T(8,128)(2,1)S(1)}, bf16[2,384,1024]{2,1,0:T(8,128)(2,1)S(1)}, f32[2,128,1024]{2,1,0:T(8,128)S(1)}) custom-call(f32[512,1024]{1,0:T(8,128)S(1)} %get-tuple-element.70.refs_0_, bf16[512,1024]{1,0:T(8,128)(2,1)S(1)} %get-tuple-element.71.refs_1_, bf16[5,384,768]{2,1,0:T(8,128)(2,1)S(1)} %get-tuple-element.53.refs_1_.refs_2_), custom_call_target="tpu_custom_call" | custom-call | flops 2000000000 | bytes 4194304 | tf_op jit(solution)/shard_map/pallas_call | solution.py:27
  45.3 2.4 %shard_map.64 = (bf16[2,384,1024]{2,1,0:T(8,128)(2,1)S(1)}, bf16[2,384,1024]{2,1,0:T(8,128)(2,1)S(1)}, f32[2,128,1024]{2,1,0:T(8,128)S(1)}) custom-call(f32[512,1024]{1,0:T(8,128)S(1)} %get-tuple-element.70.refs_0_, bf16[512,1024]{1,0:T(8,128)(2,1)S(1)} %get-tuple-element.71.refs_1_, bf16[5,384,768]{2,1,0:T(8,128)(2,1)S(1)} %get-tuple-element.53.refs_1_.refs_2_), custom_call_target="tpu_custom_call" | custom-call | flops 2000000000 | bytes 4194304 | tf_op jit(solution)/shard_map/pallas_call | solution.py:27
  48.1 2.2 %shard_map.66 = (bf16[4,128,1024]{2,1,0:T(8,128)(2,1)S(1)}, bf16[4,128,1024]{2,1,0:T(8,128)(2,1)S(1)}, f32[512,256]{1,0:T(8,128)S(1)}, f32[512,128]{1,0:T(8,128)...) custom-call(f32[64,1024]{1,0:T(8,128)S(1)} %collective-permute-done.4.refs_0_, ...), custom_call_target="tpu_custom_call" | custom-call | flops 2000000000 | bytes 4194304 | tf_op jit(solution)/shard_map/pallas_call | solution.py:27
  50.3 5.1 %collective-permute-start.8 = (f32[256,128]{1,0:T(8,128)S(1)}, f32[256,128]{1,0:T(8,128)S(1)}, u32[]{:S(2)}, u32[]{:S(2)}) collective-permute-start(f32[256,128]{1,0:T(8,128)S(1)} %get-tuple-element.82), channel_id=1, source_target_pairs={{0,1},{1,0},{2,3},{3,2},{4,5},{5,4},{6,7},{7,6},{8,9},{9,8},{10,11... | collective-permute-start | bytes 393224 | tf_op jit(solution)/shard_map/ppermute | solution.py:349
  55.4 2.0 %shard_map.68.refs_2_ = f32[256,768]{1,0:T(8,128)S(1)} custom-call(bf16[2,384,1024]{2,1,0:T(8,128)(2,1)S(1)} %get-tuple-element.74.refs_6_.refs_0_, bf16[2,384,1024]{2,1,0:T(8,128)(2,1)S(1)} %get-tuple-element.75.refs_7_.refs_1_, bf16[2,384,1024]{2,1,0:T(8,128)(2,1)S(1)} %get-tuple-element.76.refs_8_.refs_2_, ...), custom_call_target="tpu_custom_call" | custom-call | flops 1500000000 | bytes 4194304 | tf_op jit(solution)/shard_map/pallas_call | solution.py:27
  57.4 2.0 %shard_map.67.refs_1_ = f32[256,768]{1,0:T(8,128)S(1)} custom-call(bf16[2,384,1024]{2,1,0:T(8,128)(2,1)S(1)} %get-tuple-element.74.refs_6_.refs_0_, bf16[2,384,1024]{2,1,0:T(8,128)(2,1)S(1)} %get-tuple-element.75.refs_7_.refs_1_, bf16[2,384,1024]{2,1,0:T(8,128)(2,1)S(1)} %get-tuple-element.76.refs_8_.refs_2_, ...), custom_call_target="tpu_custom_call" | custom-call | flops 1500000000 | bytes 4194304 | tf_op jit(solution)/shard_map/pallas_call | solution.py:27
  61.9 2.5 %collective-permute-start.21 = (f32[8,128]{1,0:T(8,128)S(1)}, f32[8,128]{1,0:T(8,128)S(1)}, u32[]{:S(2)}, u32[]{:S(2)}) collective-permute-start(f32[8,128]{1,0:T(8,128)S(1)} %get-tuple-element.101), channel_id=1, source_target_pairs={{0,1},{1,0},{2,3},{3,2},{4,5},{5,4},{6,7},{7,6},{8,9},{9,8},{10,11... | collective-permute-start | bytes 12296 | tf_op jit(solution)/shard_map/ppermute | solution.py:360
  65.3 2.5 %collective-permute-done.22 = f32[8,128]{1,0:T(8,128)S(1)} collective-permute-done((f32[8,128]{1,0:T(8,128)S(1)}, f32[8,128]{1,0:T(8,128)S(1)}, u32[]{:S(2)}, u32[]{:S(2)}) %collective-permute-start.22) | collective-permute-done | bytes 4128 | tf_op jit(solution)/shard_map/ppermute | solution.py:360
  69.2 2.1 %collective-permute-done.23 = f32[8,128]{1,0:T(8,128)S(1)} collective-permute-done((f32[8,128]{1,0:T(8,128)S(1)}, f32[8,128]{1,0:T(8,128)S(1)}, u32[]{:S(2)}, u32[]{:S(2)}) %collective-permute-start.23) | collective-permute-done | bytes 4128 | tf_op jit(solution)/shard_map/ppermute | solution.py:360
  71.5 2.4 %collective-permute-done.24 = f32[8,128]{1,0:T(8,128)S(1)} collective-permute-done((f32[8,128]{1,0:T(8,128)S(1)}, f32[8,128]{1,0:T(8,128)S(1)}, u32[]{:S(2)}, u32[]{:S(2)}) %collective-permute-start.24) | collective-permute-done | bytes 4128 | tf_op jit(solution)/shard_map/ppermute | solution.py:360
  73.9 1.9 %collective-permute-start.25 = (f32[8,128]{1,0:T(8,128)S(1)}, f32[8,128]{1,0:T(8,128)S(1)}, u32[]{:S(2)}, u32[]{:S(2)}) collective-permute-start(f32[8,128]{1,0:T(8,128)S(1)} %add.52), channel_id=1, source_target_pairs={{0,96},{8,104},{16,112},{24,120},{32,64},{40,72},{48,80},{56,88},{... | collective-permute-start | bytes 12296 | tf_op jit(solution)/shard_map/ppermute | solution.py:360
  78.0 2.4 %shard_map.71 = (bf16[2,384,1024]{2,1,0:T(8,128)(2,1)S(1)}, bf16[2,384,1024]{2,1,0:T(8,128)(2,1)S(1)}, f32[2,128,1024]{2,1,0:T(8,128)S(1)}) custom-call(f32[512,1024]{1,0:T(8,128)S(1)} %get-tuple-element.88.refs_0_, bf16[512,1024]{1,0:T(8,128)(2,1)S(1)} %get-tuple-element.71.refs_1_, bf16[5,384,768]{2,1,0:T(8,128)(2,1)S(1)} %get-tuple-element.53.refs_1_.refs_2_), custom_call_target="tpu_custom_call" | custom-call | flops 2000000000 | bytes 4194304 | tf_op jit(solution)/shard_map/pallas_call | solution.py:27
  82.1 2.4 %shard_map.70 = (bf16[2,384,1024]{2,1,0:T(8,128)(2,1)S(1)}, bf16[2,384,1024]{2,1,0:T(8,128)(2,1)S(1)}, f32[2,128,1024]{2,1,0:T(8,128)S(1)}) custom-call(f32[512,1024]{1,0:T(8,128)S(1)} %get-tuple-element.88.refs_0_, bf16[512,1024]{1,0:T(8,128)(2,1)S(1)} %get-tuple-element.71.refs_1_, bf16[5,384,768]{2,1,0:T(8,128)(2,1)S(1)} %get-tuple-element.53.refs_1_.refs_2_), custom_call_target="tpu_custom_call" | custom-call | flops 2000000000 | bytes 4194304 | tf_op jit(solution)/shard_map/pallas_call | solution.py:27
  84.8 2.2 %shard_map.72 = (bf16[4,128,1024]{2,1,0:T(8,128)(2,1)S(1)}, bf16[4,128,1024]{2,1,0:T(8,128)(2,1)S(1)}, f32[512,256]{1,0:T(8,128)S(1)}, f32[512,128]{1,0:T(8,128)...) custom-call(f32[64,1024]{1,0:T(8,128)S(1)} %collective-permute-done.17.refs_0_, ...), custom_call_target="tpu_custom_call" | custom-call | flops 2000000000 | bytes 4194304 | tf_op jit(solution)/shard_map/pallas_call | solution.py:27
  86.9 6.5 %collective-permute-start.19 = (f32[256,128]{1,0:T(8,128)S(1)}, f32[256,128]{1,0:T(8,128)S(1)}, u32[]{:S(2)}, u32[]{:S(2)}) collective-permute-start(f32[256,128]{1,0:T(8,128)S(1)} %get-tuple-element.99), channel_id=1, source_target_pairs={{0,1},{1,0},{2,3},{3,2},{4,5},{5,4},{6,7},{7,6},{8,9},{9,8},{10,11... | collective-permute-start | bytes 393224 | tf_op jit(solution)/shard_map/ppermute | solution.py:349
  93.4 2.0 %shard_map.74.refs_2_ = f32[256,768]{1,0:T(8,128)S(1)} custom-call(bf16[2,384,1024]{2,1,0:T(8,128)(2,1)S(1)} %get-tuple-element.91.refs_6_.refs_0_, bf16[2,384,1024]{2,1,0:T(8,128)(2,1)S(1)} %get-tuple-element.92.refs_7_.refs_1_, bf16[2,384,1024]{2,1,0:T(8,128)(2,1)S(1)} %get-tuple-element.93.refs_8_.refs_2_, ...), custom_call_target="tpu_custom_call" | custom-call | flops 1500000000 | bytes 4194304 | tf_op jit(solution)/shard_map/pallas_call | solution.py:27
  95.4 2.0 %shard_map.73.refs_1_ = f32[256,768]{1,0:T(8,128)S(1)} custom-call(bf16[2,384,1024]{2,1,0:T(8,128)(2,1)S(1)} %get-tuple-element.91.refs_6_.refs_0_, bf16[2,384,1024]{2,1,0:T(8,128)(2,1)S(1)} %get-tuple-element.92.refs_7_.refs_1_, bf16[2,384,1024]{2,1,0:T(8,128)(2,1)S(1)} %get-tuple-element.93.refs_8_.refs_2_, ...), custom_call_target="tpu_custom_call" | custom-call | flops 1500000000 | bytes 4194304 | tf_op jit(solution)/shard_map/pallas_call | solution.py:27
  (66 shorter events, 30.6 us)
Async XLA Ops:
  1.8 11.7 %collective-permute-start.1 = (f32[32,1024]{1,0:T(8,128)S(1)}, f32[32,1024]{1,0:T(8,128)S(1)}, u32[]{:S(2)}, u32[]{:S(2)}) collective-permute-start(f32[32,1024]{1,0:T(8,128)S(1)} %get-tuple-element.102), channel_id=1, source_target_pairs={{8,16},{16,8},{24,32},{32,24},{40,48},{48,40},{56,64},{64,56},{72,... | collective-permute-start | bytes 393224 | tf_op jit(solution)/shard_map/ppermute | solution.py:349
  7.6 5.8 %collective-permute-start = (f32[32,1024]{1,0:T(8,128)S(1)}, f32[32,1024]{1,0:T(8,128)S(1)}, u32[]{:S(2)}, u32[]{:S(2)}) collective-permute-start(f32[32,1024]{1,0:T(8,128)S(1)} %get-tuple-element.103), channel_id=1, source_target_pairs={{0,8},{8,0},{16,24},{24,16},{32,40},{40,32},{48,56},{56,48},{64,72... | collective-permute-start | bytes 393224 | tf_op jit(solution)/shard_map/ppermute | solution.py:349
  14.2 4.0 %collective-permute-start.2 = (f32[256,128]{1,0:T(8,128)S(1)}, f32[256,128]{1,0:T(8,128)S(1)}, u32[]{:S(2)}, u32[]{:S(2)}) collective-permute-start(f32[256,128]{1,0:T(8,128)S(1)} %get-tuple-element.64), channel_id=1, source_target_pairs={{0,1},{1,0},{2,3},{3,2},{4,5},{5,4},{6,7},{7,6},{8,9},{9,8},{10,11... | collective-permute-start | bytes 393224 | tf_op jit(solution)/shard_map/ppermute | solution.py:349
  15.2 4.4 %collective-permute-start.3 = (f32[256,128]{1,0:T(8,128)S(1)}, f32[256,128]{1,0:T(8,128)S(1)}, u32[]{:S(2)}, u32[]{:S(2)}) collective-permute-start(f32[256,128]{1,0:T(8,128)S(1)} %get-tuple-element.65), channel_id=1, source_target_pairs={{1,2},{2,1},{3,4},{4,3},{5,6},{6,5},{7,0},{0,7},{9,10},{10,9},{11,... | collective-permute-start | bytes 393224 | tf_op jit(solution)/shard_map/ppermute | solution.py:349
  20.7 3.3 %collective-permute-start.10 = (f32[8,128]{1,0:T(8,128)S(1)}, f32[8,128]{1,0:T(8,128)S(1)}, u32[]{:S(2)}, u32[]{:S(2)}) collective-permute-start(f32[8,128]{1,0:T(8,128)S(1)} %get-tuple-element.84), channel_id=1, source_target_pairs={{0,1},{1,0},{2,3},{3,2},{4,5},{5,4},{6,7},{7,6},{8,9},{9,8},{10,11... | collective-permute-start | bytes 12296 | tf_op jit(solution)/shard_map/ppermute | solution.py:360
  26.5 3.9 %collective-permute-start.12 = (f32[8,128]{1,0:T(8,128)S(1)}, f32[8,128]{1,0:T(8,128)S(1)}, u32[]{:S(2)}, u32[]{:S(2)}) collective-permute-start(f32[8,128]{1,0:T(8,128)S(1)} %add.43), channel_id=1, source_target_pairs={{0,6},{1,7},{2,4},{3,5},{4,2},{5,3},{6,0},{7,1},{8,14},{9,15},{10,... | collective-permute-start | bytes 12296 | tf_op jit(solution)/shard_map/ppermute | solution.py:360
  32.9 7.1 %collective-permute-start.14 = (f32[8,128]{1,0:T(8,128)S(1)}, f32[8,128]{1,0:T(8,128)S(1)}, u32[]{:S(2)}, u32[]{:S(2)}) collective-permute-start(f32[8,128]{1,0:T(8,128)S(1)} %add.45), channel_id=1, source_target_pairs={{0,96},{8,104},{16,112},{24,120},{32,64},{40,72},{48,80},{56,88},{... | collective-permute-start | bytes 12296 | tf_op jit(solution)/shard_map/ppermute | solution.py:360
  33.4 14.7 %collective-permute-start.6 = (s32[64,1024]{1,0:T(8,128)S(1)}, s32[64,1024]{1,0:T(8,128)S(1)}, u32[]{:S(2)}, u32[]{:S(2)}) collective-permute-start(s32[64,1024]{1,0:T(8,128)S(1)} %get-tuple-element.68), channel_id=1, source_target_pairs={{0,8},{8,0},{16,24},{24,16},{32,40},{40,32},{48,56},{56,48},{64,72... | collective-permute-start | bytes 786440 | tf_op jit(solution)/shard_map/ppermute | solution.py:349
  35.2 12.9 %collective-permute-start.7 = (s32[64,1024]{1,0:T(8,128)S(1)}, s32[64,1024]{1,0:T(8,128)S(1)}, u32[]{:S(2)}, u32[]{:S(2)}) collective-permute-start(s32[64,1024]{1,0:T(8,128)S(1)} %get-tuple-element.69), channel_id=1, source_target_pairs={{8,16},{16,8},{24,32},{32,24},{40,48},{48,40},{56,64},{64,56},{72,... | collective-permute-start | bytes 786440 | tf_op jit(solution)/shard_map/ppermute | solution.py:349
  35.7 12.4 %collective-permute-start.4 = (f32[64,1024]{1,0:T(8,128)S(1)}, f32[64,1024]{1,0:T(8,128)S(1)}, u32[]{:S(2)}, u32[]{:S(2)}) collective-permute-start(f32[64,1024]{1,0:T(8,128)S(1)} %get-tuple-element.66), channel_id=1, source_target_pairs={{0,8},{8,0},{16,24},{24,16},{32,40},{40,32},{48,56},{56,48},{64,72... | collective-permute-start | bytes 786440 | tf_op jit(solution)/shard_map/ppermute | solution.py:349
  36.4 11.7 %collective-permute-start.5 = (f32[64,1024]{1,0:T(8,128)S(1)}, f32[64,1024]{1,0:T(8,128)S(1)}, u32[]{:S(2)}, u32[]{:S(2)}) collective-permute-start(f32[64,1024]{1,0:T(8,128)S(1)} %get-tuple-element.67), channel_id=1, source_target_pairs={{8,16},{16,8},{24,32},{32,24},{40,48},{48,40},{56,64},{64,56},{72,... | collective-permute-start | bytes 786440 | tf_op jit(solution)/shard_map/ppermute | solution.py:349
  40.0 3.7 %collective-permute-start.15 = (f32[8,128]{1,0:T(8,128)S(1)}, f32[8,128]{1,0:T(8,128)S(1)}, u32[]{:S(2)}, u32[]{:S(2)}) collective-permute-start(f32[8,128]{1,0:T(8,128)S(1)} %add.46), channel_id=1, source_target_pairs={{0,8},{8,0},{16,24},{24,16},{32,40},{40,32},{48,56},{56,48},{64,72... | collective-permute-start | bytes 12296 | tf_op jit(solution)/shard_map/ppermute | solution.py:360
  43.7 4.4 %collective-permute-start.16 = (f32[8,128]{1,0:T(8,128)S(1)}, f32[8,128]{1,0:T(8,128)S(1)}, u32[]{:S(2)}, u32[]{:S(2)}) collective-permute-start(f32[8,128]{1,0:T(8,128)S(1)} %add.47), channel_id=1, source_target_pairs={{0,24},{8,16},{16,8},{24,0},{32,56},{40,48},{48,40},{56,32},{64,88... | collective-permute-start | bytes 12296 | tf_op jit(solution)/shard_map/ppermute | solution.py:360
  50.3 9.1 %collective-permute-start.8 = (f32[256,128]{1,0:T(8,128)S(1)}, f32[256,128]{1,0:T(8,128)S(1)}, u32[]{:S(2)}, u32[]{:S(2)}) collective-permute-start(f32[256,128]{1,0:T(8,128)S(1)} %get-tuple-element.82), channel_id=1, source_target_pairs={{0,1},{1,0},{2,3},{3,2},{4,5},{5,4},{6,7},{7,6},{8,9},{9,8},{10,11... | collective-permute-start | bytes 393224 | tf_op jit(solution)/shard_map/ppermute | solution.py:349
  55.4 4.7 %collective-permute-start.9 = (f32[256,128]{1,0:T(8,128)S(1)}, f32[256,128]{1,0:T(8,128)S(1)}, u32[]{:S(2)}, u32[]{:S(2)}) collective-permute-start(f32[256,128]{1,0:T(8,128)S(1)} %get-tuple-element.83), channel_id=1, source_target_pairs={{1,2},{2,1},{3,4},{4,3},{5,6},{6,5},{7,0},{0,7},{9,10},{10,9},{11,... | collective-permute-start | bytes 393224 | tf_op jit(solution)/shard_map/ppermute | solution.py:349
  61.9 3.3 %collective-permute-start.21 = (f32[8,128]{1,0:T(8,128)S(1)}, f32[8,128]{1,0:T(8,128)S(1)}, u32[]{:S(2)}, u32[]{:S(2)}) collective-permute-start(f32[8,128]{1,0:T(8,128)S(1)} %get-tuple-element.101), channel_id=1, source_target_pairs={{0,1},{1,0},{2,3},{3,2},{4,5},{5,4},{6,7},{7,6},{8,9},{9,8},{10,11... | collective-permute-start | bytes 12296 | tf_op jit(solution)/shard_map/ppermute | solution.py:360
  67.7 3.7 %collective-permute-start.23 = (f32[8,128]{1,0:T(8,128)S(1)}, f32[8,128]{1,0:T(8,128)S(1)}, u32[]{:S(2)}, u32[]{:S(2)}) collective-permute-start(f32[8,128]{1,0:T(8,128)S(1)} %add.50), channel_id=1, source_target_pairs={{0,6},{1,7},{2,4},{3,5},{4,2},{5,3},{6,0},{7,1},{8,14},{9,15},{10,... | collective-permute-start | bytes 12296 | tf_op jit(solution)/shard_map/ppermute | solution.py:360
  73.9 4.1 %collective-permute-start.25 = (f32[8,128]{1,0:T(8,128)S(1)}, f32[8,128]{1,0:T(8,128)S(1)}, u32[]{:S(2)}, u32[]{:S(2)}) collective-permute-start(f32[8,128]{1,0:T(8,128)S(1)} %add.52), channel_id=1, source_target_pairs={{0,96},{8,104},{16,112},{24,120},{32,64},{40,72},{48,80},{56,88},{... | collective-permute-start | bytes 12296 | tf_op jit(solution)/shard_map/ppermute | solution.py:360
  75.8 8.9 %collective-permute-start.17 = (f32[64,1024]{1,0:T(8,128)S(1)}, f32[64,1024]{1,0:T(8,128)S(1)}, u32[]{:S(2)}, u32[]{:S(2)}) collective-permute-start(f32[64,1024]{1,0:T(8,128)S(1)} %get-tuple-element.86), channel_id=1, source_target_pairs={{0,8},{8,0},{16,24},{24,16},{32,40},{40,32},{48,56},{56,48},{64,72... | collective-permute-start | bytes 786440 | tf_op jit(solution)/shard_map/ppermute | solution.py:349
  76.1 8.7 %collective-permute-start.18 = (f32[64,1024]{1,0:T(8,128)S(1)}, f32[64,1024]{1,0:T(8,128)S(1)}, u32[]{:S(2)}, u32[]{:S(2)}) collective-permute-start(f32[64,1024]{1,0:T(8,128)S(1)} %get-tuple-element.87), channel_id=1, source_target_pairs={{8,16},{16,8},{24,32},{32,24},{40,48},{48,40},{56,64},{64,56},{72,... | collective-permute-start | bytes 786440 | tf_op jit(solution)/shard_map/ppermute | solution.py:349
  78.0 3.1 %collective-permute-start.26 = (f32[8,128]{1,0:T(8,128)S(1)}, f32[8,128]{1,0:T(8,128)S(1)}, u32[]{:S(2)}, u32[]{:S(2)}) collective-permute-start(f32[8,128]{1,0:T(8,128)S(1)} %add.53), channel_id=1, source_target_pairs={{0,8},{8,0},{16,24},{24,16},{32,40},{40,32},{48,56},{56,48},{64,72... | collective-permute-start | bytes 12296 | tf_op jit(solution)/shard_map/ppermute | solution.py:360
  81.1 3.7 %collective-permute-start.27 = (f32[8,128]{1,0:T(8,128)S(1)}, f32[8,128]{1,0:T(8,128)S(1)}, u32[]{:S(2)}, u32[]{:S(2)}) collective-permute-start(f32[8,128]{1,0:T(8,128)S(1)} %add.54), channel_id=1, source_target_pairs={{0,24},{8,16},{16,8},{24,0},{32,56},{40,48},{48,40},{56,32},{64,88... | collective-permute-start | bytes 12296 | tf_op jit(solution)/shard_map/ppermute | solution.py:360
  86.9 10.5 %collective-permute-start.19 = (f32[256,128]{1,0:T(8,128)S(1)}, f32[256,128]{1,0:T(8,128)S(1)}, u32[]{:S(2)}, u32[]{:S(2)}) collective-permute-start(f32[256,128]{1,0:T(8,128)S(1)} %get-tuple-element.99), channel_id=1, source_target_pairs={{0,1},{1,0},{2,3},{3,2},{4,5},{5,4},{6,7},{7,6},{8,9},{9,8},{10,11... | collective-permute-start | bytes 393224 | tf_op jit(solution)/shard_map/ppermute | solution.py:349
  93.4 4.7 %collective-permute-start.20 = (f32[256,128]{1,0:T(8,128)S(1)}, f32[256,128]{1,0:T(8,128)S(1)}, u32[]{:S(2)}, u32[]{:S(2)}) collective-permute-start(f32[256,128]{1,0:T(8,128)S(1)} %get-tuple-element.100), channel_id=1, source_target_pairs={{1,2},{2,1},{3,4},{4,3},{5,6},{6,5},{7,0},{0,7},{9,10},{10,9},{11,... | collective-permute-start | bytes 393224 | tf_op jit(solution)/shard_map/ppermute | solution.py:349
  (5 other events, 10.5 us)

commit v3 on v2

--- a/solution.py
+++ b/solution.py
@@ -67,61 +67,94 @@
     return [jnp.full((1, 1), value.astype(F32), F32) for value in values]
 
 
-def fill_bands(radius_ref, high_ref, low_ref, stack_ref, rim_ref):
+def fill_bands(slot, radius, high_ref, low_ref, stack_ref, rim_ref):
+    radius = jnp.full((1, 1), radius, F32)
+    inverse = 1.0 / (2.0 * (0.5 * radius) * (0.5 * radius))
+
+    def shape_of(d):
+        return jnp.where(jnp.abs(d) <= radius, jnp.exp(-(d * d) * inverse), 0.0)
+
     lane = iota((8, 128), 1).astype(F32)
     tap = jnp.where(iota((8, 128), 0) == 0, jnp.where(lane == 0, 1.0, 2.0), 0.0)
-    shift = (iota((BAND, TILE), 0) - REACH - iota((BAND, TILE), 1)).astype(F32)
-    row, column = iota((128, 128), 0), iota((128, 128), 1)
-    upper = row < 64
-    same = upper == (column < 64)
-    rim_shift = (row - column + jnp.where(upper, REACH, -REACH)).astype(F32)
-    for c in range(CLASSES + 1):
-        radius = F32(PILOT_RADIUS) if c == CLASSES else radius_ref[c].astype(F32)
-        radius = jnp.full((1, 1), radius, F32)
-        inverse = 1.0 / (2.0 * (0.5 * radius) * (0.5 * radius))
-
-        def shape_of(d):
-            return jnp.where(jnp.abs(d) <= radius, jnp.exp(-(d * d) * inverse), 0.0)
-
-        total = jnp.sum(shape_of(lane) * tap, axis=(0, 1), keepdims=True)
-        high, low = split(shape_of(shift) / total)
-        high_ref[c * BAND : (c + 1) * BAND, :] = high
-        low_ref[c * BAND : (c + 1) * BAND, :] = low
-        stack_ref[c, :, 0:TILE] = high
-        stack_ref[c, :, TILE : 2 * TILE] = low
-        stack_ref[c, :, 2 * TILE :] = high
-        high, low = split(jnp.where(same, shape_of(rim_shift) / total, 0.0))
-        rim_ref[c, :, 0:128] = high
-        rim_ref[c, :, 128:256] = high
-        rim_ref[c, :, 256:384] = low
+    total = jnp.sum(shape_of(lane) * tap, axis=(0, 1), keepdims=True)
+    column = iota((128, 128), 1)
+    shift = iota((128, 128), 0) - column
+    near = split(shape_of((shift - REACH).astype(F32)) / total)
+    far = split(shape_of((shift + REACH).astype(F32)) / total)
+    zero = jnp.zeros((128, 128), BF16)
+    side = column[:REACH] < REACH
+    zeros = jnp.zeros((REACH, 128), F32)
+    base = slot * BAND
+    for part, ref in enumerate((high_ref, low_ref)):
+        blocks = ((near[part], zero), (far[part], near[part]), (zero, far[part]))
+        for i, pair in enumerate(blocks):
+            for k, block in enumerate(pair):
+                lanes = slice(k * 128, (k + 1) * 128)
+                ref[base + i * 128 : base + (i + 1) * 128, lanes] = block
+                places = (0, 2 * TILE) if part == 0 else (TILE,)
+                for place in places:
+                    shifted = slice(place + k * 128, place + (k + 1) * 128)
+                    stack_ref[slot, i * 128 : (i + 1) * 128, shifted] = block
+        first = jnp.where(side, far[part][:REACH].astype(F32), zeros).astype(BF16)
+        second = jnp.where(side, zeros, near[part][REACH:].astype(F32)).astype(BF16)
+        for place in (0, 128) if part == 0 else (256,):
+            rim_ref[slot, :REACH, place : place + 128] = first
+            rim_ref[slot, REACH:, place : place + 128] = second
+
+
+CHUNK = 128
 
 
 def prepare_kernel(*refs):
-    (radius_ref, *fields), tables, outs, scratch = take(refs, 4, 4, 4)
-    mass_ref, label_ref, send_a, send_b = outs
-    *local, arrived = scratch
-    copies = [
-        pltpu.make_async_copy(field, kept, arrived.at[n])
-        for n, (field, kept) in enumerate(zip(fields, local))
+    (counts_in, weights_in, classes_in), tables, outs, scratch = take(refs, 3, 4, 5)
+    mass_ref, mass_a, mass_b, label_a, label_b = outs
+    counts, weights, ends, arrived, ended = scratch
+    rows = counts.shape[0]
+    copies = []
+    for n, start in enumerate(range(0, rows, CHUNK)):
+        at = slice(start, start + CHUNK)
+        pair = [
+            pltpu.make_async_copy(counts_in.at[at], counts.at[at], arrived.at[0, n]),
+            pltpu.make_async_copy(weights_in.at[at], weights.at[at], arrived.at[1, n]),
+        ]
+        for copy in pair:
+            copy.start()
+        copies.append((at, pair))
+    end_copies = [
+        pltpu.make_async_copy(classes_in.at[0:REACH], ends.at[0], ended.at[0]),
+        pltpu.make_async_copy(classes_in.at[rows - REACH : rows], ends.at[1], ended.at[1]),
     ]
-    for copy in copies:
+    for copy in end_copies:
         copy.start()
-    fill_bands(radius_ref, *tables)
-    counts, weights, classes = local
-    copies[0].wait()
-    copies[1].wait()
-    rows = counts.shape[0]
-    for start in range(0, rows, STEP):
-        at = slice(start, start + STEP)
+    fill_bands(0, F32(PILOT_RADIUS), *tables)
+    for at, pair in copies:
+        for copy in pair:
+            copy.wait()
         mass_ref[at] = counts[at].astype(F32) * weights[at]
-    copies[2].wait()
-    for start in range(0, rows, STEP):
-        at = slice(start, start + STEP)
+    odd = flags_of("row")[0]
+    top, bottom = mass_ref[0:PILOT_RADIUS], mass_ref[rows - PILOT_RADIUS :]
+    mass_a[...] = chosen(odd, top, bottom)
+    mass_b[...] = chosen(odd, bottom, top)
+    for copy in end_copies:
+        copy.wait()
+    label_a[...] = chosen(odd, ends[0], ends[1])
+    label_b[...] = chosen(odd, ends[1], ends[0])
+
+
+def bands_kernel(*refs):
+    (radius_ref, classes_in), tables, (label_ref, classes, arrived) = take(refs, 2, 4)
+    rows = classes.shape[0]
+    copies = []
+    for n, start in enumerate(range(0, rows, CHUNK)):
+        at = slice(start, start + CHUNK)
+        copy = pltpu.make_async_copy(classes_in.at[at], classes.at[at], arrived.at[n])
+        copy.start()
+        copies.append((at, copy))
+    for c in range(CLASSES):
+        fill_bands(c, radius_ref[c].astype(F32), *tables)
+    for at, copy in copies:
+        copy.wait()
         label_ref[at] = classes[at].astype(F32).astype(BF16)
-    odd = flags_of("row")[0]
-    top, bottom = classes[0:REACH], classes[rows - REACH :]
-    send_a[...] = chosen(odd, top, bottom)
-    send_b[...] = chosen(odd, bottom, top)
 
 
 def masked(pieces, labels, c):
@@ -131,8 +164,13 @@
     return [jnp.where(keep, piece, jnp.zeros_like(piece)) for piece in pieces]
 
 
-def rows_kernel(*refs, bands, labelled):
-    (field_ref,), label_refs, (stack_ref, high_ref, low_ref, edge_ref) = take(refs, 1, labelled)
+def rows_kernel(*refs, bands, labelled, carried):
+    (field_ref,), label_refs, (stack_ref,), plane, (high_ref, low_ref, edge_ref), plane_out, done = (
+        take(refs, 1, labelled, 1, carried, 3, carried)
+    )
+    copies = [pltpu.make_async_copy(*pair) for pair in zip(plane, plane_out, done)]
+    for copy in copies:
+        copy.start()
     _, columns = field_ref.shape
     for n in range(columns // TILE):
         at = slice(n * TILE, (n + 1) * TILE)
@@ -158,6 +196,8 @@
                 value_high, value_low = split(value)
                 high_ref[slot, target : target + value.shape[0], at] = value_high
                 low_ref[slot, target : target + value.shape[0], at] = value_low
+    for copy in copies:
+        copy.wait()
 
 
 def kept_row(start, rows):
@@ -294,13 +334,14 @@
 
 
 def finish_kernel(*refs, middles, scaled, following, totals):
+    leaving = scaled and not following
     (left_ref,), middle_refs, (right_ref,), come, refs = take(refs, 1, middles, 1, 2)
     pieces = (left_ref, middle_refs, right_ref)
     totals_in, mass_in, density_out, refs = take(refs, 2 * scaled, following, scaled)
     adapted_out, refs = take(refs, 4 * following)
     if scaled:
         inverse = jnp.exp(-(totals_in[0][0:1, :] / totals_in[1][1:2, :]))
-        staged, done = refs
+    staged, done = refs if leaving else (density_out[0] if scaled else None, None)
     rows = left_ref.shape[0]
     column_flags = flags_of("col")
     log_sum = jnp.zeros((8, 128), F32)
@@ -321,7 +362,7 @@
                 log_sum += jnp.sum(terms.reshape(STEP // 8, 8, 128), axis=0)
                 if totals:
                     mass_sum += jnp.sum(mass.reshape(STEP // 8, 8, 128), axis=0)
-        if scaled:
+        if leaving:
             copy = pltpu.make_async_copy(staged.at[at], density_out[0].at[at], done.at[number])
             copy.start()
             copies.append(copy)
@@ -340,13 +381,21 @@
 
 
 def exchange(first, second, axis):
+    along = 0 if axis == "row" else 1
+    sizes = [lax.axis_size("row"), lax.axis_size("col")]
     results = []
-    count = lax.axis_size(axis)
     for offset, value in ((0, first), (1, second)):
         pairs = []
-        for i in range(offset, count, 2):
-            pairs += [(i, (i + 1) % count), ((i + 1) % count, i)]
-        results.append(lax.ppermute(value, axis, pairs))
+        for index in range(sizes[0] * sizes[1]):
+            place = [index // sizes[1], index % sizes[1]]
+            own = place[along]
+            partner = own + 1 if own % 2 == offset else own - 1
+            if 0 <= partner < sizes[along]:
+                place[along] = partner
+            else:
+                place[1 - along] ^= 1
+            pairs.append((index, place[0] * sizes[1] + place[1]))
+        results.append(lax.ppermute(value, ("row", "col"), pairs))
     return results
 
 
@@ -361,21 +410,28 @@
     return stat
 
 
-def smooth(field, halo, labels, label_halo, tables, groups, cuts):
+def smooth(field, halo, labels, label_halo, tables, groups, cuts, leaving=()):
     high, low, stack, rim = tables
     rows, columns = field.shape
     labelled = labels is not None
     bands = [c for group in groups for c in group]
     highs, lows, partials = [], [], []
-    for group in groups:
+    for number, group in enumerate(groups):
         inner = (len(group), rows - 2 * REACH, columns)
         edge = (len(group), 2 * REACH, columns)
+        carried = len(leaving) if number == 0 else 0
         results = call(
-            functools.partial(rows_kernel, bands=group, labelled=labelled),
-            [(inner, BF16), (inner, BF16), (edge, F32)],
-            [field] + ([labels] if labelled else []) + [stack],
+            functools.partial(
+                rows_kernel, bands=group, labelled=labelled, carried=carried
+            ),
+            [(inner, BF16), (inner, BF16), (edge, F32)] + [(field.shape, F32)] * carried,
+            [field] + ([labels] if labelled else []) + [stack, *leaving[:carried]],
+            out_specs=[VMEM] * 3 + [HBM] * carried,
+            scratch=[pltpu.SemaphoreType.DMA] * carried,
             flops=len(group) * 1_000_000_000,
         )
+        if carried:
+            left_behind = results[3]
         for results_of, result in zip((highs, lows, partials), results):
             results_of.append(result)
     edge = (len(bands), 2 * REACH, columns)
@@ -396,14 +452,16 @@
             [*highs, *lows, edge_high, edge_low, high, low],
             flops=len(bands) * 750_000_000 // cuts,
         )
-    return [left, *middles, right, *come]
+    pieces = [left, *middles, right, *come]
+    return (pieces, left_behind) if leaving else pieces
 
 
 def finish(pieces, extra, scaled, following, totals, shape):
     plane, rim, stat = (shape, F32), ((REACH, shape[1]), F32), ((8, 128), F32)
     outs = [plane] * scaled + [plane, rim, rim, stat] * following
     scratch = []
-    if scaled:
+    leaving = scaled and not following
+    if leaving:
         scratch = [pltpu.VMEM(shape, F32), pltpu.SemaphoreType.DMA((shape[0] // STEP,))]
     return call(
         functools.partial(
@@ -415,56 +473,56 @@
         ),
         outs,
         [*pieces, *extra],
-        out_specs=[HBM] * scaled + [VMEM] * (4 * following),
+        out_specs=[HBM if leaving else VMEM] * scaled + [VMEM] * (4 * following),
         scratch=scratch,
         flops=500_000_000,
     )
 
 
+def tables_of(count):
+    return [
+        ((count * BAND, TILE), BF16),
+        ((count * BAND, TILE), BF16),
+        ((count, BAND, 3 * TILE), BF16),
+        ((count, 128, 384), BF16),
+    ]
+
+
 def body(counts, sample_weights, classes, class_radius):
     shape = rows, columns = counts.shape
-    is_odd = (lax.axis_index("row") & 1).astype(F32)
     groups = ((0, 1), (2, 3))
-    rim = (REACH, columns)
-
-    def ends(array, width):
-        top, bottom = array[:width], array[rows - width :]
-        return [jnp.where(is_odd > 0.5, *pair) for pair in ((top, bottom), (bottom, top))]
-
-    sends = [
-        number.astype(F32) * weight
-        for number, weight in zip(ends(counts, PILOT_RADIUS), ends(sample_weights, PILOT_RADIUS))
-    ]
-    mass_halo = exchange(*sends, "row")
-    wide = (CLASSES + 1) * BAND
-    *tables, mass, labels, label_a, label_b = call(
+    rim, slim = (REACH, columns), (PILOT_RADIUS, columns)
+    counts, sample_weights, classes = (
+        pltpu.with_memory_space_constraint(field, pltpu.HBM)
+        for field in (counts, sample_weights, classes)
+    )
+    chunks = rows // CHUNK
+    *pilot_tables, mass, mass_a, mass_b, label_a, label_b = call(
         prepare_kernel,
-        [
-            ((wide, TILE), BF16),
-            ((wide, TILE), BF16),
-            ((CLASSES + 1, BAND, 3 * TILE), BF16),
-            ((CLASSES + 1, 128, 384), BF16),
-            (shape, F32),
-            (shape, BF16),
-            (rim, jnp.int32),
-            (rim, jnp.int32),
-        ],
-        [class_radius]
-        + [
-            pltpu.with_memory_space_constraint(field, pltpu.HBM)
-            for field in (counts, sample_weights, classes)
-        ],
-        ins=[SMEM, HBM, HBM, HBM],
+        tables_of(1)
+        + [(shape, F32), (slim, F32), (slim, F32), (rim, jnp.int32), (rim, jnp.int32)],
+        [counts, sample_weights, classes],
+        ins=[HBM, HBM, HBM],
         scratch=[
             pltpu.VMEM(shape, jnp.int32),
             pltpu.VMEM(shape, F32),
-            pltpu.VMEM(shape, jnp.int32),
-            pltpu.SemaphoreType.DMA((3,)),
+            pltpu.VMEM((2, *rim), jnp.int32),
+            pltpu.SemaphoreType.DMA((2, chunks)),
+            pltpu.SemaphoreType.DMA((2,)),
         ],
         flops=500_000_000,
     )
+    mass_halo = exchange(mass_a, mass_b, "row")
     label_halo = exchange(label_a, label_b, "row")
-    pieces = smooth(mass, mass_halo, None, None, tables, ((CLASSES,),), 1)
+    *tables, labels = call(
+        bands_kernel,
+        tables_of(CLASSES) + [(shape, BF16)],
+        [class_radius, classes],
+        ins=[SMEM, HBM],
+        scratch=[pltpu.VMEM(shape, jnp.int32), pltpu.SemaphoreType.DMA((chunks,))],
+        flops=500_000_000,
+    )
+    pieces = smooth(mass, mass_halo, None, None, pilot_tables, ((0,),), 1)
     adapted, *sends, first_stat = finish(pieces, [mass], False, True, True, shape)
     halo = exchange(*sends, "row")
     first_total = total_over(first_stat)
@@ -474,7 +532,9 @@
     )
     halo = exchange(*sends, "row")
     second_total = total_over(second_stat)
-    pieces = smooth(adapted, halo, labels, label_halo, tables, groups, 2)
+    pieces, density_first = smooth(
+        adapted, halo, labels, label_halo, tables, groups, 2, (density_first,)
+    )
     (density_second,) = finish(
         pieces, [second_total, first_total], True, False, False, shape
     )

time: 100 us -> 94.2 us (0.942)
  waiting for transfers between devices: 20 us -> 14.9 us
  other arithmetic: 1.18 us -> 0.05 us
    ppermute x14, waiting for transfers between devices: 17.3 us -> 11.3 us  [total_over(): stat = stat + lax.ppermute(stat, axis, pairs)]
    ppermute x14, starting transfers between devices: 14.6 us -> 16 us  [total_over(): stat = stat + lax.ppermute(stat, axis, pairs)]
    mul x1 -> x0, other arithmetic: 1.14 us -> none  [body(): number.astype(F32) * weight]
    pallas_call x17 -> x18, Pallas kernels: 33.8 us -> 33.8 us  [call(): pl.pallas_call(kernel, out_shape=[jax.ShapeDtypeStruct(s, d) for s, d in...]
  transfers between devices with their start and end apart: 28 -> 28, of which waited for: 15 -> 14; matrix products, arithmetic and copies ran while one was open for 0% -> 0% of each run, Pallas kernels for 24% -> 24%
where the time goes in v3:
time: 94.2 us; the launch traced here: 94.1 us
  starting transfers between devices  44.3 us (47%)
  Pallas kernels  33.8 us (36%)
  waiting for transfers between devices  14.9 us (16%)
  between operations  1.05 us (1%)
    pallas_call x18, Pallas kernels, call(): pl.pallas_call(kernel, out_shape=[jax.ShapeDtypeStruct(s, d) for s, d in...  33.8 us
    ppermute x14, starting transfers between devices, exchange(): results.append(lax.ppermute(value, ('row', 'col'), pairs))  28.3 us
    ppermute x14, starting transfers between devices, total_over(): stat = stat + lax.ppermute(stat, axis, pairs)  16 us
    ppermute x14, waiting for transfers between devices, total_over(): stat = stat + lax.ppermute(stat, axis, pairs)  11.3 us
    ppermute x14, waiting for transfers between devices, exchange(): results.append(lax.ppermute(value, ('row', 'col'), pairs))  3.62 us
  transfers between devices with their start and end apart: 28, of which 14 were waited for; matrix products, arithmetic and copies ran while one was open for 0% of the time, Pallas kernels for 24%

profile of v3, /device:TPU:1, one launch (start us, length us, event | category | flops | bytes accessed | tf_op | source)
XLA Modules:
  0.0 94.1 jit_solution(9685154036481613685)
XLA Ops:
  0.6 2.4 %shard_map.59 = (bf16[384,256]{1,0:T(8,128)(2,1)S(1)}, bf16[384,256]{1,0:T(8,128)(2,1)S(1)}, bf16[1,384,768]{2,1,0:T(8,128)(2,1)S(1)}, bf16[1,128,384]{2,1,0:T(8...) custom-call(s32[512,1024]{1,0:T(8,128)} %refs_0_.2, ...), custom_call_target="tpu_custom_call" | custom-call | flops 500000000 | bytes 4194304 | tf_op jit(solution)/shard_map/pallas_call | solution.py:27
  3.1 2.2 %collective-permute-start = (f32[32,1024]{1,0:T(8,128)S(1)}, f32[32,1024]{1,0:T(8,128)S(1)}, u32[]{:S(2)}, u32[]{:S(2)}) collective-permute-start(f32[32,1024]{1,0:T(8,128)S(1)} %get-tuple-element.59), channel_id=1, source_target_pairs={{0,8},{1,9},{2,10},{3,11},{4,12},{5,13},{6,14},{7,15},{8,0},{9,1},... | collective-permute-start | bytes 393224 | tf_op jit(solution)/shard_map/ppermute | solution.py:398
  10.5 1.8 %collective-permute-start.3 = (f32[256,128]{1,0:T(8,128)S(1)}, f32[256,128]{1,0:T(8,128)S(1)}, u32[]{:S(2)}, u32[]{:S(2)}) collective-permute-start(f32[256,128]{1,0:T(8,128)S(1)} %get-tuple-element.74), channel_id=1, source_target_pairs={{0,8},{1,2},{2,1},{3,4},{4,3},{5,6},{6,5},{7,15},{8,0},{9,10},{10,... | collective-permute-start | bytes 393224 | tf_op jit(solution)/shard_map/ppermute | solution.py:398
  20.6 3.1 %collective-permute-start.12 = (f32[8,128]{1,0:T(8,128)S(1)}, f32[8,128]{1,0:T(8,128)S(1)}, u32[]{:S(2)}, u32[]{:S(2)}) collective-permute-start(f32[8,128]{1,0:T(8,128)S(1)} %add.43), channel_id=1, source_target_pairs={{0,6},{1,7},{2,4},{3,5},{4,2},{5,3},{6,0},{7,1},{8,14},{9,15},{10,... | collective-permute-start | bytes 12296 | tf_op jit(solution)/shard_map/ppermute | solution.py:409
  24.8 4.3 %collective-permute-start.13 = (f32[8,128]{1,0:T(8,128)S(1)}, f32[8,128]{1,0:T(8,128)S(1)}, u32[]{:S(2)}, u32[]{:S(2)}) collective-permute-start(f32[8,128]{1,0:T(8,128)S(1)} %add.44), channel_id=1, source_target_pairs={{0,32},{8,40},{16,48},{24,56},{32,0},{40,8},{48,16},{56,24},{64,96... | collective-permute-start | bytes 12296 | tf_op jit(solution)/shard_map/ppermute | solution.py:409
  29.0 2.6 %collective-permute-start.7 = (s32[64,1024]{1,0:T(8,128)S(1)}, s32[64,1024]{1,0:T(8,128)S(1)}, u32[]{:S(2)}, u32[]{:S(2)}) collective-permute-start(s32[64,1024]{1,0:T(8,128)S(1)} %get-tuple-element.78), channel_id=1, source_target_pairs={{0,1},{1,0},{2,3},{3,2},{4,5},{5,4},{6,7},{7,6},{8,16},{9,17},{10,... | collective-permute-start | bytes 786440 | tf_op jit(solution)/shard_map/ppermute | solution.py:398
  32.8 2.2 %shard_map.64 = (bf16[1536,256]{1,0:T(8,128)(2,1)S(1)}, bf16[1536,256]{1,0:T(8,128)(2,1)S(1)}, bf16[4,384,768]{2,1,0:T(8,128)(2,1)S(1)}, bf16[4,128,384]{2,1,0:T(8,128)(2,1)S(1)}, bf16[512,1024]{1,0:T(8,128)(2,1)S(1)}) custom-call(s32[4]{0:T(128)S(1)} %copy-done, s32[512,1024]{1,0:T(8,128)} %refs_1_.3), custom_call_target="tpu_custom_call" | custom-call | flops 500000000 | bytes 4194304 | tf_op jit(solution)/shard_map/pallas_call | solution.py:27
  35.9 3.8 %collective-permute-start.5 = (f32[64,1024]{1,0:T(8,128)S(1)}, f32[64,1024]{1,0:T(8,128)S(1)}, u32[]{:S(2)}, u32[]{:S(2)}) collective-permute-start(f32[64,1024]{1,0:T(8,128)S(1)} %get-tuple-element.76), channel_id=1, source_target_pairs={{0,1},{1,0},{2,3},{3,2},{4,5},{5,4},{6,7},{7,6},{8,16},{9,17},{10,... | collective-permute-start | bytes 786440 | tf_op jit(solution)/shard_map/ppermute | solution.py:398
  39.7 2.4 %shard_map.66 = (bf16[2,384,1024]{2,1,0:T(8,128)(2,1)S(1)}, bf16[2,384,1024]{2,1,0:T(8,128)(2,1)S(1)}, f32[2,128,1024]{2,1,0:T(8,128)S(1)}) custom-call(f32[512,1024]{1,0:T(8,128)S(1)} %get-tuple-element.79.refs_0_, bf16[512,1024]{1,0:T(8,128)(2,1)S(1)} %get-tuple-element.80.refs_1_, bf16[4,384,768]{2,1,0:T(8,128)(2,1)S(1)} %get-tuple-element.81.refs_2_), custom_call_target="tpu_custom_call" | custom-call | flops 2000000000 | bytes 4194304 | tf_op jit(solution)/shard_map/pallas_call | solution.py:27
  43.7 2.4 %shard_map.65 = (bf16[2,384,1024]{2,1,0:T(8,128)(2,1)S(1)}, bf16[2,384,1024]{2,1,0:T(8,128)(2,1)S(1)}, f32[2,128,1024]{2,1,0:T(8,128)S(1)}) custom-call(f32[512,1024]{1,0:T(8,128)S(1)} %get-tuple-element.79.refs_0_, bf16[512,1024]{1,0:T(8,128)(2,1)S(1)} %get-tuple-element.80.refs_1_, bf16[4,384,768]{2,1,0:T(8,128)(2,1)S(1)} %get-tuple-element.81.refs_2_), custom_call_target="tpu_custom_call" | custom-call | flops 2000000000 | bytes 4194304 | tf_op jit(solution)/shard_map/pallas_call | solution.py:27
  46.2 2.2 %shard_map.67 = (bf16[4,128,1024]{2,1,0:T(8,128)(2,1)S(1)}, bf16[4,128,1024]{2,1,0:T(8,128)(2,1)S(1)}, f32[512,256]{1,0:T(8,128)S(1)}, f32[512,128]{1,0:T(8,128)...) custom-call(f32[64,1024]{1,0:T(8,128)S(1)} %collective-permute-done.4.refs_0_, ...), custom_call_target="tpu_custom_call" | custom-call | flops 2000000000 | bytes 4194304 | tf_op jit(solution)/shard_map/pallas_call | solution.py:27
  48.4 4.0 %collective-permute-start.8 = (f32[256,128]{1,0:T(8,128)S(1)}, f32[256,128]{1,0:T(8,128)S(1)}, u32[]{:S(2)}, u32[]{:S(2)}) collective-permute-start(f32[256,128]{1,0:T(8,128)S(1)} %get-tuple-element.95), channel_id=1, source_target_pairs={{0,1},{1,0},{2,3},{3,2},{4,5},{5,4},{6,7},{7,6},{8,9},{9,8},{10,11... | collective-permute-start | bytes 393224 | tf_op jit(solution)/shard_map/ppermute | solution.py:398
  52.4 2.0 %shard_map.69.refs_2_ = f32[256,768]{1,0:T(8,128)S(1)} custom-call(bf16[2,384,1024]{2,1,0:T(8,128)(2,1)S(1)} %get-tuple-element.84.refs_6_.refs_0_, bf16[2,384,1024]{2,1,0:T(8,128)(2,1)S(1)} %get-tuple-element.85.refs_7_.refs_1_, bf16[2,384,1024]{2,1,0:T(8,128)(2,1)S(1)} %get-tuple-element.86.refs_8_.refs_2_, ...), custom_call_target="tpu_custom_call" | custom-call | flops 1500000000 | bytes 4194304 | tf_op jit(solution)/shard_map/pallas_call | solution.py:27
  54.4 2.0 %shard_map.68.refs_1_ = f32[256,768]{1,0:T(8,128)S(1)} custom-call(bf16[2,384,1024]{2,1,0:T(8,128)(2,1)S(1)} %get-tuple-element.84.refs_6_.refs_0_, bf16[2,384,1024]{2,1,0:T(8,128)(2,1)S(1)} %get-tuple-element.85.refs_7_.refs_1_, bf16[2,384,1024]{2,1,0:T(8,128)(2,1)S(1)} %get-tuple-element.86.refs_8_.refs_2_, ...), custom_call_target="tpu_custom_call" | custom-call | flops 1500000000 | bytes 4194304 | tf_op jit(solution)/shard_map/pallas_call | solution.py:27
  62.0 2.4 %collective-permute-start.23 = (f32[8,128]{1,0:T(8,128)S(1)}, f32[8,128]{1,0:T(8,128)S(1)}, u32[]{:S(2)}, u32[]{:S(2)}) collective-permute-start(f32[8,128]{1,0:T(8,128)S(1)} %add.50), channel_id=1, source_target_pairs={{0,6},{1,7},{2,4},{3,5},{4,2},{5,3},{6,0},{7,1},{8,14},{9,15},{10,... | collective-permute-start | bytes 12296 | tf_op jit(solution)/shard_map/ppermute | solution.py:409
  65.9 2.2 %collective-permute-done.24 = f32[8,128]{1,0:T(8,128)S(1)} collective-permute-done((f32[8,128]{1,0:T(8,128)S(1)}, f32[8,128]{1,0:T(8,128)S(1)}, u32[]{:S(2)}, u32[]{:S(2)}) %collective-permute-start.24) | collective-permute-done | bytes 4128 | tf_op jit(solution)/shard_map/ppermute | solution.py:409
  69.5 4.1 %collective-permute-start.18 = (f32[64,1024]{1,0:T(8,128)S(1)}, f32[64,1024]{1,0:T(8,128)S(1)}, u32[]{:S(2)}, u32[]{:S(2)}) collective-permute-start(f32[64,1024]{1,0:T(8,128)S(1)} %get-tuple-element.102), channel_id=1, source_target_pairs={{0,1},{1,0},{2,3},{3,2},{4,5},{5,4},{6,7},{7,6},{8,16},{9,17},{10,... | collective-permute-start | bytes 786440 | tf_op jit(solution)/shard_map/ppermute | solution.py:398
  73.6 2.4 %shard_map.72 = (bf16[2,384,1024]{2,1,0:T(8,128)(2,1)S(1)}, bf16[2,384,1024]{2,1,0:T(8,128)(2,1)S(1)}, f32[2,128,1024]{2,1,0:T(8,128)S(1)}) custom-call(f32[512,1024]{1,0:T(8,128)S(1)} %get-tuple-element.98.refs_0_, bf16[512,1024]{1,0:T(8,128)(2,1)S(1)} %get-tuple-element.80.refs_1_, bf16[4,384,768]{2,1,0:T(8,128)(2,1)S(1)} %get-tuple-element.81.refs_2_), custom_call_target="tpu_custom_call" | custom-call | flops 2000000000 | bytes 4194304 | tf_op jit(solution)/shard_map/pallas_call | solution.py:27
  76.6 2.4 %shard_map.71 = (bf16[2,384,1024]{2,1,0:T(8,128)(2,1)S(1)}, bf16[2,384,1024]{2,1,0:T(8,128)(2,1)S(1)}, f32[2,128,1024]{2,1,0:T(8,128)S(1)}, f32[512,1024]{1,0:T(8,128)}) custom-call(f32[512,1024]{1,0:T(8,128)S(1)} %get-tuple-element.98.refs_0_, bf16[512,1024]{1,0:T(8,128)(2,1)S(1)} %get-tuple-element.80.refs_1_, ...), custom_call_target="tpu_custom_call" | custom-call | flops 2000000000 | bytes 4194304 | tf_op jit(solution)/shard_map/pallas_call | solution.py:27
  80.1 2.2 %shard_map.73 = (bf16[4,128,1024]{2,1,0:T(8,128)(2,1)S(1)}, bf16[4,128,1024]{2,1,0:T(8,128)(2,1)S(1)}, f32[512,256]{1,0:T(8,128)S(1)}, f32[512,128]{1,0:T(8,128)...) custom-call(f32[64,1024]{1,0:T(8,128)S(1)} %collective-permute-done.17.refs_0_, ...), custom_call_target="tpu_custom_call" | custom-call | flops 2000000000 | bytes 4194304 | tf_op jit(solution)/shard_map/pallas_call | solution.py:27
  82.3 5.2 %collective-permute-start.19 = (f32[256,128]{1,0:T(8,128)S(1)}, f32[256,128]{1,0:T(8,128)S(1)}, u32[]{:S(2)}, u32[]{:S(2)}) collective-permute-start(f32[256,128]{1,0:T(8,128)S(1)} %get-tuple-element.113), channel_id=1, source_target_pairs={{0,1},{1,0},{2,3},{3,2},{4,5},{5,4},{6,7},{7,6},{8,9},{9,8},{10,11... | collective-permute-start | bytes 393224 | tf_op jit(solution)/shard_map/ppermute | solution.py:398
  87.5 2.0 %shard_map.75.refs_2_ = f32[256,768]{1,0:T(8,128)S(1)} custom-call(bf16[2,384,1024]{2,1,0:T(8,128)(2,1)S(1)} %get-tuple-element.105.refs_6_.refs_0_, bf16[2,384,1024]{2,1,0:T(8,128)(2,1)S(1)} %get-tuple-element.106.refs_7_.refs_1_, bf16[2,384,1024]{2,1,0:T(8,128)(2,1)S(1)} %get-tuple-element.107.refs_8_.refs_2_, ...), custom_call_target="tpu_custom_call" | custom-call | flops 1500000000 | bytes 4194304 | tf_op jit(solution)/shard_map/pallas_call | solution.py:27
  89.5 2.0 %shard_map.74.refs_1_ = f32[256,768]{1,0:T(8,128)S(1)} custom-call(bf16[2,384,1024]{2,1,0:T(8,128)(2,1)S(1)} %get-tuple-element.105.refs_6_.refs_0_, bf16[2,384,1024]{2,1,0:T(8,128)(2,1)S(1)} %get-tuple-element.106.refs_7_.refs_1_, bf16[2,384,1024]{2,1,0:T(8,128)(2,1)S(1)} %get-tuple-element.107.refs_8_.refs_2_, ...), custom_call_target="tpu_custom_call" | custom-call | flops 1500000000 | bytes 4194304 | tf_op jit(solution)/shard_map/pallas_call | solution.py:27
  92.1 1.8 %shard_map.76 = f32[512,1024]{1,0:T(8,128)} custom-call(f32[512,256]{1,0:T(8,128)S(1)} %get-tuple-element.109.refs_0_, f32[256,768]{1,0:T(8,128)S(1)} %shard_map.74.refs_1_, f32[256,768]{1,0:T(8,128)S(1)} %shard_map.75.refs_2_, f32[512,128]{1,0:T(8,128)S(1)} %get-tuple-element.112.refs_3_, f32[256,128]{1,0:T(8,128)S(1)} %collective-permute-done.19.refs_4_, ...), custom_call_target="tpu_custom_call" | custom-call | flops 500000000 | bytes 4194304 | tf_op jit(solution)/shard_map/pallas_call | solution.py:27
  (66 shorter events, 29.0 us)
Async XLA Ops:
  3.1 5.1 %collective-permute-start = (f32[32,1024]{1,0:T(8,128)S(1)}, f32[32,1024]{1,0:T(8,128)S(1)}, u32[]{:S(2)}, u32[]{:S(2)}) collective-permute-start(f32[32,1024]{1,0:T(8,128)S(1)} %get-tuple-element.59), channel_id=1, source_target_pairs={{0,8},{1,9},{2,10},{3,11},{4,12},{5,13},{6,14},{7,15},{8,0},{9,1},... | collective-permute-start | bytes 393224 | tf_op jit(solution)/shard_map/ppermute | solution.py:398
  5.3 2.9 %collective-permute-start.1 = (f32[32,1024]{1,0:T(8,128)S(1)}, f32[32,1024]{1,0:T(8,128)S(1)}, u32[]{:S(2)}, u32[]{:S(2)}) collective-permute-start(f32[32,1024]{1,0:T(8,128)S(1)} %get-tuple-element.60), channel_id=1, source_target_pairs={{0,1},{1,0},{2,3},{3,2},{4,5},{5,4},{6,7},{7,6},{8,16},{9,17},{10,... | collective-permute-start | bytes 393224 | tf_op jit(solution)/shard_map/ppermute | solution.py:398
  8.8 4.8 %collective-permute-start.2 = (f32[256,128]{1,0:T(8,128)S(1)}, f32[256,128]{1,0:T(8,128)S(1)}, u32[]{:S(2)}, u32[]{:S(2)}) collective-permute-start(f32[256,128]{1,0:T(8,128)S(1)} %get-tuple-element.73), channel_id=1, source_target_pairs={{0,1},{1,0},{2,3},{3,2},{4,5},{5,4},{6,7},{7,6},{8,9},{9,8},{10,11... | collective-permute-start | bytes 393224 | tf_op jit(solution)/shard_map/ppermute | solution.py:398
  10.5 4.7 %collective-permute-start.3 = (f32[256,128]{1,0:T(8,128)S(1)}, f32[256,128]{1,0:T(8,128)S(1)}, u32[]{:S(2)}, u32[]{:S(2)}) collective-permute-start(f32[256,128]{1,0:T(8,128)S(1)} %get-tuple-element.74), channel_id=1, source_target_pairs={{0,8},{1,2},{2,1},{3,4},{4,3},{5,6},{6,5},{7,15},{8,0},{9,10},{10,... | collective-permute-start | bytes 393224 | tf_op jit(solution)/shard_map/ppermute | solution.py:398
  18.2 2.5 %collective-permute-start.11 = (f32[8,128]{1,0:T(8,128)S(1)}, f32[8,128]{1,0:T(8,128)S(1)}, u32[]{:S(2)}, u32[]{:S(2)}) collective-permute-start(f32[8,128]{1,0:T(8,128)S(1)} %add.42), channel_id=1, source_target_pairs={{0,2},{1,3},{2,0},{3,1},{4,6},{5,7},{6,4},{7,5},{8,10},{9,11},{10,... | collective-permute-start | bytes 12296 | tf_op jit(solution)/shard_map/ppermute | solution.py:409
  20.6 4.1 %collective-permute-start.12 = (f32[8,128]{1,0:T(8,128)S(1)}, f32[8,128]{1,0:T(8,128)S(1)}, u32[]{:S(2)}, u32[]{:S(2)}) collective-permute-start(f32[8,128]{1,0:T(8,128)S(1)} %add.43), channel_id=1, source_target_pairs={{0,6},{1,7},{2,4},{3,5},{4,2},{5,3},{6,0},{7,1},{8,14},{9,15},{10,... | collective-permute-start | bytes 12296 | tf_op jit(solution)/shard_map/ppermute | solution.py:409
  24.8 6.9 %collective-permute-start.13 = (f32[8,128]{1,0:T(8,128)S(1)}, f32[8,128]{1,0:T(8,128)S(1)}, u32[]{:S(2)}, u32[]{:S(2)}) collective-permute-start(f32[8,128]{1,0:T(8,128)S(1)} %add.44), channel_id=1, source_target_pairs={{0,32},{8,40},{16,48},{24,56},{32,0},{40,8},{48,16},{56,24},{64,96... | collective-permute-start | bytes 12296 | tf_op jit(solution)/shard_map/ppermute | solution.py:409
  29.0 17.1 %collective-permute-start.6 = (s32[64,1024]{1,0:T(8,128)S(1)}, s32[64,1024]{1,0:T(8,128)S(1)}, u32[]{:S(2)}, u32[]{:S(2)}) collective-permute-start(s32[64,1024]{1,0:T(8,128)S(1)} %get-tuple-element.77), channel_id=1, source_target_pairs={{0,8},{1,9},{2,10},{3,11},{4,12},{5,13},{6,14},{7,15},{8,0},{9,1},... | collective-permute-start | bytes 786440 | tf_op jit(solution)/shard_map/ppermute | solution.py:398
  29.0 17.1 %collective-permute-start.7 = (s32[64,1024]{1,0:T(8,128)S(1)}, s32[64,1024]{1,0:T(8,128)S(1)}, u32[]{:S(2)}, u32[]{:S(2)}) collective-permute-start(s32[64,1024]{1,0:T(8,128)S(1)} %get-tuple-element.78), channel_id=1, source_target_pairs={{0,1},{1,0},{2,3},{3,2},{4,5},{5,4},{6,7},{7,6},{8,16},{9,17},{10,... | collective-permute-start | bytes 786440 | tf_op jit(solution)/shard_map/ppermute | solution.py:398
  31.7 8.0 %collective-permute-start.14 = (f32[8,128]{1,0:T(8,128)S(1)}, f32[8,128]{1,0:T(8,128)S(1)}, u32[]{:S(2)}, u32[]{:S(2)}) collective-permute-start(f32[8,128]{1,0:T(8,128)S(1)} %add.45), channel_id=1, source_target_pairs={{0,96},{8,104},{16,112},{24,120},{32,64},{40,72},{48,80},{56,88},{... | collective-permute-start | bytes 12296 | tf_op jit(solution)/shard_map/ppermute | solution.py:409
  35.0 11.2 %collective-permute-start.4 = (f32[64,1024]{1,0:T(8,128)S(1)}, f32[64,1024]{1,0:T(8,128)S(1)}, u32[]{:S(2)}, u32[]{:S(2)}) collective-permute-start(f32[64,1024]{1,0:T(8,128)S(1)} %get-tuple-element.75), channel_id=1, source_target_pairs={{0,8},{1,9},{2,10},{3,11},{4,12},{5,13},{6,14},{7,15},{8,0},{9,1},... | collective-permute-start | bytes 786440 | tf_op jit(solution)/shard_map/ppermute | solution.py:398
  35.9 10.3 %collective-permute-start.5 = (f32[64,1024]{1,0:T(8,128)S(1)}, f32[64,1024]{1,0:T(8,128)S(1)}, u32[]{:S(2)}, u32[]{:S(2)}) collective-permute-start(f32[64,1024]{1,0:T(8,128)S(1)} %get-tuple-element.76), channel_id=1, source_target_pairs={{0,1},{1,0},{2,3},{3,2},{4,5},{5,4},{6,7},{7,6},{8,16},{9,17},{10,... | collective-permute-start | bytes 786440 | tf_op jit(solution)/shard_map/ppermute | solution.py:398
  39.7 2.8 %collective-permute-start.15 = (f32[8,128]{1,0:T(8,128)S(1)}, f32[8,128]{1,0:T(8,128)S(1)}, u32[]{:S(2)}, u32[]{:S(2)}) collective-permute-start(f32[8,128]{1,0:T(8,128)S(1)} %add.46), channel_id=1, source_target_pairs={{0,8},{8,0},{16,24},{24,16},{32,40},{40,32},{48,56},{56,48},{64,72... | collective-permute-start | bytes 12296 | tf_op jit(solution)/shard_map/ppermute | solution.py:409
  42.5 3.7 %collective-permute-start.16 = (f32[8,128]{1,0:T(8,128)S(1)}, f32[8,128]{1,0:T(8,128)S(1)}, u32[]{:S(2)}, u32[]{:S(2)}) collective-permute-start(f32[8,128]{1,0:T(8,128)S(1)} %add.47), channel_id=1, source_target_pairs={{0,24},{8,16},{16,8},{24,0},{32,56},{40,48},{48,40},{56,32},{64,88... | collective-permute-start | bytes 12296 | tf_op jit(solution)/shard_map/ppermute | solution.py:409
  48.4 8.0 %collective-permute-start.8 = (f32[256,128]{1,0:T(8,128)S(1)}, f32[256,128]{1,0:T(8,128)S(1)}, u32[]{:S(2)}, u32[]{:S(2)}) collective-permute-start(f32[256,128]{1,0:T(8,128)S(1)} %get-tuple-element.95), channel_id=1, source_target_pairs={{0,1},{1,0},{2,3},{3,2},{4,5},{5,4},{6,7},{7,6},{8,9},{9,8},{10,11... | collective-permute-start | bytes 393224 | tf_op jit(solution)/shard_map/ppermute | solution.py:398
  52.4 4.7 %collective-permute-start.9 = (f32[256,128]{1,0:T(8,128)S(1)}, f32[256,128]{1,0:T(8,128)S(1)}, u32[]{:S(2)}, u32[]{:S(2)}) collective-permute-start(f32[256,128]{1,0:T(8,128)S(1)} %get-tuple-element.96), channel_id=1, source_target_pairs={{0,8},{1,2},{2,1},{3,4},{4,3},{5,6},{6,5},{7,15},{8,0},{9,10},{10,... | collective-permute-start | bytes 393224 | tf_op jit(solution)/shard_map/ppermute | solution.py:398
  62.0 3.7 %collective-permute-start.23 = (f32[8,128]{1,0:T(8,128)S(1)}, f32[8,128]{1,0:T(8,128)S(1)}, u32[]{:S(2)}, u32[]{:S(2)}) collective-permute-start(f32[8,128]{1,0:T(8,128)S(1)} %add.50), channel_id=1, source_target_pairs={{0,6},{1,7},{2,4},{3,5},{4,2},{5,3},{6,0},{7,1},{8,14},{9,15},{10,... | collective-permute-start | bytes 12296 | tf_op jit(solution)/shard_map/ppermute | solution.py:409
  68.2 5.4 %collective-permute-start.25 = (f32[8,128]{1,0:T(8,128)S(1)}, f32[8,128]{1,0:T(8,128)S(1)}, u32[]{:S(2)}, u32[]{:S(2)}) collective-permute-start(f32[8,128]{1,0:T(8,128)S(1)} %add.52), channel_id=1, source_target_pairs={{0,96},{8,104},{16,112},{24,120},{32,64},{40,72},{48,80},{56,88},{... | collective-permute-start | bytes 12296 | tf_op jit(solution)/shard_map/ppermute | solution.py:409
  68.4 11.6 %collective-permute-start.17 = (f32[64,1024]{1,0:T(8,128)S(1)}, f32[64,1024]{1,0:T(8,128)S(1)}, u32[]{:S(2)}, u32[]{:S(2)}) collective-permute-start(f32[64,1024]{1,0:T(8,128)S(1)} %get-tuple-element.101), channel_id=1, source_target_pairs={{0,8},{1,9},{2,10},{3,11},{4,12},{5,13},{6,14},{7,15},{8,0},{9,1},... | collective-permute-start | bytes 786440 | tf_op jit(solution)/shard_map/ppermute | solution.py:398
  69.5 10.6 %collective-permute-start.18 = (f32[64,1024]{1,0:T(8,128)S(1)}, f32[64,1024]{1,0:T(8,128)S(1)}, u32[]{:S(2)}, u32[]{:S(2)}) collective-permute-start(f32[64,1024]{1,0:T(8,128)S(1)} %get-tuple-element.102), channel_id=1, source_target_pairs={{0,1},{1,0},{2,3},{3,2},{4,5},{5,4},{6,7},{7,6},{8,16},{9,17},{10,... | collective-permute-start | bytes 786440 | tf_op jit(solution)/shard_map/ppermute | solution.py:398
  73.6 2.8 %collective-permute-start.26 = (f32[8,128]{1,0:T(8,128)S(1)}, f32[8,128]{1,0:T(8,128)S(1)}, u32[]{:S(2)}, u32[]{:S(2)}) collective-permute-start(f32[8,128]{1,0:T(8,128)S(1)} %add.53), channel_id=1, source_target_pairs={{0,8},{8,0},{16,24},{24,16},{32,40},{40,32},{48,56},{56,48},{64,72... | collective-permute-start | bytes 12296 | tf_op jit(solution)/shard_map/ppermute | solution.py:409
  76.4 3.7 %collective-permute-start.27 = (f32[8,128]{1,0:T(8,128)S(1)}, f32[8,128]{1,0:T(8,128)S(1)}, u32[]{:S(2)}, u32[]{:S(2)}) collective-permute-start(f32[8,128]{1,0:T(8,128)S(1)} %add.54), channel_id=1, source_target_pairs={{0,24},{8,16},{16,8},{24,0},{32,56},{40,48},{48,40},{56,32},{64,88... | collective-permute-start | bytes 12296 | tf_op jit(solution)/shard_map/ppermute | solution.py:409
  82.3 9.2 %collective-permute-start.19 = (f32[256,128]{1,0:T(8,128)S(1)}, f32[256,128]{1,0:T(8,128)S(1)}, u32[]{:S(2)}, u32[]{:S(2)}) collective-permute-start(f32[256,128]{1,0:T(8,128)S(1)} %get-tuple-element.113), channel_id=1, source_target_pairs={{0,1},{1,0},{2,3},{3,2},{4,5},{5,4},{6,7},{7,6},{8,9},{9,8},{10,11... | collective-permute-start | bytes 393224 | tf_op jit(solution)/shard_map/ppermute | solution.py:398
  87.5 4.7 %collective-permute-start.20 = (f32[256,128]{1,0:T(8,128)S(1)}, f32[256,128]{1,0:T(8,128)S(1)}, u32[]{:S(2)}, u32[]{:S(2)}) collective-permute-start(f32[256,128]{1,0:T(8,128)S(1)} %get-tuple-element.114), channel_id=1, source_target_pairs={{0,8},{1,2},{2,1},{3,4},{4,3},{5,6},{6,5},{7,15},{8,0},{9,10},{10,... | collective-permute-start | bytes 393224 | tf_op jit(solution)/shard_map/ppermute | solution.py:398
  (5 other events, 25.5 us)

commit v4 on v3

--- a/solution.py
+++ b/solution.py
@@ -67,7 +67,7 @@
     return [jnp.full((1, 1), value.astype(F32), F32) for value in values]
 
 
-def fill_bands(slot, radius, high_ref, low_ref, stack_ref, rim_ref):
+def fill_bands(slot, radius, high_ref, low_ref, rim_ref):
     radius = jnp.full((1, 1), radius, F32)
     inverse = 1.0 / (2.0 * (0.5 * radius) * (0.5 * radius))
 
@@ -91,10 +91,6 @@
             for k, block in enumerate(pair):
                 lanes = slice(k * 128, (k + 1) * 128)
                 ref[base + i * 128 : base + (i + 1) * 128, lanes] = block
-                places = (0, 2 * TILE) if part == 0 else (TILE,)
-                for place in places:
-                    shifted = slice(place + k * 128, place + (k + 1) * 128)
-                    stack_ref[slot, i * 128 : (i + 1) * 128, shifted] = block
         first = jnp.where(side, far[part][:REACH].astype(F32), zeros).astype(BF16)
         second = jnp.where(side, zeros, near[part][REACH:].astype(F32)).astype(BF16)
         for place in (0, 128) if part == 0 else (256,):
@@ -106,7 +102,7 @@
 
 
 def prepare_kernel(*refs):
-    (counts_in, weights_in, classes_in), tables, outs, scratch = take(refs, 3, 4, 5)
+    (counts_in, weights_in, classes_in), tables, outs, scratch = take(refs, 3, 3, 5)
     mass_ref, mass_a, mass_b, label_a, label_b = outs
     counts, weights, ends, arrived, ended = scratch
     rows = counts.shape[0]
@@ -142,7 +138,7 @@
 
 
 def bands_kernel(*refs):
-    (radius_ref, classes_in), tables, (label_ref, classes, arrived) = take(refs, 2, 4)
+    (radius_ref, classes_in), tables, (label_ref, classes, arrived) = take(refs, 2, 3)
     rows = classes.shape[0]
     copies = []
     for n, start in enumerate(range(0, rows, CHUNK)):
@@ -165,37 +161,49 @@
 
 
 def rows_kernel(*refs, bands, labelled, carried):
-    (field_ref,), label_refs, (stack_ref,), plane, (high_ref, low_ref, edge_ref), plane_out, done = (
-        take(refs, 1, labelled, 1, carried, 3, carried)
-    )
+    (field_ref,), label_refs, (band_high, band_low), plane, outs, plane_out, done = take(
+        refs, 1, labelled, 2, carried, 3, carried
+    )
+    high_ref, low_ref, edge_ref = outs
     copies = [pltpu.make_async_copy(*pair) for pair in zip(plane, plane_out, done)]
     for copy in copies:
         copy.start()
-    _, columns = field_ref.shape
+    rows, columns = field_ref.shape
+    count = rows // REACH
     for n in range(columns // TILE):
         at = slice(n * TILE, (n + 1) * TILE)
         pieces = split(field_ref[:, at])
         labels = label_refs[0][:, at] if labelled else None
         for slot, c in enumerate(bands):
             high, low = masked(pieces, labels, c)
-
-            def part(t, start):
-                own = slice(t * TILE, (t + 1) * TILE)
-                right = jnp.concatenate([high[own], high[own], low[own]], axis=0)
-                return dot(stack_ref[c, start : start + TILE + REACH, :], right)
-
-            first, second = part(0, REACH), part(1, 0)
-            edge_ref[slot, 0:REACH, at] = first[0:REACH]
-            edge_ref[slot, REACH:, at] = second[TILE:]
-            cut = TILE - REACH
-            for target, value in (
-                (0, first[REACH:cut]),
-                (cut - REACH, first[cut:] + second[: 2 * REACH]),
-                (cut + REACH, second[2 * REACH : TILE]),
-            ):
-                value_high, value_low = split(value)
-                high_ref[slot, target : target + value.shape[0], at] = value_high
-                low_ref[slot, target : target + value.shape[0], at] = value_low
+            sums = [None] * count
+
+            def add(result, first):
+                for i in range(result.shape[0] // REACH):
+                    piece = result[i * REACH : (i + 1) * REACH]
+                    own = sums[first + i]
+                    sums[first + i] = piece if own is None else own + piece
+
+            half = band_high[c * BAND : c * BAND + 2 * 128, 0:128]
+            twice = jnp.concatenate([half, half], axis=1)
+            for block in range(rows // 128):
+                own = slice(block * 128, (block + 1) * 128)
+                first = max(2 * block - 1, 0)
+                last = min(2 * block + 3, count)
+                taps = slice((first - 2 * block + 1) * REACH, (last - 2 * block + 1) * REACH)
+                add(dot(twice[taps], jnp.concatenate([high[own], low[own]])), first)
+            for tile in range(rows // TILE):
+                own = slice(tile * TILE, (tile + 1) * TILE)
+                first = max(4 * tile - 1, 0)
+                last = min(4 * tile + 5, count)
+                start = c * BAND + (first - 4 * tile + 1) * REACH
+                taps = slice(start, start + (last - first) * REACH)
+                add(dot(band_low[taps, :], high[own]), first)
+            edge_ref[slot, 0:REACH, at] = sums[0]
+            edge_ref[slot, REACH:, at] = sums[-1]
+            for i, value in enumerate(sums[1:-1]):
+                target = slice(i * REACH, (i + 1) * REACH)
+                high_ref[slot, target, at], low_ref[slot, target, at] = split(value)
     for copy in copies:
         copy.wait()
 
@@ -222,14 +230,36 @@
     return jnp.concatenate(pieces, axis=1)
 
 
-def swept(highs, lows, bands, band_refs, inputs, taps, outputs, start, stop, inner):
-    right_high, right_low = (
-        jnp.concatenate([ref[c * BAND + taps.start : c * BAND + taps.stop, outputs] for c in bands])
-        for ref in band_refs
-    )
-    high = stacked_left(highs, inputs, start, stop, inner)
-    low = stacked_left(lows, inputs, start, stop, inner)
-    return dot(high, right_high) + dot(high, right_low) + dot(low, right_high)
+def swept(highs, lows, bands, band_refs, block, width, columns, start, stop, inner):
+    high_ref, low_ref = band_refs
+
+    def window(first, last):
+        here, there = max(first, 0), min(last, columns)
+        return slice(here, there), slice(here - first, there - first)
+
+    def rights(refs_and_lanes, taps):
+        return jnp.concatenate(
+            [
+                jnp.concatenate(
+                    [ref[c * BAND + taps.start : c * BAND + taps.stop, lanes] for ref, lanes in refs_and_lanes],
+                    axis=1,
+                )
+                for c in bands
+            ]
+        )
+
+    results = []
+    origin = block * TILE - 128
+    for part in range(width // 128):
+        inputs, taps = window(origin + part * 128, origin + (part + 2) * 128)
+        left = stacked_left(highs, inputs, start, stop, inner)
+        right = rights(((high_ref, slice(0, 128)), (low_ref, slice(0, 128))), taps)
+        both = dot(left, right)
+        results.append(both[:, :128] + both[:, 128:])
+    inputs, taps = window(origin, origin + width + 128)
+    left = stacked_left(lows, inputs, start, stop, inner)
+    rest = dot(left, rights(((high_ref, slice(0, width)),), taps))
+    return [value + rest[:, k * 128 : (k + 1) * 128] for k, value in enumerate(results)]
 
 
 def edges_kernel(*refs, groups, labelled):
@@ -266,14 +296,21 @@
             edge_high[slot, :, at], edge_low[slot, :, at] = split(value)
     rows = left_ref.shape[0]
     inner = rows - 2 * REACH
-    sides = (
-        (left_ref, slice(0, TILE), slice(128, BAND), slice(0, TILE)),
-        (right_ref, slice(columns - 128, columns), slice(0, 128), slice(0, 128)),
-    )
-    for target, *window in sides:
-        target[...] = swept(
-            (highs, edge_high), (lows, edge_low), bands, band_refs, *window, 0, rows, inner
+    for target, block in ((left_ref, 0), (right_ref, columns // TILE)):
+        results = swept(
+            (highs, edge_high),
+            (lows, edge_low),
+            bands,
+            band_refs,
+            block,
+            target.shape[1],
+            columns,
+            0,
+            rows,
+            inner,
         )
+        for k, value in enumerate(results):
+            target[:, k * 128 : (k + 1) * 128] = value
     half = rows // 2
     lower = iota((half, 128), 1) < REACH
     left = left_ref[:, 0:128]
@@ -289,21 +326,21 @@
     highs, lows, (edge_high, edge_low), band_refs, (out_ref,) = take(refs, count, count, 2, 2)
     bands = [c for group in groups for c in group]
     inner = highs[0].shape[1]
-    stop = start + out_ref.shape[0]
     for j in range(out_ref.shape[1] // TILE):
-        inputs = slice(j * TILE + 128, j * TILE + 128 + BAND)
-        out_ref[:, j * TILE : (j + 1) * TILE] = swept(
+        results = swept(
             (highs, edge_high),
             (lows, edge_low),
             bands,
             band_refs,
-            inputs,
-            slice(0, BAND),
-            slice(0, TILE),
+            j + 1,
+            TILE,
+            edge_high.shape[2],
             start,
-            stop,
+            start + out_ref.shape[0],
             inner,
         )
+        for k, value in enumerate(results):
+            out_ref[:, j * TILE + k * 128 : j * TILE + (k + 1) * 128] = value
 
 
 def gathered(pieces, come, flags, start):
@@ -323,9 +360,12 @@
         come_right = pltpu.roll(come_right, REACH, 1)
     first = left_ref[at, 0:128] + jnp.where(lane >= REACH, come_left, 0.0)
     last = right_ref[at, :] + jnp.where(lane < REACH, come_right, 0.0)
-    each = middles[0].shape[0]
-    middle_ref = middles[kept // each]
-    own = slice(kept % each, kept % each + STEP)
+    own = kept
+    for middle_ref in middles:
+        if own < middle_ref.shape[0]:
+            break
+        own -= middle_ref.shape[0]
+    own = slice(own, own + STEP)
     blocks = [first, left_ref[at, 128:256]]
     blocks += [middle_ref[own, k : k + 128] for k in range(0, middle_ref.shape[1], 128)]
     blocks += [last]
@@ -399,19 +439,27 @@
     return results
 
 
-HOPS = {1: (), 2: (1,), 4: (1, 3), 8: (1, 2, 6), 16: (4, 12, 1, 3)}
+HOPS = (
+    ("col", 2, 8),
+    ("col", 6, 8),
+    ("row", 12, 16),
+    ("row", 4, 16),
+    ("row", 3, 4),
+    ("row", 1, 2),
+    ("col", 1, 2),
+)
 
 
 def total_over(stat):
-    for axis in ("col", "row"):
-        for hop in HOPS[lax.axis_size(axis)]:
+    for axis, hop, least in HOPS:
+        if lax.axis_size(axis) >= least:
             pairs = [(i, i ^ hop) for i in range(lax.axis_size(axis))]
             stat = stat + lax.ppermute(stat, axis, pairs)
     return stat
 
 
 def smooth(field, halo, labels, label_halo, tables, groups, cuts, leaving=()):
-    high, low, stack, rim = tables
+    high, low, rim = tables
     rows, columns = field.shape
     labelled = labels is not None
     bands = [c for group in groups for c in group]
@@ -425,7 +473,7 @@
                 rows_kernel, bands=group, labelled=labelled, carried=carried
             ),
             [(inner, BF16), (inner, BF16), (edge, F32)] + [(field.shape, F32)] * carried,
-            [field] + ([labels] if labelled else []) + [stack, *leaving[:carried]],
+            [field] + ([labels] if labelled else []) + [high, low, *leaving[:carried]],
             out_specs=[VMEM] * 3 + [HBM] * carried,
             scratch=[pltpu.SemaphoreType.DMA] * carried,
             flops=len(group) * 1_000_000_000,
@@ -445,13 +493,15 @@
     )
     come = exchange(send_a, send_b, "col")
     middles = []
-    for number in range(cuts):
+    start = 0
+    for count in cuts:
         middles += call(
-            functools.partial(middle_kernel, groups=groups, start=number * (rows // cuts)),
-            [((rows // cuts, columns - TILE), F32)],
+            functools.partial(middle_kernel, groups=groups, start=start),
+            [((count, columns - TILE), F32)],
             [*highs, *lows, edge_high, edge_low, high, low],
-            flops=len(bands) * 750_000_000 // cuts,
+            flops=len(bands) * 750_000_000 * count // rows,
         )
+        start += count
     pieces = [left, *middles, right, *come]
     return (pieces, left_behind) if leaving else pieces
 
@@ -483,7 +533,6 @@
     return [
         ((count * BAND, TILE), BF16),
         ((count * BAND, TILE), BF16),
-        ((count, BAND, 3 * TILE), BF16),
         ((count, 128, 384), BF16),
     ]
 
@@ -491,6 +540,7 @@
 def body(counts, sample_weights, classes, class_radius):
     shape = rows, columns = counts.shape
     groups = ((0, 1), (2, 3))
+    cuts = (rows - 192, 192)
     rim, slim = (REACH, columns), (PILOT_RADIUS, columns)
     counts, sample_weights, classes = (
         pltpu.with_memory_space_constraint(field, pltpu.HBM)
@@ -522,18 +572,18 @@
         scratch=[pltpu.VMEM(shape, jnp.int32), pltpu.SemaphoreType.DMA((chunks,))],
         flops=500_000_000,
     )
-    pieces = smooth(mass, mass_halo, None, None, pilot_tables, ((0,),), 1)
+    pieces = smooth(mass, mass_halo, None, None, pilot_tables, ((0,),), (rows,))
     adapted, *sends, first_stat = finish(pieces, [mass], False, True, True, shape)
     halo = exchange(*sends, "row")
     first_total = total_over(first_stat)
-    pieces = smooth(adapted, halo, labels, label_halo, tables, groups, 2)
+    pieces = smooth(adapted, halo, labels, label_halo, tables, groups, cuts)
     density_first, adapted, *sends, second_stat = finish(
         pieces, [first_total, first_total, mass], True, True, False, shape
     )
     halo = exchange(*sends, "row")
     second_total = total_over(second_stat)
     pieces, density_first = smooth(
-        adapted, halo, labels, label_halo, tables, groups, 2, (density_first,)
+        adapted, halo, labels, label_halo, tables, groups, cuts, (density_first,)
     )
     (density_second,) = finish(
         pieces, [second_total, first_total], True, False, False, shape

time: 94.2 us -> 96 us (1.019)
  waiting for transfers between devices: 14.9 us -> 18.8 us
  Pallas kernels: 33.8 us -> 30.1 us
  starting transfers between devices: 44.3 us -> 45.8 us
    ppermute x14, starting transfers between devices: 16 us -> 24.4 us  [total_over(): stat = stat + lax.ppermute(stat, axis, pairs)]
    ppermute x14, starting transfers between devices: 28.3 us -> 21.4 us  [exchange(): results.append(lax.ppermute(value, ('row', 'col'), pairs))]
    pallas_call x18, Pallas kernels: 33.8 us -> 30.1 us  [call(): pl.pallas_call(kernel, out_shape=[jax.ShapeDtypeStruct(s, d) for s, d in...]
    ppermute x14, waiting for transfers between devices: 3.62 us -> 5.77 us  [exchange(): results.append(lax.ppermute(value, ('row', 'col'), pairs))]
    ppermute x14, waiting for transfers between devices: 11.3 us -> 13 us  [total_over(): stat = stat + lax.ppermute(stat, axis, pairs)]
  transfers between devices with their start and end apart: 28 -> 28, of which waited for: 14 -> 13; matrix products, arithmetic and copies ran while one was open for 0% -> 0% of each run, Pallas kernels for 24% -> 20%
where the time goes in v4:
time: 96 us; the launch traced here: 95.9 us
  starting transfers between devices  45.8 us (48%)
  Pallas kernels  30.1 us (31%)
  waiting for transfers between devices  18.8 us (20%)
  between operations  1.12 us (1%)
    pallas_call x18, Pallas kernels, call(): pl.pallas_call(kernel, out_shape=[jax.ShapeDtypeStruct(s, d) for s, d in...  30.1 us
    ppermute x14, starting transfers between devices, total_over(): stat = stat + lax.ppermute(stat, axis, pairs)  24.4 us
    ppermute x14, starting transfers between devices, exchange(): results.append(lax.ppermute(value, ('row', 'col'), pairs))  21.4 us
    ppermute x14, waiting for transfers between devices, total_over(): stat = stat + lax.ppermute(stat, axis, pairs)  13 us
    ppermute x14, waiting for transfers between devices, exchange(): results.append(lax.ppermute(value, ('row', 'col'), pairs))  5.77 us
  transfers between devices with their start and end apart: 28, of which 13 were waited for; matrix products, arithmetic and copies ran while one was open for 0% of the time, Pallas kernels for 20%

profile of v4, /device:TPU:1, one launch (start us, length us, event | category | flops | bytes accessed | tf_op | source)
XLA Modules:
  0.0 95.9 jit_solution(163521554470308493)
XLA Ops:
  0.6 2.4 %shard_map.59 = (bf16[384,256]{1,0:T(8,128)(2,1)S(1)}, bf16[384,256]{1,0:T(8,128)(2,1)S(1)}, bf16[1,128,384]{2,1,0:T(8,128)(2,1)S(1)}, f32[512,1024]{1,0:T(8,128...) custom-call(s32[512,1024]{1,0:T(8,128)} %refs_0_.2, ...), custom_call_target="tpu_custom_call" | custom-call | flops 500000000 | bytes 4194304 | tf_op jit(solution)/shard_map/pallas_call | solution.py:27
  3.1 2.2 %collective-permute-start = (f32[32,1024]{1,0:T(8,128)S(1)}, f32[32,1024]{1,0:T(8,128)S(1)}, u32[]{:S(2)}, u32[]{:S(2)}) collective-permute-start(f32[32,1024]{1,0:T(8,128)S(1)} %get-tuple-element.57), channel_id=1, source_target_pairs={{0,8},{1,9},{2,10},{3,11},{4,12},{5,13},{6,14},{7,15},{8,0},{9,1},... | collective-permute-start | bytes 393224 | tf_op jit(solution)/shard_map/ppermute | solution.py:438
  10.4 1.8 %collective-permute-start.3 = (f32[256,128]{1,0:T(8,128)S(1)}, f32[256,128]{1,0:T(8,128)S(1)}, u32[]{:S(2)}, u32[]{:S(2)}) collective-permute-start(f32[256,128]{1,0:T(8,128)S(1)} %get-tuple-element.71), channel_id=1, source_target_pairs={{0,8},{1,2},{2,1},{3,4},{4,3},{5,6},{6,5},{7,15},{8,0},{9,10},{10,... | collective-permute-start | bytes 393224 | tf_op jit(solution)/shard_map/ppermute | solution.py:438
  13.2 1.9 %collective-permute-done.3.refs_4_ = f32[256,128]{1,0:T(8,128)S(1)} collective-permute-done((f32[256,128]{1,0:T(8,128)S(1)}, f32[256,128]{1,0:T(8,128)S(1)}, u32[]{:S(2)}, u32[]{:S(2)}) %collective-permute-start.3) | collective-permute-done | bytes 131104 | tf_op jit(solution)/shard_map/ppermute | solution.py:438
  18.9 3.7 %collective-permute-start.11 = (f32[8,128]{1,0:T(8,128)S(1)}, f32[8,128]{1,0:T(8,128)S(1)}, u32[]{:S(2)}, u32[]{:S(2)}) collective-permute-start(f32[8,128]{1,0:T(8,128)S(1)} %add.42), channel_id=1, source_target_pairs={{0,6},{1,7},{2,4},{3,5},{4,2},{5,3},{6,0},{7,1},{8,14},{9,15},{10,... | collective-permute-start | bytes 12296 | tf_op jit(solution)/shard_map/ppermute | solution.py:457
  23.5 5.5 %collective-permute-start.12 = (f32[8,128]{1,0:T(8,128)S(1)}, f32[8,128]{1,0:T(8,128)S(1)}, u32[]{:S(2)}, u32[]{:S(2)}) collective-permute-start(f32[8,128]{1,0:T(8,128)S(1)} %add.43), channel_id=1, source_target_pairs={{0,96},{8,104},{16,112},{24,120},{32,64},{40,72},{48,80},{56,88},{... | collective-permute-start | bytes 12296 | tf_op jit(solution)/shard_map/ppermute | solution.py:457
  30.2 3.8 %collective-permute-start.7 = (s32[64,1024]{1,0:T(8,128)S(1)}, s32[64,1024]{1,0:T(8,128)S(1)}, u32[]{:S(2)}, u32[]{:S(2)}) collective-permute-start(s32[64,1024]{1,0:T(8,128)S(1)} %get-tuple-element.75), channel_id=1, source_target_pairs={{0,1},{1,0},{2,3},{3,2},{4,5},{5,4},{6,7},{7,6},{8,16},{9,17},{10,... | collective-permute-start | bytes 786440 | tf_op jit(solution)/shard_map/ppermute | solution.py:438
  34.9 2.2 %shard_map.64 = (bf16[1536,256]{1,0:T(8,128)(2,1)S(1)}, bf16[1536,256]{1,0:T(8,128)(2,1)S(1)}, bf16[4,128,384]{2,1,0:T(8,128)(2,1)S(1)}, bf16[512,1024]{1,0:T(8,128)(2,1)S(1)}) custom-call(s32[4]{0:T(128)S(1)} %copy-done, s32[512,1024]{1,0:T(8,128)} %refs_1_.3), custom_call_target="tpu_custom_call" | custom-call | flops 500000000 | bytes 4194304 | tf_op jit(solution)/shard_map/pallas_call | solution.py:27
  37.2 4.8 %collective-permute-start.5 = (f32[64,1024]{1,0:T(8,128)S(1)}, f32[64,1024]{1,0:T(8,128)S(1)}, u32[]{:S(2)}, u32[]{:S(2)}) collective-permute-start(f32[64,1024]{1,0:T(8,128)S(1)} %get-tuple-element.73), channel_id=1, source_target_pairs={{0,1},{1,0},{2,3},{3,2},{4,5},{5,4},{6,7},{7,6},{8,16},{9,17},{10,... | collective-permute-start | bytes 786440 | tf_op jit(solution)/shard_map/ppermute | solution.py:438
  42.0 1.9 %shard_map.66 = (bf16[2,384,1024]{2,1,0:T(8,128)(2,1)S(1)}, bf16[2,384,1024]{2,1,0:T(8,128)(2,1)S(1)}, f32[2,128,1024]{2,1,0:T(8,128)S(1)}) custom-call(f32[512,1024]{1,0:T(8,128)S(1)} %get-tuple-element.76.refs_0_, bf16[512,1024]{1,0:T(8,128)(2,1)S(1)} %get-tuple-element.77.refs_1_, bf16[1536,256]{1,0:T(8,128)(2,1)S(1)} %get-tuple-element.78.refs_2_.refs_11_.refs_6_, ...), custom_call_target="tpu_custom_call" | custom-call | flops 2000000000 | bytes 4194304 | tf_op jit(solution)/shard_map/pallas_call | solution.py:27
  44.4 3.9 %collective-permute-start.16 = (f32[8,128]{1,0:T(8,128)S(1)}, f32[8,128]{1,0:T(8,128)S(1)}, u32[]{:S(2)}, u32[]{:S(2)}) collective-permute-start(f32[8,128]{1,0:T(8,128)S(1)} %add.47), channel_id=1, source_target_pairs={{0,1},{1,0},{2,3},{3,2},{4,5},{5,4},{6,7},{7,6},{8,9},{9,8},{10,11... | collective-permute-start | bytes 12296 | tf_op jit(solution)/shard_map/ppermute | solution.py:457
  48.3 1.9 %shard_map.65 = (bf16[2,384,1024]{2,1,0:T(8,128)(2,1)S(1)}, bf16[2,384,1024]{2,1,0:T(8,128)(2,1)S(1)}, f32[2,128,1024]{2,1,0:T(8,128)S(1)}) custom-call(f32[512,1024]{1,0:T(8,128)S(1)} %get-tuple-element.76.refs_0_, bf16[512,1024]{1,0:T(8,128)(2,1)S(1)} %get-tuple-element.77.refs_1_, bf16[1536,256]{1,0:T(8,128)(2,1)S(1)} %get-tuple-element.78.refs_2_.refs_11_.refs_6_, ...), custom_call_target="tpu_custom_call" | custom-call | flops 2000000000 | bytes 4194304 | tf_op jit(solution)/shard_map/pallas_call | solution.py:27
  50.3 1.9 %shard_map.67 = (bf16[4,128,1024]{2,1,0:T(8,128)(2,1)S(1)}, bf16[4,128,1024]{2,1,0:T(8,128)(2,1)S(1)}, f32[512,256]{1,0:T(8,128)S(1)}, f32[512,128]{1,0:T(8,128)...) custom-call(f32[64,1024]{1,0:T(8,128)S(1)} %collective-permute-done.4.refs_0_, ...), custom_call_target="tpu_custom_call" | custom-call | flops 2000000000 | bytes 4194304 | tf_op jit(solution)/shard_map/pallas_call | solution.py:27
  52.3 2.0 %shard_map.68.refs_1_ = f32[320,768]{1,0:T(8,128)S(1)} custom-call(bf16[2,384,1024]{2,1,0:T(8,128)(2,1)S(1)} %get-tuple-element.82.refs_6_.refs_0_, bf16[2,384,1024]{2,1,0:T(8,128)(2,1)S(1)} %get-tuple-element.83.refs_7_.refs_1_, bf16[2,384,1024]{2,1,0:T(8,128)(2,1)S(1)} %get-tuple-element.84.refs_8_.refs_2_, ...), custom_call_target="tpu_custom_call" | custom-call | flops 1875000064 | bytes 4194304 | tf_op jit(solution)/shard_map/pallas_call | solution.py:27
  58.4 2.4 %collective-permute-done.21 = f32[8,128]{1,0:T(8,128)S(1)} collective-permute-done((f32[8,128]{1,0:T(8,128)S(1)}, f32[8,128]{1,0:T(8,128)S(1)}, u32[]{:S(2)}, u32[]{:S(2)}) %collective-permute-start.21) | collective-permute-done | bytes 4128 | tf_op jit(solution)/shard_map/ppermute | solution.py:457
  60.7 2.4 %collective-permute-start.22 = (f32[8,128]{1,0:T(8,128)S(1)}, f32[8,128]{1,0:T(8,128)S(1)}, u32[]{:S(2)}, u32[]{:S(2)}) collective-permute-start(f32[8,128]{1,0:T(8,128)S(1)} %add.49), channel_id=1, source_target_pairs={{0,6},{1,7},{2,4},{3,5},{4,2},{5,3},{6,0},{7,1},{8,14},{9,15},{10,... | collective-permute-start | bytes 12296 | tf_op jit(solution)/shard_map/ppermute | solution.py:457
  65.4 2.6 %collective-permute-done.23 = f32[8,128]{1,0:T(8,128)S(1)} collective-permute-done((f32[8,128]{1,0:T(8,128)S(1)}, f32[8,128]{1,0:T(8,128)S(1)}, u32[]{:S(2)}, u32[]{:S(2)}) %collective-permute-start.23) | collective-permute-done | bytes 4128 | tf_op jit(solution)/shard_map/ppermute | solution.py:457
  68.1 2.5 %collective-permute-done.24 = f32[8,128]{1,0:T(8,128)S(1)} collective-permute-done((f32[8,128]{1,0:T(8,128)S(1)}, f32[8,128]{1,0:T(8,128)S(1)}, u32[]{:S(2)}, u32[]{:S(2)}) %collective-permute-start.24) | collective-permute-done | bytes 4128 | tf_op jit(solution)/shard_map/ppermute | solution.py:457
  71.3 5.8 %collective-permute-start.18 = (f32[64,1024]{1,0:T(8,128)S(1)}, f32[64,1024]{1,0:T(8,128)S(1)}, u32[]{:S(2)}, u32[]{:S(2)}) collective-permute-start(f32[64,1024]{1,0:T(8,128)S(1)} %get-tuple-element.98), channel_id=1, source_target_pairs={{0,1},{1,0},{2,3},{3,2},{4,5},{5,4},{6,7},{7,6},{8,16},{9,17},{10,... | collective-permute-start | bytes 786440 | tf_op jit(solution)/shard_map/ppermute | solution.py:438
  77.1 1.9 %shard_map.72 = (bf16[2,384,1024]{2,1,0:T(8,128)(2,1)S(1)}, bf16[2,384,1024]{2,1,0:T(8,128)(2,1)S(1)}, f32[2,128,1024]{2,1,0:T(8,128)S(1)}) custom-call(f32[512,1024]{1,0:T(8,128)S(1)} %get-tuple-element.94.refs_0_, bf16[512,1024]{1,0:T(8,128)(2,1)S(1)} %get-tuple-element.77.refs_1_, bf16[1536,256]{1,0:T(8,128)(2,1)S(1)} %get-tuple-element.78.refs_2_.refs_11_.refs_6_, ...), custom_call_target="tpu_custom_call" | custom-call | flops 2000000000 | bytes 4194304 | tf_op jit(solution)/shard_map/pallas_call | solution.py:27
  79.9 4.4 %collective-permute-start.27 = (f32[8,128]{1,0:T(8,128)S(1)}, f32[8,128]{1,0:T(8,128)S(1)}, u32[]{:S(2)}, u32[]{:S(2)}) collective-permute-start(f32[8,128]{1,0:T(8,128)S(1)} %add.54), channel_id=1, source_target_pairs={{0,1},{1,0},{2,3},{3,2},{4,5},{5,4},{6,7},{7,6},{8,9},{9,8},{10,11... | collective-permute-start | bytes 12296 | tf_op jit(solution)/shard_map/ppermute | solution.py:457
  84.3 2.9 %shard_map.71 = (bf16[2,384,1024]{2,1,0:T(8,128)(2,1)S(1)}, bf16[2,384,1024]{2,1,0:T(8,128)(2,1)S(1)}, f32[2,128,1024]{2,1,0:T(8,128)S(1)}, f32[512,1024]{1,0:T(8,128)}) custom-call(f32[512,1024]{1,0:T(8,128)S(1)} %get-tuple-element.94.refs_0_, bf16[512,1024]{1,0:T(8,128)(2,1)S(1)} %get-tuple-element.77.refs_1_, ...), custom_call_target="tpu_custom_call" | custom-call | flops 2000000000 | bytes 4194304 | tf_op jit(solution)/shard_map/pallas_call | solution.py:27
  87.2 1.9 %shard_map.73 = (bf16[4,128,1024]{2,1,0:T(8,128)(2,1)S(1)}, bf16[4,128,1024]{2,1,0:T(8,128)(2,1)S(1)}, f32[512,256]{1,0:T(8,128)S(1)}, f32[512,128]{1,0:T(8,128)...) custom-call(f32[64,1024]{1,0:T(8,128)S(1)} %collective-permute-done.17.refs_0_, ...), custom_call_target="tpu_custom_call" | custom-call | flops 2000000000 | bytes 4194304 | tf_op jit(solution)/shard_map/pallas_call | solution.py:27
  89.3 2.0 %shard_map.74.refs_1_ = f32[320,768]{1,0:T(8,128)S(1)} custom-call(bf16[2,384,1024]{2,1,0:T(8,128)(2,1)S(1)} %get-tuple-element.101.refs_6_.refs_0_, bf16[2,384,1024]{2,1,0:T(8,128)(2,1)S(1)} %get-tuple-element.102.refs_7_.refs_1_, bf16[2,384,1024]{2,1,0:T(8,128)(2,1)S(1)} %get-tuple-element.103.refs_8_.refs_2_, ...), custom_call_target="tpu_custom_call" | custom-call | flops 1875000064 | bytes 4194304 | tf_op jit(solution)/shard_map/pallas_call | solution.py:27
  (66 shorter events, 26.2 us)
Async XLA Ops:
  3.1 5.1 %collective-permute-start = (f32[32,1024]{1,0:T(8,128)S(1)}, f32[32,1024]{1,0:T(8,128)S(1)}, u32[]{:S(2)}, u32[]{:S(2)}) collective-permute-start(f32[32,1024]{1,0:T(8,128)S(1)} %get-tuple-element.57), channel_id=1, source_target_pairs={{0,8},{1,9},{2,10},{3,11},{4,12},{5,13},{6,14},{7,15},{8,0},{9,1},... | collective-permute-start | bytes 393224 | tf_op jit(solution)/shard_map/ppermute | solution.py:438
  5.3 2.9 %collective-permute-start.1 = (f32[32,1024]{1,0:T(8,128)S(1)}, f32[32,1024]{1,0:T(8,128)S(1)}, u32[]{:S(2)}, u32[]{:S(2)}) collective-permute-start(f32[32,1024]{1,0:T(8,128)S(1)} %get-tuple-element.58), channel_id=1, source_target_pairs={{0,1},{1,0},{2,3},{3,2},{4,5},{5,4},{6,7},{7,6},{8,16},{9,17},{10,... | collective-permute-start | bytes 393224 | tf_op jit(solution)/shard_map/ppermute | solution.py:438
  8.8 4.4 %collective-permute-start.2 = (f32[256,128]{1,0:T(8,128)S(1)}, f32[256,128]{1,0:T(8,128)S(1)}, u32[]{:S(2)}, u32[]{:S(2)}) collective-permute-start(f32[256,128]{1,0:T(8,128)S(1)} %get-tuple-element.70), channel_id=1, source_target_pairs={{0,1},{1,0},{2,3},{3,2},{4,5},{5,4},{6,7},{7,6},{8,9},{9,8},{10,11... | collective-permute-start | bytes 393224 | tf_op jit(solution)/shard_map/ppermute | solution.py:438
  10.4 4.7 %collective-permute-start.3 = (f32[256,128]{1,0:T(8,128)S(1)}, f32[256,128]{1,0:T(8,128)S(1)}, u32[]{:S(2)}, u32[]{:S(2)}) collective-permute-start(f32[256,128]{1,0:T(8,128)S(1)} %get-tuple-element.71), channel_id=1, source_target_pairs={{0,8},{1,2},{2,1},{3,4},{4,3},{5,6},{6,5},{7,15},{8,0},{9,10},{10,... | collective-permute-start | bytes 393224 | tf_op jit(solution)/shard_map/ppermute | solution.py:438
  18.9 4.7 %collective-permute-start.11 = (f32[8,128]{1,0:T(8,128)S(1)}, f32[8,128]{1,0:T(8,128)S(1)}, u32[]{:S(2)}, u32[]{:S(2)}) collective-permute-start(f32[8,128]{1,0:T(8,128)S(1)} %add.42), channel_id=1, source_target_pairs={{0,6},{1,7},{2,4},{3,5},{4,2},{5,3},{6,0},{7,1},{8,14},{9,15},{10,... | collective-permute-start | bytes 12296 | tf_op jit(solution)/shard_map/ppermute | solution.py:457
  23.5 6.5 %collective-permute-start.12 = (f32[8,128]{1,0:T(8,128)S(1)}, f32[8,128]{1,0:T(8,128)S(1)}, u32[]{:S(2)}, u32[]{:S(2)}) collective-permute-start(f32[8,128]{1,0:T(8,128)S(1)} %add.43), channel_id=1, source_target_pairs={{0,96},{8,104},{16,112},{24,120},{32,64},{40,72},{48,80},{56,88},{... | collective-permute-start | bytes 12296 | tf_op jit(solution)/shard_map/ppermute | solution.py:457
  30.0 4.0 %collective-permute-start.13 = (f32[8,128]{1,0:T(8,128)S(1)}, f32[8,128]{1,0:T(8,128)S(1)}, u32[]{:S(2)}, u32[]{:S(2)}) collective-permute-start(f32[8,128]{1,0:T(8,128)S(1)} %add.44), channel_id=1, source_target_pairs={{0,32},{8,40},{16,48},{24,56},{32,0},{40,8},{48,16},{56,24},{64,96... | collective-permute-start | bytes 12296 | tf_op jit(solution)/shard_map/ppermute | solution.py:457
  30.2 20.0 %collective-permute-start.6 = (s32[64,1024]{1,0:T(8,128)S(1)}, s32[64,1024]{1,0:T(8,128)S(1)}, u32[]{:S(2)}, u32[]{:S(2)}) collective-permute-start(s32[64,1024]{1,0:T(8,128)S(1)} %get-tuple-element.74), channel_id=1, source_target_pairs={{0,8},{1,9},{2,10},{3,11},{4,12},{5,13},{6,14},{7,15},{8,0},{9,1},... | collective-permute-start | bytes 786440 | tf_op jit(solution)/shard_map/ppermute | solution.py:438
  30.2 20.0 %collective-permute-start.7 = (s32[64,1024]{1,0:T(8,128)S(1)}, s32[64,1024]{1,0:T(8,128)S(1)}, u32[]{:S(2)}, u32[]{:S(2)}) collective-permute-start(s32[64,1024]{1,0:T(8,128)S(1)} %get-tuple-element.75), channel_id=1, source_target_pairs={{0,1},{1,0},{2,3},{3,2},{4,5},{5,4},{6,7},{7,6},{8,16},{9,17},{10,... | collective-permute-start | bytes 786440 | tf_op jit(solution)/shard_map/ppermute | solution.py:438
  34.1 7.9 %collective-permute-start.14 = (f32[8,128]{1,0:T(8,128)S(1)}, f32[8,128]{1,0:T(8,128)S(1)}, u32[]{:S(2)}, u32[]{:S(2)}) collective-permute-start(f32[8,128]{1,0:T(8,128)S(1)} %add.45), channel_id=1, source_target_pairs={{0,24},{8,16},{16,8},{24,0},{32,56},{40,48},{48,40},{56,32},{64,88... | collective-permute-start | bytes 12296 | tf_op jit(solution)/shard_map/ppermute | solution.py:457
  37.1 13.2 %collective-permute-start.4 = (f32[64,1024]{1,0:T(8,128)S(1)}, f32[64,1024]{1,0:T(8,128)S(1)}, u32[]{:S(2)}, u32[]{:S(2)}) collective-permute-start(f32[64,1024]{1,0:T(8,128)S(1)} %get-tuple-element.72), channel_id=1, source_target_pairs={{0,8},{1,9},{2,10},{3,11},{4,12},{5,13},{6,14},{7,15},{8,0},{9,1},... | collective-permute-start | bytes 786440 | tf_op jit(solution)/shard_map/ppermute | solution.py:438
  37.2 13.1 %collective-permute-start.5 = (f32[64,1024]{1,0:T(8,128)S(1)}, f32[64,1024]{1,0:T(8,128)S(1)}, u32[]{:S(2)}, u32[]{:S(2)}) collective-permute-start(f32[64,1024]{1,0:T(8,128)S(1)} %get-tuple-element.73), channel_id=1, source_target_pairs={{0,1},{1,0},{2,3},{3,2},{4,5},{5,4},{6,7},{7,6},{8,16},{9,17},{10,... | collective-permute-start | bytes 786440 | tf_op jit(solution)/shard_map/ppermute | solution.py:438
  44.4 5.8 %collective-permute-start.16 = (f32[8,128]{1,0:T(8,128)S(1)}, f32[8,128]{1,0:T(8,128)S(1)}, u32[]{:S(2)}, u32[]{:S(2)}) collective-permute-start(f32[8,128]{1,0:T(8,128)S(1)} %add.47), channel_id=1, source_target_pairs={{0,1},{1,0},{2,3},{3,2},{4,5},{5,4},{6,7},{7,6},{8,9},{9,8},{10,11... | collective-permute-start | bytes 12296 | tf_op jit(solution)/shard_map/ppermute | solution.py:457
  52.1 3.4 %collective-permute-start.8 = (f32[256,128]{1,0:T(8,128)S(1)}, f32[256,128]{1,0:T(8,128)S(1)}, u32[]{:S(2)}, u32[]{:S(2)}) collective-permute-start(f32[256,128]{1,0:T(8,128)S(1)} %get-tuple-element.91), channel_id=1, source_target_pairs={{0,1},{1,0},{2,3},{3,2},{4,5},{5,4},{6,7},{7,6},{8,9},{9,8},{10,11... | collective-permute-start | bytes 393224 | tf_op jit(solution)/shard_map/ppermute | solution.py:438
  52.2 4.8 %collective-permute-start.9 = (f32[256,128]{1,0:T(8,128)S(1)}, f32[256,128]{1,0:T(8,128)S(1)}, u32[]{:S(2)}, u32[]{:S(2)}) collective-permute-start(f32[256,128]{1,0:T(8,128)S(1)} %get-tuple-element.92), channel_id=1, source_target_pairs={{0,8},{1,2},{2,1},{3,4},{4,3},{5,6},{6,5},{7,15},{8,0},{9,10},{10,... | collective-permute-start | bytes 393224 | tf_op jit(solution)/shard_map/ppermute | solution.py:438
  60.7 3.7 %collective-permute-start.22 = (f32[8,128]{1,0:T(8,128)S(1)}, f32[8,128]{1,0:T(8,128)S(1)}, u32[]{:S(2)}, u32[]{:S(2)}) collective-permute-start(f32[8,128]{1,0:T(8,128)S(1)} %add.49), channel_id=1, source_target_pairs={{0,6},{1,7},{2,4},{3,5},{4,2},{5,3},{6,0},{7,1},{8,14},{9,15},{10,... | collective-permute-start | bytes 12296 | tf_op jit(solution)/shard_map/ppermute | solution.py:457
  64.4 3.7 %collective-permute-start.23 = (f32[8,128]{1,0:T(8,128)S(1)}, f32[8,128]{1,0:T(8,128)S(1)}, u32[]{:S(2)}, u32[]{:S(2)}) collective-permute-start(f32[8,128]{1,0:T(8,128)S(1)} %add.50), channel_id=1, source_target_pairs={{0,96},{8,104},{16,112},{24,120},{32,64},{40,72},{48,80},{56,88},{... | collective-permute-start | bytes 12296 | tf_op jit(solution)/shard_map/ppermute | solution.py:457
  70.5 6.6 %collective-permute-start.25 = (f32[8,128]{1,0:T(8,128)S(1)}, f32[8,128]{1,0:T(8,128)S(1)}, u32[]{:S(2)}, u32[]{:S(2)}) collective-permute-start(f32[8,128]{1,0:T(8,128)S(1)} %add.52), channel_id=1, source_target_pairs={{0,24},{8,16},{16,8},{24,0},{32,56},{40,48},{48,40},{56,32},{64,88... | collective-permute-start | bytes 12296 | tf_op jit(solution)/shard_map/ppermute | solution.py:457
  71.3 15.9 %collective-permute-start.17 = (f32[64,1024]{1,0:T(8,128)S(1)}, f32[64,1024]{1,0:T(8,128)S(1)}, u32[]{:S(2)}, u32[]{:S(2)}) collective-permute-start(f32[64,1024]{1,0:T(8,128)S(1)} %get-tuple-element.97), channel_id=1, source_target_pairs={{0,8},{1,9},{2,10},{3,11},{4,12},{5,13},{6,14},{7,15},{8,0},{9,1},... | collective-permute-start | bytes 786440 | tf_op jit(solution)/shard_map/ppermute | solution.py:438
  71.3 15.9 %collective-permute-start.18 = (f32[64,1024]{1,0:T(8,128)S(1)}, f32[64,1024]{1,0:T(8,128)S(1)}, u32[]{:S(2)}, u32[]{:S(2)}) collective-permute-start(f32[64,1024]{1,0:T(8,128)S(1)} %get-tuple-element.98), channel_id=1, source_target_pairs={{0,1},{1,0},{2,3},{3,2},{4,5},{5,4},{6,7},{7,6},{8,16},{9,17},{10,... | collective-permute-start | bytes 786440 | tf_op jit(solution)/shard_map/ppermute | solution.py:438
  77.1 2.8 %collective-permute-start.26 = (f32[8,128]{1,0:T(8,128)S(1)}, f32[8,128]{1,0:T(8,128)S(1)}, u32[]{:S(2)}, u32[]{:S(2)}) collective-permute-start(f32[8,128]{1,0:T(8,128)S(1)} %add.53), channel_id=1, source_target_pairs={{0,8},{8,0},{16,24},{24,16},{32,40},{40,32},{48,56},{56,48},{64,72... | collective-permute-start | bytes 12296 | tf_op jit(solution)/shard_map/ppermute | solution.py:457
  79.9 7.3 %collective-permute-start.27 = (f32[8,128]{1,0:T(8,128)S(1)}, f32[8,128]{1,0:T(8,128)S(1)}, u32[]{:S(2)}, u32[]{:S(2)}) collective-permute-start(f32[8,128]{1,0:T(8,128)S(1)} %add.54), channel_id=1, source_target_pairs={{0,1},{1,0},{2,3},{3,2},{4,5},{5,4},{6,7},{7,6},{8,9},{9,8},{10,11... | collective-permute-start | bytes 12296 | tf_op jit(solution)/shard_map/ppermute | solution.py:457
  89.1 3.4 %collective-permute-start.19 = (f32[256,128]{1,0:T(8,128)S(1)}, f32[256,128]{1,0:T(8,128)S(1)}, u32[]{:S(2)}, u32[]{:S(2)}) collective-permute-start(f32[256,128]{1,0:T(8,128)S(1)} %get-tuple-element.109), channel_id=1, source_target_pairs={{0,1},{1,0},{2,3},{3,2},{4,5},{5,4},{6,7},{7,6},{8,9},{9,8},{10,11... | collective-permute-start | bytes 393224 | tf_op jit(solution)/shard_map/ppermute | solution.py:438
  89.2 4.8 %collective-permute-start.20 = (f32[256,128]{1,0:T(8,128)S(1)}, f32[256,128]{1,0:T(8,128)S(1)}, u32[]{:S(2)}, u32[]{:S(2)}) collective-permute-start(f32[256,128]{1,0:T(8,128)S(1)} %get-tuple-element.110), channel_id=1, source_target_pairs={{0,8},{1,2},{2,1},{3,4},{4,3},{5,6},{6,5},{7,15},{8,0},{9,10},{10,... | collective-permute-start | bytes 393224 | tf_op jit(solution)/shard_map/ppermute | solution.py:438
  (5 other events, 29.7 us)

commit v5 on v4

--- a/solution.py
+++ b/solution.py
@@ -165,10 +165,14 @@
         refs, 1, labelled, 2, carried, 3, carried
     )
     high_ref, low_ref, edge_ref = outs
-    copies = [pltpu.make_async_copy(*pair) for pair in zip(plane, plane_out, done)]
+    rows, columns = field_ref.shape
+    copies = []
+    for source, target, arrived in zip(plane, plane_out, done):
+        for n, start in enumerate(range(0, rows, STEP)):
+            at = slice(start, start + STEP)
+            copies.append(pltpu.make_async_copy(source.at[at], target.at[at], arrived.at[n]))
     for copy in copies:
         copy.start()
-    rows, columns = field_ref.shape
     count = rows // REACH
     for n in range(columns // TILE):
         at = slice(n * TILE, (n + 1) * TILE)
@@ -343,15 +347,18 @@
             out_ref[:, j * TILE + k * 128 : j * TILE + (k + 1) * 128] = value
 
 
+FINE = 16
+
+
 def gathered(pieces, come, flags, start):
     left_ref, middles, right_ref = pieces
     odd, has_left, has_right = flags
     rows = left_ref.shape[0]
     half = rows // 2
     kept = kept_row(start, rows)
-    at = slice(kept, kept + STEP)
-    lane = iota((STEP, 128), 1)
-    local = slice(kept % half, kept % half + STEP)
+    at = slice(kept, kept + FINE)
+    lane = iota((FINE, 128), 1)
+    local = slice(kept % half, kept % half + FINE)
     come_left = chosen(has_left, chosen(odd, come[0][local], come[1][local]), 0.0)
     come_right = chosen(has_right, chosen(odd, come[1][local], come[0][local]), 0.0)
     if kept < half:
@@ -365,12 +372,22 @@
         if own < middle_ref.shape[0]:
             break
         own -= middle_ref.shape[0]
-    own = slice(own, own + STEP)
-    blocks = [first, left_ref[at, 128:256]]
-    blocks += [middle_ref[own, k : k + 128] for k in range(0, middle_ref.shape[1], 128)]
-    blocks += [last]
-    turned = [pltpu.roll(block, REACH, 1) for block in blocks]
-    return [jnp.where(lane < REACH, a, b) for a, b in zip(turned[:-1], turned[1:])]
+    own = slice(own, own + FINE)
+
+    def block_of(k):
+        if k == 0:
+            return first
+        if k == 1:
+            return left_ref[at, 128:256]
+        if k * 128 < TILE + middle_ref.shape[1]:
+            return middle_ref[own, k * 128 - TILE : (k + 1) * 128 - TILE]
+        return last
+
+    before = pltpu.roll(block_of(0), REACH, 1)
+    for k in range((TILE + middle_ref.shape[1]) // 128):
+        after = pltpu.roll(block_of(k + 1), REACH, 1)
+        yield jnp.where(lane < REACH, before, after)
+        before = after
 
 
 def finish_kernel(*refs, middles, scaled, following, totals):
@@ -384,11 +401,15 @@
     staged, done = refs if leaving else (density_out[0] if scaled else None, None)
     rows = left_ref.shape[0]
     column_flags = flags_of("col")
-    log_sum = jnp.zeros((8, 128), F32)
-    mass_sum = jnp.zeros((8, 128), F32)
+    columns = TILE + middle_refs[0].shape[1]
+    log_sums = [jnp.zeros((8, 128), F32)] * (columns // 128)
+    mass_sums = [jnp.zeros((8, 128), F32)] * (columns // 128)
+    if following:
+        odd_row = flags_of("row")[0]
+        adapted_ref, send_a, send_b, stat_ref = adapted_out
     copies = []
-    for number, start in enumerate(range(0, rows, STEP)):
-        at = slice(start, start + STEP)
+    for start in range(0, rows, FINE):
+        at = slice(start, start + FINE)
         for k, block in enumerate(gathered(pieces, come, column_flags, start)):
             lanes = slice(k * 128, (k + 1) * 128)
             if scaled:
@@ -397,23 +418,25 @@
             if following:
                 pilot = block + BACKGROUND
                 mass = mass_in[0][at, lanes]
-                adapted_out[0][at, lanes] = mass * pilot
+                adapted_ref[at, lanes] = mass * pilot
                 terms = mass * jnp.log(pilot)
-                log_sum += jnp.sum(terms.reshape(STEP // 8, 8, 128), axis=0)
-                if totals:
-                    mass_sum += jnp.sum(mass.reshape(STEP // 8, 8, 128), axis=0)
-        if leaving:
-            copy = pltpu.make_async_copy(staged.at[at], density_out[0].at[at], done.at[number])
+                for i in range(0, FINE, 8):
+                    log_sums[k] = log_sums[k] + terms[i : i + 8]
+                    if totals:
+                        mass_sums[k] = mass_sums[k] + mass[i : i + 8]
+        if leaving and (start + FINE) % STEP == 0:
+            at = slice(start + FINE - STEP, start + FINE)
+            copy = pltpu.make_async_copy(
+                staged.at[at], density_out[0].at[at], done.at[start // STEP]
+            )
             copy.start()
             copies.append(copy)
     if following:
-        adapted_ref, send_a, send_b, stat_ref = adapted_out
-        odd_row = flags_of("row")[0]
         top, bottom = adapted_ref[0:REACH], adapted_ref[rows - REACH :]
         send_a[...] = chosen(odd_row, top, bottom)
         send_b[...] = chosen(odd_row, bottom, top)
-        log_sum = jnp.sum(log_sum, axis=(0, 1), keepdims=True)
-        mass_sum = jnp.sum(mass_sum, axis=(0, 1), keepdims=True)
+        log_sum = jnp.sum(sum(log_sums), axis=(0, 1), keepdims=True)
+        mass_sum = jnp.sum(sum(mass_sums), axis=(0, 1), keepdims=True)
         row = iota((8, 128), 0)
         stat_ref[...] = jnp.where(row == 0, log_sum, jnp.where(row == 1, mass_sum, 0.0))
     for copy in copies:
@@ -440,21 +463,25 @@
 
 
 HOPS = (
-    ("col", 2, 8),
-    ("col", 6, 8),
-    ("row", 12, 16),
-    ("row", 4, 16),
-    ("row", 3, 4),
-    ("row", 1, 2),
-    ("col", 1, 2),
+    (0, 3, (1, 8)),
+    (0, 7, (1, 8)),
+    (12, 1, (16, 1)),
+    (4, 1, (16, 1)),
+    (3, 1, (4, 1)),
+    (1, 1, (2, 1)),
+    (0, 1, (1, 2)),
 )
 
 
 def total_over(stat):
-    for axis, hop, least in HOPS:
-        if lax.axis_size(axis) >= least:
-            pairs = [(i, i ^ hop) for i in range(lax.axis_size(axis))]
-            stat = stat + lax.ppermute(stat, axis, pairs)
+    sizes = (lax.axis_size("row"), lax.axis_size("col"))
+    for rows, columns, least in HOPS:
+        if sizes[0] >= least[0] and sizes[1] >= least[1]:
+            pairs = []
+            for index in range(sizes[0] * sizes[1]):
+                row, column = divmod(index, sizes[1])
+                pairs.append((index, (row ^ rows) * sizes[1] + (column ^ columns)))
+            stat = stat + lax.ppermute(stat, ("row", "col"), pairs)
     return stat
 
 
@@ -475,7 +502,7 @@
             [(inner, BF16), (inner, BF16), (edge, F32)] + [(field.shape, F32)] * carried,
             [field] + ([labels] if labelled else []) + [high, low, *leaving[:carried]],
             out_specs=[VMEM] * 3 + [HBM] * carried,
-            scratch=[pltpu.SemaphoreType.DMA] * carried,
+            scratch=[pltpu.SemaphoreType.DMA((rows // STEP,))] * carried,
             flops=len(group) * 1_000_000_000,
         )
         if carried:

time: 96 us -> 97.4 us (1.015)
  starting transfers between devices: 45.8 us -> 29.9 us
  waiting for transfers between devices: 18.8 us -> 32.7 us
  Pallas kernels: 30.1 us -> 33.5 us
    ppermute x14, waiting for transfers between devices: 13 us -> 26.9 us  [total_over(): stat = stat + lax.ppermute(stat, ('row', 'col'), pairs)]
    ppermute x14, starting transfers between devices: 21.4 us -> 8.78 us  [exchange(): results.append(lax.ppermute(value, ('row', 'col'), pairs))]
    pallas_call x18, Pallas kernels: 30.1 us -> 33.5 us  [call(): pl.pallas_call(kernel, out_shape=[jax.ShapeDtypeStruct(s, d) for s, d in...]
    ppermute x14, starting transfers between devices: 24.4 us -> 21.1 us  [total_over(): stat = stat + lax.ppermute(stat, ('row', 'col'), pairs)]
  transfers between devices with their start and end apart: 28 -> 28, of which waited for: 13 -> 15; matrix products, arithmetic and copies ran while one was open for 0% -> 0% of each run, Pallas kernels for 20% -> 20%
where the time goes in v5:
time: 97.4 us; the launch traced here: 97.3 us
  Pallas kernels  33.5 us (34%)
  waiting for transfers between devices  32.7 us (34%)
  starting transfers between devices  29.9 us (31%)
  between operations  1.08 us (1%)
    pallas_call x18, Pallas kernels, call(): pl.pallas_call(kernel, out_shape=[jax.ShapeDtypeStruct(s, d) for s, d in...  33.5 us
    ppermute x14, waiting for transfers between devices, total_over(): stat = stat + lax.ppermute(stat, ('row', 'col'), pairs)  26.9 us
    ppermute x14, starting transfers between devices, total_over(): stat = stat + lax.ppermute(stat, ('row', 'col'), pairs)  21.1 us
    ppermute x14, starting transfers between devices, exchange(): results.append(lax.ppermute(value, ('row', 'col'), pairs))  8.78 us
    ppermute x14, waiting for transfers between devices, exchange(): results.append(lax.ppermute(value, ('row', 'col'), pairs))  5.76 us
  transfers between devices with their start and end apart: 28, of which 15 were waited for; matrix products, arithmetic and copies ran while one was open for 0% of the time, Pallas kernels for 20%

profile of v5, /device:TPU:1, one launch (start us, length us, event | category | flops | bytes accessed | tf_op | source)
XLA Modules:
  0.0 97.3 jit_solution(16651057029517696560)
XLA Ops:
  0.6 2.4 %shard_map.59 = (bf16[384,256]{1,0:T(8,128)(2,1)S(1)}, bf16[384,256]{1,0:T(8,128)(2,1)S(1)}, bf16[1,128,384]{2,1,0:T(8,128)(2,1)S(1)}, f32[512,1024]{1,0:T(8,128...) custom-call(s32[512,1024]{1,0:T(8,128)} %refs_0_.2, ...), custom_call_target="tpu_custom_call" | custom-call | flops 500000000 | bytes 4194304 | tf_op jit(solution)/shard_map/pallas_call | solution.py:27
  3.1 2.2 %collective-permute-start = (f32[32,1024]{1,0:T(8,128)S(1)}, f32[32,1024]{1,0:T(8,128)S(1)}, u32[]{:S(2)}, u32[]{:S(2)}) collective-permute-start(f32[32,1024]{1,0:T(8,128)S(1)} %get-tuple-element.57), channel_id=1, source_target_pairs={{0,8},{1,9},{2,10},{3,11},{4,12},{5,13},{6,14},{7,15},{8,0},{9,1},... | collective-permute-start | bytes 393224 | tf_op jit(solution)/shard_map/ppermute | solution.py:461
  13.2 1.9 %collective-permute-done.3.refs_4_ = f32[256,128]{1,0:T(8,128)S(1)} collective-permute-done((f32[256,128]{1,0:T(8,128)S(1)}, f32[256,128]{1,0:T(8,128)S(1)}, u32[]{:S(2)}, u32[]{:S(2)}) %collective-permute-start.3) | collective-permute-done | bytes 131104 | tf_op jit(solution)/shard_map/ppermute | solution.py:461
  15.2 2.2 %shard_map.63 = (f32[512,1024]{1,0:T(8,128)S(1)}, f32[64,1024]{1,0:T(8,128)S(1)}, f32[64,1024]{1,0:T(8,128)S(1)}, f32[8,128]{1,0:T(8,128)S(1)}) custom-call(f32[512,256]{1,0:T(8,128)S(1)} %get-tuple-element.66.refs_0_, f32[512,768]{1,0:T(8,128)S(1)} %shard_map.62.refs_1_, f32[512,128]{1,0:T(8,128)S(1)} %get-tuple-element.69.refs_2_, ...), custom_call_target="tpu_custom_call" | custom-call | flops 500000000 | bytes 4194304 | tf_op jit(solution)/shard_map/pallas_call | solution.py:27
  20.5 3.6 %collective-permute-start.11 = (f32[8,128]{1,0:T(8,128)S(1)}, f32[8,128]{1,0:T(8,128)S(1)}, u32[]{:S(2)}, u32[]{:S(2)}) collective-permute-start(f32[8,128]{1,0:T(8,128)S(1)} %add.42), channel_id=1, source_target_pairs={{0,7},{1,6},{2,5},{3,4},{4,3},{5,2},{6,1},{7,0},{8,15},{9,14},{10,... | collective-permute-start | bytes 12296 | tf_op jit(solution)/shard_map/ppermute | solution.py:484
  25.5 5.8 %collective-permute-start.12 = (f32[8,128]{1,0:T(8,128)S(1)}, f32[8,128]{1,0:T(8,128)S(1)}, u32[]{:S(2)}, u32[]{:S(2)}) collective-permute-start(f32[8,128]{1,0:T(8,128)S(1)} %add.43), channel_id=1, source_target_pairs={{0,97},{1,96},{2,99},{3,98},{4,101},{5,100},{6,103},{7,102},{8,105... | collective-permute-start | bytes 12296 | tf_op jit(solution)/shard_map/ppermute | solution.py:484
  33.4 2.2 %collective-permute-done.13 = f32[8,128]{1,0:T(8,128)S(1)} collective-permute-done((f32[8,128]{1,0:T(8,128)S(1)}, f32[8,128]{1,0:T(8,128)S(1)}, u32[]{:S(2)}, u32[]{:S(2)}) %collective-permute-start.13) | collective-permute-done | bytes 4128 | tf_op jit(solution)/shard_map/ppermute | solution.py:484
  35.6 2.4 %collective-permute-start.14 = (f32[8,128]{1,0:T(8,128)S(1)}, f32[8,128]{1,0:T(8,128)S(1)}, u32[]{:S(2)}, u32[]{:S(2)}) collective-permute-start(f32[8,128]{1,0:T(8,128)S(1)} %add.45), channel_id=1, source_target_pairs={{0,25},{1,24},{2,27},{3,26},{4,29},{5,28},{6,31},{7,30},{8,17},{9,... | collective-permute-start | bytes 12296 | tf_op jit(solution)/shard_map/ppermute | solution.py:484
  38.0 2.2 %shard_map.64 = (bf16[1536,256]{1,0:T(8,128)(2,1)S(1)}, bf16[1536,256]{1,0:T(8,128)(2,1)S(1)}, bf16[4,128,384]{2,1,0:T(8,128)(2,1)S(1)}, bf16[512,1024]{1,0:T(8,128)(2,1)S(1)}) custom-call(s32[4]{0:T(128)S(1)} %copy-done, s32[512,1024]{1,0:T(8,128)} %refs_1_.3), custom_call_target="tpu_custom_call" | custom-call | flops 500000000 | bytes 4194304 | tf_op jit(solution)/shard_map/pallas_call | solution.py:27
  42.4 1.9 %shard_map.66 = (bf16[2,384,1024]{2,1,0:T(8,128)(2,1)S(1)}, bf16[2,384,1024]{2,1,0:T(8,128)(2,1)S(1)}, f32[2,128,1024]{2,1,0:T(8,128)S(1)}) custom-call(f32[512,1024]{1,0:T(8,128)S(1)} %get-tuple-element.76.refs_0_, bf16[512,1024]{1,0:T(8,128)(2,1)S(1)} %get-tuple-element.77.refs_1_, bf16[1536,256]{1,0:T(8,128)(2,1)S(1)} %get-tuple-element.78.refs_2_.refs_11_.refs_6_, ...), custom_call_target="tpu_custom_call" | custom-call | flops 2000000000 | bytes 4194304 | tf_op jit(solution)/shard_map/pallas_call | solution.py:27
  44.3 4.3 %collective-permute-done.15 = f32[8,128]{1,0:T(8,128)S(1)} collective-permute-done((f32[8,128]{1,0:T(8,128)S(1)}, f32[8,128]{1,0:T(8,128)S(1)}, u32[]{:S(2)}, u32[]{:S(2)}) %collective-permute-start.15) | collective-permute-done | bytes 4128 | tf_op jit(solution)/shard_map/ppermute | solution.py:484
  48.7 1.9 %shard_map.65 = (bf16[2,384,1024]{2,1,0:T(8,128)(2,1)S(1)}, bf16[2,384,1024]{2,1,0:T(8,128)(2,1)S(1)}, f32[2,128,1024]{2,1,0:T(8,128)S(1)}) custom-call(f32[512,1024]{1,0:T(8,128)S(1)} %get-tuple-element.76.refs_0_, bf16[512,1024]{1,0:T(8,128)(2,1)S(1)} %get-tuple-element.77.refs_1_, bf16[1536,256]{1,0:T(8,128)(2,1)S(1)} %get-tuple-element.78.refs_2_.refs_11_.refs_6_, ...), custom_call_target="tpu_custom_call" | custom-call | flops 2000000000 | bytes 4194304 | tf_op jit(solution)/shard_map/pallas_call | solution.py:27
  53.1 1.9 %shard_map.68.refs_1_ = f32[320,768]{1,0:T(8,128)S(1)} custom-call(bf16[2,384,1024]{2,1,0:T(8,128)(2,1)S(1)} %get-tuple-element.82.refs_6_.refs_0_, bf16[2,384,1024]{2,1,0:T(8,128)(2,1)S(1)} %get-tuple-element.83.refs_7_.refs_1_, bf16[2,384,1024]{2,1,0:T(8,128)(2,1)S(1)} %get-tuple-element.84.refs_8_.refs_2_, ...), custom_call_target="tpu_custom_call" | custom-call | flops 1875000064 | bytes 4194304 | tf_op jit(solution)/shard_map/pallas_call | solution.py:27
  57.8 2.2 %shard_map.70 = (f32[512,1024]{1,0:T(8,128)S(1)}, f32[512,1024]{1,0:T(8,128)S(1)}, f32[64,1024]{1,0:T(8,128)S(1)}, f32[64,1024]{1,0:T(8,128)S(1)}, f32[8,128]{1,0:T(8,128)S(1)}) custom-call(f32[512,256]{1,0:T(8,128)S(1)} %get-tuple-element.87.refs_0_, f32[320,768]{1,0:T(8,128)S(1)} %shard_map.68.refs_1_, f32[192,768]{1,0:T(8,128)S(1)} %shard_map.69.refs_2_, ...), custom_call_target="tpu_custom_call" | custom-call | flops 500000000 | bytes 4194304 | tf_op jit(solution)/shard_map/pallas_call | solution.py:27
  60.4 2.7 %collective-permute-done.21 = f32[8,128]{1,0:T(8,128)S(1)} collective-permute-done((f32[8,128]{1,0:T(8,128)S(1)}, f32[8,128]{1,0:T(8,128)S(1)}, u32[]{:S(2)}, u32[]{:S(2)}) %collective-permute-start.21) | collective-permute-done | bytes 4128 | tf_op jit(solution)/shard_map/ppermute | solution.py:484
  63.2 2.6 %collective-permute-start.22 = (f32[8,128]{1,0:T(8,128)S(1)}, f32[8,128]{1,0:T(8,128)S(1)}, u32[]{:S(2)}, u32[]{:S(2)}) collective-permute-start(f32[8,128]{1,0:T(8,128)S(1)} %add.49), channel_id=1, source_target_pairs={{0,7},{1,6},{2,5},{3,4},{4,3},{5,2},{6,1},{7,0},{8,15},{9,14},{10,... | collective-permute-start | bytes 12296 | tf_op jit(solution)/shard_map/ppermute | solution.py:484
  68.7 3.0 %collective-permute-done.23 = f32[8,128]{1,0:T(8,128)S(1)} collective-permute-done((f32[8,128]{1,0:T(8,128)S(1)}, f32[8,128]{1,0:T(8,128)S(1)}, u32[]{:S(2)}, u32[]{:S(2)}) %collective-permute-start.23) | collective-permute-done | bytes 4128 | tf_op jit(solution)/shard_map/ppermute | solution.py:484
  72.1 2.6 %collective-permute-done.24 = f32[8,128]{1,0:T(8,128)S(1)} collective-permute-done((f32[8,128]{1,0:T(8,128)S(1)}, f32[8,128]{1,0:T(8,128)S(1)}, u32[]{:S(2)}, u32[]{:S(2)}) %collective-permute-start.24) | collective-permute-done | bytes 4128 | tf_op jit(solution)/shard_map/ppermute | solution.py:484
  75.7 3.2 %collective-permute-done.25 = f32[8,128]{1,0:T(8,128)S(1)} collective-permute-done((f32[8,128]{1,0:T(8,128)S(1)}, f32[8,128]{1,0:T(8,128)S(1)}, u32[]{:S(2)}, u32[]{:S(2)}) %collective-permute-start.25) | collective-permute-done | bytes 4128 | tf_op jit(solution)/shard_map/ppermute | solution.py:484
  79.1 1.9 %shard_map.72 = (bf16[2,384,1024]{2,1,0:T(8,128)(2,1)S(1)}, bf16[2,384,1024]{2,1,0:T(8,128)(2,1)S(1)}, f32[2,128,1024]{2,1,0:T(8,128)S(1)}) custom-call(f32[512,1024]{1,0:T(8,128)S(1)} %get-tuple-element.94.refs_0_, bf16[512,1024]{1,0:T(8,128)(2,1)S(1)} %get-tuple-element.77.refs_1_, bf16[1536,256]{1,0:T(8,128)(2,1)S(1)} %get-tuple-element.78.refs_2_.refs_11_.refs_6_, ...), custom_call_target="tpu_custom_call" | custom-call | flops 2000000000 | bytes 4194304 | tf_op jit(solution)/shard_map/pallas_call | solution.py:27
  81.0 3.0 %collective-permute-done.26 = f32[8,128]{1,0:T(8,128)S(1)} collective-permute-done((f32[8,128]{1,0:T(8,128)S(1)}, f32[8,128]{1,0:T(8,128)S(1)}, u32[]{:S(2)}, u32[]{:S(2)}) %collective-permute-start.26) | collective-permute-done | bytes 4128 | tf_op jit(solution)/shard_map/ppermute | solution.py:484
  84.0 2.8 %shard_map.71 = (bf16[2,384,1024]{2,1,0:T(8,128)(2,1)S(1)}, bf16[2,384,1024]{2,1,0:T(8,128)(2,1)S(1)}, f32[2,128,1024]{2,1,0:T(8,128)S(1)}, f32[512,1024]{1,0:T(8,128)}) custom-call(f32[512,1024]{1,0:T(8,128)S(1)} %get-tuple-element.94.refs_0_, bf16[512,1024]{1,0:T(8,128)(2,1)S(1)} %get-tuple-element.77.refs_1_, ...), custom_call_target="tpu_custom_call" | custom-call | flops 2000000000 | bytes 4194304 | tf_op jit(solution)/shard_map/pallas_call | solution.py:27
  89.3 1.9 %shard_map.74.refs_1_ = f32[320,768]{1,0:T(8,128)S(1)} custom-call(bf16[2,384,1024]{2,1,0:T(8,128)(2,1)S(1)} %get-tuple-element.101.refs_6_.refs_0_, bf16[2,384,1024]{2,1,0:T(8,128)(2,1)S(1)} %get-tuple-element.102.refs_7_.refs_1_, bf16[2,384,1024]{2,1,0:T(8,128)(2,1)S(1)} %get-tuple-element.103.refs_8_.refs_2_, ...), custom_call_target="tpu_custom_call" | custom-call | flops 1875000064 | bytes 4194304 | tf_op jit(solution)/shard_map/pallas_call | solution.py:27
  94.0 3.1 %shard_map.76 = f32[512,1024]{1,0:T(8,128)} custom-call(f32[512,256]{1,0:T(8,128)S(1)} %get-tuple-element.105.refs_0_, f32[320,768]{1,0:T(8,128)S(1)} %shard_map.74.refs_1_, f32[192,768]{1,0:T(8,128)S(1)} %shard_map.75.refs_2_, f32[512,128]{1,0:T(8,128)S(1)} %get-tuple-element.108.refs_3_, f32[256,128]{1,0:T(8,128)S(1)} %collective-permute-done.19.refs_4_, ...), custom_call_target="tpu_custom_call" | custom-call | flops 500000000 | bytes 4194304 | tf_op jit(solution)/shard_map/pallas_call | solution.py:27
  (66 shorter events, 31.9 us)
Async XLA Ops:
  3.1 5.1 %collective-permute-start = (f32[32,1024]{1,0:T(8,128)S(1)}, f32[32,1024]{1,0:T(8,128)S(1)}, u32[]{:S(2)}, u32[]{:S(2)}) collective-permute-start(f32[32,1024]{1,0:T(8,128)S(1)} %get-tuple-element.57), channel_id=1, source_target_pairs={{0,8},{1,9},{2,10},{3,11},{4,12},{5,13},{6,14},{7,15},{8,0},{9,1},... | collective-permute-start | bytes 393224 | tf_op jit(solution)/shard_map/ppermute | solution.py:461
  8.8 4.4 %collective-permute-start.2 = (f32[256,128]{1,0:T(8,128)S(1)}, f32[256,128]{1,0:T(8,128)S(1)}, u32[]{:S(2)}, u32[]{:S(2)}) collective-permute-start(f32[256,128]{1,0:T(8,128)S(1)} %get-tuple-element.70), channel_id=1, source_target_pairs={{0,1},{1,0},{2,3},{3,2},{4,5},{5,4},{6,7},{7,6},{8,9},{9,8},{10,11... | collective-permute-start | bytes 393224 | tf_op jit(solution)/shard_map/ppermute | solution.py:461
  10.4 4.7 %collective-permute-start.3 = (f32[256,128]{1,0:T(8,128)S(1)}, f32[256,128]{1,0:T(8,128)S(1)}, u32[]{:S(2)}, u32[]{:S(2)}) collective-permute-start(f32[256,128]{1,0:T(8,128)S(1)} %get-tuple-element.71), channel_id=1, source_target_pairs={{0,8},{1,2},{2,1},{3,4},{4,3},{5,6},{6,5},{7,15},{8,0},{9,10},{10,... | collective-permute-start | bytes 393224 | tf_op jit(solution)/shard_map/ppermute | solution.py:461
  17.4 3.1 %collective-permute-start.10 = (f32[8,128]{1,0:T(8,128)S(1)}, f32[8,128]{1,0:T(8,128)S(1)}, u32[]{:S(2)}, u32[]{:S(2)}) collective-permute-start(f32[8,128]{1,0:T(8,128)S(1)} %get-tuple-element.93), channel_id=1, source_target_pairs={{0,3},{1,2},{2,1},{3,0},{4,7},{5,6},{6,5},{7,4},{8,11},{9,10},{10,... | collective-permute-start | bytes 12296 | tf_op jit(solution)/shard_map/ppermute | solution.py:484
  20.5 5.0 %collective-permute-start.11 = (f32[8,128]{1,0:T(8,128)S(1)}, f32[8,128]{1,0:T(8,128)S(1)}, u32[]{:S(2)}, u32[]{:S(2)}) collective-permute-start(f32[8,128]{1,0:T(8,128)S(1)} %add.42), channel_id=1, source_target_pairs={{0,7},{1,6},{2,5},{3,4},{4,3},{5,2},{6,1},{7,0},{8,15},{9,14},{10,... | collective-permute-start | bytes 12296 | tf_op jit(solution)/shard_map/ppermute | solution.py:484
  25.5 7.1 %collective-permute-start.12 = (f32[8,128]{1,0:T(8,128)S(1)}, f32[8,128]{1,0:T(8,128)S(1)}, u32[]{:S(2)}, u32[]{:S(2)}) collective-permute-start(f32[8,128]{1,0:T(8,128)S(1)} %add.43), channel_id=1, source_target_pairs={{0,97},{1,96},{2,99},{3,98},{4,101},{5,100},{6,103},{7,102},{8,105... | collective-permute-start | bytes 12296 | tf_op jit(solution)/shard_map/ppermute | solution.py:484
  32.6 3.0 %collective-permute-start.13 = (f32[8,128]{1,0:T(8,128)S(1)}, f32[8,128]{1,0:T(8,128)S(1)}, u32[]{:S(2)}, u32[]{:S(2)}) collective-permute-start(f32[8,128]{1,0:T(8,128)S(1)} %add.44), channel_id=1, source_target_pairs={{0,33},{1,32},{2,35},{3,34},{4,37},{5,36},{6,39},{7,38},{8,41},{9,... | collective-permute-start | bytes 12296 | tf_op jit(solution)/shard_map/ppermute | solution.py:484
  33.1 17.6 %collective-permute-start.6 = (s32[64,1024]{1,0:T(8,128)S(1)}, s32[64,1024]{1,0:T(8,128)S(1)}, u32[]{:S(2)}, u32[]{:S(2)}) collective-permute-start(s32[64,1024]{1,0:T(8,128)S(1)} %get-tuple-element.74), channel_id=1, source_target_pairs={{0,8},{1,9},{2,10},{3,11},{4,12},{5,13},{6,14},{7,15},{8,0},{9,1},... | collective-permute-start | bytes 786440 | tf_op jit(solution)/shard_map/ppermute | solution.py:461
  33.1 17.6 %collective-permute-start.7 = (s32[64,1024]{1,0:T(8,128)S(1)}, s32[64,1024]{1,0:T(8,128)S(1)}, u32[]{:S(2)}, u32[]{:S(2)}) collective-permute-start(s32[64,1024]{1,0:T(8,128)S(1)} %get-tuple-element.75), channel_id=1, source_target_pairs={{0,1},{1,0},{2,3},{3,2},{4,5},{5,4},{6,7},{7,6},{8,16},{9,17},{10,... | collective-permute-start | bytes 786440 | tf_op jit(solution)/shard_map/ppermute | solution.py:461
  35.6 5.1 %collective-permute-start.14 = (f32[8,128]{1,0:T(8,128)S(1)}, f32[8,128]{1,0:T(8,128)S(1)}, u32[]{:S(2)}, u32[]{:S(2)}) collective-permute-start(f32[8,128]{1,0:T(8,128)S(1)} %add.45), channel_id=1, source_target_pairs={{0,25},{1,24},{2,27},{3,26},{4,29},{5,28},{6,31},{7,30},{8,17},{9,... | collective-permute-start | bytes 12296 | tf_op jit(solution)/shard_map/ppermute | solution.py:484
  40.2 10.4 %collective-permute-start.4 = (f32[64,1024]{1,0:T(8,128)S(1)}, f32[64,1024]{1,0:T(8,128)S(1)}, u32[]{:S(2)}, u32[]{:S(2)}) collective-permute-start(f32[64,1024]{1,0:T(8,128)S(1)} %get-tuple-element.72), channel_id=1, source_target_pairs={{0,8},{1,9},{2,10},{3,11},{4,12},{5,13},{6,14},{7,15},{8,0},{9,1},... | collective-permute-start | bytes 786440 | tf_op jit(solution)/shard_map/ppermute | solution.py:461
  40.3 10.4 %collective-permute-start.5 = (f32[64,1024]{1,0:T(8,128)S(1)}, f32[64,1024]{1,0:T(8,128)S(1)}, u32[]{:S(2)}, u32[]{:S(2)}) collective-permute-start(f32[64,1024]{1,0:T(8,128)S(1)} %get-tuple-element.73), channel_id=1, source_target_pairs={{0,1},{1,0},{2,3},{3,2},{4,5},{5,4},{6,7},{7,6},{8,16},{9,17},{10,... | collective-permute-start | bytes 786440 | tf_op jit(solution)/shard_map/ppermute | solution.py:461
  40.7 7.9 %collective-permute-start.15 = (f32[8,128]{1,0:T(8,128)S(1)}, f32[8,128]{1,0:T(8,128)S(1)}, u32[]{:S(2)}, u32[]{:S(2)}) collective-permute-start(f32[8,128]{1,0:T(8,128)S(1)} %add.46), channel_id=1, source_target_pairs={{0,9},{1,8},{2,11},{3,10},{4,13},{5,12},{6,15},{7,14},{8,1},{9,0},... | collective-permute-start | bytes 12296 | tf_op jit(solution)/shard_map/ppermute | solution.py:484
  52.5 3.8 %collective-permute-start.8 = (f32[256,128]{1,0:T(8,128)S(1)}, f32[256,128]{1,0:T(8,128)S(1)}, u32[]{:S(2)}, u32[]{:S(2)}) collective-permute-start(f32[256,128]{1,0:T(8,128)S(1)} %get-tuple-element.91), channel_id=1, source_target_pairs={{0,1},{1,0},{2,3},{3,2},{4,5},{5,4},{6,7},{7,6},{8,9},{9,8},{10,11... | collective-permute-start | bytes 393224 | tf_op jit(solution)/shard_map/ppermute | solution.py:461
  53.1 4.7 %collective-permute-start.9 = (f32[256,128]{1,0:T(8,128)S(1)}, f32[256,128]{1,0:T(8,128)S(1)}, u32[]{:S(2)}, u32[]{:S(2)}) collective-permute-start(f32[256,128]{1,0:T(8,128)S(1)} %get-tuple-element.92), channel_id=1, source_target_pairs={{0,8},{1,2},{2,1},{3,4},{4,3},{5,6},{6,5},{7,15},{8,0},{9,10},{10,... | collective-permute-start | bytes 393224 | tf_op jit(solution)/shard_map/ppermute | solution.py:461
  60.0 3.1 %collective-permute-start.21 = (f32[8,128]{1,0:T(8,128)S(1)}, f32[8,128]{1,0:T(8,128)S(1)}, u32[]{:S(2)}, u32[]{:S(2)}) collective-permute-start(f32[8,128]{1,0:T(8,128)S(1)} %get-tuple-element.111), channel_id=1, source_target_pairs={{0,3},{1,2},{2,1},{3,0},{4,7},{5,6},{6,5},{7,4},{8,11},{9,10},{10,... | collective-permute-start | bytes 12296 | tf_op jit(solution)/shard_map/ppermute | solution.py:484
  63.2 4.2 %collective-permute-start.22 = (f32[8,128]{1,0:T(8,128)S(1)}, f32[8,128]{1,0:T(8,128)S(1)}, u32[]{:S(2)}, u32[]{:S(2)}) collective-permute-start(f32[8,128]{1,0:T(8,128)S(1)} %add.49), channel_id=1, source_target_pairs={{0,7},{1,6},{2,5},{3,4},{4,3},{5,2},{6,1},{7,0},{8,15},{9,14},{10,... | collective-permute-start | bytes 12296 | tf_op jit(solution)/shard_map/ppermute | solution.py:484
  67.4 4.2 %collective-permute-start.23 = (f32[8,128]{1,0:T(8,128)S(1)}, f32[8,128]{1,0:T(8,128)S(1)}, u32[]{:S(2)}, u32[]{:S(2)}) collective-permute-start(f32[8,128]{1,0:T(8,128)S(1)} %add.50), channel_id=1, source_target_pairs={{0,97},{1,96},{2,99},{3,98},{4,101},{5,100},{6,103},{7,102},{8,105... | collective-permute-start | bytes 12296 | tf_op jit(solution)/shard_map/ppermute | solution.py:484
  74.7 4.2 %collective-permute-start.25 = (f32[8,128]{1,0:T(8,128)S(1)}, f32[8,128]{1,0:T(8,128)S(1)}, u32[]{:S(2)}, u32[]{:S(2)}) collective-permute-start(f32[8,128]{1,0:T(8,128)S(1)} %add.52), channel_id=1, source_target_pairs={{0,25},{1,24},{2,27},{3,26},{4,29},{5,28},{6,31},{7,30},{8,17},{9,... | collective-permute-start | bytes 12296 | tf_op jit(solution)/shard_map/ppermute | solution.py:484
  75.6 11.3 %collective-permute-start.17 = (f32[64,1024]{1,0:T(8,128)S(1)}, f32[64,1024]{1,0:T(8,128)S(1)}, u32[]{:S(2)}, u32[]{:S(2)}) collective-permute-start(f32[64,1024]{1,0:T(8,128)S(1)} %get-tuple-element.97), channel_id=1, source_target_pairs={{0,8},{1,9},{2,10},{3,11},{4,12},{5,13},{6,14},{7,15},{8,0},{9,1},... | collective-permute-start | bytes 786440 | tf_op jit(solution)/shard_map/ppermute | solution.py:461
  75.6 11.3 %collective-permute-start.18 = (f32[64,1024]{1,0:T(8,128)S(1)}, f32[64,1024]{1,0:T(8,128)S(1)}, u32[]{:S(2)}, u32[]{:S(2)}) collective-permute-start(f32[64,1024]{1,0:T(8,128)S(1)} %get-tuple-element.98), channel_id=1, source_target_pairs={{0,1},{1,0},{2,3},{3,2},{4,5},{5,4},{6,7},{7,6},{8,16},{9,17},{10,... | collective-permute-start | bytes 786440 | tf_op jit(solution)/shard_map/ppermute | solution.py:461
  78.9 5.0 %collective-permute-start.26 = (f32[8,128]{1,0:T(8,128)S(1)}, f32[8,128]{1,0:T(8,128)S(1)}, u32[]{:S(2)}, u32[]{:S(2)}) collective-permute-start(f32[8,128]{1,0:T(8,128)S(1)} %add.53), channel_id=1, source_target_pairs={{0,9},{1,8},{2,11},{3,10},{4,13},{5,12},{6,15},{7,14},{8,1},{9,0},... | collective-permute-start | bytes 12296 | tf_op jit(solution)/shard_map/ppermute | solution.py:484
  88.7 3.8 %collective-permute-start.19 = (f32[256,128]{1,0:T(8,128)S(1)}, f32[256,128]{1,0:T(8,128)S(1)}, u32[]{:S(2)}, u32[]{:S(2)}) collective-permute-start(f32[256,128]{1,0:T(8,128)S(1)} %get-tuple-element.109), channel_id=1, source_target_pairs={{0,1},{1,0},{2,3},{3,2},{4,5},{5,4},{6,7},{7,6},{8,9},{9,8},{10,11... | collective-permute-start | bytes 393224 | tf_op jit(solution)/shard_map/ppermute | solution.py:461
  89.3 4.7 %collective-permute-start.20 = (f32[256,128]{1,0:T(8,128)S(1)}, f32[256,128]{1,0:T(8,128)S(1)}, u32[]{:S(2)}, u32[]{:S(2)}) collective-permute-start(f32[256,128]{1,0:T(8,128)S(1)} %get-tuple-element.110), channel_id=1, source_target_pairs={{0,8},{1,2},{2,1},{3,4},{4,3},{5,6},{6,5},{7,15},{8,0},{9,10},{10,... | collective-permute-start | bytes 393224 | tf_op jit(solution)/shard_map/ppermute | solution.py:461
  (5 other events, 33.6 us)

commit v6 on v4

--- a/solution.py
+++ b/solution.py
@@ -23,10 +23,13 @@
 SMEM = pl.BlockSpec(memory_space=pltpu.SMEM)
 
 
-def call(kernel, outs, args, ins=None, out_specs=None, scratch=(), limit=24, flops=100_000_000):
+def call(
+    kernel, outs, args, ins=None, out_specs=None, scratch=(), limit=24, flops=0, aliases=None
+):
     return pl.pallas_call(
         kernel,
         out_shape=[jax.ShapeDtypeStruct(s, d) for s, d in outs],
+        input_output_aliases=aliases or {},
         in_specs=ins or [VMEM] * len(args),
         out_specs=out_specs or [VMEM] * len(outs),
         scratch_shapes=scratch,
@@ -160,15 +163,20 @@
     return [jnp.where(keep, piece, jnp.zeros_like(piece)) for piece in pieces]
 
 
-def rows_kernel(*refs, bands, labelled, carried):
-    (field_ref,), label_refs, (band_high, band_low), plane, outs, plane_out, done = take(
-        refs, 1, labelled, 2, carried, 3, carried
+def rows_kernel(*refs, bands, labelled, leaving):
+    (field_ref,), label_refs, (band_high, band_low), plane, outs, sent = take(
+        refs, 1, labelled, 2, (1 + (leaving[0] > 0)) if leaving else 0, 3
     )
     high_ref, low_ref, edge_ref = outs
-    copies = [pltpu.make_async_copy(*pair) for pair in zip(plane, plane_out, done)]
+    rows, columns = field_ref.shape
+    copies = []
+    if leaving:
+        target, done = sent
+        for n, start in enumerate(range(*leaving, STEP)):
+            at = slice(start, start + STEP)
+            copies.append(pltpu.make_async_copy(plane[0].at[at], target.at[at], done.at[n]))
     for copy in copies:
         copy.start()
-    rows, columns = field_ref.shape
     count = rows // REACH
     for n in range(columns // TILE):
         at = slice(n * TILE, (n + 1) * TILE)
@@ -384,8 +392,9 @@
     staged, done = refs if leaving else (density_out[0] if scaled else None, None)
     rows = left_ref.shape[0]
     column_flags = flags_of("col")
-    log_sum = jnp.zeros((8, 128), F32)
-    mass_sum = jnp.zeros((8, 128), F32)
+    spans = (TILE + middle_refs[0].shape[1]) // 128
+    log_sums = [jnp.zeros((8, 128), F32)] * spans
+    mass_sums = [jnp.zeros((8, 128), F32)] * spans
     copies = []
     for number, start in enumerate(range(0, rows, STEP)):
         at = slice(start, start + STEP)
@@ -399,9 +408,9 @@
                 mass = mass_in[0][at, lanes]
                 adapted_out[0][at, lanes] = mass * pilot
                 terms = mass * jnp.log(pilot)
-                log_sum += jnp.sum(terms.reshape(STEP // 8, 8, 128), axis=0)
+                log_sums[k] += jnp.sum(terms.reshape(STEP // 8, 8, 128), axis=0)
                 if totals:
-                    mass_sum += jnp.sum(mass.reshape(STEP // 8, 8, 128), axis=0)
+                    mass_sums[k] += jnp.sum(mass.reshape(STEP // 8, 8, 128), axis=0)
         if leaving:
             copy = pltpu.make_async_copy(staged.at[at], density_out[0].at[at], done.at[number])
             copy.start()
@@ -412,8 +421,8 @@
         top, bottom = adapted_ref[0:REACH], adapted_ref[rows - REACH :]
         send_a[...] = chosen(odd_row, top, bottom)
         send_b[...] = chosen(odd_row, bottom, top)
-        log_sum = jnp.sum(log_sum, axis=(0, 1), keepdims=True)
-        mass_sum = jnp.sum(mass_sum, axis=(0, 1), keepdims=True)
+        log_sum = jnp.sum(sum(log_sums), axis=(0, 1), keepdims=True)
+        mass_sum = jnp.sum(sum(mass_sums), axis=(0, 1), keepdims=True)
         row = iota((8, 128), 0)
         stat_ref[...] = jnp.where(row == 0, log_sum, jnp.where(row == 1, mass_sum, 0.0))
     for copy in copies:
@@ -440,25 +449,29 @@
 
 
 HOPS = (
-    ("col", 2, 8),
-    ("col", 6, 8),
-    ("row", 12, 16),
-    ("row", 4, 16),
-    ("row", 3, 4),
-    ("row", 1, 2),
-    ("col", 1, 2),
+    (0, 3, (1, 8)),
+    (0, 7, (1, 8)),
+    (12, 1, (16, 1)),
+    (4, 1, (16, 1)),
+    (3, 1, (4, 1)),
+    (1, 1, (2, 1)),
+    (0, 1, (1, 2)),
 )
 
 
 def total_over(stat):
-    for axis, hop, least in HOPS:
-        if lax.axis_size(axis) >= least:
-            pairs = [(i, i ^ hop) for i in range(lax.axis_size(axis))]
-            stat = stat + lax.ppermute(stat, axis, pairs)
+    sizes = (lax.axis_size("row"), lax.axis_size("col"))
+    for rows, columns, least in HOPS:
+        if sizes[0] >= least[0] and sizes[1] >= least[1]:
+            pairs = []
+            for index in range(sizes[0] * sizes[1]):
+                row, column = divmod(index, sizes[1])
+                pairs.append((index, (row ^ rows) * sizes[1] + (column ^ columns)))
+            stat = stat + lax.ppermute(stat, ("row", "col"), pairs)
     return stat
 
 
-def smooth(field, halo, labels, label_halo, tables, groups, cuts, leaving=()):
+def smooth(field, halo, labels, label_halo, tables, groups, cuts, plane=None):
     high, low, rim = tables
     rows, columns = field.shape
     labelled = labels is not None
@@ -467,19 +480,31 @@
     for number, group in enumerate(groups):
         inner = (len(group), rows - 2 * REACH, columns)
         edge = (len(group), 2 * REACH, columns)
-        carried = len(leaving) if number == 0 else 0
+        args = [field] + ([labels] if labelled else []) + [high, low]
+        outs = [(inner, BF16), (inner, BF16), (edge, F32)]
+        ins, out_specs = [VMEM] * len(args), [VMEM] * len(outs)
+        leaving, scratch, aliases = None, [], {}
+        if plane is not None:
+            part = rows // len(groups)
+            leaving = (number * part, (number + 1) * part)
+            args, ins = [*args, plane], [*ins, VMEM]
+            if number > 0:
+                aliases = {len(args): len(outs)}
+                args, ins = [*args, plane_out], [*ins, HBM]
+            outs, out_specs = [*outs, (field.shape, F32)], [*out_specs, HBM]
+            scratch = [pltpu.SemaphoreType.DMA((part // STEP,))]
         results = call(
-            functools.partial(
-                rows_kernel, bands=group, labelled=labelled, carried=carried
-            ),
-            [(inner, BF16), (inner, BF16), (edge, F32)] + [(field.shape, F32)] * carried,
-            [field] + ([labels] if labelled else []) + [high, low, *leaving[:carried]],
-            out_specs=[VMEM] * 3 + [HBM] * carried,
-            scratch=[pltpu.SemaphoreType.DMA] * carried,
+            functools.partial(rows_kernel, bands=group, labelled=labelled, leaving=leaving),
+            outs,
+            args,
+            ins=ins,
+            out_specs=out_specs,
+            scratch=scratch,
             flops=len(group) * 1_000_000_000,
+            aliases=aliases,
         )
-        if carried:
-            left_behind = results[3]
+        if plane is not None:
+            plane_out = results[3]
         for results_of, result in zip((highs, lows, partials), results):
             results_of.append(result)
     edge = (len(bands), 2 * REACH, columns)
@@ -503,7 +528,7 @@
         )
         start += count
     pieces = [left, *middles, right, *come]
-    return (pieces, left_behind) if leaving else pieces
+    return pieces if plane is None else (pieces, plane_out)
 
 
 def finish(pieces, extra, scaled, following, totals, shape):
@@ -583,7 +608,7 @@
     halo = exchange(*sends, "row")
     second_total = total_over(second_stat)
     pieces, density_first = smooth(
-        adapted, halo, labels, label_halo, tables, groups, cuts, (density_first,)
+        adapted, halo, labels, label_halo, tables, groups, cuts, density_first
     )
     (density_second,) = finish(
         pieces, [second_total, first_total], True, False, False, shape

time: 96 us -> 93.9 us (0.978)
  starting transfers between devices: 45.8 us -> 29.9 us
  waiting for transfers between devices: 18.8 us -> 32.1 us
    ppermute x14, waiting for transfers between devices: 13 us -> 26.3 us  [total_over(): stat = stat + lax.ppermute(stat, ('row', 'col'), pairs)]
    ppermute x14, starting transfers between devices: 21.4 us -> 8.74 us  [exchange(): results.append(lax.ppermute(value, ('row', 'col'), pairs))]
    ppermute x14, starting transfers between devices: 24.4 us -> 21.1 us  [total_over(): stat = stat + lax.ppermute(stat, ('row', 'col'), pairs)]
  transfers between devices with their start and end apart: 28 -> 28, of which waited for: 13 -> 15; matrix products, arithmetic and copies ran while one was open for 0% -> 0% of each run, Pallas kernels for 20% -> 21%
where the time goes in v6:
time: 93.9 us; the launch traced here: 93.8 us
  waiting for transfers between devices  32.1 us (34%)
  Pallas kernels  30.7 us (33%)
  starting transfers between devices  29.9 us (32%)
  between operations  1.08 us (1%)
    pallas_call x18, Pallas kernels, call(): pl.pallas_call(kernel, out_shape=[jax.ShapeDtypeStruct(s, d) for s, d in...  30.7 us
    ppermute x14, waiting for transfers between devices, total_over(): stat = stat + lax.ppermute(stat, ('row', 'col'), pairs)  26.3 us
    ppermute x14, starting transfers between devices, total_over(): stat = stat + lax.ppermute(stat, ('row', 'col'), pairs)  21.1 us
    ppermute x14, starting transfers between devices, exchange(): results.append(lax.ppermute(value, ('row', 'col'), pairs))  8.74 us
    ppermute x14, waiting for transfers between devices, exchange(): results.append(lax.ppermute(value, ('row', 'col'), pairs))  5.76 us
  transfers between devices with their start and end apart: 28, of which 15 were waited for; matrix products, arithmetic and copies ran while one was open for 0% of the time, Pallas kernels for 21%

profile of v6, /device:TPU:1, one launch (start us, length us, event | category | flops | bytes accessed | tf_op | source)
XLA Modules:
  0.0 93.8 jit_solution(6490465449437660779)
XLA Ops:
  0.6 2.4 %shard_map.59 = (bf16[384,256]{1,0:T(8,128)(2,1)S(1)}, bf16[384,256]{1,0:T(8,128)(2,1)S(1)}, bf16[1,128,384]{2,1,0:T(8,128)(2,1)S(1)}, f32[512,1024]{1,0:T(8,128...) custom-call(s32[512,1024]{1,0:T(8,128)} %refs_0_.2, ...), custom_call_target="tpu_custom_call" | custom-call | flops 500000000 | bytes 4194304 | tf_op jit(solution)/shard_map/pallas_call | solution.py:29
  3.1 2.2 %collective-permute-start = (f32[32,1024]{1,0:T(8,128)S(1)}, f32[32,1024]{1,0:T(8,128)S(1)}, u32[]{:S(2)}, u32[]{:S(2)}) collective-permute-start(f32[32,1024]{1,0:T(8,128)S(1)} %get-tuple-element.58), channel_id=1, source_target_pairs={{0,8},{1,9},{2,10},{3,11},{4,12},{5,13},{6,14},{7,15},{8,0},{9,1},... | collective-permute-start | bytes 393224 | tf_op jit(solution)/shard_map/ppermute | solution.py:447
  10.4 1.8 %collective-permute-start.3 = (f32[256,128]{1,0:T(8,128)S(1)}, f32[256,128]{1,0:T(8,128)S(1)}, u32[]{:S(2)}, u32[]{:S(2)}) collective-permute-start(f32[256,128]{1,0:T(8,128)S(1)} %get-tuple-element.72), channel_id=1, source_target_pairs={{0,8},{1,2},{2,1},{3,4},{4,3},{5,6},{6,5},{7,15},{8,0},{9,10},{10,... | collective-permute-start | bytes 393224 | tf_op jit(solution)/shard_map/ppermute | solution.py:447
  13.2 1.9 %collective-permute-done.3.refs_4_ = f32[256,128]{1,0:T(8,128)S(1)} collective-permute-done((f32[256,128]{1,0:T(8,128)S(1)}, f32[256,128]{1,0:T(8,128)S(1)}, u32[]{:S(2)}, u32[]{:S(2)}) %collective-permute-start.3) | collective-permute-done | bytes 131104 | tf_op jit(solution)/shard_map/ppermute | solution.py:447
  19.4 3.6 %collective-permute-start.11 = (f32[8,128]{1,0:T(8,128)S(1)}, f32[8,128]{1,0:T(8,128)S(1)}, u32[]{:S(2)}, u32[]{:S(2)}) collective-permute-start(f32[8,128]{1,0:T(8,128)S(1)} %add.42), channel_id=1, source_target_pairs={{0,7},{1,6},{2,5},{3,4},{4,3},{5,2},{6,1},{7,0},{8,15},{9,14},{10,... | collective-permute-start | bytes 12296 | tf_op jit(solution)/shard_map/ppermute | solution.py:470
  24.4 5.8 %collective-permute-start.12 = (f32[8,128]{1,0:T(8,128)S(1)}, f32[8,128]{1,0:T(8,128)S(1)}, u32[]{:S(2)}, u32[]{:S(2)}) collective-permute-start(f32[8,128]{1,0:T(8,128)S(1)} %add.43), channel_id=1, source_target_pairs={{0,97},{1,96},{2,99},{3,98},{4,101},{5,100},{6,103},{7,102},{8,105... | collective-permute-start | bytes 12296 | tf_op jit(solution)/shard_map/ppermute | solution.py:470
  32.4 2.2 %collective-permute-done.13 = f32[8,128]{1,0:T(8,128)S(1)} collective-permute-done((f32[8,128]{1,0:T(8,128)S(1)}, f32[8,128]{1,0:T(8,128)S(1)}, u32[]{:S(2)}, u32[]{:S(2)}) %collective-permute-start.13) | collective-permute-done | bytes 4128 | tf_op jit(solution)/shard_map/ppermute | solution.py:470
  34.6 2.4 %collective-permute-start.14 = (f32[8,128]{1,0:T(8,128)S(1)}, f32[8,128]{1,0:T(8,128)S(1)}, u32[]{:S(2)}, u32[]{:S(2)}) collective-permute-start(f32[8,128]{1,0:T(8,128)S(1)} %add.45), channel_id=1, source_target_pairs={{0,25},{1,24},{2,27},{3,26},{4,29},{5,28},{6,31},{7,30},{8,17},{9,... | collective-permute-start | bytes 12296 | tf_op jit(solution)/shard_map/ppermute | solution.py:470
  36.9 2.2 %shard_map.64 = (bf16[1536,256]{1,0:T(8,128)(2,1)S(1)}, bf16[1536,256]{1,0:T(8,128)(2,1)S(1)}, bf16[4,128,384]{2,1,0:T(8,128)(2,1)S(1)}, bf16[512,1024]{1,0:T(8,128)(2,1)S(1)}) custom-call(s32[4]{0:T(128)S(1)} %copy-done, s32[512,1024]{1,0:T(8,128)} %refs_1_.3), custom_call_target="tpu_custom_call" | custom-call | flops 500000000 | bytes 4194304 | tf_op jit(solution)/shard_map/pallas_call | solution.py:29
  41.3 1.9 %shard_map.66 = (bf16[2,384,1024]{2,1,0:T(8,128)(2,1)S(1)}, bf16[2,384,1024]{2,1,0:T(8,128)(2,1)S(1)}, f32[2,128,1024]{2,1,0:T(8,128)S(1)}) custom-call(f32[512,1024]{1,0:T(8,128)S(1)} %get-tuple-element.77.refs_0_, bf16[512,1024]{1,0:T(8,128)(2,1)S(1)} %get-tuple-element.78.refs_1_, bf16[1536,256]{1,0:T(8,128)(2,1)S(1)} %get-tuple-element.79.refs_2_.refs_11_.refs_6_, ...), custom_call_target="tpu_custom_call" | custom-call | flops 2000000000 | bytes 4194304 | tf_op jit(solution)/shard_map/pallas_call | solution.py:29
  43.2 4.3 %collective-permute-done.15 = f32[8,128]{1,0:T(8,128)S(1)} collective-permute-done((f32[8,128]{1,0:T(8,128)S(1)}, f32[8,128]{1,0:T(8,128)S(1)}, u32[]{:S(2)}, u32[]{:S(2)}) %collective-permute-start.15) | collective-permute-done | bytes 4128 | tf_op jit(solution)/shard_map/ppermute | solution.py:470
  47.6 1.9 %shard_map.65 = (bf16[2,384,1024]{2,1,0:T(8,128)(2,1)S(1)}, bf16[2,384,1024]{2,1,0:T(8,128)(2,1)S(1)}, f32[2,128,1024]{2,1,0:T(8,128)S(1)}) custom-call(f32[512,1024]{1,0:T(8,128)S(1)} %get-tuple-element.77.refs_0_, bf16[512,1024]{1,0:T(8,128)(2,1)S(1)} %get-tuple-element.78.refs_1_, bf16[1536,256]{1,0:T(8,128)(2,1)S(1)} %get-tuple-element.79.refs_2_.refs_11_.refs_6_, ...), custom_call_target="tpu_custom_call" | custom-call | flops 2000000000 | bytes 4194304 | tf_op jit(solution)/shard_map/pallas_call | solution.py:29
  49.6 1.9 %shard_map.67 = (bf16[4,128,1024]{2,1,0:T(8,128)(2,1)S(1)}, bf16[4,128,1024]{2,1,0:T(8,128)(2,1)S(1)}, f32[512,256]{1,0:T(8,128)S(1)}, f32[512,128]{1,0:T(8,128)...) custom-call(f32[64,1024]{1,0:T(8,128)S(1)} %collective-permute-done.4.refs_0_, ...), custom_call_target="tpu_custom_call" | custom-call | flops 2000000000 | bytes 4194304 | tf_op jit(solution)/shard_map/pallas_call | solution.py:29
  52.1 1.9 %shard_map.68.refs_1_ = f32[320,768]{1,0:T(8,128)S(1)} custom-call(bf16[2,384,1024]{2,1,0:T(8,128)(2,1)S(1)} %get-tuple-element.83.refs_6_.refs_0_, bf16[2,384,1024]{2,1,0:T(8,128)(2,1)S(1)} %get-tuple-element.84.refs_7_.refs_1_, bf16[2,384,1024]{2,1,0:T(8,128)(2,1)S(1)} %get-tuple-element.85.refs_8_.refs_2_, ...), custom_call_target="tpu_custom_call" | custom-call | flops 1875000064 | bytes 4194304 | tf_op jit(solution)/shard_map/pallas_call | solution.py:29
  58.3 2.7 %collective-permute-done.21 = f32[8,128]{1,0:T(8,128)S(1)} collective-permute-done((f32[8,128]{1,0:T(8,128)S(1)}, f32[8,128]{1,0:T(8,128)S(1)}, u32[]{:S(2)}, u32[]{:S(2)}) %collective-permute-start.21) | collective-permute-done | bytes 4128 | tf_op jit(solution)/shard_map/ppermute | solution.py:470
  61.1 2.6 %collective-permute-start.22 = (f32[8,128]{1,0:T(8,128)S(1)}, f32[8,128]{1,0:T(8,128)S(1)}, u32[]{:S(2)}, u32[]{:S(2)}) collective-permute-start(f32[8,128]{1,0:T(8,128)S(1)} %add.49), channel_id=1, source_target_pairs={{0,7},{1,6},{2,5},{3,4},{4,3},{5,2},{6,1},{7,0},{8,15},{9,14},{10,... | collective-permute-start | bytes 12296 | tf_op jit(solution)/shard_map/ppermute | solution.py:470
  66.6 3.0 %collective-permute-done.23 = f32[8,128]{1,0:T(8,128)S(1)} collective-permute-done((f32[8,128]{1,0:T(8,128)S(1)}, f32[8,128]{1,0:T(8,128)S(1)}, u32[]{:S(2)}, u32[]{:S(2)}) %collective-permute-start.23) | collective-permute-done | bytes 4128 | tf_op jit(solution)/shard_map/ppermute | solution.py:470
  70.0 2.6 %collective-permute-done.24 = f32[8,128]{1,0:T(8,128)S(1)} collective-permute-done((f32[8,128]{1,0:T(8,128)S(1)}, f32[8,128]{1,0:T(8,128)S(1)}, u32[]{:S(2)}, u32[]{:S(2)}) %collective-permute-start.24) | collective-permute-done | bytes 4128 | tf_op jit(solution)/shard_map/ppermute | solution.py:470
  73.6 3.2 %collective-permute-done.25 = f32[8,128]{1,0:T(8,128)S(1)} collective-permute-done((f32[8,128]{1,0:T(8,128)S(1)}, f32[8,128]{1,0:T(8,128)S(1)}, u32[]{:S(2)}, u32[]{:S(2)}) %collective-permute-start.25) | collective-permute-done | bytes 4128 | tf_op jit(solution)/shard_map/ppermute | solution.py:470
  77.0 2.5 %shard_map.71 = (bf16[2,384,1024]{2,1,0:T(8,128)(2,1)S(1)}, bf16[2,384,1024]{2,1,0:T(8,128)(2,1)S(1)}, f32[2,128,1024]{2,1,0:T(8,128)S(1)}, f32[512,1024]{1,0:T(8,128)}) custom-call(f32[512,1024]{1,0:T(8,128)S(1)} %get-tuple-element.95.refs_0_, bf16[512,1024]{1,0:T(8,128)(2,1)S(1)} %get-tuple-element.78.refs_1_, ...), custom_call_target="tpu_custom_call" | custom-call | flops 2000000000 | bytes 4194304 | tf_op jit(solution)/shard_map/pallas_call | solution.py:29
  79.5 2.4 %collective-permute-done.26 = f32[8,128]{1,0:T(8,128)S(1)} collective-permute-done((f32[8,128]{1,0:T(8,128)S(1)}, f32[8,128]{1,0:T(8,128)S(1)}, u32[]{:S(2)}, u32[]{:S(2)}) %collective-permute-start.26) | collective-permute-done | bytes 4128 | tf_op jit(solution)/shard_map/ppermute | solution.py:470
  81.9 2.7 %shard_map.72 = (bf16[2,384,1024]{2,1,0:T(8,128)(2,1)S(1)}, bf16[2,384,1024]{2,1,0:T(8,128)(2,1)S(1)}, f32[2,128,1024]{2,1,0:T(8,128)S(1)}, f32[512,1024]{1,0:T(8,128)}) custom-call(f32[512,1024]{1,0:T(8,128)S(1)} %get-tuple-element.95.refs_0_, bf16[512,1024]{1,0:T(8,128)(2,1)S(1)} %get-tuple-element.78.refs_1_, ...), custom_call_target="tpu_custom_call", output_to_operand_aliasing={{3}: (5, {})} | custom-call | flops 2000000000 | bytes 4194304 | tf_op jit(solution)/shard_map/pallas_call | solution.py:29
  84.6 1.9 %shard_map.73 = (bf16[4,128,1024]{2,1,0:T(8,128)(2,1)S(1)}, bf16[4,128,1024]{2,1,0:T(8,128)(2,1)S(1)}, f32[512,256]{1,0:T(8,128)S(1)}, f32[512,128]{1,0:T(8,128)...) custom-call(f32[64,1024]{1,0:T(8,128)S(1)} %collective-permute-done.17.refs_0_, ...), custom_call_target="tpu_custom_call" | custom-call | flops 2000000000 | bytes 4194304 | tf_op jit(solution)/shard_map/pallas_call | solution.py:29
  87.1 1.9 %shard_map.74.refs_1_ = f32[320,768]{1,0:T(8,128)S(1)} custom-call(bf16[2,384,1024]{2,1,0:T(8,128)(2,1)S(1)} %get-tuple-element.103.refs_6_.refs_0_, bf16[2,384,1024]{2,1,0:T(8,128)(2,1)S(1)} %get-tuple-element.104.refs_7_.refs_1_, bf16[2,384,1024]{2,1,0:T(8,128)(2,1)S(1)} %get-tuple-element.105.refs_8_.refs_2_, ...), custom_call_target="tpu_custom_call" | custom-call | flops 1875000064 | bytes 4194304 | tf_op jit(solution)/shard_map/pallas_call | solution.py:29
  (66 shorter events, 30.5 us)
Async XLA Ops:
  3.1 5.1 %collective-permute-start = (f32[32,1024]{1,0:T(8,128)S(1)}, f32[32,1024]{1,0:T(8,128)S(1)}, u32[]{:S(2)}, u32[]{:S(2)}) collective-permute-start(f32[32,1024]{1,0:T(8,128)S(1)} %get-tuple-element.58), channel_id=1, source_target_pairs={{0,8},{1,9},{2,10},{3,11},{4,12},{5,13},{6,14},{7,15},{8,0},{9,1},... | collective-permute-start | bytes 393224 | tf_op jit(solution)/shard_map/ppermute | solution.py:447
  8.8 4.4 %collective-permute-start.2 = (f32[256,128]{1,0:T(8,128)S(1)}, f32[256,128]{1,0:T(8,128)S(1)}, u32[]{:S(2)}, u32[]{:S(2)}) collective-permute-start(f32[256,128]{1,0:T(8,128)S(1)} %get-tuple-element.71), channel_id=1, source_target_pairs={{0,1},{1,0},{2,3},{3,2},{4,5},{5,4},{6,7},{7,6},{8,9},{9,8},{10,11... | collective-permute-start | bytes 393224 | tf_op jit(solution)/shard_map/ppermute | solution.py:447
  10.4 4.7 %collective-permute-start.3 = (f32[256,128]{1,0:T(8,128)S(1)}, f32[256,128]{1,0:T(8,128)S(1)}, u32[]{:S(2)}, u32[]{:S(2)}) collective-permute-start(f32[256,128]{1,0:T(8,128)S(1)} %get-tuple-element.72), channel_id=1, source_target_pairs={{0,8},{1,2},{2,1},{3,4},{4,3},{5,6},{6,5},{7,15},{8,0},{9,10},{10,... | collective-permute-start | bytes 393224 | tf_op jit(solution)/shard_map/ppermute | solution.py:447
  16.3 3.1 %collective-permute-start.10 = (f32[8,128]{1,0:T(8,128)S(1)}, f32[8,128]{1,0:T(8,128)S(1)}, u32[]{:S(2)}, u32[]{:S(2)}) collective-permute-start(f32[8,128]{1,0:T(8,128)S(1)} %get-tuple-element.94), channel_id=1, source_target_pairs={{0,3},{1,2},{2,1},{3,0},{4,7},{5,6},{6,5},{7,4},{8,11},{9,10},{10,... | collective-permute-start | bytes 12296 | tf_op jit(solution)/shard_map/ppermute | solution.py:470
  19.4 5.0 %collective-permute-start.11 = (f32[8,128]{1,0:T(8,128)S(1)}, f32[8,128]{1,0:T(8,128)S(1)}, u32[]{:S(2)}, u32[]{:S(2)}) collective-permute-start(f32[8,128]{1,0:T(8,128)S(1)} %add.42), channel_id=1, source_target_pairs={{0,7},{1,6},{2,5},{3,4},{4,3},{5,2},{6,1},{7,0},{8,15},{9,14},{10,... | collective-permute-start | bytes 12296 | tf_op jit(solution)/shard_map/ppermute | solution.py:470
  24.4 7.1 %collective-permute-start.12 = (f32[8,128]{1,0:T(8,128)S(1)}, f32[8,128]{1,0:T(8,128)S(1)}, u32[]{:S(2)}, u32[]{:S(2)}) collective-permute-start(f32[8,128]{1,0:T(8,128)S(1)} %add.43), channel_id=1, source_target_pairs={{0,97},{1,96},{2,99},{3,98},{4,101},{5,100},{6,103},{7,102},{8,105... | collective-permute-start | bytes 12296 | tf_op jit(solution)/shard_map/ppermute | solution.py:470
  31.5 3.0 %collective-permute-start.13 = (f32[8,128]{1,0:T(8,128)S(1)}, f32[8,128]{1,0:T(8,128)S(1)}, u32[]{:S(2)}, u32[]{:S(2)}) collective-permute-start(f32[8,128]{1,0:T(8,128)S(1)} %add.44), channel_id=1, source_target_pairs={{0,33},{1,32},{2,35},{3,34},{4,37},{5,36},{6,39},{7,38},{8,41},{9,... | collective-permute-start | bytes 12296 | tf_op jit(solution)/shard_map/ppermute | solution.py:470
  32.0 17.6 %collective-permute-start.6 = (s32[64,1024]{1,0:T(8,128)S(1)}, s32[64,1024]{1,0:T(8,128)S(1)}, u32[]{:S(2)}, u32[]{:S(2)}) collective-permute-start(s32[64,1024]{1,0:T(8,128)S(1)} %get-tuple-element.75), channel_id=1, source_target_pairs={{0,8},{1,9},{2,10},{3,11},{4,12},{5,13},{6,14},{7,15},{8,0},{9,1},... | collective-permute-start | bytes 786440 | tf_op jit(solution)/shard_map/ppermute | solution.py:447
  32.0 17.6 %collective-permute-start.7 = (s32[64,1024]{1,0:T(8,128)S(1)}, s32[64,1024]{1,0:T(8,128)S(1)}, u32[]{:S(2)}, u32[]{:S(2)}) collective-permute-start(s32[64,1024]{1,0:T(8,128)S(1)} %get-tuple-element.76), channel_id=1, source_target_pairs={{0,1},{1,0},{2,3},{3,2},{4,5},{5,4},{6,7},{7,6},{8,16},{9,17},{10,... | collective-permute-start | bytes 786440 | tf_op jit(solution)/shard_map/ppermute | solution.py:447
  34.6 5.1 %collective-permute-start.14 = (f32[8,128]{1,0:T(8,128)S(1)}, f32[8,128]{1,0:T(8,128)S(1)}, u32[]{:S(2)}, u32[]{:S(2)}) collective-permute-start(f32[8,128]{1,0:T(8,128)S(1)} %add.45), channel_id=1, source_target_pairs={{0,25},{1,24},{2,27},{3,26},{4,29},{5,28},{6,31},{7,30},{8,17},{9,... | collective-permute-start | bytes 12296 | tf_op jit(solution)/shard_map/ppermute | solution.py:470
  39.1 10.5 %collective-permute-start.4 = (f32[64,1024]{1,0:T(8,128)S(1)}, f32[64,1024]{1,0:T(8,128)S(1)}, u32[]{:S(2)}, u32[]{:S(2)}) collective-permute-start(f32[64,1024]{1,0:T(8,128)S(1)} %get-tuple-element.73), channel_id=1, source_target_pairs={{0,8},{1,9},{2,10},{3,11},{4,12},{5,13},{6,14},{7,15},{8,0},{9,1},... | collective-permute-start | bytes 786440 | tf_op jit(solution)/shard_map/ppermute | solution.py:447
  39.2 10.4 %collective-permute-start.5 = (f32[64,1024]{1,0:T(8,128)S(1)}, f32[64,1024]{1,0:T(8,128)S(1)}, u32[]{:S(2)}, u32[]{:S(2)}) collective-permute-start(f32[64,1024]{1,0:T(8,128)S(1)} %get-tuple-element.74), channel_id=1, source_target_pairs={{0,1},{1,0},{2,3},{3,2},{4,5},{5,4},{6,7},{7,6},{8,16},{9,17},{10,... | collective-permute-start | bytes 786440 | tf_op jit(solution)/shard_map/ppermute | solution.py:447
  39.7 7.9 %collective-permute-start.15 = (f32[8,128]{1,0:T(8,128)S(1)}, f32[8,128]{1,0:T(8,128)S(1)}, u32[]{:S(2)}, u32[]{:S(2)}) collective-permute-start(f32[8,128]{1,0:T(8,128)S(1)} %add.46), channel_id=1, source_target_pairs={{0,9},{1,8},{2,11},{3,10},{4,13},{5,12},{6,15},{7,14},{8,1},{9,0},... | collective-permute-start | bytes 12296 | tf_op jit(solution)/shard_map/ppermute | solution.py:470
  51.5 3.8 %collective-permute-start.8 = (f32[256,128]{1,0:T(8,128)S(1)}, f32[256,128]{1,0:T(8,128)S(1)}, u32[]{:S(2)}, u32[]{:S(2)}) collective-permute-start(f32[256,128]{1,0:T(8,128)S(1)} %get-tuple-element.92), channel_id=1, source_target_pairs={{0,1},{1,0},{2,3},{3,2},{4,5},{5,4},{6,7},{7,6},{8,9},{9,8},{10,11... | collective-permute-start | bytes 393224 | tf_op jit(solution)/shard_map/ppermute | solution.py:447
  52.1 4.7 %collective-permute-start.9 = (f32[256,128]{1,0:T(8,128)S(1)}, f32[256,128]{1,0:T(8,128)S(1)}, u32[]{:S(2)}, u32[]{:S(2)}) collective-permute-start(f32[256,128]{1,0:T(8,128)S(1)} %get-tuple-element.93), channel_id=1, source_target_pairs={{0,8},{1,2},{2,1},{3,4},{4,3},{5,6},{6,5},{7,15},{8,0},{9,10},{10,... | collective-permute-start | bytes 393224 | tf_op jit(solution)/shard_map/ppermute | solution.py:447
  57.9 3.1 %collective-permute-start.21 = (f32[8,128]{1,0:T(8,128)S(1)}, f32[8,128]{1,0:T(8,128)S(1)}, u32[]{:S(2)}, u32[]{:S(2)}) collective-permute-start(f32[8,128]{1,0:T(8,128)S(1)} %get-tuple-element.113), channel_id=1, source_target_pairs={{0,3},{1,2},{2,1},{3,0},{4,7},{5,6},{6,5},{7,4},{8,11},{9,10},{10,... | collective-permute-start | bytes 12296 | tf_op jit(solution)/shard_map/ppermute | solution.py:470
  61.1 4.2 %collective-permute-start.22 = (f32[8,128]{1,0:T(8,128)S(1)}, f32[8,128]{1,0:T(8,128)S(1)}, u32[]{:S(2)}, u32[]{:S(2)}) collective-permute-start(f32[8,128]{1,0:T(8,128)S(1)} %add.49), channel_id=1, source_target_pairs={{0,7},{1,6},{2,5},{3,4},{4,3},{5,2},{6,1},{7,0},{8,15},{9,14},{10,... | collective-permute-start | bytes 12296 | tf_op jit(solution)/shard_map/ppermute | solution.py:470
  65.3 4.2 %collective-permute-start.23 = (f32[8,128]{1,0:T(8,128)S(1)}, f32[8,128]{1,0:T(8,128)S(1)}, u32[]{:S(2)}, u32[]{:S(2)}) collective-permute-start(f32[8,128]{1,0:T(8,128)S(1)} %add.50), channel_id=1, source_target_pairs={{0,97},{1,96},{2,99},{3,98},{4,101},{5,100},{6,103},{7,102},{8,105... | collective-permute-start | bytes 12296 | tf_op jit(solution)/shard_map/ppermute | solution.py:470
  72.6 4.2 %collective-permute-start.25 = (f32[8,128]{1,0:T(8,128)S(1)}, f32[8,128]{1,0:T(8,128)S(1)}, u32[]{:S(2)}, u32[]{:S(2)}) collective-permute-start(f32[8,128]{1,0:T(8,128)S(1)} %add.52), channel_id=1, source_target_pairs={{0,25},{1,24},{2,27},{3,26},{4,29},{5,28},{6,31},{7,30},{8,17},{9,... | collective-permute-start | bytes 12296 | tf_op jit(solution)/shard_map/ppermute | solution.py:470
  73.5 11.1 %collective-permute-start.17 = (f32[64,1024]{1,0:T(8,128)S(1)}, f32[64,1024]{1,0:T(8,128)S(1)}, u32[]{:S(2)}, u32[]{:S(2)}) collective-permute-start(f32[64,1024]{1,0:T(8,128)S(1)} %get-tuple-element.99), channel_id=1, source_target_pairs={{0,8},{1,9},{2,10},{3,11},{4,12},{5,13},{6,14},{7,15},{8,0},{9,1},... | collective-permute-start | bytes 786440 | tf_op jit(solution)/shard_map/ppermute | solution.py:447
  73.5 11.1 %collective-permute-start.18 = (f32[64,1024]{1,0:T(8,128)S(1)}, f32[64,1024]{1,0:T(8,128)S(1)}, u32[]{:S(2)}, u32[]{:S(2)}) collective-permute-start(f32[64,1024]{1,0:T(8,128)S(1)} %get-tuple-element.100), channel_id=1, source_target_pairs={{0,1},{1,0},{2,3},{3,2},{4,5},{5,4},{6,7},{7,6},{8,16},{9,17},{10,... | collective-permute-start | bytes 786440 | tf_op jit(solution)/shard_map/ppermute | solution.py:447
  76.8 5.0 %collective-permute-start.26 = (f32[8,128]{1,0:T(8,128)S(1)}, f32[8,128]{1,0:T(8,128)S(1)}, u32[]{:S(2)}, u32[]{:S(2)}) collective-permute-start(f32[8,128]{1,0:T(8,128)S(1)} %add.53), channel_id=1, source_target_pairs={{0,9},{1,8},{2,11},{3,10},{4,13},{5,12},{6,15},{7,14},{8,1},{9,0},... | collective-permute-start | bytes 12296 | tf_op jit(solution)/shard_map/ppermute | solution.py:470
  86.6 3.8 %collective-permute-start.19 = (f32[256,128]{1,0:T(8,128)S(1)}, f32[256,128]{1,0:T(8,128)S(1)}, u32[]{:S(2)}, u32[]{:S(2)}) collective-permute-start(f32[256,128]{1,0:T(8,128)S(1)} %get-tuple-element.111), channel_id=1, source_target_pairs={{0,1},{1,0},{2,3},{3,2},{4,5},{5,4},{6,7},{7,6},{8,9},{9,8},{10,11... | collective-permute-start | bytes 393224 | tf_op jit(solution)/shard_map/ppermute | solution.py:447
  87.1 4.7 %collective-permute-start.20 = (f32[256,128]{1,0:T(8,128)S(1)}, f32[256,128]{1,0:T(8,128)S(1)}, u32[]{:S(2)}, u32[]{:S(2)}) collective-permute-start(f32[256,128]{1,0:T(8,128)S(1)} %get-tuple-element.112), channel_id=1, source_target_pairs={{0,8},{1,2},{2,1},{3,4},{4,3},{5,6},{6,5},{7,15},{8,0},{9,10},{10,... | collective-permute-start | bytes 393224 | tf_op jit(solution)/shard_map/ppermute | solution.py:447
  (5 other events, 32.4 us)

commit v7 on v5

--- a/solution.py
+++ b/solution.py
@@ -23,7 +23,7 @@
 SMEM = pl.BlockSpec(memory_space=pltpu.SMEM)
 
 
-def call(kernel, outs, args, ins=None, out_specs=None, scratch=(), limit=24, flops=100_000_000):
+def call(kernel, outs, args, ins=None, out_specs=None, scratch=(), limit=24, flops=0):
     return pl.pallas_call(
         kernel,
         out_shape=[jax.ShapeDtypeStruct(s, d) for s, d in outs],
@@ -160,19 +160,11 @@
     return [jnp.where(keep, piece, jnp.zeros_like(piece)) for piece in pieces]
 
 
-def rows_kernel(*refs, bands, labelled, carried):
-    (field_ref,), label_refs, (band_high, band_low), plane, outs, plane_out, done = take(
-        refs, 1, labelled, 2, carried, 3, carried
-    )
-    high_ref, low_ref, edge_ref = outs
+def rows_kernel(*refs, bands, labelled):
+    (field_ref,), label_refs, (band_high, band_low, high_ref, low_ref, edge_ref) = take(
+        refs, 1, labelled
+    )
     rows, columns = field_ref.shape
-    copies = []
-    for source, target, arrived in zip(plane, plane_out, done):
-        for n, start in enumerate(range(0, rows, STEP)):
-            at = slice(start, start + STEP)
-            copies.append(pltpu.make_async_copy(source.at[at], target.at[at], arrived.at[n]))
-    for copy in copies:
-        copy.start()
     count = rows // REACH
     for n in range(columns // TILE):
         at = slice(n * TILE, (n + 1) * TILE)
@@ -208,8 +200,6 @@
             for i, value in enumerate(sums[1:-1]):
                 target = slice(i * REACH, (i + 1) * REACH)
                 high_ref[slot, target, at], low_ref[slot, target, at] = split(value)
-    for copy in copies:
-        copy.wait()
 
 
 def kept_row(start, rows):
@@ -327,111 +317,108 @@
 
 def middle_kernel(*refs, groups, start):
     count = len(groups)
-    highs, lows, (edge_high, edge_low), band_refs, (out_ref,) = take(refs, count, count, 2, 2)
+    highs, lows, (edge_high, edge_low), band_refs, (left_ref, right_ref), (out_ref,) = take(
+        refs, count, count, 2, 2, 2
+    )
     bands = [c for group in groups for c in group]
     inner = highs[0].shape[1]
-    for j in range(out_ref.shape[1] // TILE):
-        results = swept(
-            (highs, edge_high),
-            (lows, edge_low),
-            bands,
-            band_refs,
-            j + 1,
-            TILE,
-            edge_high.shape[2],
-            start,
-            start + out_ref.shape[0],
-            inner,
-        )
-        for k, value in enumerate(results):
-            out_ref[:, j * TILE + k * 128 : j * TILE + (k + 1) * 128] = value
-
-
-FINE = 16
-
-
-def gathered(pieces, come, flags, start):
-    left_ref, middles, right_ref = pieces
+    rows, columns = out_ref.shape
+    at = slice(start, start + rows)
+    lower = iota((rows, 128), 1) < REACH
+
+    def blocks():
+        for k in range(0, TILE, 128):
+            yield left_ref[at, k : k + 128]
+        for j in range(1, columns // TILE):
+            yield from swept(
+                (highs, edge_high),
+                (lows, edge_low),
+                bands,
+                band_refs,
+                j,
+                TILE,
+                columns,
+                start,
+                start + rows,
+                inner,
+            )
+        yield right_ref[at, :]
+
+    before = None
+    for k, block in enumerate(blocks()):
+        turned = pltpu.roll(block, REACH, 1)
+        if before is not None:
+            out_ref[:, (k - 1) * 128 : k * 128] = jnp.where(lower, before, turned)
+        before = turned
+
+
+def gathered(middles, come, flags, start):
     odd, has_left, has_right = flags
-    rows = left_ref.shape[0]
+    rows = sum(ref.shape[0] for ref in middles)
+    columns = middles[0].shape[1]
     half = rows // 2
     kept = kept_row(start, rows)
-    at = slice(kept, kept + FINE)
-    lane = iota((FINE, 128), 1)
-    local = slice(kept % half, kept % half + FINE)
+    lane = iota((STEP, 128), 1)
+    local = slice(kept % half, kept % half + STEP)
     come_left = chosen(has_left, chosen(odd, come[0][local], come[1][local]), 0.0)
     come_right = chosen(has_right, chosen(odd, come[1][local], come[0][local]), 0.0)
     if kept < half:
+        come_right = pltpu.roll(come_right, REACH, 1)
+    else:
         come_left = pltpu.roll(come_left, REACH, 1)
-    else:
-        come_right = pltpu.roll(come_right, REACH, 1)
-    first = left_ref[at, 0:128] + jnp.where(lane >= REACH, come_left, 0.0)
-    last = right_ref[at, :] + jnp.where(lane < REACH, come_right, 0.0)
     own = kept
     for middle_ref in middles:
         if own < middle_ref.shape[0]:
             break
         own -= middle_ref.shape[0]
-    own = slice(own, own + FINE)
-
-    def block_of(k):
+    for k in range(0, columns, 128):
+        block = middle_ref[own : own + STEP, k : k + 128]
         if k == 0:
-            return first
-        if k == 1:
-            return left_ref[at, 128:256]
-        if k * 128 < TILE + middle_ref.shape[1]:
-            return middle_ref[own, k * 128 - TILE : (k + 1) * 128 - TILE]
-        return last
-
-    before = pltpu.roll(block_of(0), REACH, 1)
-    for k in range((TILE + middle_ref.shape[1]) // 128):
-        after = pltpu.roll(block_of(k + 1), REACH, 1)
-        yield jnp.where(lane < REACH, before, after)
-        before = after
+            block = block + jnp.where(lane < REACH, come_left, 0.0)
+        if k == columns - 128:
+            block = block + jnp.where(lane >= REACH, come_right, 0.0)
+        yield block
 
 
 def finish_kernel(*refs, middles, scaled, following, totals):
-    leaving = scaled and not following
-    (left_ref,), middle_refs, (right_ref,), come, refs = take(refs, 1, middles, 1, 2)
-    pieces = (left_ref, middle_refs, right_ref)
-    totals_in, mass_in, density_out, refs = take(refs, 2 * scaled, following, scaled)
+    middle_refs, come, totals_in, mass_in, density_out, refs = take(
+        refs, middles, 2, 2 * scaled, following, scaled
+    )
     adapted_out, refs = take(refs, 4 * following)
+    rows = sum(ref.shape[0] for ref in middle_refs)
+    columns = middle_refs[0].shape[1]
+    column_flags = flags_of("col")
+    copies = []
     if scaled:
         inverse = jnp.exp(-(totals_in[0][0:1, :] / totals_in[1][1:2, :]))
-    staged, done = refs if leaving else (density_out[0] if scaled else None, None)
-    rows = left_ref.shape[0]
-    column_flags = flags_of("col")
-    columns = TILE + middle_refs[0].shape[1]
-    log_sums = [jnp.zeros((8, 128), F32)] * (columns // 128)
-    mass_sums = [jnp.zeros((8, 128), F32)] * (columns // 128)
+        staged, done = refs
+        for number, start in enumerate(range(0, rows, STEP)):
+            at = slice(start, start + STEP)
+            for k, block in enumerate(gathered(middle_refs, come, column_flags, start)):
+                staged[at, k * 128 : (k + 1) * 128] = block * inverse
+            copy = pltpu.make_async_copy(staged.at[at], density_out[0].at[at], done.at[number])
+            copy.start()
+            copies.append(copy)
     if following:
+        adapted_ref, send_a, send_b, stat_ref = adapted_out
         odd_row = flags_of("row")[0]
-        adapted_ref, send_a, send_b, stat_ref = adapted_out
-    copies = []
-    for start in range(0, rows, FINE):
-        at = slice(start, start + FINE)
-        for k, block in enumerate(gathered(pieces, come, column_flags, start)):
-            lanes = slice(k * 128, (k + 1) * 128)
+        log_sums = [jnp.zeros((8, 128), F32)] * (columns // 128)
+        mass_sums = [jnp.zeros((8, 128), F32)] * (columns // 128)
+        for start in range(0, rows, STEP):
+            at = slice(start, start + STEP)
             if scaled:
-                block = block * inverse
-                staged[at, lanes] = block
-            if following:
+                blocks = (staged[at, k : k + 128] for k in range(0, columns, 128))
+            else:
+                blocks = gathered(middle_refs, come, column_flags, start)
+            for k, block in enumerate(blocks):
+                lanes = slice(k * 128, (k + 1) * 128)
                 pilot = block + BACKGROUND
                 mass = mass_in[0][at, lanes]
                 adapted_ref[at, lanes] = mass * pilot
                 terms = mass * jnp.log(pilot)
-                for i in range(0, FINE, 8):
-                    log_sums[k] = log_sums[k] + terms[i : i + 8]
-                    if totals:
-                        mass_sums[k] = mass_sums[k] + mass[i : i + 8]
-        if leaving and (start + FINE) % STEP == 0:
-            at = slice(start + FINE - STEP, start + FINE)
-            copy = pltpu.make_async_copy(
-                staged.at[at], density_out[0].at[at], done.at[start // STEP]
-            )
-            copy.start()
-            copies.append(copy)
-    if following:
+                log_sums[k] += jnp.sum(terms.reshape(STEP // 8, 8, 128), axis=0)
+                if totals:
+                    mass_sums[k] += jnp.sum(mass.reshape(STEP // 8, 8, 128), axis=0)
         top, bottom = adapted_ref[0:REACH], adapted_ref[rows - REACH :]
         send_a[...] = chosen(odd_row, top, bottom)
         send_b[...] = chosen(odd_row, bottom, top)
@@ -463,13 +450,13 @@
 
 
 HOPS = (
+    (0, 7, (1, 8)),
     (0, 3, (1, 8)),
-    (0, 7, (1, 8)),
     (12, 1, (16, 1)),
     (4, 1, (16, 1)),
+    (0, 1, (1, 2)),
     (3, 1, (4, 1)),
     (1, 1, (2, 1)),
-    (0, 1, (1, 2)),
 )
 
 
@@ -485,28 +472,21 @@
     return stat
 
 
-def smooth(field, halo, labels, label_halo, tables, groups, cuts, leaving=()):
+def smooth(field, halo, labels, label_halo, tables, groups, cuts):
     high, low, rim = tables
     rows, columns = field.shape
     labelled = labels is not None
     bands = [c for group in groups for c in group]
     highs, lows, partials = [], [], []
-    for number, group in enumerate(groups):
+    for group in groups:
         inner = (len(group), rows - 2 * REACH, columns)
         edge = (len(group), 2 * REACH, columns)
-        carried = len(leaving) if number == 0 else 0
         results = call(
-            functools.partial(
-                rows_kernel, bands=group, labelled=labelled, carried=carried
-            ),
-            [(inner, BF16), (inner, BF16), (edge, F32)] + [(field.shape, F32)] * carried,
-            [field] + ([labels] if labelled else []) + [high, low, *leaving[:carried]],
-            out_specs=[VMEM] * 3 + [HBM] * carried,
-            scratch=[pltpu.SemaphoreType.DMA((rows // STEP,))] * carried,
+            functools.partial(rows_kernel, bands=group, labelled=labelled),
+            [(inner, BF16), (inner, BF16), (edge, F32)],
+            [field] + ([labels] if labelled else []) + [high, low],
             flops=len(group) * 1_000_000_000,
         )
-        if carried:
-            left_behind = results[3]
         for results_of, result in zip((highs, lows, partials), results):
             results_of.append(result)
     edge = (len(bands), 2 * REACH, columns)
@@ -524,33 +504,31 @@
     for count in cuts:
         middles += call(
             functools.partial(middle_kernel, groups=groups, start=start),
-            [((count, columns - TILE), F32)],
-            [*highs, *lows, edge_high, edge_low, high, low],
+            [((count, columns), F32)],
+            [*highs, *lows, edge_high, edge_low, high, low, left, right],
             flops=len(bands) * 750_000_000 * count // rows,
         )
         start += count
-    pieces = [left, *middles, right, *come]
-    return (pieces, left_behind) if leaving else pieces
+    return [*middles, *come]
 
 
 def finish(pieces, extra, scaled, following, totals, shape):
     plane, rim, stat = (shape, F32), ((REACH, shape[1]), F32), ((8, 128), F32)
     outs = [plane] * scaled + [plane, rim, rim, stat] * following
     scratch = []
-    leaving = scaled and not following
-    if leaving:
+    if scaled:
         scratch = [pltpu.VMEM(shape, F32), pltpu.SemaphoreType.DMA((shape[0] // STEP,))]
     return call(
         functools.partial(
             finish_kernel,
-            middles=len(pieces) - 4,
+            middles=len(pieces) - 2,
             scaled=scaled,
             following=following,
             totals=totals,
         ),
         outs,
         [*pieces, *extra],
-        out_specs=[HBM if leaving else VMEM] * scaled + [VMEM] * (4 * following),
+        out_specs=[HBM] * scaled + [VMEM] * (4 * following),
         scratch=scratch,
         flops=500_000_000,
     )
@@ -609,9 +587,7 @@
     )
     halo = exchange(*sends, "row")
     second_total = total_over(second_stat)
-    pieces, density_first = smooth(
-        adapted, halo, labels, label_halo, tables, groups, cuts, (density_first,)
-    )
+    pieces = smooth(adapted, halo, labels, label_halo, tables, groups, cuts)
     (density_second,) = finish(
         pieces, [second_total, first_total], True, False, False, shape
     )

time: 97.4 us -> 93.6 us (0.961)
  starting transfers between devices: 29.9 us -> 40.9 us
  waiting for transfers between devices: 32.7 us -> 21.8 us
  Pallas kernels: 33.5 us -> 29.6 us
    ppermute x14, waiting for transfers between devices: 26.9 us -> 16.4 us  [total_over(): stat = stat + lax.ppermute(stat, ('row', 'col'), pairs)]
    ppermute x14, starting transfers between devices: 21.1 us -> 29.7 us  [total_over(): stat = stat + lax.ppermute(stat, ('row', 'col'), pairs)]
    pallas_call x18, Pallas kernels: 33.5 us -> 29.6 us  [call(): pl.pallas_call(kernel, out_shape=[jax.ShapeDtypeStruct(s, d) for s, d in...]
    ppermute x14, starting transfers between devices: 8.78 us -> 11.2 us  [exchange(): results.append(lax.ppermute(value, ('row', 'col'), pairs))]
  transfers between devices with their start and end apart: 28 -> 28, of which waited for: 15 -> 12; matrix products, arithmetic and copies ran while one was open for 0% -> 0% of each run, Pallas kernels for 20% -> 20%
where the time goes in v7:
time: 93.6 us; the launch traced here: 93.5 us
  starting transfers between devices  40.9 us (44%)
  Pallas kernels  29.6 us (32%)
  waiting for transfers between devices  21.8 us (23%)
  between operations  1.11 us (1%)
    ppermute x14, starting transfers between devices, total_over(): stat = stat + lax.ppermute(stat, ('row', 'col'), pairs)  29.7 us
    pallas_call x18, Pallas kernels, call(): pl.pallas_call(kernel, out_shape=[jax.ShapeDtypeStruct(s, d) for s, d in...  29.6 us
    ppermute x14, waiting for transfers between devices, total_over(): stat = stat + lax.ppermute(stat, ('row', 'col'), pairs)  16.4 us
    ppermute x14, starting transfers between devices, exchange(): results.append(lax.ppermute(value, ('row', 'col'), pairs))  11.2 us
    ppermute x14, waiting for transfers between devices, exchange(): results.append(lax.ppermute(value, ('row', 'col'), pairs))  5.37 us
  transfers between devices with their start and end apart: 28, of which 12 were waited for; matrix products, arithmetic and copies ran while one was open for 0% of the time, Pallas kernels for 20%

profile of v7, /device:TPU:1, one launch (start us, length us, event | category | flops | bytes accessed | tf_op | source)
XLA Modules:
  0.0 93.5 jit_solution(2218985821497735984)
XLA Ops:
  0.6 2.4 %shard_map.59 = (bf16[384,256]{1,0:T(8,128)(2,1)S(1)}, bf16[384,256]{1,0:T(8,128)(2,1)S(1)}, bf16[1,128,384]{2,1,0:T(8,128)(2,1)S(1)}, f32[512,1024]{1,0:T(8,128...) custom-call(s32[512,1024]{1,0:T(8,128)} %refs_0_.2, ...), custom_call_target="tpu_custom_call" | custom-call | flops 500000000 | bytes 4194304 | tf_op jit(solution)/shard_map/pallas_call | solution.py:27
  3.1 2.2 %collective-permute-start = (f32[32,1024]{1,0:T(8,128)S(1)}, f32[32,1024]{1,0:T(8,128)S(1)}, u32[]{:S(2)}, u32[]{:S(2)}) collective-permute-start(f32[32,1024]{1,0:T(8,128)S(1)} %get-tuple-element.61), channel_id=1, source_target_pairs={{0,8},{1,9},{2,10},{3,11},{4,12},{5,13},{6,14},{7,15},{8,0},{9,1},... | collective-permute-start | bytes 393224 | tf_op jit(solution)/shard_map/ppermute | solution.py:448
  13.3 1.9 %collective-permute-done.3.refs_2_ = f32[256,128]{1,0:T(8,128)S(1)} collective-permute-done((f32[256,128]{1,0:T(8,128)S(1)}, f32[256,128]{1,0:T(8,128)S(1)}, u32[]{:S(2)}, u32[]{:S(2)}) %collective-permute-start.3) | collective-permute-done | bytes 131104 | tf_op jit(solution)/shard_map/ppermute | solution.py:448
  16.1 3.6 %collective-permute-start.10 = (f32[8,128]{1,0:T(8,128)S(1)}, f32[8,128]{1,0:T(8,128)S(1)}, u32[]{:S(2)}, u32[]{:S(2)}) collective-permute-start(f32[8,128]{1,0:T(8,128)S(1)} %get-tuple-element.92), channel_id=1, source_target_pairs={{0,7},{1,6},{2,5},{3,4},{4,3},{5,2},{6,1},{7,0},{8,15},{9,14},{10,... | collective-permute-start | bytes 12296 | tf_op jit(solution)/shard_map/ppermute | solution.py:471
  21.2 3.1 %collective-permute-done.11 = f32[8,128]{1,0:T(8,128)S(1)} collective-permute-done((f32[8,128]{1,0:T(8,128)S(1)}, f32[8,128]{1,0:T(8,128)S(1)}, u32[]{:S(2)}, u32[]{:S(2)}) %collective-permute-start.11) | collective-permute-done | bytes 4128 | tf_op jit(solution)/shard_map/ppermute | solution.py:471
  24.3 5.8 %collective-permute-start.12 = (f32[8,128]{1,0:T(8,128)S(1)}, f32[8,128]{1,0:T(8,128)S(1)}, u32[]{:S(2)}, u32[]{:S(2)}) collective-permute-start(f32[8,128]{1,0:T(8,128)S(1)} %add.43), channel_id=1, source_target_pairs={{0,97},{1,96},{2,99},{3,98},{4,101},{5,100},{6,103},{7,102},{8,105... | collective-permute-start | bytes 12296 | tf_op jit(solution)/shard_map/ppermute | solution.py:471
  32.2 2.2 %collective-permute-done.13 = f32[8,128]{1,0:T(8,128)S(1)} collective-permute-done((f32[8,128]{1,0:T(8,128)S(1)}, f32[8,128]{1,0:T(8,128)S(1)}, u32[]{:S(2)}, u32[]{:S(2)}) %collective-permute-start.13) | collective-permute-done | bytes 4128 | tf_op jit(solution)/shard_map/ppermute | solution.py:471
  34.8 2.2 %shard_map.64 = (bf16[1536,256]{1,0:T(8,128)(2,1)S(1)}, bf16[1536,256]{1,0:T(8,128)(2,1)S(1)}, bf16[4,128,384]{2,1,0:T(8,128)(2,1)S(1)}, bf16[512,1024]{1,0:T(8,128)(2,1)S(1)}) custom-call(s32[4]{0:T(128)S(1)} %copy-done, s32[512,1024]{1,0:T(8,128)} %refs_1_.3), custom_call_target="tpu_custom_call" | custom-call | flops 500000000 | bytes 4194304 | tf_op jit(solution)/shard_map/pallas_call | solution.py:27
  38.1 4.0 %collective-permute-start.15 = (f32[8,128]{1,0:T(8,128)S(1)}, f32[8,128]{1,0:T(8,128)S(1)}, u32[]{:S(2)}, u32[]{:S(2)}) collective-permute-start(f32[8,128]{1,0:T(8,128)S(1)} %add.46), channel_id=1, source_target_pairs={{0,25},{1,24},{2,27},{3,26},{4,29},{5,28},{6,31},{7,30},{8,17},{9,... | collective-permute-start | bytes 12296 | tf_op jit(solution)/shard_map/ppermute | solution.py:471
  42.1 1.9 %shard_map.66 = (bf16[2,384,1024]{2,1,0:T(8,128)(2,1)S(1)}, bf16[2,384,1024]{2,1,0:T(8,128)(2,1)S(1)}, f32[2,128,1024]{2,1,0:T(8,128)S(1)}) custom-call(f32[512,1024]{1,0:T(8,128)S(1)} %get-tuple-element.71.refs_0_, bf16[512,1024]{1,0:T(8,128)(2,1)S(1)} %get-tuple-element.72.refs_1_, bf16[1536,256]{1,0:T(8,128)(2,1)S(1)} %get-tuple-element.73.refs_2_.refs_11_.refs_6_, ...), custom_call_target="tpu_custom_call" | custom-call | flops 2000000000 | bytes 4194304 | tf_op jit(solution)/shard_map/pallas_call | solution.py:27
  44.1 3.1 %collective-permute-start.16 = (f32[8,128]{1,0:T(8,128)S(1)}, f32[8,128]{1,0:T(8,128)S(1)}, u32[]{:S(2)}, u32[]{:S(2)}) collective-permute-start(f32[8,128]{1,0:T(8,128)S(1)} %add.47), channel_id=1, source_target_pairs={{0,9},{1,8},{2,11},{3,10},{4,13},{5,12},{6,15},{7,14},{8,1},{9,0},... | collective-permute-start | bytes 12296 | tf_op jit(solution)/shard_map/ppermute | solution.py:471
  47.1 1.9 %shard_map.65 = (bf16[2,384,1024]{2,1,0:T(8,128)(2,1)S(1)}, bf16[2,384,1024]{2,1,0:T(8,128)(2,1)S(1)}, f32[2,128,1024]{2,1,0:T(8,128)S(1)}) custom-call(f32[512,1024]{1,0:T(8,128)S(1)} %get-tuple-element.71.refs_0_, bf16[512,1024]{1,0:T(8,128)(2,1)S(1)} %get-tuple-element.72.refs_1_, bf16[1536,256]{1,0:T(8,128)(2,1)S(1)} %get-tuple-element.73.refs_2_.refs_11_.refs_6_, ...), custom_call_target="tpu_custom_call" | custom-call | flops 2000000000 | bytes 4194304 | tf_op jit(solution)/shard_map/pallas_call | solution.py:27
  49.1 1.9 %shard_map.67 = (bf16[4,128,1024]{2,1,0:T(8,128)(2,1)S(1)}, bf16[4,128,1024]{2,1,0:T(8,128)(2,1)S(1)}, f32[512,256]{1,0:T(8,128)S(1)}, f32[512,128]{1,0:T(8,128)...) custom-call(f32[64,1024]{1,0:T(8,128)S(1)} %collective-permute-done.4.refs_0_, ...), custom_call_target="tpu_custom_call" | custom-call | flops 2000000000 | bytes 4194304 | tf_op jit(solution)/shard_map/pallas_call | solution.py:27
  51.6 2.0 %shard_map.68.refs_0_ = f32[320,1024]{1,0:T(8,128)S(1)} custom-call(bf16[2,384,1024]{2,1,0:T(8,128)(2,1)S(1)} %get-tuple-element.75.refs_6_.refs_0_, bf16[2,384,1024]{2,1,0:T(8,128)(2,1)S(1)} %get-tuple-element.76.refs_7_.refs_1_, bf16[2,384,1024]{2,1,0:T(8,128)(2,1)S(1)} %get-tuple-element.77.refs_8_.refs_2_, ...), custom_call_target="tpu_custom_call" | custom-call | flops 1875000064 | bytes 4194304 | tf_op jit(solution)/shard_map/pallas_call | solution.py:27
  57.9 2.7 %collective-permute-start.21 = (f32[8,128]{1,0:T(8,128)S(1)}, f32[8,128]{1,0:T(8,128)S(1)}, u32[]{:S(2)}, u32[]{:S(2)}) collective-permute-start(f32[8,128]{1,0:T(8,128)S(1)} %get-tuple-element.109), channel_id=1, source_target_pairs={{0,7},{1,6},{2,5},{3,4},{4,3},{5,2},{6,1},{7,0},{8,15},{9,14},{10,... | collective-permute-start | bytes 12296 | tf_op jit(solution)/shard_map/ppermute | solution.py:471
  62.2 3.0 %collective-permute-done.22 = f32[8,128]{1,0:T(8,128)S(1)} collective-permute-done((f32[8,128]{1,0:T(8,128)S(1)}, f32[8,128]{1,0:T(8,128)S(1)}, u32[]{:S(2)}, u32[]{:S(2)}) %collective-permute-start.22) | collective-permute-done | bytes 4128 | tf_op jit(solution)/shard_map/ppermute | solution.py:471
  65.2 2.8 %collective-permute-start.23 = (f32[8,128]{1,0:T(8,128)S(1)}, f32[8,128]{1,0:T(8,128)S(1)}, u32[]{:S(2)}, u32[]{:S(2)}) collective-permute-start(f32[8,128]{1,0:T(8,128)S(1)} %add.50), channel_id=1, source_target_pairs={{0,97},{1,96},{2,99},{3,98},{4,101},{5,100},{6,103},{7,102},{8,105... | collective-permute-start | bytes 12296 | tf_op jit(solution)/shard_map/ppermute | solution.py:471
  70.2 2.3 %collective-permute-done.24 = f32[8,128]{1,0:T(8,128)S(1)} collective-permute-done((f32[8,128]{1,0:T(8,128)S(1)}, f32[8,128]{1,0:T(8,128)S(1)}, u32[]{:S(2)}, u32[]{:S(2)}) %collective-permute-start.24) | collective-permute-done | bytes 4128 | tf_op jit(solution)/shard_map/ppermute | solution.py:471
  74.4 3.2 %collective-permute-start.26 = (f32[8,128]{1,0:T(8,128)S(1)}, f32[8,128]{1,0:T(8,128)S(1)}, u32[]{:S(2)}, u32[]{:S(2)}) collective-permute-start(f32[8,128]{1,0:T(8,128)S(1)} %add.53), channel_id=1, source_target_pairs={{0,25},{1,24},{2,27},{3,26},{4,29},{5,28},{6,31},{7,30},{8,17},{9,... | collective-permute-start | bytes 12296 | tf_op jit(solution)/shard_map/ppermute | solution.py:471
  77.6 2.0 %shard_map.72 = (bf16[2,384,1024]{2,1,0:T(8,128)(2,1)S(1)}, bf16[2,384,1024]{2,1,0:T(8,128)(2,1)S(1)}, f32[2,128,1024]{2,1,0:T(8,128)S(1)}) custom-call(f32[512,1024]{1,0:T(8,128)S(1)} %get-tuple-element.94.refs_0_, bf16[512,1024]{1,0:T(8,128)(2,1)S(1)} %get-tuple-element.72.refs_1_, bf16[1536,256]{1,0:T(8,128)(2,1)S(1)} %get-tuple-element.73.refs_2_.refs_11_.refs_6_, ...), custom_call_target="tpu_custom_call" | custom-call | flops 2000000000 | bytes 4194304 | tf_op jit(solution)/shard_map/pallas_call | solution.py:27
  79.7 2.5 %collective-permute-start.27 = (f32[8,128]{1,0:T(8,128)S(1)}, f32[8,128]{1,0:T(8,128)S(1)}, u32[]{:S(2)}, u32[]{:S(2)}) collective-permute-start(f32[8,128]{1,0:T(8,128)S(1)} %add.54), channel_id=1, source_target_pairs={{0,9},{1,8},{2,11},{3,10},{4,13},{5,12},{6,15},{7,14},{8,1},{9,0},... | collective-permute-start | bytes 12296 | tf_op jit(solution)/shard_map/ppermute | solution.py:471
  82.2 2.0 %shard_map.71 = (bf16[2,384,1024]{2,1,0:T(8,128)(2,1)S(1)}, bf16[2,384,1024]{2,1,0:T(8,128)(2,1)S(1)}, f32[2,128,1024]{2,1,0:T(8,128)S(1)}) custom-call(f32[512,1024]{1,0:T(8,128)S(1)} %get-tuple-element.94.refs_0_, bf16[512,1024]{1,0:T(8,128)(2,1)S(1)} %get-tuple-element.72.refs_1_, bf16[1536,256]{1,0:T(8,128)(2,1)S(1)} %get-tuple-element.73.refs_2_.refs_11_.refs_6_, ...), custom_call_target="tpu_custom_call" | custom-call | flops 2000000000 | bytes 4194304 | tf_op jit(solution)/shard_map/pallas_call | solution.py:27
  84.3 1.9 %shard_map.73 = (bf16[4,128,1024]{2,1,0:T(8,128)(2,1)S(1)}, bf16[4,128,1024]{2,1,0:T(8,128)(2,1)S(1)}, f32[512,256]{1,0:T(8,128)S(1)}, f32[512,128]{1,0:T(8,128)...) custom-call(f32[64,1024]{1,0:T(8,128)S(1)} %collective-permute-done.17.refs_0_, ...), custom_call_target="tpu_custom_call" | custom-call | flops 2000000000 | bytes 4194304 | tf_op jit(solution)/shard_map/pallas_call | solution.py:27
  87.1 2.0 %shard_map.74.refs_0_ = f32[320,1024]{1,0:T(8,128)S(1)} custom-call(bf16[2,384,1024]{2,1,0:T(8,128)(2,1)S(1)} %get-tuple-element.95.refs_6_.refs_0_, bf16[2,384,1024]{2,1,0:T(8,128)(2,1)S(1)} %get-tuple-element.96.refs_7_.refs_1_, bf16[2,384,1024]{2,1,0:T(8,128)(2,1)S(1)} %get-tuple-element.97.refs_8_.refs_2_, ...), custom_call_target="tpu_custom_call" | custom-call | flops 1875000064 | bytes 4194304 | tf_op jit(solution)/shard_map/pallas_call | solution.py:27
  (66 shorter events, 29.7 us)
Async XLA Ops:
  3.1 5.1 %collective-permute-start = (f32[32,1024]{1,0:T(8,128)S(1)}, f32[32,1024]{1,0:T(8,128)S(1)}, u32[]{:S(2)}, u32[]{:S(2)}) collective-permute-start(f32[32,1024]{1,0:T(8,128)S(1)} %get-tuple-element.61), channel_id=1, source_target_pairs={{0,8},{1,9},{2,10},{3,11},{4,12},{5,13},{6,14},{7,15},{8,0},{9,1},... | collective-permute-start | bytes 393224 | tf_op jit(solution)/shard_map/ppermute | solution.py:448
  8.8 4.5 %collective-permute-start.2 = (f32[256,128]{1,0:T(8,128)S(1)}, f32[256,128]{1,0:T(8,128)S(1)}, u32[]{:S(2)}, u32[]{:S(2)}) collective-permute-start(f32[256,128]{1,0:T(8,128)S(1)} %get-tuple-element.69), channel_id=1, source_target_pairs={{0,1},{1,0},{2,3},{3,2},{4,5},{5,4},{6,7},{7,6},{8,9},{9,8},{10,11... | collective-permute-start | bytes 393224 | tf_op jit(solution)/shard_map/ppermute | solution.py:448
  10.4 4.7 %collective-permute-start.3 = (f32[256,128]{1,0:T(8,128)S(1)}, f32[256,128]{1,0:T(8,128)S(1)}, u32[]{:S(2)}, u32[]{:S(2)}) collective-permute-start(f32[256,128]{1,0:T(8,128)S(1)} %get-tuple-element.70), channel_id=1, source_target_pairs={{0,8},{1,2},{2,1},{3,4},{4,3},{5,6},{6,5},{7,15},{8,0},{9,10},{10,... | collective-permute-start | bytes 393224 | tf_op jit(solution)/shard_map/ppermute | solution.py:448
  16.1 5.0 %collective-permute-start.10 = (f32[8,128]{1,0:T(8,128)S(1)}, f32[8,128]{1,0:T(8,128)S(1)}, u32[]{:S(2)}, u32[]{:S(2)}) collective-permute-start(f32[8,128]{1,0:T(8,128)S(1)} %get-tuple-element.92), channel_id=1, source_target_pairs={{0,7},{1,6},{2,5},{3,4},{4,3},{5,2},{6,1},{7,0},{8,15},{9,14},{10,... | collective-permute-start | bytes 12296 | tf_op jit(solution)/shard_map/ppermute | solution.py:471
  21.2 3.1 %collective-permute-start.11 = (f32[8,128]{1,0:T(8,128)S(1)}, f32[8,128]{1,0:T(8,128)S(1)}, u32[]{:S(2)}, u32[]{:S(2)}) collective-permute-start(f32[8,128]{1,0:T(8,128)S(1)} %add.42), channel_id=1, source_target_pairs={{0,3},{1,2},{2,1},{3,0},{4,7},{5,6},{6,5},{7,4},{8,11},{9,10},{10,... | collective-permute-start | bytes 12296 | tf_op jit(solution)/shard_map/ppermute | solution.py:471
  24.3 7.1 %collective-permute-start.12 = (f32[8,128]{1,0:T(8,128)S(1)}, f32[8,128]{1,0:T(8,128)S(1)}, u32[]{:S(2)}, u32[]{:S(2)}) collective-permute-start(f32[8,128]{1,0:T(8,128)S(1)} %add.43), channel_id=1, source_target_pairs={{0,97},{1,96},{2,99},{3,98},{4,101},{5,100},{6,103},{7,102},{8,105... | collective-permute-start | bytes 12296 | tf_op jit(solution)/shard_map/ppermute | solution.py:471
  31.3 3.0 %collective-permute-start.13 = (f32[8,128]{1,0:T(8,128)S(1)}, f32[8,128]{1,0:T(8,128)S(1)}, u32[]{:S(2)}, u32[]{:S(2)}) collective-permute-start(f32[8,128]{1,0:T(8,128)S(1)} %add.44), channel_id=1, source_target_pairs={{0,33},{1,32},{2,35},{3,34},{4,37},{5,36},{6,39},{7,38},{8,41},{9,... | collective-permute-start | bytes 12296 | tf_op jit(solution)/shard_map/ppermute | solution.py:471
  31.8 17.3 %collective-permute-start.6 = (s32[64,1024]{1,0:T(8,128)S(1)}, s32[64,1024]{1,0:T(8,128)S(1)}, u32[]{:S(2)}, u32[]{:S(2)}) collective-permute-start(s32[64,1024]{1,0:T(8,128)S(1)} %get-tuple-element.81), channel_id=1, source_target_pairs={{0,8},{1,9},{2,10},{3,11},{4,12},{5,13},{6,14},{7,15},{8,0},{9,1},... | collective-permute-start | bytes 786440 | tf_op jit(solution)/shard_map/ppermute | solution.py:448
  31.8 17.3 %collective-permute-start.7 = (s32[64,1024]{1,0:T(8,128)S(1)}, s32[64,1024]{1,0:T(8,128)S(1)}, u32[]{:S(2)}, u32[]{:S(2)}) collective-permute-start(s32[64,1024]{1,0:T(8,128)S(1)} %get-tuple-element.82), channel_id=1, source_target_pairs={{0,1},{1,0},{2,3},{3,2},{4,5},{5,4},{6,7},{7,6},{8,16},{9,17},{10,... | collective-permute-start | bytes 786440 | tf_op jit(solution)/shard_map/ppermute | solution.py:448
  34.4 3.7 %collective-permute-start.14 = (f32[8,128]{1,0:T(8,128)S(1)}, f32[8,128]{1,0:T(8,128)S(1)}, u32[]{:S(2)}, u32[]{:S(2)}) collective-permute-start(f32[8,128]{1,0:T(8,128)S(1)} %add.45), channel_id=1, source_target_pairs={{0,1},{1,0},{2,3},{3,2},{4,5},{5,4},{6,7},{7,6},{8,9},{9,8},{10,11... | collective-permute-start | bytes 12296 | tf_op jit(solution)/shard_map/ppermute | solution.py:471
  37.0 12.2 %collective-permute-start.4 = (f32[64,1024]{1,0:T(8,128)S(1)}, f32[64,1024]{1,0:T(8,128)S(1)}, u32[]{:S(2)}, u32[]{:S(2)}) collective-permute-start(f32[64,1024]{1,0:T(8,128)S(1)} %get-tuple-element.79), channel_id=1, source_target_pairs={{0,8},{1,9},{2,10},{3,11},{4,12},{5,13},{6,14},{7,15},{8,0},{9,1},... | collective-permute-start | bytes 786440 | tf_op jit(solution)/shard_map/ppermute | solution.py:448
  37.8 11.4 %collective-permute-start.5 = (f32[64,1024]{1,0:T(8,128)S(1)}, f32[64,1024]{1,0:T(8,128)S(1)}, u32[]{:S(2)}, u32[]{:S(2)}) collective-permute-start(f32[64,1024]{1,0:T(8,128)S(1)} %get-tuple-element.80), channel_id=1, source_target_pairs={{0,1},{1,0},{2,3},{3,2},{4,5},{5,4},{6,7},{7,6},{8,16},{9,17},{10,... | collective-permute-start | bytes 786440 | tf_op jit(solution)/shard_map/ppermute | solution.py:448
  38.1 6.0 %collective-permute-start.15 = (f32[8,128]{1,0:T(8,128)S(1)}, f32[8,128]{1,0:T(8,128)S(1)}, u32[]{:S(2)}, u32[]{:S(2)}) collective-permute-start(f32[8,128]{1,0:T(8,128)S(1)} %add.46), channel_id=1, source_target_pairs={{0,25},{1,24},{2,27},{3,26},{4,29},{5,28},{6,31},{7,30},{8,17},{9,... | collective-permute-start | bytes 12296 | tf_op jit(solution)/shard_map/ppermute | solution.py:471
  44.1 5.0 %collective-permute-start.16 = (f32[8,128]{1,0:T(8,128)S(1)}, f32[8,128]{1,0:T(8,128)S(1)}, u32[]{:S(2)}, u32[]{:S(2)}) collective-permute-start(f32[8,128]{1,0:T(8,128)S(1)} %add.47), channel_id=1, source_target_pairs={{0,9},{1,8},{2,11},{3,10},{4,13},{5,12},{6,15},{7,14},{8,1},{9,0},... | collective-permute-start | bytes 12296 | tf_op jit(solution)/shard_map/ppermute | solution.py:471
  51.0 4.0 %collective-permute-start.8 = (f32[256,128]{1,0:T(8,128)S(1)}, f32[256,128]{1,0:T(8,128)S(1)}, u32[]{:S(2)}, u32[]{:S(2)}) collective-permute-start(f32[256,128]{1,0:T(8,128)S(1)} %get-tuple-element.90), channel_id=1, source_target_pairs={{0,1},{1,0},{2,3},{3,2},{4,5},{5,4},{6,7},{7,6},{8,9},{9,8},{10,11... | collective-permute-start | bytes 393224 | tf_op jit(solution)/shard_map/ppermute | solution.py:448
  51.6 4.7 %collective-permute-start.9 = (f32[256,128]{1,0:T(8,128)S(1)}, f32[256,128]{1,0:T(8,128)S(1)}, u32[]{:S(2)}, u32[]{:S(2)}) collective-permute-start(f32[256,128]{1,0:T(8,128)S(1)} %get-tuple-element.91), channel_id=1, source_target_pairs={{0,8},{1,2},{2,1},{3,4},{4,3},{5,6},{6,5},{7,15},{8,0},{9,10},{10,... | collective-permute-start | bytes 393224 | tf_op jit(solution)/shard_map/ppermute | solution.py:448
  57.9 4.3 %collective-permute-start.21 = (f32[8,128]{1,0:T(8,128)S(1)}, f32[8,128]{1,0:T(8,128)S(1)}, u32[]{:S(2)}, u32[]{:S(2)}) collective-permute-start(f32[8,128]{1,0:T(8,128)S(1)} %get-tuple-element.109), channel_id=1, source_target_pairs={{0,7},{1,6},{2,5},{3,4},{4,3},{5,2},{6,1},{7,0},{8,15},{9,14},{10,... | collective-permute-start | bytes 12296 | tf_op jit(solution)/shard_map/ppermute | solution.py:471
  65.2 4.2 %collective-permute-start.23 = (f32[8,128]{1,0:T(8,128)S(1)}, f32[8,128]{1,0:T(8,128)S(1)}, u32[]{:S(2)}, u32[]{:S(2)}) collective-permute-start(f32[8,128]{1,0:T(8,128)S(1)} %add.50), channel_id=1, source_target_pairs={{0,97},{1,96},{2,99},{3,98},{4,101},{5,100},{6,103},{7,102},{8,105... | collective-permute-start | bytes 12296 | tf_op jit(solution)/shard_map/ppermute | solution.py:471
  72.9 11.3 %collective-permute-start.17 = (f32[64,1024]{1,0:T(8,128)S(1)}, f32[64,1024]{1,0:T(8,128)S(1)}, u32[]{:S(2)}, u32[]{:S(2)}) collective-permute-start(f32[64,1024]{1,0:T(8,128)S(1)} %get-tuple-element.99), channel_id=1, source_target_pairs={{0,8},{1,9},{2,10},{3,11},{4,12},{5,13},{6,14},{7,15},{8,0},{9,1},... | collective-permute-start | bytes 786440 | tf_op jit(solution)/shard_map/ppermute | solution.py:448
  74.0 10.2 %collective-permute-start.18 = (f32[64,1024]{1,0:T(8,128)S(1)}, f32[64,1024]{1,0:T(8,128)S(1)}, u32[]{:S(2)}, u32[]{:S(2)}) collective-permute-start(f32[64,1024]{1,0:T(8,128)S(1)} %get-tuple-element.100), channel_id=1, source_target_pairs={{0,1},{1,0},{2,3},{3,2},{4,5},{5,4},{6,7},{7,6},{8,16},{9,17},{10,... | collective-permute-start | bytes 786440 | tf_op jit(solution)/shard_map/ppermute | solution.py:448
  74.4 5.2 %collective-permute-start.26 = (f32[8,128]{1,0:T(8,128)S(1)}, f32[8,128]{1,0:T(8,128)S(1)}, u32[]{:S(2)}, u32[]{:S(2)}) collective-permute-start(f32[8,128]{1,0:T(8,128)S(1)} %add.53), channel_id=1, source_target_pairs={{0,25},{1,24},{2,27},{3,26},{4,29},{5,28},{6,31},{7,30},{8,17},{9,... | collective-permute-start | bytes 12296 | tf_op jit(solution)/shard_map/ppermute | solution.py:471
  79.7 4.5 %collective-permute-start.27 = (f32[8,128]{1,0:T(8,128)S(1)}, f32[8,128]{1,0:T(8,128)S(1)}, u32[]{:S(2)}, u32[]{:S(2)}) collective-permute-start(f32[8,128]{1,0:T(8,128)S(1)} %add.54), channel_id=1, source_target_pairs={{0,9},{1,8},{2,11},{3,10},{4,13},{5,12},{6,15},{7,14},{8,1},{9,0},... | collective-permute-start | bytes 12296 | tf_op jit(solution)/shard_map/ppermute | solution.py:471
  86.1 4.4 %collective-permute-start.19 = (f32[256,128]{1,0:T(8,128)S(1)}, f32[256,128]{1,0:T(8,128)S(1)}, u32[]{:S(2)}, u32[]{:S(2)}) collective-permute-start(f32[256,128]{1,0:T(8,128)S(1)} %get-tuple-element.107), channel_id=1, source_target_pairs={{0,1},{1,0},{2,3},{3,2},{4,5},{5,4},{6,7},{7,6},{8,9},{9,8},{10,11... | collective-permute-start | bytes 393224 | tf_op jit(solution)/shard_map/ppermute | solution.py:448
  87.1 4.7 %collective-permute-start.20 = (f32[256,128]{1,0:T(8,128)S(1)}, f32[256,128]{1,0:T(8,128)S(1)}, u32[]{:S(2)}, u32[]{:S(2)}) collective-permute-start(f32[256,128]{1,0:T(8,128)S(1)} %get-tuple-element.108), channel_id=1, source_target_pairs={{0,8},{1,2},{2,1},{3,4},{4,3},{5,6},{6,5},{7,15},{8,0},{9,10},{10,... | collective-permute-start | bytes 393224 | tf_op jit(solution)/shard_map/ppermute | solution.py:448
  (5 other events, 32.3 us)

commit v8 on v7

--- a/solution.py
+++ b/solution.py
@@ -380,52 +380,72 @@
         yield block
 
 
-def finish_kernel(*refs, middles, scaled, following, totals):
-    middle_refs, come, totals_in, mass_in, density_out, refs = take(
-        refs, middles, 2, 2 * scaled, following, scaled
-    )
-    adapted_out, refs = take(refs, 4 * following)
-    rows = sum(ref.shape[0] for ref in middle_refs)
-    columns = middle_refs[0].shape[1]
-    column_flags = flags_of("col")
-    copies = []
+def tally_kernel(*refs, middles, scaled, totals):
+    middle_refs, come, totals_in, (mass_ref, plane_ref, stat_ref) = take(
+        refs, middles, 2, 2 * scaled
+    )
+    rows, columns = plane_ref.shape
+    flags = flags_of("col")
     if scaled:
         inverse = jnp.exp(-(totals_in[0][0:1, :] / totals_in[1][1:2, :]))
-        staged, done = refs
+    log_sums = [jnp.zeros((8, 128), F32)] * (columns // 128)
+    mass_sums = [jnp.zeros((8, 128), F32)] * (columns // 128)
+    for start in range(0, rows, STEP):
+        at = slice(start, start + STEP)
+        for k, block in enumerate(gathered(middle_refs, come, flags, start)):
+            lanes = slice(k * 128, (k + 1) * 128)
+            if scaled:
+                block = block * inverse
+            plane_ref[at, lanes] = block
+            mass = mass_ref[at, lanes]
+            terms = mass * jnp.log(block + BACKGROUND)
+            log_sums[k] += jnp.sum(terms.reshape(STEP // 8, 8, 128), axis=0)
+            if totals:
+                mass_sums[k] += jnp.sum(mass.reshape(STEP // 8, 8, 128), axis=0)
+    log_sum = jnp.sum(sum(log_sums), axis=(0, 1), keepdims=True)
+    mass_sum = jnp.sum(sum(mass_sums), axis=(0, 1), keepdims=True)
+    row = iota((8, 128), 0)
+    stat_ref[...] = jnp.where(row == 0, log_sum, jnp.where(row == 1, mass_sum, 0.0))
+
+
+def adapt_kernel(*refs, kept):
+    (plane_ref, mass_ref, adapted_ref, send_a, send_b), density_out, done = take(refs, 5, kept)
+    rows = plane_ref.shape[0]
+    copies = []
+    if kept:
         for number, start in enumerate(range(0, rows, STEP)):
             at = slice(start, start + STEP)
-            for k, block in enumerate(gathered(middle_refs, come, column_flags, start)):
-                staged[at, k * 128 : (k + 1) * 128] = block * inverse
-            copy = pltpu.make_async_copy(staged.at[at], density_out[0].at[at], done.at[number])
-            copy.start()
-            copies.append(copy)
-    if following:
-        adapted_ref, send_a, send_b, stat_ref = adapted_out
-        odd_row = flags_of("row")[0]
-        log_sums = [jnp.zeros((8, 128), F32)] * (columns // 128)
-        mass_sums = [jnp.zeros((8, 128), F32)] * (columns // 128)
-        for start in range(0, rows, STEP):
-            at = slice(start, start + STEP)
-            if scaled:
-                blocks = (staged[at, k : k + 128] for k in range(0, columns, 128))
-            else:
-                blocks = gathered(middle_refs, come, column_flags, start)
-            for k, block in enumerate(blocks):
-                lanes = slice(k * 128, (k + 1) * 128)
-                pilot = block + BACKGROUND
-                mass = mass_in[0][at, lanes]
-                adapted_ref[at, lanes] = mass * pilot
-                terms = mass * jnp.log(pilot)
-                log_sums[k] += jnp.sum(terms.reshape(STEP // 8, 8, 128), axis=0)
-                if totals:
-                    mass_sums[k] += jnp.sum(mass.reshape(STEP // 8, 8, 128), axis=0)
-        top, bottom = adapted_ref[0:REACH], adapted_ref[rows - REACH :]
-        send_a[...] = chosen(odd_row, top, bottom)
-        send_b[...] = chosen(odd_row, bottom, top)
-        log_sum = jnp.sum(sum(log_sums), axis=(0, 1), keepdims=True)
-        mass_sum = jnp.sum(sum(mass_sums), axis=(0, 1), keepdims=True)
-        row = iota((8, 128), 0)
-        stat_ref[...] = jnp.where(row == 0, log_sum, jnp.where(row == 1, mass_sum, 0.0))
+            copies.append(
+                pltpu.make_async_copy(
+                    plane_ref.at[at], density_out[0].at[at], done[0].at[number]
+                )
+            )
+    for copy in copies:
+        copy.start()
+    for start in range(0, rows, STEP):
+        at = slice(start, start + STEP)
+        adapted_ref[at] = mass_ref[at] * (plane_ref[at] + BACKGROUND)
+    odd = flags_of("row")[0]
+    top, bottom = adapted_ref[0:REACH], adapted_ref[rows - REACH :]
+    send_a[...] = chosen(odd, top, bottom)
+    send_b[...] = chosen(odd, bottom, top)
+    for copy in copies:
+        copy.wait()
+
+
+def finish_kernel(*refs, middles):
+    middle_refs, come, totals_in, (density_ref, staged, done) = take(refs, middles, 2, 2)
+    rows, _ = staged.shape
+    flags = flags_of("col")
+    inverse = jnp.exp(-(totals_in[0][0:1, :] / totals_in[1][1:2, :]))
+    copies = []
+    for number, start in enumerate(range(0, rows, STEP)):
+        at = slice(start, start + STEP)
+        for k, block in enumerate(gathered(middle_refs, come, flags, start)):
+            staged[at, k * 128 : (k + 1) * 128] = block * inverse
+        copy = pltpu.make_async_copy(staged.at[at], density_ref.at[at], done.at[number])
+        copy.start()
+        copies.append(copy)
     for copy in copies:
         copy.wait()
 
@@ -512,24 +532,45 @@
     return [*middles, *come]
 
 
-def finish(pieces, extra, scaled, following, totals, shape):
-    plane, rim, stat = (shape, F32), ((REACH, shape[1]), F32), ((8, 128), F32)
-    outs = [plane] * scaled + [plane, rim, rim, stat] * following
-    scratch = []
-    if scaled:
-        scratch = [pltpu.VMEM(shape, F32), pltpu.SemaphoreType.DMA((shape[0] // STEP,))]
+def leaving(shape):
+    return pltpu.SemaphoreType.DMA((shape[0] // STEP,))
+
+
+def tally(pieces, totals_in, mass):
+    shape = mass.shape
     return call(
         functools.partial(
-            finish_kernel,
+            tally_kernel,
             middles=len(pieces) - 2,
-            scaled=scaled,
-            following=following,
-            totals=totals,
+            scaled=bool(totals_in),
+            totals=not totals_in,
         ),
-        outs,
-        [*pieces, *extra],
-        out_specs=[HBM] * scaled + [VMEM] * (4 * following),
-        scratch=scratch,
+        [(shape, F32), ((8, 128), F32)],
+        [*pieces, *totals_in, mass],
+        flops=500_000_000,
+    )
+
+
+def adapt(plane, mass, kept):
+    shape = mass.shape
+    rim = (REACH, shape[1])
+    return call(
+        functools.partial(adapt_kernel, kept=kept),
+        [(shape, F32), (rim, F32), (rim, F32)] + [(shape, F32)] * kept,
+        [plane, mass],
+        out_specs=[VMEM] * 3 + [HBM] * kept,
+        scratch=[leaving(shape)] * kept,
+        flops=500_000_000,
+    )
+
+
+def finish(pieces, totals_in, shape):
+    return call(
+        functools.partial(finish_kernel, middles=len(pieces) - 2),
+        [(shape, F32)],
+        [*pieces, *totals_in],
+        out_specs=[HBM],
+        scratch=[pltpu.VMEM(shape, F32), leaving(shape)],
         flops=500_000_000,
     )
 
@@ -578,19 +619,17 @@
         flops=500_000_000,
     )
     pieces = smooth(mass, mass_halo, None, None, pilot_tables, ((0,),), (rows,))
-    adapted, *sends, first_stat = finish(pieces, [mass], False, True, True, shape)
+    plane, stat = tally(pieces, [], mass)
+    first_total = total_over(stat)
+    adapted, *sends = adapt(plane, mass, False)
     halo = exchange(*sends, "row")
-    first_total = total_over(first_stat)
     pieces = smooth(adapted, halo, labels, label_halo, tables, groups, cuts)
-    density_first, adapted, *sends, second_stat = finish(
-        pieces, [first_total, first_total, mass], True, True, False, shape
-    )
+    plane, stat = tally(pieces, [first_total, first_total], mass)
+    second_total = total_over(stat)
+    adapted, *sends, density_first = adapt(plane, mass, True)
     halo = exchange(*sends, "row")
-    second_total = total_over(second_stat)
     pieces = smooth(adapted, halo, labels, label_halo, tables, groups, cuts)
-    (density_second,) = finish(
-        pieces, [second_total, first_total], True, False, False, shape
-    )
+    (density_second,) = finish(pieces, [second_total, first_total], shape)
     return density_first, density_second
 
 

time: 93.6 us -> 95.5 us (1.020)
  waiting for transfers between devices: 21.8 us -> 26.2 us
  starting transfers between devices: 40.9 us -> 38 us
    ppermute x14, waiting for transfers between devices: 16.4 us -> 20.8 us  [total_over(): stat = stat + lax.ppermute(stat, ('row', 'col'), pairs)]
    ppermute x14, starting transfers between devices: 29.7 us -> 26.4 us  [total_over(): stat = stat + lax.ppermute(stat, ('row', 'col'), pairs)]
    pallas_call x18 -> x20, Pallas kernels: 29.6 us -> 30 us  [call(): pl.pallas_call(kernel, out_shape=[jax.ShapeDtypeStruct(s, d) for s, d in...]
  transfers between devices with their start and end apart: 28 -> 28, of which waited for: 12 -> 14; matrix products, arithmetic and copies ran while one was open for 0% -> 0% of each run, Pallas kernels for 20% -> 21%
where the time goes in v8:
time: 95.5 us; the launch traced here: 95.4 us
  starting transfers between devices  38 us (40%)
  Pallas kernels  30 us (31%)
  waiting for transfers between devices  26.2 us (27%)
  between operations  1.11 us (1%)
    pallas_call x20, Pallas kernels, call(): pl.pallas_call(kernel, out_shape=[jax.ShapeDtypeStruct(s, d) for s, d in...  30 us
    ppermute x14, starting transfers between devices, total_over(): stat = stat + lax.ppermute(stat, ('row', 'col'), pairs)  26.4 us
    ppermute x14, waiting for transfers between devices, total_over(): stat = stat + lax.ppermute(stat, ('row', 'col'), pairs)  20.8 us
    ppermute x14, starting transfers between devices, exchange(): results.append(lax.ppermute(value, ('row', 'col'), pairs))  11.6 us
    ppermute x14, waiting for transfers between devices, exchange(): results.append(lax.ppermute(value, ('row', 'col'), pairs))  5.37 us
  transfers between devices with their start and end apart: 28, of which 14 were waited for; matrix products, arithmetic and copies ran while one was open for 0% of the time, Pallas kernels for 21%

profile of v8, /device:TPU:1, one launch (start us, length us, event | category | flops | bytes accessed | tf_op | source)
XLA Modules:
  0.0 95.4 jit_solution(8811396825300861084)
XLA Ops:
  0.6 2.4 %shard_map.59 = (bf16[384,256]{1,0:T(8,128)(2,1)S(1)}, bf16[384,256]{1,0:T(8,128)(2,1)S(1)}, bf16[1,128,384]{2,1,0:T(8,128)(2,1)S(1)}, f32[512,1024]{1,0:T(8,128...) custom-call(s32[512,1024]{1,0:T(8,128)} %refs_0_.2, ...), custom_call_target="tpu_custom_call" | custom-call | flops 500000000 | bytes 4194304 | tf_op jit(solution)/shard_map/pallas_call | solution.py:27
  3.1 2.2 %collective-permute-start = (f32[32,1024]{1,0:T(8,128)S(1)}, f32[32,1024]{1,0:T(8,128)S(1)}, u32[]{:S(2)}, u32[]{:S(2)}) collective-permute-start(f32[32,1024]{1,0:T(8,128)S(1)} %get-tuple-element.63), channel_id=1, source_target_pairs={{0,8},{1,9},{2,10},{3,11},{4,12},{5,13},{6,14},{7,15},{8,0},{9,1},... | collective-permute-start | bytes 393224 | tf_op jit(solution)/shard_map/ppermute | solution.py:468
  13.3 1.9 %collective-permute-done.3.refs_2_ = f32[256,128]{1,0:T(8,128)S(1)} collective-permute-done((f32[256,128]{1,0:T(8,128)S(1)}, f32[256,128]{1,0:T(8,128)S(1)}, u32[]{:S(2)}, u32[]{:S(2)}) %collective-permute-start.3) | collective-permute-done | bytes 131104 | tf_op jit(solution)/shard_map/ppermute | solution.py:468
  15.9 3.6 %collective-permute-start.10 = (f32[8,128]{1,0:T(8,128)S(1)}, f32[8,128]{1,0:T(8,128)S(1)}, u32[]{:S(2)}, u32[]{:S(2)}) collective-permute-start(f32[8,128]{1,0:T(8,128)S(1)} %get-tuple-element.95), channel_id=1, source_target_pairs={{0,7},{1,6},{2,5},{3,4},{4,3},{5,2},{6,1},{7,0},{8,15},{9,14},{10,... | collective-permute-start | bytes 12296 | tf_op jit(solution)/shard_map/ppermute | solution.py:491
  21.0 3.1 %collective-permute-done.11 = f32[8,128]{1,0:T(8,128)S(1)} collective-permute-done((f32[8,128]{1,0:T(8,128)S(1)}, f32[8,128]{1,0:T(8,128)S(1)}, u32[]{:S(2)}, u32[]{:S(2)}) %collective-permute-start.11) | collective-permute-done | bytes 4128 | tf_op jit(solution)/shard_map/ppermute | solution.py:491
  24.0 5.8 %collective-permute-start.12 = (f32[8,128]{1,0:T(8,128)S(1)}, f32[8,128]{1,0:T(8,128)S(1)}, u32[]{:S(2)}, u32[]{:S(2)}) collective-permute-start(f32[8,128]{1,0:T(8,128)S(1)} %add.43), channel_id=1, source_target_pairs={{0,97},{1,96},{2,99},{3,98},{4,101},{5,100},{6,103},{7,102},{8,105... | collective-permute-start | bytes 12296 | tf_op jit(solution)/shard_map/ppermute | solution.py:491
  32.6 2.2 %shard_map.65 = (bf16[1536,256]{1,0:T(8,128)(2,1)S(1)}, bf16[1536,256]{1,0:T(8,128)(2,1)S(1)}, bf16[4,128,384]{2,1,0:T(8,128)(2,1)S(1)}, bf16[512,1024]{1,0:T(8,128)(2,1)S(1)}) custom-call(s32[4]{0:T(128)S(1)} %copy-done, s32[512,1024]{1,0:T(8,128)} %refs_1_.3), custom_call_target="tpu_custom_call" | custom-call | flops 500000000 | bytes 4194304 | tf_op jit(solution)/shard_map/pallas_call | solution.py:27
  34.8 3.7 %collective-permute-done.13 = f32[8,128]{1,0:T(8,128)S(1)} collective-permute-done((f32[8,128]{1,0:T(8,128)S(1)}, f32[8,128]{1,0:T(8,128)S(1)}, u32[]{:S(2)}, u32[]{:S(2)}) %collective-permute-start.13) | collective-permute-done | bytes 4128 | tf_op jit(solution)/shard_map/ppermute | solution.py:491
  39.6 1.9 %collective-permute-start.15 = (f32[8,128]{1,0:T(8,128)S(1)}, f32[8,128]{1,0:T(8,128)S(1)}, u32[]{:S(2)}, u32[]{:S(2)}) collective-permute-start(f32[8,128]{1,0:T(8,128)S(1)} %add.46), channel_id=1, source_target_pairs={{0,25},{1,24},{2,27},{3,26},{4,29},{5,28},{6,31},{7,30},{8,17},{9,... | collective-permute-start | bytes 12296 | tf_op jit(solution)/shard_map/ppermute | solution.py:491
  41.5 1.9 %shard_map.67 = (bf16[2,384,1024]{2,1,0:T(8,128)(2,1)S(1)}, bf16[2,384,1024]{2,1,0:T(8,128)(2,1)S(1)}, f32[2,128,1024]{2,1,0:T(8,128)S(1)}) custom-call(f32[512,1024]{1,0:T(8,128)S(1)} %get-tuple-element.74.refs_0_, bf16[512,1024]{1,0:T(8,128)(2,1)S(1)} %get-tuple-element.75.refs_1_, bf16[1536,256]{1,0:T(8,128)(2,1)S(1)} %get-tuple-element.76.refs_2_.refs_11_.refs_6_, ...), custom_call_target="tpu_custom_call" | custom-call | flops 2000000000 | bytes 4194304 | tf_op jit(solution)/shard_map/pallas_call | solution.py:27
  43.9 3.9 %collective-permute-start.16 = (f32[8,128]{1,0:T(8,128)S(1)}, f32[8,128]{1,0:T(8,128)S(1)}, u32[]{:S(2)}, u32[]{:S(2)}) collective-permute-start(f32[8,128]{1,0:T(8,128)S(1)} %add.47), channel_id=1, source_target_pairs={{0,9},{1,8},{2,11},{3,10},{4,13},{5,12},{6,15},{7,14},{8,1},{9,0},... | collective-permute-start | bytes 12296 | tf_op jit(solution)/shard_map/ppermute | solution.py:491
  47.8 1.9 %shard_map.66 = (bf16[2,384,1024]{2,1,0:T(8,128)(2,1)S(1)}, bf16[2,384,1024]{2,1,0:T(8,128)(2,1)S(1)}, f32[2,128,1024]{2,1,0:T(8,128)S(1)}) custom-call(f32[512,1024]{1,0:T(8,128)S(1)} %get-tuple-element.74.refs_0_, bf16[512,1024]{1,0:T(8,128)(2,1)S(1)} %get-tuple-element.75.refs_1_, bf16[1536,256]{1,0:T(8,128)(2,1)S(1)} %get-tuple-element.76.refs_2_.refs_11_.refs_6_, ...), custom_call_target="tpu_custom_call" | custom-call | flops 2000000000 | bytes 4194304 | tf_op jit(solution)/shard_map/pallas_call | solution.py:27
  49.8 1.9 %shard_map.68 = (bf16[4,128,1024]{2,1,0:T(8,128)(2,1)S(1)}, bf16[4,128,1024]{2,1,0:T(8,128)(2,1)S(1)}, f32[512,256]{1,0:T(8,128)S(1)}, f32[512,128]{1,0:T(8,128)...) custom-call(f32[64,1024]{1,0:T(8,128)S(1)} %collective-permute-done.4.refs_0_, ...), custom_call_target="tpu_custom_call" | custom-call | flops 2000000000 | bytes 4194304 | tf_op jit(solution)/shard_map/pallas_call | solution.py:27
  53.1 2.0 %shard_map.69.refs_0_ = f32[320,1024]{1,0:T(8,128)S(1)} custom-call(bf16[2,384,1024]{2,1,0:T(8,128)(2,1)S(1)} %get-tuple-element.78.refs_6_.refs_0_, bf16[2,384,1024]{2,1,0:T(8,128)(2,1)S(1)} %get-tuple-element.79.refs_7_.refs_1_, bf16[2,384,1024]{2,1,0:T(8,128)(2,1)S(1)} %get-tuple-element.80.refs_8_.refs_2_, ...), custom_call_target="tpu_custom_call" | custom-call | flops 1875000064 | bytes 4194304 | tf_op jit(solution)/shard_map/pallas_call | solution.py:27
  58.4 2.7 %collective-permute-start.21 = (f32[8,128]{1,0:T(8,128)S(1)}, f32[8,128]{1,0:T(8,128)S(1)}, u32[]{:S(2)}, u32[]{:S(2)}) collective-permute-start(f32[8,128]{1,0:T(8,128)S(1)} %get-tuple-element.113), channel_id=1, source_target_pairs={{0,7},{1,6},{2,5},{3,4},{4,3},{5,2},{6,1},{7,0},{8,15},{9,14},{10,... | collective-permute-start | bytes 12296 | tf_op jit(solution)/shard_map/ppermute | solution.py:491
  62.7 3.0 %collective-permute-done.22 = f32[8,128]{1,0:T(8,128)S(1)} collective-permute-done((f32[8,128]{1,0:T(8,128)S(1)}, f32[8,128]{1,0:T(8,128)S(1)}, u32[]{:S(2)}, u32[]{:S(2)}) %collective-permute-start.22) | collective-permute-done | bytes 4128 | tf_op jit(solution)/shard_map/ppermute | solution.py:491
  66.4 3.5 %collective-permute-done.23 = f32[8,128]{1,0:T(8,128)S(1)} collective-permute-done((f32[8,128]{1,0:T(8,128)S(1)}, f32[8,128]{1,0:T(8,128)S(1)}, u32[]{:S(2)}, u32[]{:S(2)}) %collective-permute-start.23) | collective-permute-done | bytes 4128 | tf_op jit(solution)/shard_map/ppermute | solution.py:491
  70.0 3.0 %collective-permute-done.24 = f32[8,128]{1,0:T(8,128)S(1)} collective-permute-done((f32[8,128]{1,0:T(8,128)S(1)}, f32[8,128]{1,0:T(8,128)S(1)}, u32[]{:S(2)}, u32[]{:S(2)}) %collective-permute-start.24) | collective-permute-done | bytes 4128 | tf_op jit(solution)/shard_map/ppermute | solution.py:491
  76.4 2.6 %collective-permute-start.26 = (f32[8,128]{1,0:T(8,128)S(1)}, f32[8,128]{1,0:T(8,128)S(1)}, u32[]{:S(2)}, u32[]{:S(2)}) collective-permute-start(f32[8,128]{1,0:T(8,128)S(1)} %add.53), channel_id=1, source_target_pairs={{0,25},{1,24},{2,27},{3,26},{4,29},{5,28},{6,31},{7,30},{8,17},{9,... | collective-permute-start | bytes 12296 | tf_op jit(solution)/shard_map/ppermute | solution.py:491
  78.9 1.9 %shard_map.74 = (bf16[2,384,1024]{2,1,0:T(8,128)(2,1)S(1)}, bf16[2,384,1024]{2,1,0:T(8,128)(2,1)S(1)}, f32[2,128,1024]{2,1,0:T(8,128)S(1)}) custom-call(f32[512,1024]{1,0:T(8,128)S(1)} %get-tuple-element.98.refs_0_, bf16[512,1024]{1,0:T(8,128)(2,1)S(1)} %get-tuple-element.75.refs_1_, bf16[1536,256]{1,0:T(8,128)(2,1)S(1)} %get-tuple-element.76.refs_2_.refs_11_.refs_6_, ...), custom_call_target="tpu_custom_call" | custom-call | flops 2000000000 | bytes 4194304 | tf_op jit(solution)/shard_map/pallas_call | solution.py:27
  80.9 3.3 %collective-permute-start.27 = (f32[8,128]{1,0:T(8,128)S(1)}, f32[8,128]{1,0:T(8,128)S(1)}, u32[]{:S(2)}, u32[]{:S(2)}) collective-permute-start(f32[8,128]{1,0:T(8,128)S(1)} %add.54), channel_id=1, source_target_pairs={{0,9},{1,8},{2,11},{3,10},{4,13},{5,12},{6,15},{7,14},{8,1},{9,0},... | collective-permute-start | bytes 12296 | tf_op jit(solution)/shard_map/ppermute | solution.py:491
  84.2 1.9 %shard_map.73 = (bf16[2,384,1024]{2,1,0:T(8,128)(2,1)S(1)}, bf16[2,384,1024]{2,1,0:T(8,128)(2,1)S(1)}, f32[2,128,1024]{2,1,0:T(8,128)S(1)}) custom-call(f32[512,1024]{1,0:T(8,128)S(1)} %get-tuple-element.98.refs_0_, bf16[512,1024]{1,0:T(8,128)(2,1)S(1)} %get-tuple-element.75.refs_1_, bf16[1536,256]{1,0:T(8,128)(2,1)S(1)} %get-tuple-element.76.refs_2_.refs_11_.refs_6_, ...), custom_call_target="tpu_custom_call" | custom-call | flops 2000000000 | bytes 4194304 | tf_op jit(solution)/shard_map/pallas_call | solution.py:27
  86.2 1.9 %shard_map.75 = (bf16[4,128,1024]{2,1,0:T(8,128)(2,1)S(1)}, bf16[4,128,1024]{2,1,0:T(8,128)(2,1)S(1)}, f32[512,256]{1,0:T(8,128)S(1)}, f32[512,128]{1,0:T(8,128)...) custom-call(f32[64,1024]{1,0:T(8,128)S(1)} %collective-permute-done.17.refs_0_, ...), custom_call_target="tpu_custom_call" | custom-call | flops 2000000000 | bytes 4194304 | tf_op jit(solution)/shard_map/pallas_call | solution.py:27
  89.0 2.0 %shard_map.76.refs_0_ = f32[320,1024]{1,0:T(8,128)S(1)} custom-call(bf16[2,384,1024]{2,1,0:T(8,128)(2,1)S(1)} %get-tuple-element.99.refs_6_.refs_0_, bf16[2,384,1024]{2,1,0:T(8,128)(2,1)S(1)} %get-tuple-element.100.refs_7_.refs_1_, bf16[2,384,1024]{2,1,0:T(8,128)(2,1)S(1)} %get-tuple-element.101.refs_8_.refs_2_, ...), custom_call_target="tpu_custom_call" | custom-call | flops 1875000064 | bytes 4194304 | tf_op jit(solution)/shard_map/pallas_call | solution.py:27
  (68 shorter events, 30.0 us)
Async XLA Ops:
  3.1 5.1 %collective-permute-start = (f32[32,1024]{1,0:T(8,128)S(1)}, f32[32,1024]{1,0:T(8,128)S(1)}, u32[]{:S(2)}, u32[]{:S(2)}) collective-permute-start(f32[32,1024]{1,0:T(8,128)S(1)} %get-tuple-element.63), channel_id=1, source_target_pairs={{0,8},{1,9},{2,10},{3,11},{4,12},{5,13},{6,14},{7,15},{8,0},{9,1},... | collective-permute-start | bytes 393224 | tf_op jit(solution)/shard_map/ppermute | solution.py:468
  8.8 4.5 %collective-permute-start.2 = (f32[256,128]{1,0:T(8,128)S(1)}, f32[256,128]{1,0:T(8,128)S(1)}, u32[]{:S(2)}, u32[]{:S(2)}) collective-permute-start(f32[256,128]{1,0:T(8,128)S(1)} %get-tuple-element.71), channel_id=1, source_target_pairs={{0,1},{1,0},{2,3},{3,2},{4,5},{5,4},{6,7},{7,6},{8,9},{9,8},{10,11... | collective-permute-start | bytes 393224 | tf_op jit(solution)/shard_map/ppermute | solution.py:468
  10.4 4.7 %collective-permute-start.3 = (f32[256,128]{1,0:T(8,128)S(1)}, f32[256,128]{1,0:T(8,128)S(1)}, u32[]{:S(2)}, u32[]{:S(2)}) collective-permute-start(f32[256,128]{1,0:T(8,128)S(1)} %get-tuple-element.72), channel_id=1, source_target_pairs={{0,8},{1,2},{2,1},{3,4},{4,3},{5,6},{6,5},{7,15},{8,0},{9,10},{10,... | collective-permute-start | bytes 393224 | tf_op jit(solution)/shard_map/ppermute | solution.py:468
  15.9 5.0 %collective-permute-start.10 = (f32[8,128]{1,0:T(8,128)S(1)}, f32[8,128]{1,0:T(8,128)S(1)}, u32[]{:S(2)}, u32[]{:S(2)}) collective-permute-start(f32[8,128]{1,0:T(8,128)S(1)} %get-tuple-element.95), channel_id=1, source_target_pairs={{0,7},{1,6},{2,5},{3,4},{4,3},{5,2},{6,1},{7,0},{8,15},{9,14},{10,... | collective-permute-start | bytes 12296 | tf_op jit(solution)/shard_map/ppermute | solution.py:491
  21.0 3.1 %collective-permute-start.11 = (f32[8,128]{1,0:T(8,128)S(1)}, f32[8,128]{1,0:T(8,128)S(1)}, u32[]{:S(2)}, u32[]{:S(2)}) collective-permute-start(f32[8,128]{1,0:T(8,128)S(1)} %add.42), channel_id=1, source_target_pairs={{0,3},{1,2},{2,1},{3,0},{4,7},{5,6},{6,5},{7,4},{8,11},{9,10},{10,... | collective-permute-start | bytes 12296 | tf_op jit(solution)/shard_map/ppermute | solution.py:491
  24.0 7.1 %collective-permute-start.12 = (f32[8,128]{1,0:T(8,128)S(1)}, f32[8,128]{1,0:T(8,128)S(1)}, u32[]{:S(2)}, u32[]{:S(2)}) collective-permute-start(f32[8,128]{1,0:T(8,128)S(1)} %add.43), channel_id=1, source_target_pairs={{0,97},{1,96},{2,99},{3,98},{4,101},{5,100},{6,103},{7,102},{8,105... | collective-permute-start | bytes 12296 | tf_op jit(solution)/shard_map/ppermute | solution.py:491
  29.8 20.0 %collective-permute-start.6 = (s32[64,1024]{1,0:T(8,128)S(1)}, s32[64,1024]{1,0:T(8,128)S(1)}, u32[]{:S(2)}, u32[]{:S(2)}) collective-permute-start(s32[64,1024]{1,0:T(8,128)S(1)} %get-tuple-element.84), channel_id=1, source_target_pairs={{0,8},{1,9},{2,10},{3,11},{4,12},{5,13},{6,14},{7,15},{8,0},{9,1},... | collective-permute-start | bytes 786440 | tf_op jit(solution)/shard_map/ppermute | solution.py:468
  29.8 20.0 %collective-permute-start.7 = (s32[64,1024]{1,0:T(8,128)S(1)}, s32[64,1024]{1,0:T(8,128)S(1)}, u32[]{:S(2)}, u32[]{:S(2)}) collective-permute-start(s32[64,1024]{1,0:T(8,128)S(1)} %get-tuple-element.85), channel_id=1, source_target_pairs={{0,1},{1,0},{2,3},{3,2},{4,5},{5,4},{6,7},{7,6},{8,16},{9,17},{10,... | collective-permute-start | bytes 786440 | tf_op jit(solution)/shard_map/ppermute | solution.py:468
  31.1 7.3 %collective-permute-start.13 = (f32[8,128]{1,0:T(8,128)S(1)}, f32[8,128]{1,0:T(8,128)S(1)}, u32[]{:S(2)}, u32[]{:S(2)}) collective-permute-start(f32[8,128]{1,0:T(8,128)S(1)} %add.44), channel_id=1, source_target_pairs={{0,33},{1,32},{2,35},{3,34},{4,37},{5,36},{6,39},{7,38},{8,41},{9,... | collective-permute-start | bytes 12296 | tf_op jit(solution)/shard_map/ppermute | solution.py:491
  38.8 11.0 %collective-permute-start.4 = (f32[64,1024]{1,0:T(8,128)S(1)}, f32[64,1024]{1,0:T(8,128)S(1)}, u32[]{:S(2)}, u32[]{:S(2)}) collective-permute-start(f32[64,1024]{1,0:T(8,128)S(1)} %get-tuple-element.82), channel_id=1, source_target_pairs={{0,8},{1,9},{2,10},{3,11},{4,12},{5,13},{6,14},{7,15},{8,0},{9,1},... | collective-permute-start | bytes 786440 | tf_op jit(solution)/shard_map/ppermute | solution.py:468
  38.9 10.9 %collective-permute-start.5 = (f32[64,1024]{1,0:T(8,128)S(1)}, f32[64,1024]{1,0:T(8,128)S(1)}, u32[]{:S(2)}, u32[]{:S(2)}) collective-permute-start(f32[64,1024]{1,0:T(8,128)S(1)} %get-tuple-element.83), channel_id=1, source_target_pairs={{0,1},{1,0},{2,3},{3,2},{4,5},{5,4},{6,7},{7,6},{8,16},{9,17},{10,... | collective-permute-start | bytes 786440 | tf_op jit(solution)/shard_map/ppermute | solution.py:468
  39.6 4.2 %collective-permute-start.15 = (f32[8,128]{1,0:T(8,128)S(1)}, f32[8,128]{1,0:T(8,128)S(1)}, u32[]{:S(2)}, u32[]{:S(2)}) collective-permute-start(f32[8,128]{1,0:T(8,128)S(1)} %add.46), channel_id=1, source_target_pairs={{0,25},{1,24},{2,27},{3,26},{4,29},{5,28},{6,31},{7,30},{8,17},{9,... | collective-permute-start | bytes 12296 | tf_op jit(solution)/shard_map/ppermute | solution.py:491
  43.9 5.9 %collective-permute-start.16 = (f32[8,128]{1,0:T(8,128)S(1)}, f32[8,128]{1,0:T(8,128)S(1)}, u32[]{:S(2)}, u32[]{:S(2)}) collective-permute-start(f32[8,128]{1,0:T(8,128)S(1)} %add.47), channel_id=1, source_target_pairs={{0,9},{1,8},{2,11},{3,10},{4,13},{5,12},{6,15},{7,14},{8,1},{9,0},... | collective-permute-start | bytes 12296 | tf_op jit(solution)/shard_map/ppermute | solution.py:491
  51.7 4.8 %collective-permute-start.8 = (f32[256,128]{1,0:T(8,128)S(1)}, f32[256,128]{1,0:T(8,128)S(1)}, u32[]{:S(2)}, u32[]{:S(2)}) collective-permute-start(f32[256,128]{1,0:T(8,128)S(1)} %get-tuple-element.93), channel_id=1, source_target_pairs={{0,1},{1,0},{2,3},{3,2},{4,5},{5,4},{6,7},{7,6},{8,9},{9,8},{10,11... | collective-permute-start | bytes 393224 | tf_op jit(solution)/shard_map/ppermute | solution.py:468
  53.1 4.7 %collective-permute-start.9 = (f32[256,128]{1,0:T(8,128)S(1)}, f32[256,128]{1,0:T(8,128)S(1)}, u32[]{:S(2)}, u32[]{:S(2)}) collective-permute-start(f32[256,128]{1,0:T(8,128)S(1)} %get-tuple-element.94), channel_id=1, source_target_pairs={{0,8},{1,2},{2,1},{3,4},{4,3},{5,6},{6,5},{7,15},{8,0},{9,10},{10,... | collective-permute-start | bytes 393224 | tf_op jit(solution)/shard_map/ppermute | solution.py:468
  58.4 4.3 %collective-permute-start.21 = (f32[8,128]{1,0:T(8,128)S(1)}, f32[8,128]{1,0:T(8,128)S(1)}, u32[]{:S(2)}, u32[]{:S(2)}) collective-permute-start(f32[8,128]{1,0:T(8,128)S(1)} %get-tuple-element.113), channel_id=1, source_target_pairs={{0,7},{1,6},{2,5},{3,4},{4,3},{5,2},{6,1},{7,0},{8,15},{9,14},{10,... | collective-permute-start | bytes 12296 | tf_op jit(solution)/shard_map/ppermute | solution.py:491
  65.7 4.2 %collective-permute-start.23 = (f32[8,128]{1,0:T(8,128)S(1)}, f32[8,128]{1,0:T(8,128)S(1)}, u32[]{:S(2)}, u32[]{:S(2)}) collective-permute-start(f32[8,128]{1,0:T(8,128)S(1)} %add.50), channel_id=1, source_target_pairs={{0,97},{1,96},{2,99},{3,98},{4,101},{5,100},{6,103},{7,102},{8,105... | collective-permute-start | bytes 12296 | tf_op jit(solution)/shard_map/ppermute | solution.py:491
  73.0 3.4 %collective-permute-start.25 = (f32[8,128]{1,0:T(8,128)S(1)}, f32[8,128]{1,0:T(8,128)S(1)}, u32[]{:S(2)}, u32[]{:S(2)}) collective-permute-start(f32[8,128]{1,0:T(8,128)S(1)} %add.52), channel_id=1, source_target_pairs={{0,1},{1,0},{2,3},{3,2},{4,5},{5,4},{6,7},{7,6},{8,9},{9,8},{10,11... | collective-permute-start | bytes 12296 | tf_op jit(solution)/shard_map/ppermute | solution.py:491
  74.8 11.4 %collective-permute-start.17 = (f32[64,1024]{1,0:T(8,128)S(1)}, f32[64,1024]{1,0:T(8,128)S(1)}, u32[]{:S(2)}, u32[]{:S(2)}) collective-permute-start(f32[64,1024]{1,0:T(8,128)S(1)} %get-tuple-element.103), channel_id=1, source_target_pairs={{0,8},{1,9},{2,10},{3,11},{4,12},{5,13},{6,14},{7,15},{8,0},{9,1},... | collective-permute-start | bytes 786440 | tf_op jit(solution)/shard_map/ppermute | solution.py:468
  76.0 10.2 %collective-permute-start.18 = (f32[64,1024]{1,0:T(8,128)S(1)}, f32[64,1024]{1,0:T(8,128)S(1)}, u32[]{:S(2)}, u32[]{:S(2)}) collective-permute-start(f32[64,1024]{1,0:T(8,128)S(1)} %get-tuple-element.104), channel_id=1, source_target_pairs={{0,1},{1,0},{2,3},{3,2},{4,5},{5,4},{6,7},{7,6},{8,16},{9,17},{10,... | collective-permute-start | bytes 786440 | tf_op jit(solution)/shard_map/ppermute | solution.py:468
  76.4 4.5 %collective-permute-start.26 = (f32[8,128]{1,0:T(8,128)S(1)}, f32[8,128]{1,0:T(8,128)S(1)}, u32[]{:S(2)}, u32[]{:S(2)}) collective-permute-start(f32[8,128]{1,0:T(8,128)S(1)} %add.53), channel_id=1, source_target_pairs={{0,25},{1,24},{2,27},{3,26},{4,29},{5,28},{6,31},{7,30},{8,17},{9,... | collective-permute-start | bytes 12296 | tf_op jit(solution)/shard_map/ppermute | solution.py:491
  80.9 5.2 %collective-permute-start.27 = (f32[8,128]{1,0:T(8,128)S(1)}, f32[8,128]{1,0:T(8,128)S(1)}, u32[]{:S(2)}, u32[]{:S(2)}) collective-permute-start(f32[8,128]{1,0:T(8,128)S(1)} %add.54), channel_id=1, source_target_pairs={{0,9},{1,8},{2,11},{3,10},{4,13},{5,12},{6,15},{7,14},{8,1},{9,0},... | collective-permute-start | bytes 12296 | tf_op jit(solution)/shard_map/ppermute | solution.py:491
  88.0 4.4 %collective-permute-start.19 = (f32[256,128]{1,0:T(8,128)S(1)}, f32[256,128]{1,0:T(8,128)S(1)}, u32[]{:S(2)}, u32[]{:S(2)}) collective-permute-start(f32[256,128]{1,0:T(8,128)S(1)} %get-tuple-element.111), channel_id=1, source_target_pairs={{0,1},{1,0},{2,3},{3,2},{4,5},{5,4},{6,7},{7,6},{8,9},{9,8},{10,11... | collective-permute-start | bytes 393224 | tf_op jit(solution)/shard_map/ppermute | solution.py:468
  89.0 4.7 %collective-permute-start.20 = (f32[256,128]{1,0:T(8,128)S(1)}, f32[256,128]{1,0:T(8,128)S(1)}, u32[]{:S(2)}, u32[]{:S(2)}) collective-permute-start(f32[256,128]{1,0:T(8,128)S(1)} %get-tuple-element.112), channel_id=1, source_target_pairs={{0,8},{1,2},{2,1},{3,4},{4,3},{5,6},{6,5},{7,15},{8,0},{9,10},{10,... | collective-permute-start | bytes 393224 | tf_op jit(solution)/shard_map/ppermute | solution.py:468
  (5 other events, 29.4 us)

commit v9 on v8

--- a/solution.py
+++ b/solution.py
@@ -315,11 +315,21 @@
     send_b[...] = chosen(odd_column, right, left)
 
 
-def middle_kernel(*refs, groups, start):
+def middle_kernel(*refs, groups, start, kept):
     count = len(groups)
-    highs, lows, (edge_high, edge_low), band_refs, (left_ref, right_ref), (out_ref,) = take(
+    highs, lows, (edge_high, edge_low), band_refs, (left_ref, right_ref), refs = take(
         refs, count, count, 2, 2, 2
     )
+    plane, (out_ref,), plane_out, done = take(refs, kept, 1, kept)
+    copies = []
+    for source, target, arrived in zip(plane, plane_out, done):
+        for number, first in enumerate(range(0, source.shape[0], STEP)):
+            part = slice(first, first + STEP)
+            copies.append(
+                pltpu.make_async_copy(source.at[part], target.at[part], arrived.at[number])
+            )
+    for copy in copies:
+        copy.start()
     bands = [c for group in groups for c in group]
     inner = highs[0].shape[1]
     rows, columns = out_ref.shape
@@ -350,6 +360,8 @@
         if before is not None:
             out_ref[:, (k - 1) * 128 : k * 128] = jnp.where(lower, before, turned)
         before = turned
+    for copy in copies:
+        copy.wait()
 
 
 def gathered(middles, come, flags, start):
@@ -492,7 +504,7 @@
     return stat
 
 
-def smooth(field, halo, labels, label_halo, tables, groups, cuts):
+def smooth(field, halo, labels, label_halo, tables, groups, cuts, plane=None):
     high, low, rim = tables
     rows, columns = field.shape
     labelled = labels is not None
@@ -521,15 +533,20 @@
     come = exchange(send_a, send_b, "col")
     middles = []
     start = 0
-    for count in cuts:
-        middles += call(
-            functools.partial(middle_kernel, groups=groups, start=start),
-            [((count, columns), F32)],
-            [*highs, *lows, edge_high, edge_low, high, low, left, right],
+    for number, count in enumerate(cuts):
+        kept = int(plane is not None and number == len(cuts) - 1)
+        middle, *gone = call(
+            functools.partial(middle_kernel, groups=groups, start=start, kept=kept),
+            [((count, columns), F32)] + [(field.shape, F32)] * kept,
+            [*highs, *lows, edge_high, edge_low, high, low, left, right] + [plane] * kept,
+            out_specs=[VMEM] + [HBM] * kept,
+            scratch=[leaving(field.shape)] * kept,
             flops=len(bands) * 750_000_000 * count // rows,
         )
+        middles.append(middle)
         start += count
-    return [*middles, *come]
+    pieces = [*middles, *come]
+    return pieces if plane is None else (pieces, *gone)
 
 
 def leaving(shape):
@@ -626,9 +643,9 @@
     pieces = smooth(adapted, halo, labels, label_halo, tables, groups, cuts)
     plane, stat = tally(pieces, [first_total, first_total], mass)
     second_total = total_over(stat)
-    adapted, *sends, density_first = adapt(plane, mass, True)
+    adapted, *sends = adapt(plane, mass, False)
     halo = exchange(*sends, "row")
-    pieces = smooth(adapted, halo, labels, label_halo, tables, groups, cuts)
+    pieces, density_first = smooth(adapted, halo, labels, label_halo, tables, groups, cuts, plane)
     (density_second,) = finish(pieces, [second_total, first_total], shape)
     return density_first, density_second
 

time: 95.5 us -> 94.5 us (0.990)
  waiting for transfers between devices: 26.2 us -> 25 us
    ppermute x14, waiting for transfers between devices: 5.37 us -> 4.2 us  [exchange(): results.append(lax.ppermute(value, ('row', 'col'), pairs))]
  transfers between devices with their start and end apart: 28 -> 28, of which waited for: 14 -> 14; matrix products, arithmetic and copies ran while one was open for 0% -> 0% of each run, Pallas kernels for 21% -> 22%
where the time goes in v9:
time: 94.5 us; the launch traced here: 94.3 us
  starting transfers between devices  38 us (40%)
  Pallas kernels  30.1 us (32%)
  waiting for transfers between devices  25 us (26%)
  between operations  1.11 us (1%)
    pallas_call x20, Pallas kernels, call(): pl.pallas_call(kernel, out_shape=[jax.ShapeDtypeStruct(s, d) for s, d in...  30.1 us
    ppermute x14, starting transfers between devices, total_over(): stat = stat + lax.ppermute(stat, ('row', 'col'), pairs)  26.4 us
    ppermute x14, waiting for transfers between devices, total_over(): stat = stat + lax.ppermute(stat, ('row', 'col'), pairs)  20.8 us
    ppermute x14, starting transfers between devices, exchange(): results.append(lax.ppermute(value, ('row', 'col'), pairs))  11.6 us
    ppermute x14, waiting for transfers between devices, exchange(): results.append(lax.ppermute(value, ('row', 'col'), pairs))  4.2 us
  transfers between devices with their start and end apart: 28, of which 14 were waited for; matrix products, arithmetic and copies ran while one was open for 0% of the time, Pallas kernels for 22%

profile of v9, /device:TPU:1, one launch (start us, length us, event | category | flops | bytes accessed | tf_op | source)
XLA Modules:
  0.0 94.3 jit_solution(4510257012580977470)
XLA Ops:
  0.6 2.4 %shard_map.59 = (bf16[384,256]{1,0:T(8,128)(2,1)S(1)}, bf16[384,256]{1,0:T(8,128)(2,1)S(1)}, bf16[1,128,384]{2,1,0:T(8,128)(2,1)S(1)}, f32[512,1024]{1,0:T(8,128...) custom-call(s32[512,1024]{1,0:T(8,128)} %refs_0_.2, ...), custom_call_target="tpu_custom_call" | custom-call | flops 500000000 | bytes 4194304 | tf_op jit(solution)/shard_map/pallas_call | solution.py:27
  3.1 2.2 %collective-permute-start = (f32[32,1024]{1,0:T(8,128)S(1)}, f32[32,1024]{1,0:T(8,128)S(1)}, u32[]{:S(2)}, u32[]{:S(2)}) collective-permute-start(f32[32,1024]{1,0:T(8,128)S(1)} %get-tuple-element.64), channel_id=1, source_target_pairs={{0,8},{1,9},{2,10},{3,11},{4,12},{5,13},{6,14},{7,15},{8,0},{9,1},... | collective-permute-start | bytes 393224 | tf_op jit(solution)/shard_map/ppermute | solution.py:480
  15.9 3.6 %collective-permute-start.10 = (f32[8,128]{1,0:T(8,128)S(1)}, f32[8,128]{1,0:T(8,128)S(1)}, u32[]{:S(2)}, u32[]{:S(2)}) collective-permute-start(f32[8,128]{1,0:T(8,128)S(1)} %get-tuple-element.96), channel_id=1, source_target_pairs={{0,7},{1,6},{2,5},{3,4},{4,3},{5,2},{6,1},{7,0},{8,15},{9,14},{10,... | collective-permute-start | bytes 12296 | tf_op jit(solution)/shard_map/ppermute | solution.py:503
  21.0 3.1 %collective-permute-done.11 = f32[8,128]{1,0:T(8,128)S(1)} collective-permute-done((f32[8,128]{1,0:T(8,128)S(1)}, f32[8,128]{1,0:T(8,128)S(1)}, u32[]{:S(2)}, u32[]{:S(2)}) %collective-permute-start.11) | collective-permute-done | bytes 4128 | tf_op jit(solution)/shard_map/ppermute | solution.py:503
  24.0 5.8 %collective-permute-start.12 = (f32[8,128]{1,0:T(8,128)S(1)}, f32[8,128]{1,0:T(8,128)S(1)}, u32[]{:S(2)}, u32[]{:S(2)}) collective-permute-start(f32[8,128]{1,0:T(8,128)S(1)} %add.43), channel_id=1, source_target_pairs={{0,97},{1,96},{2,99},{3,98},{4,101},{5,100},{6,103},{7,102},{8,105... | collective-permute-start | bytes 12296 | tf_op jit(solution)/shard_map/ppermute | solution.py:503
  32.6 2.2 %shard_map.65 = (bf16[1536,256]{1,0:T(8,128)(2,1)S(1)}, bf16[1536,256]{1,0:T(8,128)(2,1)S(1)}, bf16[4,128,384]{2,1,0:T(8,128)(2,1)S(1)}, bf16[512,1024]{1,0:T(8,128)(2,1)S(1)}) custom-call(s32[4]{0:T(128)S(1)} %copy-done, s32[512,1024]{1,0:T(8,128)} %refs_1_.3), custom_call_target="tpu_custom_call" | custom-call | flops 500000000 | bytes 4194304 | tf_op jit(solution)/shard_map/pallas_call | solution.py:27
  34.8 3.7 %collective-permute-done.13 = f32[8,128]{1,0:T(8,128)S(1)} collective-permute-done((f32[8,128]{1,0:T(8,128)S(1)}, f32[8,128]{1,0:T(8,128)S(1)}, u32[]{:S(2)}, u32[]{:S(2)}) %collective-permute-start.13) | collective-permute-done | bytes 4128 | tf_op jit(solution)/shard_map/ppermute | solution.py:503
  39.6 1.9 %collective-permute-start.15 = (f32[8,128]{1,0:T(8,128)S(1)}, f32[8,128]{1,0:T(8,128)S(1)}, u32[]{:S(2)}, u32[]{:S(2)}) collective-permute-start(f32[8,128]{1,0:T(8,128)S(1)} %add.46), channel_id=1, source_target_pairs={{0,25},{1,24},{2,27},{3,26},{4,29},{5,28},{6,31},{7,30},{8,17},{9,... | collective-permute-start | bytes 12296 | tf_op jit(solution)/shard_map/ppermute | solution.py:503
  41.5 1.9 %shard_map.67 = (bf16[2,384,1024]{2,1,0:T(8,128)(2,1)S(1)}, bf16[2,384,1024]{2,1,0:T(8,128)(2,1)S(1)}, f32[2,128,1024]{2,1,0:T(8,128)S(1)}) custom-call(f32[512,1024]{1,0:T(8,128)S(1)} %get-tuple-element.75.refs_0_, bf16[512,1024]{1,0:T(8,128)(2,1)S(1)} %get-tuple-element.76.refs_1_, bf16[1536,256]{1,0:T(8,128)(2,1)S(1)} %get-tuple-element.77.refs_2_.refs_11_.refs_6_, ...), custom_call_target="tpu_custom_call" | custom-call | flops 2000000000 | bytes 4194304 | tf_op jit(solution)/shard_map/pallas_call | solution.py:27
  43.9 3.9 %collective-permute-start.16 = (f32[8,128]{1,0:T(8,128)S(1)}, f32[8,128]{1,0:T(8,128)S(1)}, u32[]{:S(2)}, u32[]{:S(2)}) collective-permute-start(f32[8,128]{1,0:T(8,128)S(1)} %add.47), channel_id=1, source_target_pairs={{0,9},{1,8},{2,11},{3,10},{4,13},{5,12},{6,15},{7,14},{8,1},{9,0},... | collective-permute-start | bytes 12296 | tf_op jit(solution)/shard_map/ppermute | solution.py:503
  47.8 1.9 %shard_map.66 = (bf16[2,384,1024]{2,1,0:T(8,128)(2,1)S(1)}, bf16[2,384,1024]{2,1,0:T(8,128)(2,1)S(1)}, f32[2,128,1024]{2,1,0:T(8,128)S(1)}) custom-call(f32[512,1024]{1,0:T(8,128)S(1)} %get-tuple-element.75.refs_0_, bf16[512,1024]{1,0:T(8,128)(2,1)S(1)} %get-tuple-element.76.refs_1_, bf16[1536,256]{1,0:T(8,128)(2,1)S(1)} %get-tuple-element.77.refs_2_.refs_11_.refs_6_, ...), custom_call_target="tpu_custom_call" | custom-call | flops 2000000000 | bytes 4194304 | tf_op jit(solution)/shard_map/pallas_call | solution.py:27
  49.8 1.9 %shard_map.68 = (bf16[4,128,1024]{2,1,0:T(8,128)(2,1)S(1)}, bf16[4,128,1024]{2,1,0:T(8,128)(2,1)S(1)}, f32[512,256]{1,0:T(8,128)S(1)}, f32[512,128]{1,0:T(8,128)...) custom-call(f32[64,1024]{1,0:T(8,128)S(1)} %collective-permute-done.4.refs_0_, ...), custom_call_target="tpu_custom_call" | custom-call | flops 2000000000 | bytes 4194304 | tf_op jit(solution)/shard_map/pallas_call | solution.py:27
  53.1 2.0 %shard_map.69.refs_0_ = f32[320,1024]{1,0:T(8,128)S(1)} custom-call(bf16[2,384,1024]{2,1,0:T(8,128)(2,1)S(1)} %get-tuple-element.79.refs_6_.refs_0_, bf16[2,384,1024]{2,1,0:T(8,128)(2,1)S(1)} %get-tuple-element.80.refs_7_.refs_1_, bf16[2,384,1024]{2,1,0:T(8,128)(2,1)S(1)} %get-tuple-element.81.refs_8_.refs_2_, ...), custom_call_target="tpu_custom_call" | custom-call | flops 1875000064 | bytes 4194304 | tf_op jit(solution)/shard_map/pallas_call | solution.py:27
  58.4 2.7 %collective-permute-start.21 = (f32[8,128]{1,0:T(8,128)S(1)}, f32[8,128]{1,0:T(8,128)S(1)}, u32[]{:S(2)}, u32[]{:S(2)}) collective-permute-start(f32[8,128]{1,0:T(8,128)S(1)} %get-tuple-element.115), channel_id=1, source_target_pairs={{0,7},{1,6},{2,5},{3,4},{4,3},{5,2},{6,1},{7,0},{8,15},{9,14},{10,... | collective-permute-start | bytes 12296 | tf_op jit(solution)/shard_map/ppermute | solution.py:503
  62.7 3.0 %collective-permute-done.22 = f32[8,128]{1,0:T(8,128)S(1)} collective-permute-done((f32[8,128]{1,0:T(8,128)S(1)}, f32[8,128]{1,0:T(8,128)S(1)}, u32[]{:S(2)}, u32[]{:S(2)}) %collective-permute-start.22) | collective-permute-done | bytes 4128 | tf_op jit(solution)/shard_map/ppermute | solution.py:503
  66.4 3.5 %collective-permute-done.23 = f32[8,128]{1,0:T(8,128)S(1)} collective-permute-done((f32[8,128]{1,0:T(8,128)S(1)}, f32[8,128]{1,0:T(8,128)S(1)}, u32[]{:S(2)}, u32[]{:S(2)}) %collective-permute-start.23) | collective-permute-done | bytes 4128 | tf_op jit(solution)/shard_map/ppermute | solution.py:503
  70.0 3.0 %collective-permute-done.24 = f32[8,128]{1,0:T(8,128)S(1)} collective-permute-done((f32[8,128]{1,0:T(8,128)S(1)}, f32[8,128]{1,0:T(8,128)S(1)}, u32[]{:S(2)}, u32[]{:S(2)}) %collective-permute-start.24) | collective-permute-done | bytes 4128 | tf_op jit(solution)/shard_map/ppermute | solution.py:503
  75.3 2.6 %collective-permute-start.26 = (f32[8,128]{1,0:T(8,128)S(1)}, f32[8,128]{1,0:T(8,128)S(1)}, u32[]{:S(2)}, u32[]{:S(2)}) collective-permute-start(f32[8,128]{1,0:T(8,128)S(1)} %add.53), channel_id=1, source_target_pairs={{0,25},{1,24},{2,27},{3,26},{4,29},{5,28},{6,31},{7,30},{8,17},{9,... | collective-permute-start | bytes 12296 | tf_op jit(solution)/shard_map/ppermute | solution.py:503
  77.9 1.9 %shard_map.74 = (bf16[2,384,1024]{2,1,0:T(8,128)(2,1)S(1)}, bf16[2,384,1024]{2,1,0:T(8,128)(2,1)S(1)}, f32[2,128,1024]{2,1,0:T(8,128)S(1)}) custom-call(f32[512,1024]{1,0:T(8,128)S(1)} %get-tuple-element.98.refs_0_, bf16[512,1024]{1,0:T(8,128)(2,1)S(1)} %get-tuple-element.76.refs_1_, bf16[1536,256]{1,0:T(8,128)(2,1)S(1)} %get-tuple-element.77.refs_2_.refs_11_.refs_6_, ...), custom_call_target="tpu_custom_call" | custom-call | flops 2000000000 | bytes 4194304 | tf_op jit(solution)/shard_map/pallas_call | solution.py:27
  79.8 3.3 %collective-permute-start.27 = (f32[8,128]{1,0:T(8,128)S(1)}, f32[8,128]{1,0:T(8,128)S(1)}, u32[]{:S(2)}, u32[]{:S(2)}) collective-permute-start(f32[8,128]{1,0:T(8,128)S(1)} %add.54), channel_id=1, source_target_pairs={{0,9},{1,8},{2,11},{3,10},{4,13},{5,12},{6,15},{7,14},{8,1},{9,0},... | collective-permute-start | bytes 12296 | tf_op jit(solution)/shard_map/ppermute | solution.py:503
  83.1 1.9 %shard_map.73 = (bf16[2,384,1024]{2,1,0:T(8,128)(2,1)S(1)}, bf16[2,384,1024]{2,1,0:T(8,128)(2,1)S(1)}, f32[2,128,1024]{2,1,0:T(8,128)S(1)}) custom-call(f32[512,1024]{1,0:T(8,128)S(1)} %get-tuple-element.98.refs_0_, bf16[512,1024]{1,0:T(8,128)(2,1)S(1)} %get-tuple-element.76.refs_1_, bf16[1536,256]{1,0:T(8,128)(2,1)S(1)} %get-tuple-element.77.refs_2_.refs_11_.refs_6_, ...), custom_call_target="tpu_custom_call" | custom-call | flops 2000000000 | bytes 4194304 | tf_op jit(solution)/shard_map/pallas_call | solution.py:27
  85.1 1.9 %shard_map.75 = (bf16[4,128,1024]{2,1,0:T(8,128)(2,1)S(1)}, bf16[4,128,1024]{2,1,0:T(8,128)(2,1)S(1)}, f32[512,256]{1,0:T(8,128)S(1)}, f32[512,128]{1,0:T(8,128)...) custom-call(f32[64,1024]{1,0:T(8,128)S(1)} %collective-permute-done.17.refs_0_, ...), custom_call_target="tpu_custom_call" | custom-call | flops 2000000000 | bytes 4194304 | tf_op jit(solution)/shard_map/pallas_call | solution.py:27
  88.0 2.0 %shard_map.77.refs_0_ = f32[320,1024]{1,0:T(8,128)S(1)} custom-call(bf16[2,384,1024]{2,1,0:T(8,128)(2,1)S(1)} %get-tuple-element.99.refs_6_.refs_0_, bf16[2,384,1024]{2,1,0:T(8,128)(2,1)S(1)} %get-tuple-element.100.refs_7_.refs_1_, bf16[2,384,1024]{2,1,0:T(8,128)(2,1)S(1)} %get-tuple-element.101.refs_8_.refs_2_, ...), custom_call_target="tpu_custom_call" | custom-call | flops 1875000064 | bytes 4194304 | tf_op jit(solution)/shard_map/pallas_call | solution.py:27
  90.0 2.5 %shard_map.76 = (f32[192,1024]{1,0:T(8,128)S(1)}, f32[512,1024]{1,0:T(8,128)}) custom-call(bf16[2,384,1024]{2,1,0:T(8,128)(2,1)S(1)} %get-tuple-element.99.refs_6_.refs_0_, bf16[2,384,1024]{2,1,0:T(8,128)(2,1)S(1)} %get-tuple-element.100.refs_7_.refs_1_, bf16[2,384,1024]{2,1,0:T(8,128)(2,1)S(1)} %get-tuple-element.101.refs_8_.refs_2_, ...), custom_call_target="tpu_custom_call" | custom-call | flops 1124999936 | bytes 4194304 | tf_op jit(solution)/shard_map/pallas_call | solution.py:27
  (68 shorter events, 28.2 us)
Async XLA Ops:
  3.1 5.1 %collective-permute-start = (f32[32,1024]{1,0:T(8,128)S(1)}, f32[32,1024]{1,0:T(8,128)S(1)}, u32[]{:S(2)}, u32[]{:S(2)}) collective-permute-start(f32[32,1024]{1,0:T(8,128)S(1)} %get-tuple-element.64), channel_id=1, source_target_pairs={{0,8},{1,9},{2,10},{3,11},{4,12},{5,13},{6,14},{7,15},{8,0},{9,1},... | collective-permute-start | bytes 393224 | tf_op jit(solution)/shard_map/ppermute | solution.py:480
  8.8 4.5 %collective-permute-start.2 = (f32[256,128]{1,0:T(8,128)S(1)}, f32[256,128]{1,0:T(8,128)S(1)}, u32[]{:S(2)}, u32[]{:S(2)}) collective-permute-start(f32[256,128]{1,0:T(8,128)S(1)} %get-tuple-element.72), channel_id=1, source_target_pairs={{0,1},{1,0},{2,3},{3,2},{4,5},{5,4},{6,7},{7,6},{8,9},{9,8},{10,11... | collective-permute-start | bytes 393224 | tf_op jit(solution)/shard_map/ppermute | solution.py:480
  10.4 4.7 %collective-permute-start.3 = (f32[256,128]{1,0:T(8,128)S(1)}, f32[256,128]{1,0:T(8,128)S(1)}, u32[]{:S(2)}, u32[]{:S(2)}) collective-permute-start(f32[256,128]{1,0:T(8,128)S(1)} %get-tuple-element.73), channel_id=1, source_target_pairs={{0,8},{1,2},{2,1},{3,4},{4,3},{5,6},{6,5},{7,15},{8,0},{9,10},{10,... | collective-permute-start | bytes 393224 | tf_op jit(solution)/shard_map/ppermute | solution.py:480
  15.9 5.0 %collective-permute-start.10 = (f32[8,128]{1,0:T(8,128)S(1)}, f32[8,128]{1,0:T(8,128)S(1)}, u32[]{:S(2)}, u32[]{:S(2)}) collective-permute-start(f32[8,128]{1,0:T(8,128)S(1)} %get-tuple-element.96), channel_id=1, source_target_pairs={{0,7},{1,6},{2,5},{3,4},{4,3},{5,2},{6,1},{7,0},{8,15},{9,14},{10,... | collective-permute-start | bytes 12296 | tf_op jit(solution)/shard_map/ppermute | solution.py:503
  21.0 3.1 %collective-permute-start.11 = (f32[8,128]{1,0:T(8,128)S(1)}, f32[8,128]{1,0:T(8,128)S(1)}, u32[]{:S(2)}, u32[]{:S(2)}) collective-permute-start(f32[8,128]{1,0:T(8,128)S(1)} %add.42), channel_id=1, source_target_pairs={{0,3},{1,2},{2,1},{3,0},{4,7},{5,6},{6,5},{7,4},{8,11},{9,10},{10,... | collective-permute-start | bytes 12296 | tf_op jit(solution)/shard_map/ppermute | solution.py:503
  24.0 7.1 %collective-permute-start.12 = (f32[8,128]{1,0:T(8,128)S(1)}, f32[8,128]{1,0:T(8,128)S(1)}, u32[]{:S(2)}, u32[]{:S(2)}) collective-permute-start(f32[8,128]{1,0:T(8,128)S(1)} %add.43), channel_id=1, source_target_pairs={{0,97},{1,96},{2,99},{3,98},{4,101},{5,100},{6,103},{7,102},{8,105... | collective-permute-start | bytes 12296 | tf_op jit(solution)/shard_map/ppermute | solution.py:503
  29.8 20.0 %collective-permute-start.6 = (s32[64,1024]{1,0:T(8,128)S(1)}, s32[64,1024]{1,0:T(8,128)S(1)}, u32[]{:S(2)}, u32[]{:S(2)}) collective-permute-start(s32[64,1024]{1,0:T(8,128)S(1)} %get-tuple-element.85), channel_id=1, source_target_pairs={{0,8},{1,9},{2,10},{3,11},{4,12},{5,13},{6,14},{7,15},{8,0},{9,1},... | collective-permute-start | bytes 786440 | tf_op jit(solution)/shard_map/ppermute | solution.py:480
  29.8 20.0 %collective-permute-start.7 = (s32[64,1024]{1,0:T(8,128)S(1)}, s32[64,1024]{1,0:T(8,128)S(1)}, u32[]{:S(2)}, u32[]{:S(2)}) collective-permute-start(s32[64,1024]{1,0:T(8,128)S(1)} %get-tuple-element.86), channel_id=1, source_target_pairs={{0,1},{1,0},{2,3},{3,2},{4,5},{5,4},{6,7},{7,6},{8,16},{9,17},{10,... | collective-permute-start | bytes 786440 | tf_op jit(solution)/shard_map/ppermute | solution.py:480
  31.1 7.3 %collective-permute-start.13 = (f32[8,128]{1,0:T(8,128)S(1)}, f32[8,128]{1,0:T(8,128)S(1)}, u32[]{:S(2)}, u32[]{:S(2)}) collective-permute-start(f32[8,128]{1,0:T(8,128)S(1)} %add.44), channel_id=1, source_target_pairs={{0,33},{1,32},{2,35},{3,34},{4,37},{5,36},{6,39},{7,38},{8,41},{9,... | collective-permute-start | bytes 12296 | tf_op jit(solution)/shard_map/ppermute | solution.py:503
  38.8 11.0 %collective-permute-start.4 = (f32[64,1024]{1,0:T(8,128)S(1)}, f32[64,1024]{1,0:T(8,128)S(1)}, u32[]{:S(2)}, u32[]{:S(2)}) collective-permute-start(f32[64,1024]{1,0:T(8,128)S(1)} %get-tuple-element.83), channel_id=1, source_target_pairs={{0,8},{1,9},{2,10},{3,11},{4,12},{5,13},{6,14},{7,15},{8,0},{9,1},... | collective-permute-start | bytes 786440 | tf_op jit(solution)/shard_map/ppermute | solution.py:480
  38.9 10.9 %collective-permute-start.5 = (f32[64,1024]{1,0:T(8,128)S(1)}, f32[64,1024]{1,0:T(8,128)S(1)}, u32[]{:S(2)}, u32[]{:S(2)}) collective-permute-start(f32[64,1024]{1,0:T(8,128)S(1)} %get-tuple-element.84), channel_id=1, source_target_pairs={{0,1},{1,0},{2,3},{3,2},{4,5},{5,4},{6,7},{7,6},{8,16},{9,17},{10,... | collective-permute-start | bytes 786440 | tf_op jit(solution)/shard_map/ppermute | solution.py:480
  39.6 4.2 %collective-permute-start.15 = (f32[8,128]{1,0:T(8,128)S(1)}, f32[8,128]{1,0:T(8,128)S(1)}, u32[]{:S(2)}, u32[]{:S(2)}) collective-permute-start(f32[8,128]{1,0:T(8,128)S(1)} %add.46), channel_id=1, source_target_pairs={{0,25},{1,24},{2,27},{3,26},{4,29},{5,28},{6,31},{7,30},{8,17},{9,... | collective-permute-start | bytes 12296 | tf_op jit(solution)/shard_map/ppermute | solution.py:503
  43.9 5.9 %collective-permute-start.16 = (f32[8,128]{1,0:T(8,128)S(1)}, f32[8,128]{1,0:T(8,128)S(1)}, u32[]{:S(2)}, u32[]{:S(2)}) collective-permute-start(f32[8,128]{1,0:T(8,128)S(1)} %add.47), channel_id=1, source_target_pairs={{0,9},{1,8},{2,11},{3,10},{4,13},{5,12},{6,15},{7,14},{8,1},{9,0},... | collective-permute-start | bytes 12296 | tf_op jit(solution)/shard_map/ppermute | solution.py:503
  51.7 4.8 %collective-permute-start.8 = (f32[256,128]{1,0:T(8,128)S(1)}, f32[256,128]{1,0:T(8,128)S(1)}, u32[]{:S(2)}, u32[]{:S(2)}) collective-permute-start(f32[256,128]{1,0:T(8,128)S(1)} %get-tuple-element.94), channel_id=1, source_target_pairs={{0,1},{1,0},{2,3},{3,2},{4,5},{5,4},{6,7},{7,6},{8,9},{9,8},{10,11... | collective-permute-start | bytes 393224 | tf_op jit(solution)/shard_map/ppermute | solution.py:480
  53.1 4.7 %collective-permute-start.9 = (f32[256,128]{1,0:T(8,128)S(1)}, f32[256,128]{1,0:T(8,128)S(1)}, u32[]{:S(2)}, u32[]{:S(2)}) collective-permute-start(f32[256,128]{1,0:T(8,128)S(1)} %get-tuple-element.95), channel_id=1, source_target_pairs={{0,8},{1,2},{2,1},{3,4},{4,3},{5,6},{6,5},{7,15},{8,0},{9,10},{10,... | collective-permute-start | bytes 393224 | tf_op jit(solution)/shard_map/ppermute | solution.py:480
  58.4 4.3 %collective-permute-start.21 = (f32[8,128]{1,0:T(8,128)S(1)}, f32[8,128]{1,0:T(8,128)S(1)}, u32[]{:S(2)}, u32[]{:S(2)}) collective-permute-start(f32[8,128]{1,0:T(8,128)S(1)} %get-tuple-element.115), channel_id=1, source_target_pairs={{0,7},{1,6},{2,5},{3,4},{4,3},{5,2},{6,1},{7,0},{8,15},{9,14},{10,... | collective-permute-start | bytes 12296 | tf_op jit(solution)/shard_map/ppermute | solution.py:503
  62.7 3.0 %collective-permute-start.22 = (f32[8,128]{1,0:T(8,128)S(1)}, f32[8,128]{1,0:T(8,128)S(1)}, u32[]{:S(2)}, u32[]{:S(2)}) collective-permute-start(f32[8,128]{1,0:T(8,128)S(1)} %add.49), channel_id=1, source_target_pairs={{0,3},{1,2},{2,1},{3,0},{4,7},{5,6},{6,5},{7,4},{8,11},{9,10},{10,... | collective-permute-start | bytes 12296 | tf_op jit(solution)/shard_map/ppermute | solution.py:503
  65.7 4.2 %collective-permute-start.23 = (f32[8,128]{1,0:T(8,128)S(1)}, f32[8,128]{1,0:T(8,128)S(1)}, u32[]{:S(2)}, u32[]{:S(2)}) collective-permute-start(f32[8,128]{1,0:T(8,128)S(1)} %add.50), channel_id=1, source_target_pairs={{0,97},{1,96},{2,99},{3,98},{4,101},{5,100},{6,103},{7,102},{8,105... | collective-permute-start | bytes 12296 | tf_op jit(solution)/shard_map/ppermute | solution.py:503
  73.7 11.4 %collective-permute-start.17 = (f32[64,1024]{1,0:T(8,128)S(1)}, f32[64,1024]{1,0:T(8,128)S(1)}, u32[]{:S(2)}, u32[]{:S(2)}) collective-permute-start(f32[64,1024]{1,0:T(8,128)S(1)} %get-tuple-element.103), channel_id=1, source_target_pairs={{0,8},{1,9},{2,10},{3,11},{4,12},{5,13},{6,14},{7,15},{8,0},{9,1},... | collective-permute-start | bytes 786440 | tf_op jit(solution)/shard_map/ppermute | solution.py:480
  74.9 10.2 %collective-permute-start.18 = (f32[64,1024]{1,0:T(8,128)S(1)}, f32[64,1024]{1,0:T(8,128)S(1)}, u32[]{:S(2)}, u32[]{:S(2)}) collective-permute-start(f32[64,1024]{1,0:T(8,128)S(1)} %get-tuple-element.104), channel_id=1, source_target_pairs={{0,1},{1,0},{2,3},{3,2},{4,5},{5,4},{6,7},{7,6},{8,16},{9,17},{10,... | collective-permute-start | bytes 786440 | tf_op jit(solution)/shard_map/ppermute | solution.py:480
  75.3 4.5 %collective-permute-start.26 = (f32[8,128]{1,0:T(8,128)S(1)}, f32[8,128]{1,0:T(8,128)S(1)}, u32[]{:S(2)}, u32[]{:S(2)}) collective-permute-start(f32[8,128]{1,0:T(8,128)S(1)} %add.53), channel_id=1, source_target_pairs={{0,25},{1,24},{2,27},{3,26},{4,29},{5,28},{6,31},{7,30},{8,17},{9,... | collective-permute-start | bytes 12296 | tf_op jit(solution)/shard_map/ppermute | solution.py:503
  79.8 5.2 %collective-permute-start.27 = (f32[8,128]{1,0:T(8,128)S(1)}, f32[8,128]{1,0:T(8,128)S(1)}, u32[]{:S(2)}, u32[]{:S(2)}) collective-permute-start(f32[8,128]{1,0:T(8,128)S(1)} %add.54), channel_id=1, source_target_pairs={{0,9},{1,8},{2,11},{3,10},{4,13},{5,12},{6,15},{7,14},{8,1},{9,0},... | collective-permute-start | bytes 12296 | tf_op jit(solution)/shard_map/ppermute | solution.py:503
  87.0 5.5 %collective-permute-start.19 = (f32[256,128]{1,0:T(8,128)S(1)}, f32[256,128]{1,0:T(8,128)S(1)}, u32[]{:S(2)}, u32[]{:S(2)}) collective-permute-start(f32[256,128]{1,0:T(8,128)S(1)} %get-tuple-element.113), channel_id=1, source_target_pairs={{0,1},{1,0},{2,3},{3,2},{4,5},{5,4},{6,7},{7,6},{8,9},{9,8},{10,11... | collective-permute-start | bytes 393224 | tf_op jit(solution)/shard_map/ppermute | solution.py:480
  88.0 4.7 %collective-permute-start.20 = (f32[256,128]{1,0:T(8,128)S(1)}, f32[256,128]{1,0:T(8,128)S(1)}, u32[]{:S(2)}, u32[]{:S(2)}) collective-permute-start(f32[256,128]{1,0:T(8,128)S(1)} %get-tuple-element.114), channel_id=1, source_target_pairs={{0,8},{1,2},{2,1},{3,4},{4,3},{5,6},{6,5},{7,15},{8,0},{9,10},{10,... | collective-permute-start | bytes 393224 | tf_op jit(solution)/shard_map/ppermute | solution.py:480
  (5 other events, 28.7 us)
